TPU v7x, 256 devices: a whole 4x4x8 slice. The times are simulated.
256 devices in a mesh: grp: 8 (over x_lo, y), smp: 32 (over x_hi, z, core).
Axes of the slice: x: 4 (x_hi: 2, x_lo: 2; x = x_hi * 2 + x_lo), y: 4, z: 8, core: 2. Of those that a mesh axis runs over, the one named last changes fastest.
Arguments:
- spins_packed: int32 [32, 32768], P(None, 'smp'), may hold values from -2147483648 to 2147483646
- weight: bfloat16 [1024, 8192], P(None, 'grp'), may hold values from -0.1875 to 0.1875
- hidden_bias: float32 [8192], P('grp'), may hold values from -1.5 to 1.5
- force_w: float32 [1024, 8192], P('smp', 'grp'), may hold values from -6 to 6
- force_b: float32 [8192], P('grp'), may hold values from -6 to 6
Outputs:
- update_w: float32 [1024, 8192], P('smp', 'grp')
- update_b: float32 [8192], P('grp')
All inputs are finite; a program needn't handle non-finite values.
Results may differ from a plain program's by a relative error of at most 0.0003.
Values sent between devices are 32-bit elements; how exact they have to be, the bound alone decides.
No kernel may reach another device: no remote copies, remote signals or barrier semaphores. Data moves between devices by JAX's collectives and lax.ppermute only.
A program may use at most 64 MiB of HBM per device.

v0:
```python
import functools

import jax
import jax.numpy as jnp
from jax import lax
from jax.sharding import Mesh
from jax.sharding import PartitionSpec as P

ITERS = 2
GRP = ("grp_0", "grp_1")
SMP = ("smp_0", "smp_1", "smp_2")
GRP_SMP = ("grp_0", "grp_1", "smp_0", "smp_1", "smp_2")


diag_shift = 0.01


def one_axis_at_a_time(value, axes):
    return functools.reduce(lax.psum, axes, value)


def joined_along(tiles, dim):
    shape = list(tiles.shape[1:])
    shape[dim] *= tiles.shape[0]
    return jnp.moveaxis(tiles, 0, dim).reshape(shape)


def all_blocks(value, axes, order):
    tiles = value
    for k in order:
        tiles = lax.all_gather(tiles, axes[k])
    done = order[::-1]
    back = [done.index(k) for k in range(len(axes))]
    tiles = tiles.transpose(*back, *range(len(axes), tiles.ndim))
    return tiles.reshape(-1, *value.shape)


def gather_axes(value, axes, order, dim):
    return joined_along(all_blocks(value, axes, order), dim)


def sent_to_all(value, axis):
    size = lax.axis_size(axis)
    return lax.all_to_all(
        jnp.broadcast_to(value[None], (size, *value.shape)), axis, 0, 0, tiled=True
    )


def over_copies(value, axis):
    return sent_to_all(value, axis).sum(axis=0)


def unpack(packed):
    shifts = jnp.arange(32, dtype=jnp.int32)
    bit_values = jnp.bitwise_and(jnp.right_shift(packed[:, None, :], shifts[None, :, None]), 1)
    signs = 2 * bit_values - 1
    return signs.reshape(packed.shape[0] * 32, packed.shape[1]).astype(jnp.bfloat16)


def body(spins_packed, weight, hidden_bias, force_w, force_b):
    group_size = lax.axis_size(GRP)
    shard_size = lax.axis_size(SMP)
    spins = unpack(spins_packed)
    sample_count = spins.shape[1] * shard_size
    pre_activation = jnp.einsum("it,ih->th", spins, weight, preferred_element_type=jnp.float32)
    hidden = jnp.tanh(pre_activation + hidden_bias)

    def vector_dot(first_w, first_b, second_w, second_b):
        local_sum = jnp.sum(first_w * second_w) + jnp.sum(first_b * second_b) / shard_size
        return one_axis_at_a_time(local_sum, GRP_SMP)

    solution_w = jnp.zeros_like(force_w)
    solution_b = jnp.zeros_like(force_b)
    residual_w, residual_b = (force_w, force_b)
    direction_w, direction_b = (force_w, force_b)
    norm_now = vector_dot(residual_w, residual_b, residual_w, residual_b)
    for iteration in range(ITERS):
        final_turn = iteration + 1 == ITERS
        projected = jnp.einsum(
            "it,ih->th",
            spins,
            gather_axes(direction_w, SMP, (0, 1, 2), 0),
            precision=lax.Precision.HIGHEST,
            preferred_element_type=jnp.float32,
        )
        partial_value = jnp.sum(hidden * (projected + direction_b), axis=1)
        sample_values = over_copies(partial_value, GRP)
        mean_value = over_copies(jnp.sum(sample_values), SMP) / sample_count
        centred = sample_values - mean_value
        local_sum = jnp.sum(centred * centred) / (sample_count * group_size)
        local_sum = local_sum + diag_shift * (
            jnp.sum(direction_w * direction_w) + jnp.sum(direction_b * direction_b) / shard_size
        )
        curvature = one_axis_at_a_time(local_sum, GRP_SMP)
        if not final_turn:
            scaled = centred / sample_count
            weighted = scaled[:, None] * hidden
            image_w = (
                lax.psum_scatter(
                    jnp.einsum(
                        "it,th->ih",
                        spins,
                        weighted,
                        precision=lax.Precision.HIGHEST,
                        preferred_element_type=jnp.float32,
                    ),
                    SMP,
                    scatter_dimension=0,
                    tiled=True,
                )
                + diag_shift * direction_w
            )
            bias_term = jnp.dot(
                scaled, hidden, precision=lax.Precision.HIGHEST, preferred_element_type=jnp.float32
            )
            image_b = over_copies(bias_term, SMP) + diag_shift * direction_b
            image_w, image_b = (image_w, image_b)
        step_size = norm_now / curvature
        solution_w = solution_w + step_size * direction_w
        solution_b = solution_b + step_size * direction_b
        if not final_turn:
            residual_w = residual_w - step_size * image_w
            residual_b = residual_b - step_size * image_b
            norm_next = vector_dot(residual_w, residual_b, residual_w, residual_b)
            direction_w = residual_w + norm_next / norm_now * direction_w
            direction_b = residual_b + norm_next / norm_now * direction_b
            norm_now = norm_next
    return (solution_w, solution_b)


def solution(mesh):
    torus = Mesh(mesh.devices.reshape(2, 4, 2, 8, 2), ("grp_0", "grp_1", "smp_0", "smp_1", "smp_2"))
    in_specs = (P(None, SMP), P(None, GRP), P(GRP), P(SMP, GRP), P(GRP))
    out_specs = (P(SMP, GRP), P(GRP))
    return jax.shard_map(body, mesh=torus, in_specs=in_specs, out_specs=out_specs, check_vma=False)
```

profile of v0, /device:TPU:1, one launch (start us, length us, event | category | flops | bytes accessed | tf_op | source)
XLA Modules:
  0.0 466.7 jit_solution(8668620236048288955)
XLA Ops:
  7.2 8.6 %all-gather = f32[64,1024]{1,0:T(8,128)} all-gather(f32[32,1024]{1,0:T(8,128)} %param.8), channel_id=2, replica_groups=mesh['grp_0'=2,'grp_1'=4,'smp_0'=2,'smp_1'=8,'smp_2'=2] {'smp_0'}, dimensions={0}, use_global_device_ids=true | all-gather | bytes 393216 | tf_op jit(solution)/shard_map/all_gather | solution.py:31
  15.9 39.8 %all-gather.11.cloned.1.call-done = f32[16,32,1024]{2,1,0:T(8,128)} async-done(((f32[2,32,1024]{2,1,0:T(8,128)}), f32[16,32,1024]{2,1,0:T(8,128)}) %all-gather.11.cloned.1.call-update) | async-done | bytes 2097168 | tf_op jit(solution)/shard_map/all_gather | solution.py:31
  55.9 1.7 fusion.3
  57.6 2.3 add_convert_fusion
  60.0 4.3 fusion.12
  64.3 15.7 %all-gather.13.cloned.1.call-done = f32[16,2,32,1024]{3,2,1,0:T(8,128)} async-done(((f32[8,2,32,1024]{3,2,1,0:T(8,128)}), f32[16,2,32,1024]{3,2,1,0:T(8,128)}) %all-gather.13.cloned.1.call-update) | async-done | bytes 4194320 | tf_op jit(solution)/shard_map/all_gather | solution.py:31
  80.0 2.7 copy.13
  82.7 0.8 copy-done.1
  83.5 0.7 copy-done.4
  84.2 8.1 %multiply_reduce_fusion.1 = f32[1024]{0:T(1024)S(1)} fusion(f32[1024,1024]{0,1:T(8,128)S(1)} %copy-done.1, f32[1024]{0:T(1024)S(1)} %copy-done.8, f32[1024]{0:T(1024)S(1)} %copy-done.9, bf16[1024,1024]{1,0:T(8,128)(2,1)S(1)} %bitcast.37, f32[1024,1024]{1,0:T(8,128)S(1)} %bitcast.36), kind=kOutput, calls=%fused_computation.8 | convolution fusion | flops 12889095168 | bytes 10498048 | tf_op jit(solution)/shard_map/it,ih->th/dot_general | solution.py:79
  92.3 9.6 %all_to_all.30 = f32[8,1,1024]{2,1,0:T(1,128)S(1)} all-to-all(f32[8,1,1024]{2,1,0:T(1,128)S(1)} %broadcast_in_dim.10), channel_id=1, replica_groups=mesh['grp_0'=2,'grp_1'=4,'smp_0'=2,'smp_1'=8,'smp_2'=2] {'grp_0','grp_1'}, dimensions={0} | all-to-all | bytes 65536 | tf_op jit(solution)/shard_map/all_to_all | solution.py:44
  103.2 20.1 %all_to_all.31 = f32[32,1,1]{2,1,0:T(1,128)S(1)} all-to-all(f32[32,1,1]{2,1,0:T(1,128)S(1)} %broadcast_in_dim.11), channel_id=1, replica_groups=mesh['grp_0'=2,'grp_1'=4,'smp_0'=2,'smp_1'=8,'smp_2'=2] {'smp_0','smp_1'..., dimensions={0} | all-to-all | bytes 256 | tf_op jit(solution)/shard_map/all_to_all | solution.py:44
  125.2 11.3 %fusion.4 = f32[1024,1024]{1,0:T(8,128)} fusion(bf16[1024,1024]{1,0:T(8,128)(2,1)} %copy-done.6, f32[1024,1024]{0,1:T(8,128)} %fusion.12, f32[1024]{0:T(1024)S(1)} %get-tuple-element.21, f32[1024]{0:T(1024)S(1)} %copy-done.9), kind=kOutput, calls=%fused_computation.6 | convolution fusion | flops 12886999040 | bytes 10493952 | tf_op jit(solution)/shard_map/it,th->ih/dot_general | solution.py:100
  136.5 5.9 %fusion.6 = f32[1,1024]{1,0:T(1,128)S(1)} fusion(f32[1024,1]{0,1:T(1,128)S(1)} %bitcast.44, f32[1024,1024]{0,1:T(8,128)} %fusion.12, f32[1024]{0:T(1024)S(1)} %copy-done.9), kind=kOutput, calls=%fused_computation.11 | convolution fusion | flops 13631488 | bytes 4206592 | tf_op jit(solution)/shard_map/dot_general | solution.py:113
  142.5 0.7 broadcast_in_dim.12
  143.2 4.3 all-to-all-start.2
  147.6 0.7 multiply_reduce_fusion.9
  149.0 0.7 multiply_reduce_fusion.4
  151.0 4.6 all-reduce.4
  155.7 7.6 %all-reduce.1 = (f32[]{:T(128)}, f32[]{:T(128)}) all-reduce(f32[]{:T(128)} %get-tuple-element.14, f32[]{:T(128)} %get-tuple-element.15), channel_id=1, replica_groups=mesh['grp_0'=2,'grp_1'=4,'smp_0'=2,'smp_1'=8,'smp_2'=2] {'grp_1'}, use_global_device_ids=true, to_apply=%region_3.0 | all-reduce | flops 2 | bytes 16 | tf_op jit(solution)/shard_map/psum | solution.py:19
  163.3 5.9 %all-reduce.3 = (f32[]{:T(128)}, f32[]{:T(128)}) all-reduce(f32[]{:T(128)} %get-tuple-element.8, f32[]{:T(128)} %get-tuple-element.9), channel_id=1, replica_groups=mesh['grp_0'=2,'grp_1'=4,'smp_0'=2,'smp_1'=8,'smp_2'=2] {'smp_0'}, use_global_device_ids=true, to_apply=%region_4.0 | all-reduce | flops 2 | bytes 16 | tf_op jit(solution)/shard_map/psum | solution.py:19
  169.2 14.0 %all-reduce = (f32[]{:T(128)}, f32[]{:T(128)}) all-reduce(f32[]{:T(128)} %get-tuple-element.12, f32[]{:T(128)} %get-tuple-element.13), channel_id=1, replica_groups=mesh['grp_0'=2,'grp_1'=4,'smp_0'=2,'smp_1'=8,'smp_2'=2] {'smp_1'}, use_global_device_ids=true, to_apply=%region_5.0 | all-reduce | flops 2 | bytes 16 | tf_op jit(solution)/shard_map/psum | solution.py:19
  183.2 10.8 %all-reduce.2 = (f32[]{:T(128)}, f32[]{:T(128)}) all-reduce(f32[]{:T(128)} %get-tuple-element.6, f32[]{:T(128)} %get-tuple-element.7), channel_id=1, replica_groups=mesh['grp_0'=2,'grp_1'=4,'smp_0'=2,'smp_1'=8,'smp_2'=2] {'smp_2'}, use_global_device_ids=true, to_apply=%region_6.0 | all-reduce | flops 2 | bytes 16 | tf_op jit(solution)/shard_map/psum | solution.py:19
  196.7 55.0 %reduce-scatter.2.cloned.1.call-done = f32[32,1024]{1,0:T(8,128)} async-done(((f32[1024,1024]{1,0:T(8,128)}), f32[32,1024]{1,0:T(8,128)}) %reduce-scatter.2.cloned.1.call-update) | async-done | bytes 131088 | tf_op jit(solution)/shard_map/reduce_scatter | solution.py:99
  251.7 1.5 multiply_reduce_fusion.3
  253.9 4.3 psum.150
  258.2 9.1 %psum.151 = f32[]{:T(128)} all-reduce(f32[]{:T(128)} %psum.150), channel_id=1, replica_groups=mesh['grp_0'=2,'grp_1'=4,'smp_0'=2,'smp_1'=8,'smp_2'=2] {'grp_1'}, use_global_device_ids=true, to_apply=%region_22.0 | all-reduce | flops 1 | bytes 8 | tf_op jit(solution)/shard_map/psum | solution.py:19
  267.3 5.9 %psum.152 = f32[]{:T(128)} all-reduce(f32[]{:T(128)} %psum.151), channel_id=1, replica_groups=mesh['grp_0'=2,'grp_1'=4,'smp_0'=2,'smp_1'=8,'smp_2'=2] {'smp_0'}, use_global_device_ids=true, to_apply=%region_23.0 | all-reduce | flops 1 | bytes 8 | tf_op jit(solution)/shard_map/psum | solution.py:19
  273.2 13.3 %psum.153 = f32[]{:T(128)} all-reduce(f32[]{:T(128)} %psum.152), channel_id=1, replica_groups=mesh['grp_0'=2,'grp_1'=4,'smp_0'=2,'smp_1'=8,'smp_2'=2] {'smp_1'}, use_global_device_ids=true, to_apply=%region_24.0 | all-reduce | flops 1 | bytes 8 | tf_op jit(solution)/shard_map/psum | solution.py:19
  286.5 16.3 %psum.154 = f32[]{:T(128)} all-reduce(f32[]{:T(128)} %psum.153), channel_id=1, replica_groups=mesh['grp_0'=2,'grp_1'=4,'smp_0'=2,'smp_1'=8,'smp_2'=2] {'smp_2'}, use_global_device_ids=true, to_apply=%region_25.0 | all-reduce | flops 1 | bytes 8 | tf_op jit(solution)/shard_map/psum | solution.py:19
  304.1 1.6 multiply_reduce_fusion.2
  305.6 7.0 %all-gather.3 = f32[64,1024]{1,0:T(8,128)} all-gather(f32[32,1024]{1,0:T(8,128)S(1)} %get-tuple-element.19), channel_id=5, replica_groups=mesh['grp_0'=2,'grp_1'=4,'smp_0'=2,'smp_1'=8,'smp_2'=2] {'smp_0'}, dimensions={0}, use_global_device_ids=true | all-gather | bytes 393216 | tf_op jit(solution)/shard_map/all_gather | solution.py:31
  312.9 33.0 %all-gather.15.cloned.1.call-done = f32[16,32,1024]{2,1,0:T(8,128)} async-done(((f32[2,32,1024]{2,1,0:T(8,128)}), f32[16,32,1024]{2,1,0:T(8,128)}) %all-gather.15.cloned.1.call-update) | async-done | bytes 2097168 | tf_op jit(solution)/shard_map/all_gather | solution.py:31
  346.6 23.5 %all-gather.17.cloned.1.call-done = f32[16,2,32,1024]{3,2,1,0:T(8,128)} async-done(((f32[8,2,32,1024]{3,2,1,0:T(8,128)}), f32[16,2,32,1024]{3,2,1,0:T(8,128)}) %all-gather.17.cloned.1.call-update) | async-done | bytes 4194320 | tf_op jit(solution)/shard_map/all_gather | solution.py:31
  370.0 2.7 copy.18
  372.7 0.8 copy-done.2
  373.5 0.7 copy-done.5
  374.2 8.1 %multiply_reduce_fusion = f32[1024]{0:T(1024)S(1)} fusion(f32[1024,1024]{0,1:T(8,128)S(1)} %copy-done.2, f32[1024]{0:T(1024)S(1)} %get-tuple-element.17, f32[1024]{0:T(1024)S(1)} %copy-done.9, bf16[1024,1024]{1,0:T(8,128)(2,1)S(1)} %bitcast.38, f32[1024,1024]{1,0:T(8,128)S(1)} %bitcast.35), kind=kOutput, calls=%fused_computation.5 | convolution fusion | flops 12889095168 | bytes 10498048 | tf_op jit(solution)/shard_map/it,ih->th/dot_general | solution.py:79
  382.3 9.6 %all_to_all.32 = f32[8,1,1024]{2,1,0:T(1,128)S(1)} all-to-all(f32[8,1,1024]{2,1,0:T(1,128)S(1)} %broadcast_in_dim.13), channel_id=1, replica_groups=mesh['grp_0'=2,'grp_1'=4,'smp_0'=2,'smp_1'=8,'smp_2'=2] {'grp_0','grp_1'}, dimensions={0} | all-to-all | bytes 65536 | tf_op jit(solution)/shard_map/all_to_all | solution.py:44
  391.9 0.7 fusion.10
  392.6 1.3 broadcast_in_dim.14
  393.9 10.9 %all-to-all-start.4 = ((f32[32,1,1]{2,1,0:T(1,128)}), f32[32,1,1]{2,1,0:T(1,128)S(1)}, u32[]{:S(2)}, u32[]{:S(2)}) async-start(f32[32,1,1]{2,1,0:T(1,128)} %broadcast_in_dim.14), calls=%async_computation.5 | async-start | bytes 32768 | tf_op jit(solution)/shard_map/all_to_all | solution.py:44
  406.2 8.0 %all-to-all-done.4 = f32[32,1,1]{2,1,0:T(1,128)S(1)} async-done(((f32[32,1,1]{2,1,0:T(1,128)}), f32[32,1,1]{2,1,0:T(1,128)S(1)}, u32[]{:S(2)}, u32[]{:S(2)}) %all-to-all-start.4) | async-done | bytes 160 | tf_op jit(solution)/shard_map/all_to_all | solution.py:44
  416.7 4.3 psum.155
  421.0 7.5 %psum.156 = f32[]{:T(128)} all-reduce(f32[]{:T(128)} %psum.155), channel_id=1, replica_groups=mesh['grp_0'=2,'grp_1'=4,'smp_0'=2,'smp_1'=8,'smp_2'=2] {'grp_1'}, use_global_device_ids=true, to_apply=%region_34.0 | all-reduce | flops 1 | bytes 8 | tf_op jit(solution)/shard_map/psum | solution.py:19
  428.5 5.9 %psum.157 = f32[]{:T(128)} all-reduce(f32[]{:T(128)} %psum.156), channel_id=1, replica_groups=mesh['grp_0'=2,'grp_1'=4,'smp_0'=2,'smp_1'=8,'smp_2'=2] {'smp_0'}, use_global_device_ids=true, to_apply=%region_35.0 | all-reduce | flops 1 | bytes 8 | tf_op jit(solution)/shard_map/psum | solution.py:19
  434.3 11.7 %psum.158 = f32[]{:T(128)} all-reduce(f32[]{:T(128)} %psum.157), channel_id=1, replica_groups=mesh['grp_0'=2,'grp_1'=4,'smp_0'=2,'smp_1'=8,'smp_2'=2] {'smp_1'}, use_global_device_ids=true, to_apply=%region_36.0 | all-reduce | flops 1 | bytes 8 | tf_op jit(solution)/shard_map/psum | solution.py:19
  446.0 11.6 %psum.159 = f32[]{:T(128)} all-reduce(f32[]{:T(128)} %psum.158), channel_id=1, replica_groups=mesh['grp_0'=2,'grp_1'=4,'smp_0'=2,'smp_1'=8,'smp_2'=2] {'smp_2'}, use_global_device_ids=true, to_apply=%region_37.0 | all-reduce | flops 1 | bytes 8 | tf_op jit(solution)/shard_map/psum | solution.py:19
  (42 shorter events, 7.1 us)
Async XLA Ops:
  7.2 52.8 %copy-start = (bf16[1024,1024]{1,0:T(8,128)(2,1)S(1)}, bf16[1024,1024]{1,0:T(8,128)(2,1)}, u32[]{:S(2)}) copy-start(bf16[1024,1024]{1,0:T(8,128)(2,1)} %param.6) | copy-start | bytes 6291460
  7.2 50.4 %copy-start.7 = (s32[32,1024]{1,0:T(8,128)S(1)}, s32[32,1024]{1,0:T(8,128)}, u32[]{:S(2)}) copy-start(s32[32,1024]{1,0:T(8,128)} %param.5) | copy-start | bytes 393220
  7.2 48.5 %all-gather.11.cloned.1.call-start = ((), (), s32[]{:S(2)}) async-start(), calls=%async_computation.7 | async-start | bytes 2359296 | tf_op jit(solution)/shard_map/all_gather | solution.py:31
  15.8 64.2 %all-gather.13.cloned.1.call-start = ((), (), s32[]{:S(2)}) async-start(), calls=%async_computation.8 | async-start | bytes 6291456 | tf_op jit(solution)/shard_map/all_gather | solution.py:31
  55.8 196.0 %reduce-scatter.2.cloned.1.call-start = ((), (), s32[]{:S(2)}) async-start(), calls=%async_computation.6 | async-start | bytes 4325376 | tf_op jit(solution)/shard_map/reduce_scatter | solution.py:99
  57.6 2.4 copy-start.6
  80.0 3.4 copy-start.1
  80.0 4.1 copy-start.4
  80.0 4.1 copy-start.8
  80.0 4.1 copy-start.9
  136.5 12.5 %copy-start.3 = (f32[32,1024]{1,0:T(8,128)S(1)}, f32[32,1024]{1,0:T(8,128)}, u32[]{:S(2)}) copy-start(f32[32,1024]{1,0:T(8,128)} %param.8) | copy-start | bytes 393220
  143.2 52.1 %all-to-all-start.2 = ((f32[32,1,1024]{2,1,0:T(1,128)}), f32[32,1,1024]{2,1,0:T(1,128)S(1)}, u32[]{:S(2)}, u32[]{:S(2)}) async-start(f32[32,1,1024]{2,1,0:T(1,128)} %broadcast_in_dim.12), calls=%async_computation.3 | async-start | bytes 262144 | tf_op jit(solution)/shard_map/all_to_all | solution.py:44
  147.5 198.4 %all-gather.15.cloned.1.call-start = ((), (), s32[]{:S(2)}) async-start(), calls=%async_computation.9 | async-start | bytes 2359296 | tf_op jit(solution)/shard_map/all_gather | solution.py:31
  312.6 57.4 %all-gather.17.cloned.1.call-start = ((), (), s32[]{:S(2)}) async-start(), calls=%async_computation.10 | async-start | bytes 6291456 | tf_op jit(solution)/shard_map/all_gather | solution.py:31
  370.0 3.4 copy-start.2
  370.0 4.1 copy-start.5
  393.9 20.2 %all-to-all-start.4 = ((f32[32,1,1]{2,1,0:T(1,128)}), f32[32,1,1]{2,1,0:T(1,128)S(1)}, u32[]{:S(2)}, u32[]{:S(2)}) async-start(f32[32,1,1]{2,1,0:T(1,128)} %broadcast_in_dim.14), calls=%async_computation.5 | async-start | bytes 32768 | tf_op jit(solution)/shard_map/all_to_all | solution.py:44
Sparse Core Ops, SparseCore 0:
  16.0 39.7 all-gather.10
  57.5 22.4 all-gather.12
  136.6 115.0 reduce-scatter.1
  312.8 33.0 all-gather.14
  347.5 22.4 all-gather.16
where the time goes:
time: 468 us; the launch traced here: 467 us
  blocking collectives  187 us (40%)
  waiting for transfers between devices  175 us (37%)
  matrix products  37.8 us (8%)
  between operations  24.5 us (5%)
  starting transfers between devices  15.7 us (3%)
  other arithmetic  15.1 us (3%)
  local copies, waits for them, and re-layouts  11.1 us (2%)
    psum x15, blocking collectives, one_axis_at_a_time(): return functools.reduce(lax.psum, axes, value)  133 us
    all_gather x4, waiting for transfers between devices, all_blocks(): tiles = lax.all_gather(tiles, axes[k])  112 us
    reduce_scatter x1, waiting for transfers between devices, body(): lax.psum_scatter(jnp.einsum('it,th->ih', spins, weighted, precision=lax.P...  55 us
    all_to_all x3, blocking collectives, sent_to_all(): lax.all_to_all(jnp.broadcast_to(value[None], (size, *value.shape)), axis,...  39.2 us
    dot_general x2, matrix products, body(): jnp.einsum('it,ih->th', spins, gather_axes(direction_w, SMP, (0, 1, 2), 0...  16.2 us
    all_gather x2, blocking collectives, all_blocks(): tiles = lax.all_gather(tiles, axes[k])  15.5 us
    all_to_all x2, starting transfers between devices, sent_to_all(): lax.all_to_all(jnp.broadcast_to(value[None], (size, *value.shape)), axis,...  15.3 us
    dot_general x1, matrix products, body(): jnp.einsum('it,th->ih', spins, weighted, precision=lax.Precision.HIGHEST,...  11.3 us
  transfers between devices with their start and end apart: 7, of which 6 were waited for; matrix products, arithmetic and copies ran while one was open for 4% of the time, Pallas kernels for 0%

commit v1 on v0

v1 whole, which is shorter than its diff:
```python
import functools

import jax
import jax.numpy as jnp
from jax import lax
from jax.experimental import pallas as pl
from jax.experimental.pallas import tpu as pltpu
from jax.sharding import Mesh
from jax.sharding import PartitionSpec as P

GRP = ("xl", "y")
SMP = ("xh", "zh", "zl", "c")
SUM = ("xl", "y", "zh")
SWAP = [(0, 1), (1, 0)]
LAM = 0.01
ROWS = 32
NB = 8
F32, BF16 = jnp.float32, jnp.bfloat16


def swap(x, axis):
    return lax.ppermute(x, axis, SWAP)


def split_terms(x):
    hi = x.astype(BF16)
    return hi, (x - hi.astype(F32)).astype(BF16)


def to_all(x, axes, size):
    return lax.all_to_all(jnp.broadcast_to(x[None], (size, *x.shape)), axes, 0, 0, tiled=True)


def params(limit=56 << 20):
    return pltpu.CompilerParams(dimension_semantics=("arbitrary",), vmem_limit_bytes=limit)


def unpack_tile(words_ref, packed_ref, out_ref):
    bits = lax.broadcasted_iota(jnp.int32, (ROWS, packed_ref.shape[1]), 0)
    for q in range(32):
        word = packed_ref[pl.ds(words_ref[q], 1), :]
        up = jnp.left_shift(jnp.broadcast_to(word, bits.shape), 31 - bits) < 0
        out_ref[q * ROWS : (q + 1) * ROWS, :] = jnp.where(up, 1.0, -1.0).astype(BF16)


def first_kernel(words_ref, packed_ref, wt_ref, f_ref, hb_ref, fb_ref, s_ref, h_ref, p_ref, n_ref, lhs):
    units = wt_ref.shape[0]

    @pl.when(pl.program_id(0) == 0)
    def _():
        lhs[:units, :] = wt_ref[...]
        total = jnp.zeros((units, 128), F32)
        for b in range(NB):
            block = f_ref[b]
            hi, lo = split_terms(block)
            lhs[units : 2 * units, b * 128 : (b + 1) * 128] = hi
            lhs[2 * units :, b * 128 : (b + 1) * 128] = lo
            total = total + block * block
        fb = fb_ref[...]
        n_ref[...] = jnp.full(n_ref.shape, jnp.sum(total) + jnp.sum(fb * fb), F32)

    unpack_tile(words_ref, packed_ref, s_ref)
    out = jnp.dot(lhs[...], s_ref[...], preferred_element_type=F32)
    hidden = jnp.tanh(out[:units] + hb_ref[...])
    h_ref[...] = hidden
    proj = out[units : 2 * units] + out[2 * units :] + fb_ref[...]
    p_ref[...] = jnp.sum(hidden * proj, axis=0, keepdims=True)


def first_pass(words, packed, wt, f, hb, fb):
    parts, _, tile = packed.shape
    units = wt.shape[0]
    n = parts * tile
    full = lambda shape: pl.BlockSpec(shape, lambda t: (0,) * len(shape))
    return pl.pallas_call(
        first_kernel,
        grid=(parts,),
        in_specs=[
            pl.BlockSpec(memory_space=pltpu.SMEM),
            pl.BlockSpec((None, ROWS, tile), lambda t: (t, 0, 0)),
            full(wt.shape),
            full(f.shape),
            full(hb.shape),
            full(fb.shape),
        ],
        out_specs=[
            pl.BlockSpec((NB * 128, tile), lambda t: (0, t)),
            pl.BlockSpec((units, tile), lambda t: (0, t)),
            pl.BlockSpec((1, tile), lambda t: (0, t)),
            full((1, 128)),
        ],
        out_shape=[
            jax.ShapeDtypeStruct((NB * 128, n), BF16),
            jax.ShapeDtypeStruct((units, n), F32),
            jax.ShapeDtypeStruct((1, n), F32),
            jax.ShapeDtypeStruct((1, 128), F32),
        ],
        scratch_shapes=[pltpu.VMEM((3 * units, NB * 128), BF16)],
        compiler_params=params(),
        name="first_pass",
    )(words, packed, wt, f, hb, fb)


def image_kernel(s_ref, h_ref, c_ref, keep_ref, send_ref, acc, bsum):
    units = h_ref.shape[0]
    step = pl.program_id(0)
    r = h_ref[...] * c_ref[...]
    hi, lo = split_terms(r)
    both = jnp.concatenate([hi, lo], axis=0)
    out = lax.dot_general(both, s_ref[...], (((1,), (1,)), ((), ())), preferred_element_type=F32)
    part = out[:units] + out[units:]
    lanes = r[:, :128]
    for k in range(1, r.shape[1] // 128):
        lanes = lanes + r[:, k * 128 : (k + 1) * 128]

    @pl.when(step == 0)
    def _():
        acc[...] = part
        bsum[...] = lanes

    @pl.when(step > 0)
    def _():
        acc[...] += part
        bsum[...] += lanes

    @pl.when(step == pl.num_programs(0) - 1)
    def _():
        half = NB // 2
        for b in range(half):
            keep_ref[b * units : (b + 1) * units, :] = acc[:, b * 128 : (b + 1) * 128]
            send_ref[b * units : (b + 1) * units, :] = acc[:, (b + half) * 128 : (b + half + 1) * 128]
        tail = pl.ds(half * units, 8)
        keep_ref[tail, :] = jnp.zeros((8, 128), F32)
        send_ref[tail, :] = jnp.zeros((8, 128), F32)
        for k in range(units // 128):
            row = jnp.sum(bsum[k * 128 : (k + 1) * 128, :].T, axis=0, keepdims=True)
            keep_ref[half * units + k : half * units + k + 1, :] = row
            send_ref[half * units + k : half * units + k + 1, :] = row


def image_pass(spins, hidden, c, tile=1024):
    units, n = hidden.shape
    rows = NB // 2 * units + 8
    full = lambda shape: pl.BlockSpec(shape, lambda t: (0,) * len(shape))
    return pl.pallas_call(
        image_kernel,
        grid=(n // tile,),
        in_specs=[
            pl.BlockSpec((NB * 128, tile), lambda t: (0, t)),
            pl.BlockSpec((units, tile), lambda t: (0, t)),
            pl.BlockSpec((1, tile), lambda t: (0, t)),
        ],
        out_specs=[full((rows, 128))] * 2,
        out_shape=[jax.ShapeDtypeStruct((rows, 128), F32)] * 2,
        scratch_shapes=[pltpu.VMEM((units, NB * 128), F32), pltpu.VMEM((units, 128), F32)],
        compiler_params=params(),
        name="image_pass",
    )(spins, hidden, c)


def second_kernel(step_ref, s_ref, h_ref, f_ref, g0_ref, g1_ref, fb_ref, gb_ref, p_ref, n_ref, lhs, rb):
    units = h_ref.shape[0]

    @pl.when(pl.program_id(0) == 0)
    def _():
        a = step_ref[0]
        rr = jnp.zeros((units, 128), F32)
        rf = jnp.zeros((units, 128), F32)
        for b in range(NB):
            f = f_ref[b]
            g_ref = g0_ref if b < NB // 2 else g1_ref
            row = (b % (NB // 2)) * units
            r = f - a * (g_ref[row : row + units, :] + LAM * f)
            hi, lo = split_terms(r)
            lhs[:units, b * 128 : (b + 1) * 128] = hi
            lhs[units:, b * 128 : (b + 1) * 128] = lo
            rr = rr + r * r
            rf = rf + r * f
        fb = fb_ref[...]
        r = fb - a * (gb_ref[...] + LAM * fb)
        rb[...] = r
        n_ref[...] = jnp.concatenate(
            [
                jnp.full((1, 128), jnp.sum(rr) + jnp.sum(r * r), F32),
                jnp.full((1, 128), jnp.sum(rf) + jnp.sum(r * fb), F32),
            ],
            axis=1,
        )

    out = jnp.dot(lhs[...], s_ref[...], preferred_element_type=F32)
    proj = out[:units] + out[units:] + rb[...]
    p_ref[...] = jnp.sum(h_ref[...] * proj, axis=0, keepdims=True)


def second_pass(step_size, spins, hidden, f, g0, g1, fb, gb, tile=1024):
    units, n = hidden.shape
    full = lambda shape: pl.BlockSpec(shape, lambda t: (0,) * len(shape))
    return pl.pallas_call(
        second_kernel,
        grid=(n // tile,),
        in_specs=[
            pl.BlockSpec(memory_space=pltpu.SMEM),
            pl.BlockSpec((NB * 128, tile), lambda t: (0, t)),
            pl.BlockSpec((units, tile), lambda t: (0, t)),
            full(f.shape),
            full(g0.shape),
            full(g1.shape),
            full(fb.shape),
            full(gb.shape),
        ],
        out_specs=[pl.BlockSpec((1, tile), lambda t: (0, t)), full((1, 256))],
        out_shape=[jax.ShapeDtypeStruct((1, n), F32), jax.ShapeDtypeStruct((1, 256), F32)],
        scratch_shapes=[pltpu.VMEM((2 * units, NB * 128), BF16), pltpu.VMEM((units, 1), F32)],
        compiler_params=params(),
        name="second_pass",
    )(step_size, spins, hidden, f, g0, g1, fb, gb)


def merged(mean, spread, count, axis):
    got = swap(jnp.stack([mean, spread]).reshape(1, 2), axis)
    delta = got[0, 0] - mean
    return 0.5 * (mean + got[0, 0]), spread + got[0, 1] + (0.5 * count) * delta * delta


def stats(values):
    count = values.size
    mean = jnp.sum(values) / count
    spread = jnp.sum((values - mean) ** 2)
    for axis in ("c", "zl", "xh"):
        mean, spread = merged(mean, spread, count, axis)
        count *= 2
    return mean, spread


def body(spins_packed, weight, hidden_bias, force_w, force_b):
    xh, zh, zl, c = (lax.axis_index(a) for a in SMP)
    parts = lax.axis_size("zh")
    summed = lax.axis_size(SUM)
    units = weight.shape[1] // parts
    samples = spins_packed.shape[1] * lax.axis_size(SMP)

    q = jnp.arange(32, dtype=jnp.int32)
    words = (((q >> 2) & 1) ^ xh) * 16 + (q & 3) * 4 + (((q >> 3) & 1) ^ zl) * 2 + ((q >> 4) ^ c)

    f_cols = force_w.reshape(ROWS, parts, units).transpose(1, 0, 2)
    f_rows = lax.all_to_all(f_cols, "zh", 0, 0, tiled=True).reshape(parts * ROWS, units)
    f = f_rows.T[None]
    for axis in ("xh", "zl", "c"):
        f = jnp.concatenate([f, swap(f, axis)], axis=0)

    packed = to_all(spins_packed, "zh", parts)

    w = lax.dynamic_slice_in_dim(weight, zh * units, units, 1).reshape(2, parts, 2, 2, ROWS, units)
    for dim, bit in ((0, xh), (2, zl), (3, c)):
        w = jnp.where(bit == 1, jnp.flip(w, dim), w)
    wt = w.transpose(3, 2, 0, 1, 4, 5).reshape(NB * 128, units).T
    hb = lax.dynamic_slice_in_dim(hidden_bias, zh * units, units, 0).reshape(units, 1)
    fb = lax.dynamic_slice_in_dim(force_b, zh * units, units, 0).reshape(units, 1)

    spins, hidden, partial, norm = first_pass(words, packed, wt, f, hb, fb)
    gathered = to_all(jnp.concatenate([partial, norm], axis=1), SUM, summed).sum(axis=0)
    n = partial.shape[1]
    values = gathered[:, :n]
    norm_now = gathered[0, n]
    mean, spread = stats(values)
    curvature = spread / samples + LAM * norm_now
    step0 = norm_now / curvature

    keep, send = image_pass(spins, hidden, (values - mean) / samples)
    g = keep + swap(send, "c")
    rows = 2 * units
    g = jnp.concatenate([g[:rows], g[2 * rows :]], axis=0) + swap(g[rows:], "zl")
    got = swap(g, "xh")
    g = g + jnp.concatenate([got[units:rows], got[:units], got[rows:]], axis=0)
    gb = g[rows : rows + units // 128].reshape(units)
    g_mine = g[:units].T.reshape(parts, ROWS, units)
    g_mine = jnp.concatenate([g_mine, jnp.broadcast_to(gb, (parts, 8, units))], axis=1)
    g = g[:rows]
    g = jnp.concatenate([g, swap(g, "zl")], axis=0)
    g1 = swap(g, "c")
    g_mine = lax.all_to_all(g_mine, "zh", 0, 0, tiled=True)
    gw = g_mine[:, :ROWS].transpose(1, 0, 2).reshape(ROWS, parts * units)
    gb_all = g_mine[:, ROWS].reshape(parts * units)

    partial, norms = second_pass(step0.reshape(1), spins, hidden, f, g, g1, fb, gb.reshape(units, 1))
    gathered = to_all(jnp.concatenate([partial, norms], axis=1), SUM, summed).sum(axis=0)
    norm_next = gathered[0, n]
    cross = gathered[0, n + 128]
    beta = norm_next / norm_now
    _, spread = stats(gathered[:, :n] + beta * values)
    length = norm_next + 2.0 * beta * cross + beta * beta * norm_now
    step1 = norm_next / (spread / samples + LAM * length)

    def update(f0, g0):
        r = f0 - step0 * (g0 + LAM * f0)
        return step0 * f0 + step1 * (r + beta * f0)

    return update(force_w, gw), update(force_b, gb_all)


def solution(mesh):
    torus = Mesh(mesh.devices.reshape(2, 4, 2, 4, 2, 2), ("xl", "y", "xh", "zh", "zl", "c"))
    in_specs = (P(None, SMP), P(None, GRP), P(GRP), P(SMP, GRP), P(GRP))
    out_specs = (P(SMP, GRP), P(GRP))
    return jax.shard_map(body, mesh=torus, in_specs=in_specs, out_specs=out_specs, check_vma=False)
```

time: 468 us -> 228 us (0.49)
  blocking collectives: 187 us -> 40.3 us
  waiting for transfers between devices: 175 us -> 58.4 us
  matrix products: 37.8 us -> 0 us
  Pallas kernels: 0 us -> 30.3 us
  starting transfers between devices: 15.7 us -> 44.3 us
  between operations: 24.5 us -> 19.3 us
  local copies, waits for them, and re-layouts: 11.1 us -> 16 us
    psum x15 -> x0, blocking collectives: 133 us -> none  [one_axis_at_a_time(): return functools.reduce(lax.psum, axes, value)]
    all_gather x4 -> x0, waiting for transfers between devices: 112 us -> none  [all_blocks(): tiles = lax.all_gather(tiles, axes[k])]
    reduce_scatter x1 -> x0, waiting for transfers between devices: 55 us -> none  [body(): lax.psum_scatter(jnp.einsum('it,th->ih', spins, weighted, precision=lax.P...]
    ppermute x0 -> x14, waiting for transfers between devices: none -> 41.6 us  [swap(): return lax.ppermute(x, axis, SWAP)]
    dot_general x5 -> x0, matrix products: 37.8 us -> none  [the longest x2 16.2 us: body(): jnp.einsum('it,ih->th', spins, gather_axes(direction_w, SMP, (0, 1, 2), 0...]
    pallas_call x0 -> x3, Pallas kernels: none -> 30.3 us  [the longest x1 11.2 us: first_pass(): pl.pallas_call(first_kernel, grid=(parts,), in_specs=[pl.BlockSpec(memory...]
    ppermute x0 -> x14, starting transfers between devices: none -> 27.9 us  [swap(): return lax.ppermute(x, axis, SWAP)]
    all_gather x2 -> x0, blocking collectives: 15.5 us -> none  [all_blocks(): tiles = lax.all_gather(tiles, axes[k])]
  transfers between devices with their start and end apart: 7 -> 17, of which waited for: 6 -> 12; matrix products, arithmetic and copies ran while one was open for 4% -> 6% of each run, Pallas kernels for 0% -> 4%
where the time goes in v1:
time: 228 us; the launch traced here: 226 us
  waiting for transfers between devices  58.4 us (26%)
  starting transfers between devices  44.3 us (19%)
  blocking collectives  40.3 us (18%)
  Pallas kernels  30.3 us (13%)
  between operations  19.3 us (8%)
  other arithmetic  17.7 us (8%)
  local copies, waits for them, and re-layouts  16 us (7%)
    ppermute x14, waiting for transfers between devices, swap(): return lax.ppermute(x, axis, SWAP)  41.6 us
    ppermute x14, starting transfers between devices, swap(): return lax.ppermute(x, axis, SWAP)  27.9 us
    all_to_all x1, blocking collectives, to_all(): lax.all_to_all(jnp.broadcast_to(x[None], (size, *x.shape)), axes, 0, 0, t...  24.2 us
    all_to_all x2, waiting for transfers between devices, to_all(): lax.all_to_all(jnp.broadcast_to(x[None], (size, *x.shape)), axes, 0, 0, t...  16.9 us
    all_to_all x1, blocking collectives, body(): lax.all_to_all(f_cols, 'zh', 0, 0, tiled=True).reshape(parts * ROWS, units)  16 us
    all_to_all x2, starting transfers between devices, to_all(): lax.all_to_all(jnp.broadcast_to(x[None], (size, *x.shape)), axes, 0, 0, t...  13.1 us
    pallas_call x1, Pallas kernels, first_pass(): pl.pallas_call(first_kernel, grid=(parts,), in_specs=[pl.BlockSpec(memory...  11.2 us
    pallas_call x1, Pallas kernels, second_pass(): pl.pallas_call(second_kernel, grid=(n // tile,), in_specs=[pl.BlockSpec(m...  9.85 us
  transfers between devices with their start and end apart: 17, of which 12 were waited for; matrix products, arithmetic and copies ran while one was open for 6% of the time, Pallas kernels for 4%

profile of v1, /device:TPU:1, one launch (start us, length us, event | category | flops | bytes accessed | tf_op | source)
XLA Modules:
  0.0 226.2 jit_solution(8597595053992498264)
XLA Ops:
  0.7 1.1 reshape.63
  1.8 16.0 %all_to_all.25 = f32[4,32,256]{2,1,0:T(8,128)S(1)} all-to-all(f32[4,32,256]{2,1,0:T(8,128)S(1)} %copy.49), channel_id=1, replica_groups=mesh['xl'=2,'y'=4,'xh'=2,'zh'=4,'zl'=2,'c'=2] {'zh'}, dimensions={0} | all-to-all | bytes 262144 | tf_op jit(solution)/shard_map/all_to_all | solution.py:246
  17.9 2.8 %collective-permute-start = (f32[1,256,128]{2,1,0:T(8,128)S(1)}, f32[1,256,128]{2,1,0:T(8,128)S(1)}, u32[]{:S(2)}, u32[]{:S(2)}) collective-permute-start(f32[1,256,128]{2,1,0:T(8,128)S(1)} %bitcast.66), channel_id=1, source_target_pairs={{0,16},{16,0},{1,17},{17,1},{2,18},{18,2},{3,19},{19,3},{4,20},{20... | collective-permute-start | bytes 393224 | tf_op jit(solution)/shard_map/ppermute | solution.py:22
  20.8 1.7 broadcast_in_dim.28
  22.5 3.5 %all-to-all-start = ((s32[4,32,1024]{2,1,0:T(8,128)}), s32[4,32,1024]{2,1,0:T(8,128)S(1)}, u32[]{:S(2)}, u32[]{:S(2)}) async-start(s32[4,32,1024]{2,1,0:T(8,128)} %broadcast_in_dim.28), calls=%async_computation | async-start | bytes 1048576 | tf_op jit(solution)/shard_map/all_to_all | solution.py:31
  28.4 0.8 copy.52.fb_ref
  29.2 0.8 copy.51.hb_ref
  30.1 11.0 %collective-permute-done.1 = f32[2,256,128]{2,1,0:T(8,128)} collective-permute-done((f32[2,256,128]{2,1,0:T(8,128)}, f32[2,256,128]{2,1,0:T(8,128)}, u32[]{:S(2)}, u32[]{:S(2)}) %collective-permute-start.1) | collective-permute-done | bytes 262176 | tf_op jit(solution)/shard_map/ppermute | solution.py:22
  41.1 1.8 pad_maximum_fusion.1
  42.9 4.4 %collective-permute-start.2 = (f32[4,256,128]{2,1,0:T(8,128)}, f32[4,256,128]{2,1,0:T(8,128)}, u32[]{:S(2)}, u32[]{:S(2)}) collective-permute-start(f32[4,256,128]{2,1,0:T(8,128)} %pad_maximum_fusion.1), channel_id=1, source_target_pairs={{0,1},{1,0},{2,3},{3,2},{4,5},{5,4},{6,7},{7,6},{8,9},{9,8},{10,11... | collective-permute-start | bytes 1572872 | tf_op jit(solution)/shard_map/ppermute | solution.py:22
  47.7 1.0 copy.48
  49.2 2.2 pad_maximum_fusion.f_ref
  51.5 0.8 copy-done.1
  52.3 11.2 %first_pass.1 = (bf16[1024,4096]{1,0:T(8,128)(2,1)}, f32[256,4096]{1,0:T(8,128)}, f32[1,4096]{1,0:T(1,128)}, f32[1,128]{1,0:T(1,128)}) custom-call(s32[32]{0:T(128)} %xor_add_fusion.words_ref, s32[4,32,1024]{2,1,0:T(8,128)} %copy-done.1, bf16[256,1024]{1,0:T(8,128)(2,1)} %bitcast.63, f32[8,256,128]{2,1,0:T(8,128)} %pad_maximum_fusion.f_ref, ...), custom_call_target="tpu_custom_call" | custom-call | tf_op jit(solution)/shard_map/first_pass/pallas_call | solution.py:75
  64.5 24.2 %all_to_all.26 = f32[32,1,4224]{2,1,0:T(1,128)S(1)} all-to-all(f32[32,1,4224]{2,1,0:T(1,128)S(1)} %broadcast_in_dim.31), channel_id=1, replica_groups=mesh['xl'=2,'y'=4,'xh'=2,'zh'=4,'zl'=2,'c'=2] {'xl','y','zh'}, dimensions={0} | all-to-all | bytes 1081344 | tf_op jit(solution)/shard_map/all_to_all | solution.py:31
  91.7 4.0 %collective-permute-start.3 = (f32[1,2]{1,0:T(1,128)S(1)}, f32[1,2]{1,0:T(1,128)S(1)}, u32[]{:S(2)}, u32[]{:S(2)}) collective-permute-start(f32[1,2]{1,0:T(1,128)S(1)} %maximum_bitcast_fusion), channel_id=1, source_target_pairs={{0,1},{1,0},{2,3},{3,2},{4,5},{5,4},{6,7},{7,6},{8,9},{9,8},{10,11... | collective-permute-start | bytes 32 | tf_op jit(solution)/shard_map/ppermute | solution.py:22
  95.7 0.8 collective-permute-done.3
  99.6 0.8 collective-permute-start.4
  100.4 1.7 collective-permute-done.4
  104.5 1.7 collective-permute-start.5
  106.2 2.2 collective-permute-done.5
  110.2 9.2 %image_pass.1 = (f32[1032,128]{1,0:T(8,128)}, f32[1032,128]{1,0:T(8,128)}) custom-call(bf16[1024,4096]{1,0:T(8,128)(2,1)} %get-tuple-element.12.s_ref, f32[256,4096]{1,0:T(8,128)} %get-tuple-element.13.h_ref, f32[1,4096]{1,0:T(1,128)} %subtract_multiply_fusion.c_ref), custom_call_target="tpu_custom_call" | custom-call | tf_op jit(solution)/shard_map/image_pass/pallas_call | solution.py:145
  119.5 2.6 %collective-permute-start.6 = (f32[1032,128]{1,0:T(8,128)}, f32[1032,128]{1,0:T(8,128)S(1)}, u32[]{:S(2)}, u32[]{:S(2)}) collective-permute-start(f32[1032,128]{1,0:T(8,128)} %get-tuple-element.15), channel_id=1, source_target_pairs={{0,1},{1,0},{2,3},{3,2},{4,5},{5,4},{6,7},{7,6},{8,9},{9,8},{10,11... | collective-permute-start | bytes 1585160 | tf_op jit(solution)/shard_map/ppermute | solution.py:22
  122.1 1.8 collective-permute-done.6
  123.9 1.1 add.121
  125.0 0.9 collective-permute-start.7
  125.9 6.8 %collective-permute-done.7 = f32[520,128]{1,0:T(8,128)S(1)} collective-permute-done((f32[520,128]{1,0:T(8,128)S(1)}, f32[520,128]{1,0:T(8,128)S(1)}, u32[]{:S(2)}, u32[]{:S(2)}) %collective-permute-start.7) | collective-permute-done | bytes 266272 | tf_op jit(solution)/shard_map/ppermute | solution.py:22
  132.7 1.8 collective-permute-start.8
  134.5 6.5 %collective-permute-done.8 = f32[520,128]{1,0:T(8,128)S(1)} collective-permute-done((f32[520,128]{1,0:T(8,128)S(1)}, f32[520,128]{1,0:T(8,128)S(1)}, u32[]{:S(2)}, u32[]{:S(2)}) %collective-permute-start.8) | collective-permute-done | bytes 266272 | tf_op jit(solution)/shard_map/ppermute | solution.py:22
  141.1 1.0 collective-permute-start.9
  142.3 5.0 %collective-permute-done.9 = f32[512,128]{1,0:T(8,128)} collective-permute-done((f32[512,128]{1,0:T(8,128)S(1)}, f32[512,128]{1,0:T(8,128)}, u32[]{:S(2)}, u32[]{:S(2)}) %collective-permute-start.9) | collective-permute-done | bytes 262176 | tf_op jit(solution)/shard_map/ppermute | solution.py:22
  147.3 1.0 pad_maximum_fusion.2.g0_ref
  148.3 3.0 %collective-permute-start.10 = (f32[1024,128]{1,0:T(8,128)S(1)}, f32[1024,128]{1,0:T(8,128)S(1)}, u32[]{:S(2)}, u32[]{:S(2)}) collective-permute-start(f32[1024,128]{1,0:T(8,128)S(1)} %pad_maximum_fusion.2.g0_ref), channel_id=1, source_target_pairs={{0,1},{1,0},{2,3},{3,2},{4,5},{5,4},{6,7},{7,6},{8,9},{9,8},{10,11... | collective-permute-start | bytes 1572872 | tf_op jit(solution)/shard_map/ppermute | solution.py:22
  152.0 3.3 %all-to-all-start.4 = ((f32[4,40,256]{2,1,0:T(8,128)}), f32[4,40,256]{2,1,0:T(8,128)S(1)}, u32[]{:S(2)}, u32[]{:S(2)}) async-start(f32[4,40,256]{2,1,0:T(8,128)} %pad_maximum_fusion.4), calls=%async_computation.4 | async-start | bytes 327680 | tf_op jit(solution)/shard_map/all_to_all | solution.py:281
  155.3 1.3 slice.117
  159.2 0.8 copy.55.gb_ref
  160.0 0.8 copy-done.3
  160.8 9.8 %second_pass.1 = (f32[1,4096]{1,0:T(1,128)}, f32[1,256]{1,0:T(1,128)}) custom-call(f32[1]{0:T(128)} %bitcast.27.step_ref, bf16[1024,4096]{1,0:T(8,128)(2,1)} %get-tuple-element.12.s_ref, f32[256,4096]{1,0:T(8,128)} %get-tuple-element.13.h_ref, f32[8,256,128]{2,1,0:T(8,128)} %pad_maximum_fusion.f_ref, f32[1024,128]{1,0:T(8,128)} %copy-done.2, ...), custom_call_target="tpu_custom_call" | custom-call | tf_op jit(solution)/shard_map/second_pass/pallas_call | solution.py:198
  170.6 0.8 maximum_reduce_fusion
  171.4 1.1 broadcast_in_dim.33
  172.5 9.6 %all-to-all-start.3 = ((f32[32,1,4352]{2,1,0:T(1,128)}), f32[32,1,4352]{2,1,0:T(1,128)S(1)}, u32[]{:S(2)}, u32[]{:S(2)}) async-start(f32[32,1,4352]{2,1,0:T(1,128)} %broadcast_in_dim.33), calls=%async_computation.3 | async-start | bytes 1114112 | tf_op jit(solution)/shard_map/all_to_all | solution.py:31
  182.2 16.8 %all-to-all-done.3 = f32[32,1,4352]{2,1,0:T(1,128)S(1)} async-done(((f32[32,1,4352]{2,1,0:T(1,128)}), f32[32,1,4352]{2,1,0:T(1,128)S(1)}, u32[]{:S(2)}, u32[]{:S(2)}) %all-to-all-start.3) | async-done | bytes 557088 | tf_op jit(solution)/shard_map/all_to_all | solution.py:31
  201.3 1.4 fusion.1
  206.8 2.6 %collective-permute-start.11 = (f32[1,2]{1,0:T(1,128)S(1)}, f32[1,2]{1,0:T(1,128)S(1)}, u32[]{:S(2)}, u32[]{:S(2)}) collective-permute-start(f32[1,2]{1,0:T(1,128)S(1)} %maximum_bitcast_fusion.3), channel_id=1, source_target_pairs={{0,1},{1,0},{2,3},{3,2},{4,5},{5,4},{6,7},{7,6},{8,9},{9,8},{10,11... | collective-permute-start | bytes 32 | tf_op jit(solution)/shard_map/ppermute | solution.py:22
  209.4 0.8 collective-permute-done.11
  213.6 2.2 collective-permute-done.12
  218.4 1.2 collective-permute-start.13
  219.6 2.7 %collective-permute-done.13 = f32[1,2]{1,0:T(1,128)S(1)} collective-permute-done((f32[1,2]{1,0:T(1,128)S(1)}, f32[1,2]{1,0:T(1,128)S(1)}, u32[]{:S(2)}, u32[]{:S(2)}) %collective-permute-start.13) | collective-permute-done | bytes 40 | tf_op jit(solution)/shard_map/ppermute | solution.py:22
  (71 shorter events, 16.1 us)
Async XLA Ops:
  0.6 26.8 %copy-start = (bf16[1024,1024]{1,0:T(8,128)(2,1)S(1)}, bf16[1024,1024]{1,0:T(8,128)(2,1)}, u32[]{:S(2)}) copy-start(bf16[1024,1024]{1,0:T(8,128)(2,1)} %param.6) | copy-start | bytes 6291460
  0.6 27.7 %copy-start.6 = (f32[1024]{0:T(1024)S(1)}, f32[1024]{0:T(1024)}, u32[]{:S(2)}) copy-start(f32[1024]{0:T(1024)} %param.9) | copy-start | bytes 12292
  17.9 8.1 %collective-permute-start = (f32[1,256,128]{2,1,0:T(8,128)S(1)}, f32[1,256,128]{2,1,0:T(8,128)S(1)}, u32[]{:S(2)}, u32[]{:S(2)}) collective-permute-start(f32[1,256,128]{2,1,0:T(8,128)S(1)} %bitcast.66), channel_id=1, source_target_pairs={{0,16},{16,0},{1,17},{17,1},{2,18},{18,2},{3,19},{19,3},{4,20},{20... | collective-permute-start | bytes 393224 | tf_op jit(solution)/shard_map/ppermute | solution.py:22
  22.5 29.0 %all-to-all-start = ((s32[4,32,1024]{2,1,0:T(8,128)}), s32[4,32,1024]{2,1,0:T(8,128)S(1)}, u32[]{:S(2)}, u32[]{:S(2)}) async-start(s32[4,32,1024]{2,1,0:T(8,128)} %broadcast_in_dim.28), calls=%async_computation | async-start | bytes 1048576 | tf_op jit(solution)/shard_map/all_to_all | solution.py:31
  26.7 14.4 %collective-permute-start.1 = (f32[2,256,128]{2,1,0:T(8,128)}, f32[2,256,128]{2,1,0:T(8,128)}, u32[]{:S(2)}, u32[]{:S(2)}) collective-permute-start(f32[2,256,128]{2,1,0:T(8,128)} %pad_maximum_fusion.3), channel_id=1, source_target_pairs={{0,2},{2,0},{1,3},{3,1},{4,6},{6,4},{5,7},{7,5},{8,10},{10,8},{9,1... | collective-permute-start | bytes 786440 | tf_op jit(solution)/shard_map/ppermute | solution.py:22
  42.9 6.3 %collective-permute-start.2 = (f32[4,256,128]{2,1,0:T(8,128)}, f32[4,256,128]{2,1,0:T(8,128)}, u32[]{:S(2)}, u32[]{:S(2)}) collective-permute-start(f32[4,256,128]{2,1,0:T(8,128)} %pad_maximum_fusion.1), channel_id=1, source_target_pairs={{0,1},{1,0},{2,3},{3,2},{4,5},{5,4},{6,7},{7,6},{8,9},{9,8},{10,11... | collective-permute-start | bytes 1572872 | tf_op jit(solution)/shard_map/ppermute | solution.py:22
  51.5 0.8 copy-start.1
  89.1 36.8 %copy-start.5 = (f32[1,4224]{1,0:T(1,128)}, f32[1,4224]{1,0:T(1,128)S(1)}, u32[]{:S(2)}) copy-start(f32[1,4224]{1,0:T(1,128)S(1)} %reduce_sum.59) | copy-start | bytes 50692
  91.7 4.8 %collective-permute-start.3 = (f32[1,2]{1,0:T(1,128)S(1)}, f32[1,2]{1,0:T(1,128)S(1)}, u32[]{:S(2)}, u32[]{:S(2)}) collective-permute-start(f32[1,2]{1,0:T(1,128)S(1)} %maximum_bitcast_fusion), channel_id=1, source_target_pairs={{0,1},{1,0},{2,3},{3,2},{4,5},{5,4},{6,7},{7,6},{8,9},{9,8},{10,11... | collective-permute-start | bytes 32 | tf_op jit(solution)/shard_map/ppermute | solution.py:22
  99.6 2.4 %collective-permute-start.4 = (f32[1,2]{1,0:T(1,128)S(1)}, f32[1,2]{1,0:T(1,128)S(1)}, u32[]{:S(2)}, u32[]{:S(2)}) collective-permute-start(f32[1,2]{1,0:T(1,128)S(1)} %maximum_bitcast_fusion.1), channel_id=1, source_target_pairs={{0,2},{2,0},{1,3},{3,1},{4,6},{6,4},{5,7},{7,5},{8,10},{10,8},{9,1... | collective-permute-start | bytes 32 | tf_op jit(solution)/shard_map/ppermute | solution.py:22
  104.5 4.0 %collective-permute-start.5 = (f32[1,2]{1,0:T(1,128)S(1)}, f32[1,2]{1,0:T(1,128)S(1)}, u32[]{:S(2)}, u32[]{:S(2)}) collective-permute-start(f32[1,2]{1,0:T(1,128)S(1)} %maximum_bitcast_fusion.2), channel_id=1, source_target_pairs={{0,16},{16,0},{1,17},{17,1},{2,18},{18,2},{3,19},{19,3},{4,20},{20... | collective-permute-start | bytes 32 | tf_op jit(solution)/shard_map/ppermute | solution.py:22
  119.5 4.4 %collective-permute-start.6 = (f32[1032,128]{1,0:T(8,128)}, f32[1032,128]{1,0:T(8,128)S(1)}, u32[]{:S(2)}, u32[]{:S(2)}) collective-permute-start(f32[1032,128]{1,0:T(8,128)} %get-tuple-element.15), channel_id=1, source_target_pairs={{0,1},{1,0},{2,3},{3,2},{4,5},{5,4},{6,7},{7,6},{8,9},{9,8},{10,11... | collective-permute-start | bytes 1585160 | tf_op jit(solution)/shard_map/ppermute | solution.py:22
  125.0 7.7 %collective-permute-start.7 = (f32[520,128]{1,0:T(8,128)S(1)}, f32[520,128]{1,0:T(8,128)S(1)}, u32[]{:S(2)}, u32[]{:S(2)}) collective-permute-start(f32[520,128]{1,0:T(8,128)S(1)} %slice.121), channel_id=1, source_target_pairs={{0,2},{2,0},{1,3},{3,1},{4,6},{6,4},{5,7},{7,5},{8,10},{10,8},{9,1... | collective-permute-start | bytes 798728 | tf_op jit(solution)/shard_map/ppermute | solution.py:22
  132.7 8.3 %collective-permute-start.8 = (f32[520,128]{1,0:T(8,128)S(1)}, f32[520,128]{1,0:T(8,128)S(1)}, u32[]{:S(2)}, u32[]{:S(2)}) collective-permute-start(f32[520,128]{1,0:T(8,128)S(1)} %maximum_add_fusion), channel_id=1, source_target_pairs={{0,16},{16,0},{1,17},{17,1},{2,18},{18,2},{3,19},{19,3},{4,20},{20... | collective-permute-start | bytes 798728 | tf_op jit(solution)/shard_map/ppermute | solution.py:22
  141.1 6.2 %collective-permute-start.9 = (f32[512,128]{1,0:T(8,128)S(1)}, f32[512,128]{1,0:T(8,128)}, u32[]{:S(2)}, u32[]{:S(2)}) collective-permute-start(f32[512,128]{1,0:T(8,128)S(1)} %slice.125), channel_id=1, source_target_pairs={{0,2},{2,0},{1,3},{3,1},{4,6},{6,4},{5,7},{7,5},{8,10},{10,8},{9,1... | collective-permute-start | bytes 786440 | tf_op jit(solution)/shard_map/ppermute | solution.py:22
  148.3 11.7 %copy-start.2 = (f32[1024,128]{1,0:T(8,128)}, f32[1024,128]{1,0:T(8,128)S(1)}, u32[]{:S(2)}) copy-start(f32[1024,128]{1,0:T(8,128)S(1)} %pad_maximum_fusion.2.g0_ref) | copy-start | bytes 1572868
  148.3 11.7 %collective-permute-start.10 = (f32[1024,128]{1,0:T(8,128)S(1)}, f32[1024,128]{1,0:T(8,128)S(1)}, u32[]{:S(2)}, u32[]{:S(2)}) collective-permute-start(f32[1024,128]{1,0:T(8,128)S(1)} %pad_maximum_fusion.2.g0_ref), channel_id=1, source_target_pairs={{0,1},{1,0},{2,3},{3,2},{4,5},{5,4},{6,7},{7,6},{8,9},{9,8},{10,11... | collective-permute-start | bytes 1572872 | tf_op jit(solution)/shard_map/ppermute | solution.py:22
  152.0 19.4 %all-to-all-start.4 = ((f32[4,40,256]{2,1,0:T(8,128)}), f32[4,40,256]{2,1,0:T(8,128)S(1)}, u32[]{:S(2)}, u32[]{:S(2)}) async-start(f32[4,40,256]{2,1,0:T(8,128)} %pad_maximum_fusion.4), calls=%async_computation.4 | async-start | bytes 327680 | tf_op jit(solution)/shard_map/all_to_all | solution.py:281
  160.0 0.8 copy-start.3
  160.8 64.7 %copy-start.4 = (f32[32,1024]{1,0:T(8,128)S(1)}, f32[32,1024]{1,0:T(8,128)}, u32[]{:S(2)}) copy-start(f32[32,1024]{1,0:T(8,128)} %param.8) | copy-start | bytes 393220
  172.5 26.5 %all-to-all-start.3 = ((f32[32,1,4352]{2,1,0:T(1,128)}), f32[32,1,4352]{2,1,0:T(1,128)S(1)}, u32[]{:S(2)}, u32[]{:S(2)}) async-start(f32[32,1,4352]{2,1,0:T(1,128)} %broadcast_in_dim.33), calls=%async_computation.3 | async-start | bytes 1114112 | tf_op jit(solution)/shard_map/all_to_all | solution.py:31
  206.8 3.4 %collective-permute-start.11 = (f32[1,2]{1,0:T(1,128)S(1)}, f32[1,2]{1,0:T(1,128)S(1)}, u32[]{:S(2)}, u32[]{:S(2)}) collective-permute-start(f32[1,2]{1,0:T(1,128)S(1)} %maximum_bitcast_fusion.3), channel_id=1, source_target_pairs={{0,1},{1,0},{2,3},{3,2},{4,5},{5,4},{6,7},{7,6},{8,9},{9,8},{10,11... | collective-permute-start | bytes 32 | tf_op jit(solution)/shard_map/ppermute | solution.py:22
  213.4 2.4 %collective-permute-start.12 = (f32[1,2]{1,0:T(1,128)S(1)}, f32[1,2]{1,0:T(1,128)S(1)}, u32[]{:S(2)}, u32[]{:S(2)}) collective-permute-start(f32[1,2]{1,0:T(1,128)S(1)} %maximum_bitcast_fusion.4), channel_id=1, source_target_pairs={{0,2},{2,0},{1,3},{3,1},{4,6},{6,4},{5,7},{7,5},{8,10},{10,8},{9,1... | collective-permute-start | bytes 32 | tf_op jit(solution)/shard_map/ppermute | solution.py:22
  218.4 4.0 %collective-permute-start.13 = (f32[1,2]{1,0:T(1,128)S(1)}, f32[1,2]{1,0:T(1,128)S(1)}, u32[]{:S(2)}, u32[]{:S(2)}) collective-permute-start(f32[1,2]{1,0:T(1,128)S(1)} %maximum_bitcast_fusion.5), channel_id=1, source_target_pairs={{0,16},{16,0},{1,17},{17,1},{2,18},{18,2},{3,19},{19,3},{4,20},{20... | collective-permute-start | bytes 32 | tf_op jit(solution)/shard_map/ppermute | solution.py:22

commit v2 on v0

v2 whole, which is shorter than its diff:
```python
import functools

import jax
import jax.numpy as jnp
from jax import lax
from jax.experimental import pallas as pl
from jax.experimental.pallas import tpu as pltpu
from jax.sharding import Mesh
from jax.sharding import PartitionSpec as P

GRP = ("xl", "y")
SMP = ("xh", "zh", "zl", "c")
SUM = ("zh", "xl", "y")
QUAD = ("xh", "zl")
SWAP = [(0, 1), (1, 0)]
LAM = 0.01
ROWS = 32
NB = 8
TILE = 1024
EXTRA = 128
F32, BF16 = jnp.float32, jnp.bfloat16
VMEM = pl.BlockSpec(memory_space=pltpu.VMEM)
SMEM = pl.BlockSpec(memory_space=pltpu.SMEM)


def swap(x, axis):
    return lax.ppermute(x, axis, SWAP)


def to_all(x, axes, size):
    return lax.all_to_all(jnp.broadcast_to(x[None], (size, *x.shape)), axes, 0, 0, tiled=True)


def split_terms(x):
    hi = x.astype(BF16)
    return hi, (x - hi.astype(F32)).astype(BF16)


def resident(x):
    return pltpu.with_memory_space_constraint(x, pltpu.VMEM)


def call(kernel, ins, outs, scratch=(), flops=0, name=None):
    return pl.pallas_call(
        kernel,
        in_specs=ins,
        out_specs=[VMEM] * len(outs),
        out_shape=outs,
        scratch_shapes=scratch,
        compiler_params=pltpu.CompilerParams(vmem_limit_bytes=40 << 20),
        cost_estimate=pl.CostEstimate(flops=flops, bytes_accessed=1 << 20, transcendentals=0),
        name=name,
    )


def cols(t):
    return pl.ds(pl.multiple_of(t * TILE, TILE), TILE)


def rows_to_column(rows):
    return jnp.concatenate(
        [jnp.broadcast_to(rows[k : k + 1, :], (128, 128)).T[:, :1] for k in range(rows.shape[0])], axis=0
    )


def total(x):
    return jnp.full((1, EXTRA), jnp.sum(x), F32)


def hidden_kernel(pos_ref, packed_ref, wt_ref, hb_ref, s_ref, h_ref):
    units = wt_ref.shape[0]
    shifts = 31 - lax.broadcasted_iota(jnp.int32, (ROWS, TILE), 0)
    hb = rows_to_column(hb_ref[pl.ds(pos_ref[32] * (units // 128), units // 128), :])

    def step(t, carry):
        for q in range(32):
            word = packed_ref[t, pl.ds(pos_ref[q], 1), :]
            up = jnp.left_shift(jnp.broadcast_to(word, (ROWS, TILE)), shifts) < 0
            s_ref[q * ROWS : (q + 1) * ROWS, cols(t)] = jnp.where(up, 1.0, -1.0).astype(BF16)
        pre = jnp.dot(wt_ref[...], s_ref[:, cols(t)], preferred_element_type=F32)
        h_ref[:, cols(t)] = jnp.tanh(pre + hb)
        return carry

    lax.fori_loop(0, packed_ref.shape[0], step, 0)


def hidden_pass(pos, packed, wt, hb):
    units, n = wt.shape[0], packed.shape[0] * TILE
    return call(
        hidden_kernel,
        [SMEM, VMEM, VMEM, VMEM],
        [pltpu.VMEM((NB * 128, n), BF16), pltpu.VMEM((units, n), F32)],
        flops=4 * 10**9,
        name="hidden_pass",
    )(pos, packed, wt, hb)


def project(s_ref, h_ref, lhs, bias, p_ref):
    units = h_ref.shape[0]

    def step(t, carry):
        out = jnp.dot(lhs[...], s_ref[:, cols(t)], preferred_element_type=F32)
        proj = out[:units] + out[units:] + bias
        p_ref[pl.ds(t, 1), :TILE] = jnp.sum(h_ref[:, cols(t)] * proj, axis=0, keepdims=True)
        return carry

    lax.fori_loop(0, s_ref.shape[1] // TILE, step, 0)


def set_block(lhs, b, x):
    units = x.shape[0]
    hi, lo = split_terms(x)
    lhs[:units, b * 128 : (b + 1) * 128] = hi
    lhs[units:, b * 128 : (b + 1) * 128] = lo


def my_rows(pos_ref, ref, units):
    return ref[pl.ds(pos_ref[32] * (units // 128), units // 128), :]


def first_kernel(pos_ref, s_ref, h_ref, f0, f1, f2, f3, fb_ref, p_ref, lhs):
    units = h_ref.shape[0]
    norm = jnp.zeros((units, 128), F32)
    for b in range(NB):
        x = (f0, f1, f2, f3)[b // 2][b % 2]
        set_block(lhs, b, x)
        norm = norm + x * x
    fb = my_rows(pos_ref, fb_ref, units)
    p_ref[:, TILE:] = jnp.zeros((p_ref.shape[0], EXTRA), F32)
    p_ref[0:1, TILE:] = total(norm) + total(fb * fb)
    project(s_ref, h_ref, lhs, rows_to_column(fb), p_ref)


def first_pass(pos, spins, hidden, f, fb):
    units, n = hidden.shape
    return call(
        first_kernel,
        [SMEM] + [VMEM] * 7,
        [jax.ShapeDtypeStruct((n // TILE, TILE + EXTRA), F32)],
        [pltpu.VMEM((2 * units, NB * 128), BF16)],
        flops=4 * 10**9,
        name="first_pass",
    )(pos, resident(spins), resident(hidden), *f, fb)[0]


def step_of(norm, spread, samples, length):
    return norm / (spread / samples + LAM * length)


def second_kernel(samples, pos_ref, s_ref, h_ref, f0, f1, f2, f3, fb_ref, g0, g1, st_ref, norm_ref, p_ref, lhs):
    units = h_ref.shape[0]
    norm0 = norm_ref[0:1, :]
    a = step_of(norm0, st_ref[1:2, :], samples, norm0)
    rr = jnp.zeros((units, 128), F32)
    rf = jnp.zeros((units, 128), F32)
    for b in range(NB):
        f = (f0, f1, f2, f3)[b // 2][b % 2]
        g = (g0, g1)[b // 4][pos_ref[33 + b % 4], :units, :]
        r = f - a * (g + LAM * f)
        set_block(lhs, b, r)
        rr = rr + r * r
        rf = rf + r * f
    fb = my_rows(pos_ref, fb_ref, units)
    rb = fb - a * (g0[0, units : units + units // 128, :] + LAM * fb)
    p_ref[:, TILE:] = jnp.zeros((p_ref.shape[0], EXTRA), F32)
    p_ref[0:1, TILE:] = total(rr) + total(rb * rb)
    p_ref[1:2, TILE:] = total(rf) + total(rb * fb)
    project(s_ref, h_ref, lhs, rows_to_column(rb), p_ref)


def second_pass(samples, pos, spins, hidden, f, fb, g0, g1, st, norm):
    units, n = hidden.shape
    return call(
        functools.partial(second_kernel, samples),
        [SMEM] + [VMEM] * 11,
        [jax.ShapeDtypeStruct((n // TILE, TILE + EXTRA), F32)],
        [pltpu.VMEM((2 * units, NB * 128), BF16)],
        flops=4 * 10**9,
        name="second_pass",
    )(pos, resident(spins), resident(hidden), *f, fb, g0, g1, st, norm)[0]


def put_stats(v, st_ref):
    mean = jnp.sum(v) / v.size
    st_ref[0:1, :] = jnp.full((1, 128), mean, F32)
    st_ref[1:2, :] = total((v - mean) ** 2)


def first_sum_kernel(got_ref, v_ref, st_ref, norm_ref):
    x = got_ref[0]
    for k in range(1, got_ref.shape[0]):
        x = x + got_ref[k]
    v = x[:, :TILE]
    v_ref[...] = v
    norm_ref[...] = x[:, TILE:]
    put_stats(v, st_ref)


def first_sum(got):
    parts = got.shape[1]
    shape = lambda *s: jax.ShapeDtypeStruct(s, F32)
    return call(first_sum_kernel, [VMEM], [shape(parts, TILE), shape(2, 128), shape(parts, EXTRA)], name="first_sum")(
        got
    )


def second_sum_kernel(got_ref, v_ref, norm_ref, st_ref, next_ref):
    x = got_ref[0]
    for k in range(1, got_ref.shape[0]):
        x = x + got_ref[k]
    next_ref[...] = x[:, TILE:]
    beta = x[0:1, TILE : TILE + 1] / norm_ref[0:1, 0:1]
    put_stats(x[:, :TILE] + beta * v_ref[...], st_ref)


def second_sum(got, values, norm):
    shape = lambda *s: jax.ShapeDtypeStruct(s, F32)
    return call(second_sum_kernel, [VMEM] * 3, [shape(2, 128), shape(got.shape[1], EXTRA)], name="second_sum")(
        got, values, norm
    )


def merged(st, count, axis):
    got = swap(st, axis)
    delta = got[0:1] - st[0:1]
    first = lax.broadcasted_iota(jnp.int32, st.shape, 0) == 0
    return jnp.where(first, 0.5 * (st + got), st + got + (0.5 * count) * delta * delta)


def over_sets(st, count):
    for axis in ("c", "zl", "xh"):
        st = merged(st, count, axis)
        count *= 2
    return st


def image_kernel(samples, pos_ref, s_ref, h_ref, v_ref, st_ref, keep_ref, send_ref, acc, lanes):
    units = h_ref.shape[0]
    mean = st_ref[0:1, 0:1]
    acc[...] = jnp.zeros(acc.shape, F32)
    lanes[...] = jnp.zeros(lanes.shape, F32)

    def step(t, carry):
        r = h_ref[:, cols(t)] * ((v_ref[pl.ds(t, 1), :] - mean) * (1.0 / samples))
        both = jnp.concatenate(split_terms(r), axis=0)
        out = lax.dot_general(both, s_ref[:, cols(t)], (((1,), (1,)), ((), ())), preferred_element_type=F32)
        acc[...] += out[:units] + out[units:]
        part = r[:, :128]
        for k in range(1, TILE // 128):
            part = part + r[:, k * 128 : (k + 1) * 128]
        lanes[...] += part
        return carry

    lax.fori_loop(0, s_ref.shape[1] // TILE, step, 0)
    bias = [
        jnp.sum(lanes[k * 128 : (k + 1) * 128, :].T, axis=0, keepdims=True) for k in range(units // 128)
    ] + [jnp.zeros((8 - units // 128, 128), F32)]
    bias = jnp.concatenate(bias, axis=0)
    for b in range(NB):
        ref = (keep_ref, send_ref)[b // 4]
        at = pos_ref[33 + b % 4]
        ref[at, :units, :] = acc[:, b * 128 : (b + 1) * 128]
        ref[at, units:, :] = bias


def image_pass(samples, pos, spins, hidden, values, st):
    units = hidden.shape[0]
    return call(
        functools.partial(image_kernel, samples),
        [SMEM] + [VMEM] * 4,
        [jax.ShapeDtypeStruct((4, units + 8, 128), F32)] * 2,
        [pltpu.VMEM((units, NB * 128), F32), pltpu.VMEM((units, 128), F32)],
        flops=4 * 10**9,
        name="image_pass",
    )(pos, resident(spins), resident(hidden), values, st)


def update_kernel(samples, f_ref, fb_ref, g_ref, st0_ref, norm_ref, st1_ref, next_ref, w_ref, b_ref):
    norm0, norm1 = norm_ref[0:1, 0:1], next_ref[0:1, 0:1]
    cross = next_ref[1:2, 0:1]
    beta = norm1 / norm0
    step0 = step_of(norm0, st0_ref[1:2, 0:1], samples, norm0)
    step1 = step_of(norm1, st1_ref[1:2, 0:1], samples, norm1 + 2.0 * beta * cross + beta * beta * norm0)

    def update(f, g):
        r = f - step0 * (g + LAM * f)
        return step0 * f + step1 * (r + beta * f)

    units = g_ref.shape[2]
    for k in range(g_ref.shape[0]):
        at = slice(k * units, (k + 1) * units)
        w_ref[:, at] = update(f_ref[:, at], g_ref[k, :ROWS, :])
        for h in range(units // 128):
            row = slice(k * (units // 128) + h, k * (units // 128) + h + 1)
            b_ref[row, :] = update(fb_ref[row, :], g_ref[k, ROWS : ROWS + 1, h * 128 : (h + 1) * 128])


def update_pass(samples, f, fb, g, st0, norm, st1, norms):
    shape = lambda s: jax.ShapeDtypeStruct(s, F32)
    return call(
        functools.partial(update_kernel, samples), [VMEM] * 7, [shape(f.shape), shape(fb.shape)], name="update_pass"
    )(f, fb, g, st0, norm, st1, norms)


def body(spins_packed, weight, hidden_bias, force_w, force_b):
    xh, zh, zl, c = (lax.axis_index(a) for a in SMP)
    parts = lax.axis_size("zh")
    summed = lax.axis_size(SUM)
    units = weight.shape[1] // parts
    samples = spins_packed.shape[1] * lax.axis_size(SMP)
    hb = hidden_bias.reshape(-1, 128)
    fb = force_b.reshape(-1, 128)

    q = jnp.arange(32, dtype=jnp.int32)
    words = (((q >> 2) & 1) ^ xh) * 16 + (q & 3) * 4 + (((q >> 3) & 1) ^ zl) * 2 + ((q >> 4) ^ c)
    k = jnp.arange(4, dtype=jnp.int32)
    blocks = ((k & 1) ^ xh) * 2 + ((k >> 1) ^ zl)
    pos = jnp.concatenate([words, zh.reshape(1), blocks])

    f_cols = force_w.reshape(ROWS, parts, units).transpose(1, 0, 2)
    f = lax.all_to_all(f_cols, "zh", 0, 0, tiled=True).reshape(parts * ROWS, units).T[None]
    f = jnp.concatenate([f, swap(f, "xh")], axis=0)
    f_zl = swap(f, "zl")
    f = (f, f_zl, swap(f, "c"), swap(f_zl, "c"))

    packed = to_all(spins_packed, "zh", parts)
    w = lax.dynamic_slice_in_dim(weight, zh * units, units, 1).reshape(2, parts, 2, 2, ROWS, units)
    for dim, bit in ((0, xh), (2, zl), (3, c)):
        w = jnp.where(bit == 1, jnp.flip(w, dim), w)
    wt = w.transpose(3, 2, 0, 1, 4, 5).reshape(NB * 128, units).T

    spins, hidden = hidden_pass(pos, packed, wt, hb)
    partial = first_pass(pos, spins, hidden, f, fb)
    values, st, norm = first_sum(to_all(partial, SUM, summed))
    n = values.size
    st0 = over_sets(st, n)

    keep, send = image_pass(samples, pos, spins, hidden, values, st0)
    g = keep + swap(send, "c")
    g = lax.all_to_all(g, QUAD, 0, 0, tiled=True).sum(axis=0)
    g_mine = g[:units].T.reshape(parts, ROWS, units)
    gb = jnp.broadcast_to(g[units : units + units // 128].reshape(1, 1, units), (parts, 8, units))
    g_mine = lax.all_to_all(jnp.concatenate([g_mine, gb], axis=1), "zh", 0, 0, tiled=True)
    g = to_all(g, QUAD, 4)

    partial = second_pass(samples, pos, spins, hidden, f, fb, g, swap(g, "c"), st0, norm)
    st, norms = second_sum(to_all(partial, SUM, summed), values, norm)
    st1 = over_sets(st, n)
    out_w, out_b = update_pass(samples, force_w, fb, g_mine, st0, norm, st1, norms)
    return out_w, out_b.reshape(-1)


def solution(mesh):
    torus = Mesh(mesh.devices.reshape(2, 4, 2, 4, 2, 2), ("xl", "y", "xh", "zh", "zl", "c"))
    in_specs = (P(None, SMP), P(None, GRP), P(GRP), P(SMP, GRP), P(GRP))
    out_specs = (P(SMP, GRP), P(GRP))
    return jax.shard_map(body, mesh=torus, in_specs=in_specs, out_specs=out_specs, check_vma=False)
```

time: 468 us -> 195 us (0.42)
  waiting for transfers between devices: 175 us -> 29.1 us
  blocking collectives: 187 us -> 75.8 us
  matrix products: 37.8 us -> 0 us
  Pallas kernels: 0 us -> 26.6 us
  starting transfers between devices: 15.7 us -> 40.3 us
  between operations: 24.5 us -> 0.88 us
  other arithmetic: 15.1 us -> 3.81 us
  local copies, waits for them, and re-layouts: 11.1 us -> 16 us
    psum x15 -> x0, blocking collectives: 133 us -> none  [one_axis_at_a_time(): return functools.reduce(lax.psum, axes, value)]
    all_gather x4 -> x0, waiting for transfers between devices: 112 us -> none  [all_blocks(): tiles = lax.all_gather(tiles, axes[k])]
    reduce_scatter x1 -> x0, waiting for transfers between devices: 55 us -> none  [body(): lax.psum_scatter(jnp.einsum('it,th->ih', spins, weighted, precision=lax.P...]
    dot_general x5 -> x0, matrix products: 37.8 us -> none  [the longest x2 16.2 us: body(): jnp.einsum('it,ih->th', spins, gather_axes(direction_w, SMP, (0, 1, 2), 0...]
    all_to_all x3 -> x4, blocking collectives: 39.2 us -> 75.8 us  [the longest x3 61.2 us: to_all(): lax.all_to_all(jnp.broadcast_to(x[None], (size, *x.shape)), axes, 0, 0, t...]
    pallas_call x0 -> x7, Pallas kernels: none -> 26.6 us  [the longest x1 7.43 us: first_pass(): call(first_kernel, [SMEM] + [VMEM] * 7, [jax.ShapeDtypeStruct((n // TILE,...]
    ppermute x0 -> x12, starting transfers between devices: none -> 23.8 us  [swap(): return lax.ppermute(x, axis, SWAP)]
    ppermute x0 -> x12, waiting for transfers between devices: none -> 15.6 us  [swap(): return lax.ppermute(x, axis, SWAP)]
  transfers between devices with their start and end apart: 7 -> 15, of which waited for: 6 -> 11; matrix products, arithmetic and copies ran while one was open for 4% -> 3% of each run, Pallas kernels for 0% -> 2%
where the time goes in v2:
time: 195 us; the launch traced here: 193 us
  blocking collectives  75.8 us (39%)
  starting transfers between devices  40.3 us (21%)
  waiting for transfers between devices  29.1 us (15%)
  Pallas kernels  26.6 us (14%)
  local copies, waits for them, and re-layouts  16 us (8%)
  other arithmetic  3.81 us (2%)
    all_to_all x3, blocking collectives, to_all(): lax.all_to_all(jnp.broadcast_to(x[None], (size, *x.shape)), axes, 0, 0, t...  61.2 us
    ppermute x12, starting transfers between devices, swap(): return lax.ppermute(x, axis, SWAP)  23.8 us
    ppermute x12, waiting for transfers between devices, swap(): return lax.ppermute(x, axis, SWAP)  15.6 us
    all_to_all x1, blocking collectives, body(): g = lax.all_to_all(g, QUAD, 0, 0, tiled=True).sum(axis=0)  14.6 us
    unnamed x20, local copies, waits for them, and re-layouts  9.84 us
    all_to_all x1, starting transfers between devices, body(): lax.all_to_all(f_cols, 'zh', 0, 0, tiled=True).reshape(parts * ROWS, units)  9 us
    pallas_call x1, Pallas kernels, first_pass(): call(first_kernel, [SMEM] + [VMEM] * 7, [jax.ShapeDtypeStruct((n // TILE,...  7.43 us
    pallas_call x1, Pallas kernels, second_pass(): call(functools.partial(second_kernel, samples), [SMEM] + [VMEM] * 11, [ja...  7.39 us
  transfers between devices with their start and end apart: 15, of which 11 were waited for; matrix products, arithmetic and copies ran while one was open for 3% of the time, Pallas kernels for 2%

profile of v2, /device:TPU:1, one launch (start us, length us, event | category | flops | bytes accessed | tf_op | source)
XLA Modules:
  0.0 192.6 jit_solution(6261979531824915310)
XLA Ops:
  0.6 1.1 reshape.42
  1.8 0.7 copy.20
  2.4 9.0 %all-to-all-start.1 = ((f32[4,32,256]{2,1,0:T(8,128)}), f32[4,32,256]{2,1,0:T(8,128)S(1)}, u32[]{:S(2)}, u32[]{:S(2)}) async-start(f32[4,32,256]{2,1,0:T(8,128)} %copy.20), calls=%async_computation.1 | async-start | bytes 262144 | tf_op jit(solution)/shard_map/all_to_all | solution.py:321
  11.5 0.9 reverse_select_fusion.2
  12.4 6.2 %all-to-all-done.1 = f32[4,32,256]{2,1,0:T(8,128)S(1)} async-done(((f32[4,32,256]{2,1,0:T(8,128)}), f32[4,32,256]{2,1,0:T(8,128)S(1)}, u32[]{:S(2)}, u32[]{:S(2)}) %all-to-all-start.1) | async-done | bytes 131104 | tf_op jit(solution)/shard_map/all_to_all | solution.py:321
  18.7 1.8 broadcast_in_dim.14
  20.4 3.5 %all-to-all-start = ((s32[4,32,1024]{2,1,0:T(8,128)}), s32[4,32,1024]{2,1,0:T(8,128)S(1)}, u32[]{:S(2)}, u32[]{:S(2)}) async-start(s32[4,32,1024]{2,1,0:T(8,128)} %broadcast_in_dim.14), calls=%async_computation | async-start | bytes 1048576 | tf_op jit(solution)/shard_map/all_to_all | solution.py:31
  23.9 1.4 reverse_select_fusion.1
  25.4 2.8 %collective-permute-start = (f32[1,256,128]{2,1,0:T(8,128)S(1)}, f32[1,256,128]{2,1,0:T(8,128)S(1)}, u32[]{:S(2)}, u32[]{:S(2)}) collective-permute-start(f32[1,256,128]{2,1,0:T(8,128)S(1)} %bitcast.41), channel_id=1, source_target_pairs={{0,16},{16,0},{1,17},{17,1},{2,18},{18,2},{3,19},{19,3},{4,20},{20... | collective-permute-start | bytes 393224 | tf_op jit(solution)/shard_map/ppermute | solution.py:27
  28.4 2.4 %collective-permute-done = f32[1,256,128]{2,1,0:T(8,128)S(1)} collective-permute-done((f32[1,256,128]{2,1,0:T(8,128)S(1)}, f32[1,256,128]{2,1,0:T(8,128)S(1)}, u32[]{:S(2)}, u32[]{:S(2)}) %collective-permute-start) | collective-permute-done | bytes 131104 | tf_op jit(solution)/shard_map/ppermute | solution.py:27
  30.8 0.8 collective-permute-start.1
  31.7 0.8 copy.18
  32.5 1.2 copy.19
  33.9 4.4 %collective-permute-start.2 = (f32[2,256,128]{2,1,0:T(8,128)S(1)}, f32[2,256,128]{2,1,0:T(8,128)}, u32[]{:S(2)}, u32[]{:S(2)}) collective-permute-start(f32[2,256,128]{2,1,0:T(8,128)S(1)} %pad_maximum_fusion.f0), channel_id=1, source_target_pairs={{0,1},{1,0},{2,3},{3,2},{4,5},{5,4},{6,7},{7,6},{8,9},{9,8},{10,11... | collective-permute-start | bytes 786440 | tf_op jit(solution)/shard_map/ppermute | solution.py:27
  38.3 3.8 %collective-permute-done.1.f1 = f32[2,256,128]{2,1,0:T(8,128)} collective-permute-done((f32[2,256,128]{2,1,0:T(8,128)S(1)}, f32[2,256,128]{2,1,0:T(8,128)}, u32[]{:S(2)}, u32[]{:S(2)}) %collective-permute-start.1) | collective-permute-done | bytes 262176 | tf_op jit(solution)/shard_map/ppermute | solution.py:27
  42.1 1.4 collective-permute-start.3
  43.5 4.3 %hidden_pass.1 = (bf16[1024,4096]{1,0:T(8,128)(2,1)S(1)}, f32[256,4096]{1,0:T(8,128)S(1)}) custom-call(s32[37]{0:T(128)S(1)} %pad_add_fusion.pos_ref, s32[4,32,1024]{2,1,0:T(8,128)S(1)} %all-to-all-done.packed_ref, bf16[256,1024]{1,0:T(8,128)(2,1)S(1)} %bitcast.31, f32[8,128]{1,0:T(8,128)S(1)} %bitcast.35), custom_call_target="tpu_custom_call" | custom-call | flops 4000000000 | bytes 1048576 | tf_op jit(solution)/shard_map/hidden_pass/pallas_call | solution.py:89
  47.8 7.4 %first_pass.1 = f32[4,1152]{1,0:T(4,128)S(1)} custom-call(s32[37]{0:T(128)S(1)} %pad_add_fusion.pos_ref, bf16[1024,4096]{1,0:T(8,128)(2,1)S(1)} %get-tuple-element.13.s_ref, f32[256,4096]{1,0:T(8,128)S(1)} %get-tuple-element.14.h_ref, f32[2,256,128]{2,1,0:T(8,128)S(1)} %pad_maximum_fusion.f0, f32[2,256,128]{2,1,0:T(8,128)} %collective-permute-done.1.f1, ...), custom_call_target="tpu_custom_call" | custom-call | flops 4000000000 | bytes 1048576 | tf_op jit(solution)/shard_map/first_pass/pallas_call | solution.py:136
  55.4 26.5 %all_to_all.35.got_ref = f32[32,4,1152]{2,1,0:T(4,128)S(1)} all-to-all(f32[32,4,1152]{2,1,0:T(4,128)S(1)} %broadcast_in_dim.16), channel_id=1, replica_groups=mesh['xl'=2,'y'=4,'xh'=2,'zh'=4,'zl'=2,'c'=2] {'zh','xl','y'}, dimensions={0} | all-to-all | bytes 1179648 | tf_op jit(solution)/shard_map/all_to_all | solution.py:31
  81.9 0.3 first_sum.1
  82.2 2.9 %collective-permute-start.4 = (f32[2,128]{1,0:T(2,128)S(1)}, f32[2,128]{1,0:T(2,128)S(1)}, u32[]{:S(2)}, u32[]{:S(2)}) collective-permute-start(f32[2,128]{1,0:T(2,128)S(1)} %get-tuple-element.16), channel_id=1, source_target_pairs={{0,1},{1,0},{2,3},{3,2},{4,5},{5,4},{6,7},{7,6},{8,9},{9,8},{10,11... | collective-permute-start | bytes 3080 | tf_op jit(solution)/shard_map/ppermute | solution.py:27
  85.1 0.8 collective-permute-done.4
  86.0 1.5 collective-permute-start.5
  87.5 1.0 collective-permute-done.5
  88.5 2.6 %collective-permute-start.6 = (f32[2,128]{1,0:T(2,128)S(1)}, f32[2,128]{1,0:T(2,128)S(1)}, u32[]{:S(2)}, u32[]{:S(2)}) collective-permute-start(f32[2,128]{1,0:T(2,128)S(1)} %add_select_fusion.4), channel_id=1, source_target_pairs={{0,16},{16,0},{1,17},{17,1},{2,18},{18,2},{3,19},{19,3},{4,20},{20... | collective-permute-start | bytes 3080 | tf_op jit(solution)/shard_map/ppermute | solution.py:27
  91.1 1.3 collective-permute-done.6
  92.6 3.4 %copy-done.5 = bf16[1024,4096]{1,0:T(8,128)(2,1)S(1)} copy-done((bf16[1024,4096]{1,0:T(8,128)(2,1)S(1)}, bf16[1024,4096]{1,0:T(8,128)(2,1)}, u32[]{:S(2)}) %copy-start.5) | copy-done | bytes 8388632
  95.9 6.2 %image_pass.1 = (f32[4,264,128]{2,1,0:T(8,128)S(1)}, f32[4,264,128]{2,1,0:T(8,128)S(1)}) custom-call(s32[37]{0:T(128)S(1)} %pad_add_fusion.pos_ref, bf16[1024,4096]{1,0:T(8,128)(2,1)S(1)} %copy-done.5, f32[256,4096]{1,0:T(8,128)S(1)} %get-tuple-element.14.h_ref, f32[4,1024]{1,0:T(4,128)S(1)} %get-tuple-element.15.v_ref, ...), custom_call_target="tpu_custom_call" | custom-call | flops 4000000000 | bytes 1048576 | tf_op jit(solution)/shard_map/image_pass/pallas_call | solution.py:268
  102.1 2.7 %collective-permute-start.7 = (f32[4,264,128]{2,1,0:T(8,128)S(1)}, f32[4,264,128]{2,1,0:T(8,128)S(1)}, u32[]{:S(2)}, u32[]{:S(2)}) collective-permute-start(f32[4,264,128]{2,1,0:T(8,128)S(1)} %get-tuple-element.18), channel_id=1, source_target_pairs={{0,1},{1,0},{2,3},{3,2},{4,5},{5,4},{6,7},{7,6},{8,9},{9,8},{10,11... | collective-permute-start | bytes 1622024 | tf_op jit(solution)/shard_map/ppermute | solution.py:27
  104.8 1.6 collective-permute-done.7
  106.4 14.6 %all_to_all.36 = f32[4,264,128]{2,1,0:T(8,128)S(1)} all-to-all(f32[4,264,128]{2,1,0:T(8,128)S(1)} %add.119), channel_id=1, replica_groups=mesh['xl'=2,'y'=4,'xh'=2,'zh'=4,'zl'=2,'c'=2] {'xh','zl'}, dimensions={0} | all-to-all | bytes 1081344 | tf_op jit(solution)/shard_map/all_to_all | solution.py:340
  121.1 11.4 %all_to_all.37.g0 = f32[4,264,128]{2,1,0:T(8,128)S(1)} all-to-all(f32[4,264,128]{2,1,0:T(8,128)S(1)} %broadcast_in_dim.19), channel_id=1, replica_groups=mesh['xl'=2,'y'=4,'xh'=2,'zh'=4,'zl'=2,'c'=2] {'xh','zl'}, dimensions={0} | all-to-all | bytes 1081344 | tf_op jit(solution)/shard_map/all_to_all | solution.py:31
  132.5 2.5 %collective-permute-start.8 = (f32[4,264,128]{2,1,0:T(8,128)S(1)}, f32[4,264,128]{2,1,0:T(8,128)S(1)}, u32[]{:S(2)}, u32[]{:S(2)}) collective-permute-start(f32[4,264,128]{2,1,0:T(8,128)S(1)} %all_to_all.37.g0), channel_id=1, source_target_pairs={{0,1},{1,0},{2,3},{3,2},{4,5},{5,4},{6,7},{7,6},{8,9},{9,8},{10,11... | collective-permute-start | bytes 1622024 | tf_op jit(solution)/shard_map/ppermute | solution.py:27
  135.0 1.6 collective-permute-done.8.g1
  136.5 0.9 copy-done.9
  137.4 3.4 %copy-done.6 = bf16[1024,4096]{1,0:T(8,128)(2,1)S(1)} copy-done((bf16[1024,4096]{1,0:T(8,128)(2,1)S(1)}, bf16[1024,4096]{1,0:T(8,128)(2,1)}, u32[]{:S(2)}) %copy-start.6) | copy-done | bytes 8388632
  140.8 2.2 %copy-done.8 = f32[256,4096]{1,0:T(8,128)S(1)} copy-done((f32[256,4096]{1,0:T(8,128)S(1)}, f32[256,4096]{1,0:T(8,128)}, u32[]{:S(2)}) %copy-start.8) | copy-done | bytes 4194328
  143.0 7.4 %second_pass.1 = f32[4,1152]{1,0:T(4,128)S(1)} custom-call(s32[37]{0:T(128)S(1)} %pad_add_fusion.pos_ref, bf16[1024,4096]{1,0:T(8,128)(2,1)S(1)} %copy-done.6, f32[256,4096]{1,0:T(8,128)S(1)} %copy-done.8, f32[2,256,128]{2,1,0:T(8,128)S(1)} %pad_maximum_fusion.f0, f32[2,256,128]{2,1,0:T(8,128)} %collective-permute-done.1.f1, ...), custom_call_target="tpu_custom_call" | custom-call | flops 4000000000 | bytes 1048576 | tf_op jit(solution)/shard_map/second_pass/pallas_call | solution.py:173
  150.4 23.3 %all_to_all.38.got_ref = f32[32,4,1152]{2,1,0:T(4,128)S(1)} all-to-all(f32[32,4,1152]{2,1,0:T(4,128)S(1)} %broadcast_in_dim.40), channel_id=1, replica_groups=mesh['xl'=2,'y'=4,'xh'=2,'zh'=4,'zl'=2,'c'=2] {'zh','xl','y'}, dimensions={0} | all-to-all | bytes 1179648 | tf_op jit(solution)/shard_map/all_to_all | solution.py:31
  173.8 0.3 second_sum.1
  174.1 1.9 collective-permute-start.9
  176.0 0.8 collective-permute-done.9
  177.0 2.3 %collective-permute-done.10 = f32[2,128]{1,0:T(2,128)S(1)} collective-permute-done((f32[2,128]{1,0:T(2,128)S(1)}, f32[2,128]{1,0:T(2,128)S(1)}, u32[]{:S(2)}, u32[]{:S(2)}) %collective-permute-start.10) | collective-permute-done | bytes 1056 | tf_op jit(solution)/shard_map/ppermute | solution.py:27
  179.4 0.3 collective-permute-start.11
  179.7 0.7 pad_maximum_fusion.1
  180.3 4.1 %all-to-all-start.4 = ((f32[4,40,256]{2,1,0:T(8,128)}), f32[4,40,256]{2,1,0:T(8,128)S(1)}, u32[]{:S(2)}, u32[]{:S(2)}) async-start(f32[4,40,256]{2,1,0:T(8,128)} %pad_maximum_fusion.1), calls=%async_computation.4 | async-start | bytes 327680 | tf_op jit(solution)/shard_map/all_to_all | solution.py:343
  184.5 7.3 %all-to-all-done.4.g_ref = f32[4,40,256]{2,1,0:T(8,128)S(1)} async-done(((f32[4,40,256]{2,1,0:T(8,128)}), f32[4,40,256]{2,1,0:T(8,128)S(1)}, u32[]{:S(2)}, u32[]{:S(2)}) %all-to-all-start.4) | async-done | bytes 163872 | tf_op jit(solution)/shard_map/all_to_all | solution.py:343
  191.9 0.7 update_pass.1
  (50 shorter events, 1.3 us)
Async XLA Ops:
  0.6 10.8 %copy-start = (bf16[1024,1024]{1,0:T(8,128)(2,1)S(1)}, bf16[1024,1024]{1,0:T(8,128)(2,1)}, u32[]{:S(2)}) copy-start(bf16[1024,1024]{1,0:T(8,128)(2,1)} %param.6) | copy-start | bytes 6291460
  2.4 16.2 %all-to-all-start.1 = ((f32[4,32,256]{2,1,0:T(8,128)}), f32[4,32,256]{2,1,0:T(8,128)S(1)}, u32[]{:S(2)}, u32[]{:S(2)}) async-start(f32[4,32,256]{2,1,0:T(8,128)} %copy.20), calls=%async_computation.1 | async-start | bytes 262144 | tf_op jit(solution)/shard_map/all_to_all | solution.py:321
  11.4 32.1 %copy-start.3 = (f32[1024]{0:T(1024)S(1)}, f32[1024]{0:T(1024)}, u32[]{:S(2)}) copy-start(f32[1024]{0:T(1024)} %param.7) | copy-start | bytes 12292
  20.4 23.1 %all-to-all-start = ((s32[4,32,1024]{2,1,0:T(8,128)}), s32[4,32,1024]{2,1,0:T(8,128)S(1)}, u32[]{:S(2)}, u32[]{:S(2)}) async-start(s32[4,32,1024]{2,1,0:T(8,128)} %broadcast_in_dim.14), calls=%async_computation | async-start | bytes 1048576 | tf_op jit(solution)/shard_map/all_to_all | solution.py:31
  25.4 5.4 %collective-permute-start = (f32[1,256,128]{2,1,0:T(8,128)S(1)}, f32[1,256,128]{2,1,0:T(8,128)S(1)}, u32[]{:S(2)}, u32[]{:S(2)}) collective-permute-start(f32[1,256,128]{2,1,0:T(8,128)S(1)} %bitcast.41), channel_id=1, source_target_pairs={{0,16},{16,0},{1,17},{17,1},{2,18},{18,2},{3,19},{19,3},{4,20},{20... | collective-permute-start | bytes 393224 | tf_op jit(solution)/shard_map/ppermute | solution.py:27
  30.8 11.2 %collective-permute-start.1 = (f32[2,256,128]{2,1,0:T(8,128)S(1)}, f32[2,256,128]{2,1,0:T(8,128)}, u32[]{:S(2)}, u32[]{:S(2)}) collective-permute-start(f32[2,256,128]{2,1,0:T(8,128)S(1)} %pad_maximum_fusion.f0), channel_id=1, source_target_pairs={{0,2},{2,0},{1,3},{3,1},{4,6},{6,4},{5,7},{7,5},{8,10},{10,8},{9,1... | collective-permute-start | bytes 786440 | tf_op jit(solution)/shard_map/ppermute | solution.py:27
  33.9 13.9 %collective-permute-start.2 = (f32[2,256,128]{2,1,0:T(8,128)S(1)}, f32[2,256,128]{2,1,0:T(8,128)}, u32[]{:S(2)}, u32[]{:S(2)}) collective-permute-start(f32[2,256,128]{2,1,0:T(8,128)S(1)} %pad_maximum_fusion.f0), channel_id=1, source_target_pairs={{0,1},{1,0},{2,3},{3,2},{4,5},{5,4},{6,7},{7,6},{8,9},{9,8},{10,11... | collective-permute-start | bytes 786440 | tf_op jit(solution)/shard_map/ppermute | solution.py:27
  42.1 5.8 %collective-permute-start.3 = (f32[2,256,128]{2,1,0:T(8,128)}, f32[2,256,128]{2,1,0:T(8,128)}, u32[]{:S(2)}, u32[]{:S(2)}) collective-permute-start(f32[2,256,128]{2,1,0:T(8,128)} %collective-permute-done.1.f1), channel_id=1, source_target_pairs={{0,1},{1,0},{2,3},{3,2},{4,5},{5,4},{6,7},{7,6},{8,9},{9,8},{10,11... | collective-permute-start | bytes 786440 | tf_op jit(solution)/shard_map/ppermute | solution.py:27
  43.5 4.3 %copy-start.2 = (f32[1024]{0:T(1024)S(1)}, f32[1024]{0:T(1024)}, u32[]{:S(2)}) copy-start(f32[1024]{0:T(1024)} %param.9) | copy-start | bytes 12292
  47.8 7.5 %copy-start.4 = (bf16[1024,4096]{1,0:T(8,128)(2,1)}, bf16[1024,4096]{1,0:T(8,128)(2,1)S(1)}, u32[]{:S(2)}) copy-start(bf16[1024,4096]{1,0:T(8,128)(2,1)S(1)} %get-tuple-element.13.s_ref) | copy-start | bytes 25165828
  47.8 44.8 %copy-start.7 = (f32[256,4096]{1,0:T(8,128)}, f32[256,4096]{1,0:T(8,128)S(1)}, u32[]{:S(2)}) copy-start(f32[256,4096]{1,0:T(8,128)S(1)} %get-tuple-element.14.h_ref) | copy-start | bytes 12582916
  82.2 3.7 %collective-permute-start.4 = (f32[2,128]{1,0:T(2,128)S(1)}, f32[2,128]{1,0:T(2,128)S(1)}, u32[]{:S(2)}, u32[]{:S(2)}) collective-permute-start(f32[2,128]{1,0:T(2,128)S(1)} %get-tuple-element.16), channel_id=1, source_target_pairs={{0,1},{1,0},{2,3},{3,2},{4,5},{5,4},{6,7},{7,6},{8,9},{9,8},{10,11... | collective-permute-start | bytes 3080 | tf_op jit(solution)/shard_map/ppermute | solution.py:27
  86.0 2.5 %collective-permute-start.5 = (f32[2,128]{1,0:T(2,128)S(1)}, f32[2,128]{1,0:T(2,128)S(1)}, u32[]{:S(2)}, u32[]{:S(2)}) collective-permute-start(f32[2,128]{1,0:T(2,128)S(1)} %add_select_fusion.5), channel_id=1, source_target_pairs={{0,2},{2,0},{1,3},{3,1},{4,6},{6,4},{5,7},{7,5},{8,10},{10,8},{9,1... | collective-permute-start | bytes 3080 | tf_op jit(solution)/shard_map/ppermute | solution.py:27
  88.5 3.9 %collective-permute-start.6 = (f32[2,128]{1,0:T(2,128)S(1)}, f32[2,128]{1,0:T(2,128)S(1)}, u32[]{:S(2)}, u32[]{:S(2)}) collective-permute-start(f32[2,128]{1,0:T(2,128)S(1)} %add_select_fusion.4), channel_id=1, source_target_pairs={{0,16},{16,0},{1,17},{17,1},{2,18},{18,2},{3,19},{19,3},{4,20},{20... | collective-permute-start | bytes 3080 | tf_op jit(solution)/shard_map/ppermute | solution.py:27
  92.6 3.4 %copy-start.5 = (bf16[1024,4096]{1,0:T(8,128)(2,1)S(1)}, bf16[1024,4096]{1,0:T(8,128)(2,1)}, u32[]{:S(2)}) copy-start(bf16[1024,4096]{1,0:T(8,128)(2,1)} %copy-done.4) | copy-start | bytes 25165828
  102.1 4.2 %collective-permute-start.7 = (f32[4,264,128]{2,1,0:T(8,128)S(1)}, f32[4,264,128]{2,1,0:T(8,128)S(1)}, u32[]{:S(2)}, u32[]{:S(2)}) collective-permute-start(f32[4,264,128]{2,1,0:T(8,128)S(1)} %get-tuple-element.18), channel_id=1, source_target_pairs={{0,1},{1,0},{2,3},{3,2},{4,5},{5,4},{6,7},{7,6},{8,9},{9,8},{10,11... | collective-permute-start | bytes 1622024 | tf_op jit(solution)/shard_map/ppermute | solution.py:27
  132.5 4.0 %collective-permute-start.8 = (f32[4,264,128]{2,1,0:T(8,128)S(1)}, f32[4,264,128]{2,1,0:T(8,128)S(1)}, u32[]{:S(2)}, u32[]{:S(2)}) collective-permute-start(f32[4,264,128]{2,1,0:T(8,128)S(1)} %all_to_all.37.g0), channel_id=1, source_target_pairs={{0,1},{1,0},{2,3},{3,2},{4,5},{5,4},{6,7},{7,6},{8,9},{9,8},{10,11... | collective-permute-start | bytes 1622024 | tf_op jit(solution)/shard_map/ppermute | solution.py:27
  136.5 0.9 copy-start.9
  137.4 3.4 %copy-start.6 = (bf16[1024,4096]{1,0:T(8,128)(2,1)S(1)}, bf16[1024,4096]{1,0:T(8,128)(2,1)}, u32[]{:S(2)}) copy-start(bf16[1024,4096]{1,0:T(8,128)(2,1)} %copy-done.4) | copy-start | bytes 25165828
  140.8 2.2 %copy-start.8 = (f32[256,4096]{1,0:T(8,128)S(1)}, f32[256,4096]{1,0:T(8,128)}, u32[]{:S(2)}) copy-start(f32[256,4096]{1,0:T(8,128)} %copy-done.7) | copy-start | bytes 12582916
  143.0 48.9 %copy-start.1 = (f32[32,1024]{1,0:T(8,128)S(1)}, f32[32,1024]{1,0:T(8,128)}, u32[]{:S(2)}) copy-start(f32[32,1024]{1,0:T(8,128)} %f_ref.1) | copy-start | bytes 393220
  174.1 2.7 %collective-permute-start.9 = (f32[2,128]{1,0:T(2,128)S(1)}, f32[2,128]{1,0:T(2,128)S(1)}, u32[]{:S(2)}, u32[]{:S(2)}) collective-permute-start(f32[2,128]{1,0:T(2,128)S(1)} %get-tuple-element.20), channel_id=1, source_target_pairs={{0,1},{1,0},{2,3},{3,2},{4,5},{5,4},{6,7},{7,6},{8,9},{9,8},{10,11... | collective-permute-start | bytes 3080 | tf_op jit(solution)/shard_map/ppermute | solution.py:27
  176.9 2.4 %collective-permute-start.10 = (f32[2,128]{1,0:T(2,128)S(1)}, f32[2,128]{1,0:T(2,128)S(1)}, u32[]{:S(2)}, u32[]{:S(2)}) collective-permute-start(f32[2,128]{1,0:T(2,128)S(1)} %add_select_fusion.2), channel_id=1, source_target_pairs={{0,2},{2,0},{1,3},{3,1},{4,6},{6,4},{5,7},{7,5},{8,10},{10,8},{9,1... | collective-permute-start | bytes 3080 | tf_op jit(solution)/shard_map/ppermute | solution.py:27
  179.4 5.0 %collective-permute-start.11 = (f32[2,128]{1,0:T(2,128)S(1)}, f32[2,128]{1,0:T(2,128)S(1)}, u32[]{:S(2)}, u32[]{:S(2)}) collective-permute-start(f32[2,128]{1,0:T(2,128)S(1)} %add_select_fusion.1), channel_id=1, source_target_pairs={{0,16},{16,0},{1,17},{17,1},{2,18},{18,2},{3,19},{19,3},{4,20},{20... | collective-permute-start | bytes 3080 | tf_op jit(solution)/shard_map/ppermute | solution.py:27
  180.3 11.5 %all-to-all-start.4 = ((f32[4,40,256]{2,1,0:T(8,128)}), f32[4,40,256]{2,1,0:T(8,128)S(1)}, u32[]{:S(2)}, u32[]{:S(2)}) async-start(f32[4,40,256]{2,1,0:T(8,128)} %pad_maximum_fusion.1), calls=%async_computation.4 | async-start | bytes 327680 | tf_op jit(solution)/shard_map/all_to_all | solution.py:343

commit v3 on v2

--- a/solution.py
+++ b/solution.py
@@ -7,6 +7,7 @@
 from jax.experimental.pallas import tpu as pltpu
 from jax.sharding import Mesh
 from jax.sharding import PartitionSpec as P
+
 
 GRP = ("xl", "y")
 SMP = ("xh", "zh", "zl", "c")
@@ -17,6 +18,7 @@
 ROWS = 32
 NB = 8
 TILE = 1024
+LIMIT = 14
 EXTRA = 128
 F32, BF16 = jnp.float32, jnp.bfloat16
 VMEM = pl.BlockSpec(memory_space=pltpu.VMEM)
@@ -40,16 +42,15 @@
     return pltpu.with_memory_space_constraint(x, pltpu.VMEM)
 
 
-def call(kernel, ins, outs, scratch=(), flops=0, name=None):
+def call(kernel, ins, outs, scratch=(), flops=0):
     return pl.pallas_call(
         kernel,
         in_specs=ins,
         out_specs=[VMEM] * len(outs),
         out_shape=outs,
         scratch_shapes=scratch,
-        compiler_params=pltpu.CompilerParams(vmem_limit_bytes=40 << 20),
+        compiler_params=pltpu.CompilerParams(vmem_limit_bytes=LIMIT << 20),
         cost_estimate=pl.CostEstimate(flops=flops, bytes_accessed=1 << 20, transcendentals=0),
-        name=name,
     )
 
 
@@ -67,32 +68,37 @@
     return jnp.full((1, EXTRA), jnp.sum(x), F32)
 
 
-def hidden_kernel(pos_ref, packed_ref, wt_ref, hb_ref, s_ref, h_ref):
-    units = wt_ref.shape[0]
+def hidden_kernel(pos_ref, packed_ref, w_ref, hb_ref, s_ref, h_ref, wt):
+    units = wt.shape[0]
+    mine = pl.ds(pl.multiple_of(pos_ref[32] * units, units), units)
+    for b in range(NB):
+        rows = [w_ref[pl.ds(pl.multiple_of(pos_ref[4 * b + k] * ROWS, ROWS), ROWS), mine] for k in range(4)]
+        block = jnp.concatenate(rows, axis=0).astype(F32)
+        wt[:, b * 128 : (b + 1) * 128] = block.T.astype(BF16)
     shifts = 31 - lax.broadcasted_iota(jnp.int32, (ROWS, TILE), 0)
-    hb = rows_to_column(hb_ref[pl.ds(pos_ref[32] * (units // 128), units // 128), :])
+    hb = rows_to_column(my_rows(pos_ref, hb_ref, units))
 
     def step(t, carry):
         for q in range(32):
             word = packed_ref[t, pl.ds(pos_ref[q], 1), :]
             up = jnp.left_shift(jnp.broadcast_to(word, (ROWS, TILE)), shifts) < 0
             s_ref[q * ROWS : (q + 1) * ROWS, cols(t)] = jnp.where(up, 1.0, -1.0).astype(BF16)
-        pre = jnp.dot(wt_ref[...], s_ref[:, cols(t)], preferred_element_type=F32)
+        pre = jnp.dot(wt[...], s_ref[:, cols(t)], preferred_element_type=F32)
         h_ref[:, cols(t)] = jnp.tanh(pre + hb)
         return carry
 
     lax.fori_loop(0, packed_ref.shape[0], step, 0)
 
 
-def hidden_pass(pos, packed, wt, hb):
-    units, n = wt.shape[0], packed.shape[0] * TILE
+def hidden_pass(pos, packed, w, hb, units):
+    n = packed.shape[0] * TILE
     return call(
         hidden_kernel,
         [SMEM, VMEM, VMEM, VMEM],
         [pltpu.VMEM((NB * 128, n), BF16), pltpu.VMEM((units, n), F32)],
+        [pltpu.VMEM((units, NB * 128), BF16)],
         flops=4 * 10**9,
-        name="hidden_pass",
-    )(pos, packed, wt, hb)
+    )(pos, packed, w, hb)
 
 
 def project(s_ref, h_ref, lhs, bias, p_ref):
@@ -139,7 +145,6 @@
         [jax.ShapeDtypeStruct((n // TILE, TILE + EXTRA), F32)],
         [pltpu.VMEM((2 * units, NB * 128), BF16)],
         flops=4 * 10**9,
-        name="first_pass",
     )(pos, resident(spins), resident(hidden), *f, fb)[0]
 
 
@@ -176,7 +181,6 @@
         [jax.ShapeDtypeStruct((n // TILE, TILE + EXTRA), F32)],
         [pltpu.VMEM((2 * units, NB * 128), BF16)],
         flops=4 * 10**9,
-        name="second_pass",
     )(pos, resident(spins), resident(hidden), *f, fb, g0, g1, st, norm)[0]
 
 
@@ -199,9 +203,7 @@
 def first_sum(got):
     parts = got.shape[1]
     shape = lambda *s: jax.ShapeDtypeStruct(s, F32)
-    return call(first_sum_kernel, [VMEM], [shape(parts, TILE), shape(2, 128), shape(parts, EXTRA)], name="first_sum")(
-        got
-    )
+    return call(first_sum_kernel, [VMEM], [shape(parts, TILE), shape(2, 128), shape(parts, EXTRA)])(got)
 
 
 def second_sum_kernel(got_ref, v_ref, norm_ref, st_ref, next_ref):
@@ -215,9 +217,7 @@
 
 def second_sum(got, values, norm):
     shape = lambda *s: jax.ShapeDtypeStruct(s, F32)
-    return call(second_sum_kernel, [VMEM] * 3, [shape(2, 128), shape(got.shape[1], EXTRA)], name="second_sum")(
-        got, values, norm
-    )
+    return call(second_sum_kernel, [VMEM] * 3, [shape(2, 128), shape(got.shape[1], EXTRA)])(got, values, norm)
 
 
 def merged(st, count, axis):
@@ -271,11 +271,33 @@
         [jax.ShapeDtypeStruct((4, units + 8, 128), F32)] * 2,
         [pltpu.VMEM((units, NB * 128), F32), pltpu.VMEM((units, 128), F32)],
         flops=4 * 10**9,
-        name="image_pass",
     )(pos, resident(spins), resident(hidden), values, st)
 
 
-def update_kernel(samples, f_ref, fb_ref, g_ref, st0_ref, norm_ref, st1_ref, next_ref, w_ref, b_ref):
+def image_sum_kernel(pos_ref, got_ref, all_ref, r0, r1, r2, r3, turned):
+    units = r0.shape[1]
+    x = got_ref[0] + got_ref[1] + (got_ref[2] + got_ref[3])
+    for k in range(4):
+        all_ref[k] = x
+    turned[...] = x[:units].T
+    bias = jnp.concatenate([x[units + k : units + k + 1, :] for k in range(units // 128)], axis=1)
+    for d, ref in enumerate((r0, r1, r2, r3)):
+        to = (pos_ref[32] + d) % 4
+        ref[:ROWS, :] = turned[pl.ds(pl.multiple_of(to * ROWS, ROWS), ROWS), :]
+        ref[ROWS:, :] = jnp.broadcast_to(bias, (ref.shape[0] - ROWS, units))
+
+
+def image_sum(pos, got, units):
+    shape = lambda *s: jax.ShapeDtypeStruct(s, F32)
+    return call(
+        image_sum_kernel,
+        [SMEM, VMEM],
+        [shape(*got.shape)] + [shape(ROWS + 8, units)] * 4,
+        [pltpu.VMEM((128, units), F32)],
+    )(pos, got)
+
+
+def update_kernel(samples, pos_ref, f_ref, fb_ref, g0, g1, g2, g3, st0_ref, norm_ref, st1_ref, next_ref, w_ref, b_ref):
     norm0, norm1 = norm_ref[0:1, 0:1], next_ref[0:1, 0:1]
     cross = next_ref[1:2, 0:1]
     beta = norm1 / norm0
@@ -286,20 +308,21 @@
         r = f - step0 * (g + LAM * f)
         return step0 * f + step1 * (r + beta * f)
 
-    units = g_ref.shape[2]
-    for k in range(g_ref.shape[0]):
-        at = slice(k * units, (k + 1) * units)
-        w_ref[:, at] = update(f_ref[:, at], g_ref[k, :ROWS, :])
+    units = g0.shape[1]
+    for d, g_ref in enumerate((g0, g1, g2, g3)):
+        source = (pos_ref[32] + 4 - d) % 4
+        at = pl.ds(pl.multiple_of(source * units, units), units)
+        w_ref[:, at] = update(f_ref[:, at], g_ref[:ROWS, :])
         for h in range(units // 128):
-            row = slice(k * (units // 128) + h, k * (units // 128) + h + 1)
-            b_ref[row, :] = update(fb_ref[row, :], g_ref[k, ROWS : ROWS + 1, h * 128 : (h + 1) * 128])
-
-
-def update_pass(samples, f, fb, g, st0, norm, st1, norms):
+            row = pl.ds(source * (units // 128) + h, 1)
+            b_ref[row, :] = update(fb_ref[row, :], g_ref[ROWS : ROWS + 1, h * 128 : (h + 1) * 128])
+
+
+def update_pass(samples, pos, f, fb, g, st0, norm, st1, norms):
     shape = lambda s: jax.ShapeDtypeStruct(s, F32)
     return call(
-        functools.partial(update_kernel, samples), [VMEM] * 7, [shape(f.shape), shape(fb.shape)], name="update_pass"
-    )(f, fb, g, st0, norm, st1, norms)
+        functools.partial(update_kernel, samples), [SMEM] + [VMEM] * 10, [shape(f.shape), shape(fb.shape)]
+    )(pos, f, fb, *g, st0, norm, st1, norms)
 
 
 def body(spins_packed, weight, hidden_bias, force_w, force_b):
@@ -317,19 +340,14 @@
     blocks = ((k & 1) ^ xh) * 2 + ((k >> 1) ^ zl)
     pos = jnp.concatenate([words, zh.reshape(1), blocks])
 
-    f_cols = force_w.reshape(ROWS, parts, units).transpose(1, 0, 2)
+    f_cols = jnp.stack([force_w[:, k * units : (k + 1) * units] for k in range(parts)])
     f = lax.all_to_all(f_cols, "zh", 0, 0, tiled=True).reshape(parts * ROWS, units).T[None]
     f = jnp.concatenate([f, swap(f, "xh")], axis=0)
     f_zl = swap(f, "zl")
     f = (f, f_zl, swap(f, "c"), swap(f_zl, "c"))
 
     packed = to_all(spins_packed, "zh", parts)
-    w = lax.dynamic_slice_in_dim(weight, zh * units, units, 1).reshape(2, parts, 2, 2, ROWS, units)
-    for dim, bit in ((0, xh), (2, zl), (3, c)):
-        w = jnp.where(bit == 1, jnp.flip(w, dim), w)
-    wt = w.transpose(3, 2, 0, 1, 4, 5).reshape(NB * 128, units).T
-
-    spins, hidden = hidden_pass(pos, packed, wt, hb)
+    spins, hidden = hidden_pass(pos, packed, weight, hb, units)
     partial = first_pass(pos, spins, hidden, f, fb)
     values, st, norm = first_sum(to_all(partial, SUM, summed))
     n = values.size
@@ -337,16 +355,14 @@
 
     keep, send = image_pass(samples, pos, spins, hidden, values, st0)
     g = keep + swap(send, "c")
-    g = lax.all_to_all(g, QUAD, 0, 0, tiled=True).sum(axis=0)
-    g_mine = g[:units].T.reshape(parts, ROWS, units)
-    gb = jnp.broadcast_to(g[units : units + units // 128].reshape(1, 1, units), (parts, 8, units))
-    g_mine = lax.all_to_all(jnp.concatenate([g_mine, gb], axis=1), "zh", 0, 0, tiled=True)
-    g = to_all(g, QUAD, 4)
+    g, *rows = image_sum(pos, lax.all_to_all(g, QUAD, 0, 0, tiled=True), units)
+    rows = [rows[0]] + [lax.ppermute(rows[d], "zh", [(i, (i + d) % 4) for i in range(4)]) for d in (1, 2, 3)]
+    g = lax.all_to_all(g, QUAD, 0, 0, tiled=True)
 
     partial = second_pass(samples, pos, spins, hidden, f, fb, g, swap(g, "c"), st0, norm)
     st, norms = second_sum(to_all(partial, SUM, summed), values, norm)
     st1 = over_sets(st, n)
-    out_w, out_b = update_pass(samples, force_w, fb, g_mine, st0, norm, st1, norms)
+    out_w, out_b = update_pass(samples, pos, force_w, fb, rows, st0, norm, st1, norms)
     return out_w, out_b.reshape(-1)
 
 

time: 195 us -> 183 us (0.938)
  blocking collectives: 75.8 us -> 92.6 us
  local copies, waits for them, and re-layouts: 16 us -> 5.12 us
  waiting for transfers between devices: 29.1 us -> 21.7 us
  starting transfers between devices: 40.3 us -> 33.7 us
  other arithmetic: 3.81 us -> 0.66 us
    all_to_all x1 -> x3, blocking collectives: 14.6 us -> 41.8 us  [the longest x1 16 us: body(): lax.all_to_all(f_cols, 'zh', 0, 0, tiled=True).reshape(parts * ROWS, units)]
    all_to_all x2 -> x0, waiting for transfers between devices: 13.6 us -> none  [the longest x1 7.34 us: body(): lax.all_to_all(jnp.concatenate([g_mine, gb], axis=1), 'zh', 0, 0, tiled=T...]
    all_to_all x2 -> x0, starting transfers between devices: 13.1 us -> none  [the longest x1 9 us: body(): lax.all_to_all(f_cols, 'zh', 0, 0, tiled=True).reshape(parts * ROWS, units)]
    all_to_all x3 -> x2, blocking collectives: 61.2 us -> 50.7 us  [to_all(): lax.all_to_all(jnp.broadcast_to(x[None], (size, *x.shape)), axes, 0, 0, t...]
    unnamed x20 -> x8, local copies, waits for them, and re-layouts: 9.84 us -> 2.29 us
    ppermute x0 -> x3, starting transfers between devices: none -> 6.38 us  [body(): lax.ppermute(rows[d], 'zh', [(i, (i + d) % 4) for i in range(4)])]
    ppermute x0 -> x3, waiting for transfers between devices: none -> 3.1 us  [body(): lax.ppermute(rows[d], 'zh', [(i, (i + d) % 4) for i in range(4)])]
    ppermute x12, waiting for transfers between devices: 15.6 us -> 18.6 us  [swap(): return lax.ppermute(x, axis, SWAP)]
  transfers between devices with their start and end apart: 15 -> 16, of which waited for: 11 -> 10; matrix products, arithmetic and copies ran while one was open for 3% -> 0% of each run, Pallas kernels for 2% -> 2%
where the time goes in v3:
time: 183 us; the launch traced here: 181 us
  blocking collectives  92.6 us (51%)
  starting transfers between devices  33.7 us (18%)
  Pallas kernels  25.9 us (14%)
  waiting for transfers between devices  21.7 us (12%)
  local copies, waits for them, and re-layouts  5.12 us (3%)
    all_to_all x2, blocking collectives, to_all(): lax.all_to_all(jnp.broadcast_to(x[None], (size, *x.shape)), axes, 0, 0, t...  50.7 us
    ppermute x12, starting transfers between devices, swap(): return lax.ppermute(x, axis, SWAP)  23.9 us
    ppermute x12, waiting for transfers between devices, swap(): return lax.ppermute(x, axis, SWAP)  18.6 us
    all_to_all x1, blocking collectives, body(): lax.all_to_all(f_cols, 'zh', 0, 0, tiled=True).reshape(parts * ROWS, units)  16 us
    all_to_all x1, blocking collectives, body(): g, *rows = image_sum(pos, lax.all_to_all(g, QUAD, 0, 0, tiled=True), units)  14.4 us
    all_to_all x1, blocking collectives, body(): g = lax.all_to_all(g, QUAD, 0, 0, tiled=True)  11.4 us
    pallas_call x1, Pallas kernels, second_pass(): call(functools.partial(second_kernel, samples), [SMEM] + [VMEM] * 11, [ja...  6.57 us
    ppermute x3, starting transfers between devices, body(): lax.ppermute(rows[d], 'zh', [(i, (i + d) % 4) for i in range(4)])  6.38 us
  transfers between devices with their start and end apart: 16, of which 10 were waited for; matrix products, arithmetic and copies ran while one was open for 0% of the time, Pallas kernels for 2%

profile of v3, /device:TPU:1, one launch (start us, length us, event | category | flops | bytes accessed | tf_op | source)
XLA Modules:
  0.0 180.5 jit_solution(479430452340054163)
XLA Ops:
  0.6 0.8 slice_bitcast_fusion.3
  1.5 16.0 %all_to_all.30 = f32[4,32,256]{2,1,0:T(8,128)S(1)} all-to-all(f32[4,32,256]{2,1,0:T(8,128)S(1)} %pad_maximum_fusion.1), channel_id=1, replica_groups=mesh['xl'=2,'y'=4,'xh'=2,'zh'=4,'zl'=2,'c'=2] {'zh'}, dimensions={0} | all-to-all | bytes 262144 | tf_op jit(solution)/shard_map/all_to_all | solution.py:344
  17.5 1.8 broadcast_in_dim.8
  19.3 3.5 %all-to-all-start = ((s32[4,32,1024]{2,1,0:T(8,128)}), s32[4,32,1024]{2,1,0:T(8,128)S(1)}, u32[]{:S(2)}, u32[]{:S(2)}) async-start(s32[4,32,1024]{2,1,0:T(8,128)} %broadcast_in_dim.8), calls=%async_computation | async-start | bytes 1048576 | tf_op jit(solution)/shard_map/all_to_all | solution.py:33
  22.7 0.1 copy.8
  22.8 2.8 %collective-permute-start = (f32[1,256,128]{2,1,0:T(8,128)S(1)}, f32[1,256,128]{2,1,0:T(8,128)S(1)}, u32[]{:S(2)}, u32[]{:S(2)}) collective-permute-start(f32[1,256,128]{2,1,0:T(8,128)S(1)} %bitcast.33), channel_id=1, source_target_pairs={{0,16},{16,0},{1,17},{17,1},{2,18},{18,2},{3,19},{19,3},{4,20},{20... | collective-permute-start | bytes 393224 | tf_op jit(solution)/shard_map/ppermute | solution.py:29
  25.7 2.6 %collective-permute-done = f32[1,256,128]{2,1,0:T(8,128)S(1)} collective-permute-done((f32[1,256,128]{2,1,0:T(8,128)S(1)}, f32[1,256,128]{2,1,0:T(8,128)S(1)}, u32[]{:S(2)}, u32[]{:S(2)}) %collective-permute-start) | collective-permute-done | bytes 131104 | tf_op jit(solution)/shard_map/ppermute | solution.py:29
  28.3 0.8 collective-permute-start.1
  29.1 0.1 pad_add_fusion.pos_ref
  29.2 4.4 %collective-permute-start.2 = (f32[2,256,128]{2,1,0:T(8,128)S(1)}, f32[2,256,128]{2,1,0:T(8,128)S(1)}, u32[]{:S(2)}, u32[]{:S(2)}) collective-permute-start(f32[2,256,128]{2,1,0:T(8,128)S(1)} %pad_maximum_fusion.f0), channel_id=1, source_target_pairs={{0,1},{1,0},{2,3},{3,2},{4,5},{5,4},{6,7},{7,6},{8,9},{9,8},{10,11... | collective-permute-start | bytes 786440 | tf_op jit(solution)/shard_map/ppermute | solution.py:29
  33.6 6.2 %collective-permute-done.1.f1 = f32[2,256,128]{2,1,0:T(8,128)S(1)} collective-permute-done((f32[2,256,128]{2,1,0:T(8,128)S(1)}, f32[2,256,128]{2,1,0:T(8,128)S(1)}, u32[]{:S(2)}, u32[]{:S(2)}) %collective-permute-start.1) | collective-permute-done | bytes 262176 | tf_op jit(solution)/shard_map/ppermute | solution.py:29
  39.8 2.4 %collective-permute-start.3 = (f32[2,256,128]{2,1,0:T(8,128)S(1)}, f32[2,256,128]{2,1,0:T(8,128)S(1)}, u32[]{:S(2)}, u32[]{:S(2)}) collective-permute-start(f32[2,256,128]{2,1,0:T(8,128)S(1)} %collective-permute-done.1.f1), channel_id=1, source_target_pairs={{0,1},{1,0},{2,3},{3,2},{4,5},{5,4},{6,7},{7,6},{8,9},{9,8},{10,11... | collective-permute-start | bytes 786440 | tf_op jit(solution)/shard_map/ppermute | solution.py:29
  42.2 1.6 copy-done.2
  43.8 0.7 copy-done.3
  44.5 4.4 %shard_map.68 = (bf16[1024,4096]{1,0:T(8,128)(2,1)S(1)}, f32[256,4096]{1,0:T(8,128)S(1)}) custom-call(s32[37]{0:T(128)S(1)} %pad_add_fusion.pos_ref, s32[4,32,1024]{2,1,0:T(8,128)S(1)} %all-to-all-done.packed_ref, bf16[1024,1024]{1,0:T(8,128)(2,1)S(1)} %copy-done.2, f32[8,128]{1,0:T(8,128)S(1)} %bitcast.31), custom_call_target="tpu_custom_call" | custom-call | flops 4000000000 | bytes 1048576 | tf_op jit(solution)/shard_map/pallas_call | solution.py:95
  49.0 6.2 %shard_map.69 = f32[4,1152]{1,0:T(4,128)S(1)} custom-call(s32[37]{0:T(128)S(1)} %pad_add_fusion.pos_ref, bf16[1024,4096]{1,0:T(8,128)(2,1)S(1)} %get-tuple-element.18.s_ref, f32[256,4096]{1,0:T(8,128)S(1)} %get-tuple-element.19.h_ref, f32[2,256,128]{2,1,0:T(8,128)S(1)} %pad_maximum_fusion.f0, f32[2,256,128]{2,1,0:T(8,128)S(1)} %collective-permute-done.1.f1, ...), custom_call_target="tpu_custom_call" | custom-call | flops 4000000000 | bytes 1048576 | tf_op jit(solution)/shard_map/pallas_call | solution.py:142
  55.2 0.1 broadcast_in_dim.10
  55.3 27.2 %all_to_all.31.got_ref = f32[32,4,1152]{2,1,0:T(4,128)S(1)} all-to-all(f32[32,4,1152]{2,1,0:T(4,128)S(1)} %broadcast_in_dim.10), channel_id=1, replica_groups=mesh['xl'=2,'y'=4,'xh'=2,'zh'=4,'zl'=2,'c'=2] {'zh','xl','y'}, dimensions={0} | all-to-all | bytes 1179648 | tf_op jit(solution)/shard_map/all_to_all | solution.py:33
  82.5 0.3 shard_map.70
  82.8 2.4 %collective-permute-start.4 = (f32[2,128]{1,0:T(2,128)S(1)}, f32[2,128]{1,0:T(2,128)S(1)}, u32[]{:S(2)}, u32[]{:S(2)}) collective-permute-start(f32[2,128]{1,0:T(2,128)S(1)} %get-tuple-element.21), channel_id=1, source_target_pairs={{0,1},{1,0},{2,3},{3,2},{4,5},{5,4},{6,7},{7,6},{8,9},{9,8},{10,11... | collective-permute-start | bytes 3080 | tf_op jit(solution)/shard_map/ppermute | solution.py:29
  85.2 0.8 collective-permute-done.4
  86.0 0.1 add_select_fusion.5
  86.1 1.3 collective-permute-start.5
  87.4 1.1 collective-permute-done.5
  88.5 0.1 add_select_fusion.4
  88.6 2.4 %collective-permute-start.6 = (f32[2,128]{1,0:T(2,128)S(1)}, f32[2,128]{1,0:T(2,128)S(1)}, u32[]{:S(2)}, u32[]{:S(2)}) collective-permute-start(f32[2,128]{1,0:T(2,128)S(1)} %add_select_fusion.4), channel_id=1, source_target_pairs={{0,16},{16,0},{1,17},{17,1},{2,18},{18,2},{3,19},{19,3},{4,20},{20... | collective-permute-start | bytes 3080 | tf_op jit(solution)/shard_map/ppermute | solution.py:29
  91.0 1.6 collective-permute-done.6
  92.6 6.2 %shard_map.71 = (f32[4,264,128]{2,1,0:T(8,128)S(1)}, f32[4,264,128]{2,1,0:T(8,128)S(1)}) custom-call(s32[37]{0:T(128)S(1)} %pad_add_fusion.pos_ref, bf16[1024,4096]{1,0:T(8,128)(2,1)S(1)} %get-tuple-element.18.s_ref, f32[256,4096]{1,0:T(8,128)S(1)} %get-tuple-element.19.h_ref, f32[4,1024]{1,0:T(4,128)S(1)} %get-tuple-element.20.v_ref, ...), custom_call_target="tpu_custom_call" | custom-call | flops 4000000000 | bytes 1048576 | tf_op jit(solution)/shard_map/pallas_call | solution.py:268
  98.8 2.7 %collective-permute-start.7 = (f32[4,264,128]{2,1,0:T(8,128)S(1)}, f32[4,264,128]{2,1,0:T(8,128)S(1)}, u32[]{:S(2)}, u32[]{:S(2)}) collective-permute-start(f32[4,264,128]{2,1,0:T(8,128)S(1)} %get-tuple-element.23), channel_id=1, source_target_pairs={{0,1},{1,0},{2,3},{3,2},{4,5},{5,4},{6,7},{7,6},{8,9},{9,8},{10,11... | collective-permute-start | bytes 1622024 | tf_op jit(solution)/shard_map/ppermute | solution.py:29
  101.5 1.6 collective-permute-done.7
  103.1 14.4 %all_to_all.32.got_ref = f32[4,264,128]{2,1,0:T(8,128)S(1)} all-to-all(f32[4,264,128]{2,1,0:T(8,128)S(1)} %add.115), channel_id=1, replica_groups=mesh['xl'=2,'y'=4,'xh'=2,'zh'=4,'zl'=2,'c'=2] {'xh','zl'}, dimensions={0} | all-to-all | bytes 1081344 | tf_op jit(solution)/shard_map/all_to_all | solution.py:358
  117.6 0.7 shard_map.72
  118.2 11.4 %all_to_all.33.g0 = f32[4,264,128]{2,1,0:T(8,128)S(1)} all-to-all(f32[4,264,128]{2,1,0:T(8,128)S(1)} %get-tuple-element.29), channel_id=1, replica_groups=mesh['xl'=2,'y'=4,'xh'=2,'zh'=4,'zl'=2,'c'=2] {'xh','zl'}, dimensions={0} | all-to-all | bytes 1081344 | tf_op jit(solution)/shard_map/all_to_all | solution.py:360
  129.6 2.5 %collective-permute-start.11 = (f32[4,264,128]{2,1,0:T(8,128)S(1)}, f32[4,264,128]{2,1,0:T(8,128)S(1)}, u32[]{:S(2)}, u32[]{:S(2)}) collective-permute-start(f32[4,264,128]{2,1,0:T(8,128)S(1)} %all_to_all.33.g0), channel_id=1, source_target_pairs={{0,1},{1,0},{2,3},{3,2},{4,5},{5,4},{6,7},{7,6},{8,9},{9,8},{10,11... | collective-permute-start | bytes 1622024 | tf_op jit(solution)/shard_map/ppermute | solution.py:29
  132.0 1.6 collective-permute-done.11.g1
  133.6 6.6 %shard_map.73 = f32[4,1152]{1,0:T(4,128)S(1)} custom-call(s32[37]{0:T(128)S(1)} %pad_add_fusion.pos_ref, bf16[1024,4096]{1,0:T(8,128)(2,1)S(1)} %get-tuple-element.18.s_ref, f32[256,4096]{1,0:T(8,128)S(1)} %get-tuple-element.19.h_ref, f32[2,256,128]{2,1,0:T(8,128)S(1)} %pad_maximum_fusion.f0, f32[2,256,128]{2,1,0:T(8,128)S(1)} %collective-permute-done.1.f1, ...), custom_call_target="tpu_custom_call" | custom-call | flops 4000000000 | bytes 1048576 | tf_op jit(solution)/shard_map/pallas_call | solution.py:178
  140.2 0.1 broadcast_in_dim.11
  140.3 23.5 %all_to_all.34.got_ref = f32[32,4,1152]{2,1,0:T(4,128)S(1)} all-to-all(f32[32,4,1152]{2,1,0:T(4,128)S(1)} %broadcast_in_dim.11), channel_id=1, replica_groups=mesh['xl'=2,'y'=4,'xh'=2,'zh'=4,'zl'=2,'c'=2] {'zh','xl','y'}, dimensions={0} | all-to-all | bytes 1179648 | tf_op jit(solution)/shard_map/all_to_all | solution.py:33
  163.8 0.3 shard_map.74
  164.1 1.8 %collective-permute-start.12 = (f32[2,128]{1,0:T(2,128)S(1)}, f32[2,128]{1,0:T(2,128)S(1)}, u32[]{:S(2)}, u32[]{:S(2)}) collective-permute-start(f32[2,128]{1,0:T(2,128)S(1)} %get-tuple-element.30), channel_id=1, source_target_pairs={{0,1},{1,0},{2,3},{3,2},{4,5},{5,4},{6,7},{7,6},{8,9},{9,8},{10,11... | collective-permute-start | bytes 3080 | tf_op jit(solution)/shard_map/ppermute | solution.py:29
  166.0 0.8 collective-permute-done.12
  166.9 2.4 %collective-permute-done.13 = f32[2,128]{1,0:T(2,128)S(1)} collective-permute-done((f32[2,128]{1,0:T(2,128)S(1)}, f32[2,128]{1,0:T(2,128)S(1)}, u32[]{:S(2)}, u32[]{:S(2)}) %collective-permute-start.13) | collective-permute-done | bytes 1056 | tf_op jit(solution)/shard_map/ppermute | solution.py:29
  169.4 0.3 collective-permute-start.14
  169.7 2.8 %collective-permute-start.8 = (f32[40,256]{1,0:T(8,128)S(1)}, f32[40,256]{1,0:T(8,128)S(1)}, u32[]{:S(2)}, u32[]{:S(2)}) collective-permute-start(f32[40,256]{1,0:T(8,128)S(1)} %get-tuple-element.25), channel_id=1, source_target_pairs={{0,4},{4,8},{8,12},{12,0},{1,5},{5,9},{9,13},{13,1},{2,6},{6,10},{... | collective-permute-start | bytes 122888 | tf_op jit(solution)/shard_map/ppermute | solution.py:359
  172.5 0.4 collective-permute-start.9
  172.9 3.2 %collective-permute-start.10 = (f32[40,256]{1,0:T(8,128)S(1)}, f32[40,256]{1,0:T(8,128)S(1)}, u32[]{:S(2)}, u32[]{:S(2)}) collective-permute-start(f32[40,256]{1,0:T(8,128)S(1)} %get-tuple-element.27), channel_id=1, source_target_pairs={{0,12},{4,0},{8,4},{12,8},{1,13},{5,1},{9,5},{13,9},{2,14},{6,2},{... | collective-permute-start | bytes 122888 | tf_op jit(solution)/shard_map/ppermute | solution.py:359
  176.2 3.1 %collective-permute-done.9.g2 = f32[40,256]{1,0:T(8,128)S(1)} collective-permute-done((f32[40,256]{1,0:T(8,128)S(1)}, f32[40,256]{1,0:T(8,128)S(1)}, u32[]{:S(2)}, u32[]{:S(2)}) %collective-permute-start.9) | collective-permute-done | bytes 40992 | tf_op jit(solution)/shard_map/ppermute | solution.py:359
  179.3 1.3 shard_map.75
  (29 shorter events, 0.5 us)
Async XLA Ops:
  19.3 22.9 %all-to-all-start = ((s32[4,32,1024]{2,1,0:T(8,128)}), s32[4,32,1024]{2,1,0:T(8,128)S(1)}, u32[]{:S(2)}, u32[]{:S(2)}) async-start(s32[4,32,1024]{2,1,0:T(8,128)} %broadcast_in_dim.8), calls=%async_computation | async-start | bytes 1048576 | tf_op jit(solution)/shard_map/all_to_all | solution.py:33
  22.8 5.4 %collective-permute-start = (f32[1,256,128]{2,1,0:T(8,128)S(1)}, f32[1,256,128]{2,1,0:T(8,128)S(1)}, u32[]{:S(2)}, u32[]{:S(2)}) collective-permute-start(f32[1,256,128]{2,1,0:T(8,128)S(1)} %bitcast.33), channel_id=1, source_target_pairs={{0,16},{16,0},{1,17},{17,1},{2,18},{18,2},{3,19},{19,3},{4,20},{20... | collective-permute-start | bytes 393224 | tf_op jit(solution)/shard_map/ppermute | solution.py:29
  28.3 11.5 %collective-permute-start.1 = (f32[2,256,128]{2,1,0:T(8,128)S(1)}, f32[2,256,128]{2,1,0:T(8,128)S(1)}, u32[]{:S(2)}, u32[]{:S(2)}) collective-permute-start(f32[2,256,128]{2,1,0:T(8,128)S(1)} %pad_maximum_fusion.f0), channel_id=1, source_target_pairs={{0,2},{2,0},{1,3},{3,1},{4,6},{6,4},{5,7},{7,5},{8,10},{10,8},{9,1... | collective-permute-start | bytes 786440 | tf_op jit(solution)/shard_map/ppermute | solution.py:29
  29.2 19.7 %collective-permute-start.2 = (f32[2,256,128]{2,1,0:T(8,128)S(1)}, f32[2,256,128]{2,1,0:T(8,128)S(1)}, u32[]{:S(2)}, u32[]{:S(2)}) collective-permute-start(f32[2,256,128]{2,1,0:T(8,128)S(1)} %pad_maximum_fusion.f0), channel_id=1, source_target_pairs={{0,1},{1,0},{2,3},{3,2},{4,5},{5,4},{6,7},{7,6},{8,9},{9,8},{10,11... | collective-permute-start | bytes 786440 | tf_op jit(solution)/shard_map/ppermute | solution.py:29
  39.8 9.2 %collective-permute-start.3 = (f32[2,256,128]{2,1,0:T(8,128)S(1)}, f32[2,256,128]{2,1,0:T(8,128)S(1)}, u32[]{:S(2)}, u32[]{:S(2)}) collective-permute-start(f32[2,256,128]{2,1,0:T(8,128)S(1)} %collective-permute-done.1.f1), channel_id=1, source_target_pairs={{0,1},{1,0},{2,3},{3,2},{4,5},{5,4},{6,7},{7,6},{8,9},{9,8},{10,11... | collective-permute-start | bytes 786440 | tf_op jit(solution)/shard_map/ppermute | solution.py:29
  42.2 1.6 copy-start.2
  43.8 0.7 copy-start.3
  44.5 4.4 %copy-start.1 = (f32[1024]{0:T(1024)S(1)}, f32[1024]{0:T(1024)}, u32[]{:S(2)}) copy-start(f32[1024]{0:T(1024)} %param.9) | copy-start | bytes 12292
  82.8 3.2 %collective-permute-start.4 = (f32[2,128]{1,0:T(2,128)S(1)}, f32[2,128]{1,0:T(2,128)S(1)}, u32[]{:S(2)}, u32[]{:S(2)}) collective-permute-start(f32[2,128]{1,0:T(2,128)S(1)} %get-tuple-element.21), channel_id=1, source_target_pairs={{0,1},{1,0},{2,3},{3,2},{4,5},{5,4},{6,7},{7,6},{8,9},{9,8},{10,11... | collective-permute-start | bytes 3080 | tf_op jit(solution)/shard_map/ppermute | solution.py:29
  86.1 2.4 %collective-permute-start.5 = (f32[2,128]{1,0:T(2,128)S(1)}, f32[2,128]{1,0:T(2,128)S(1)}, u32[]{:S(2)}, u32[]{:S(2)}) collective-permute-start(f32[2,128]{1,0:T(2,128)S(1)} %add_select_fusion.5), channel_id=1, source_target_pairs={{0,2},{2,0},{1,3},{3,1},{4,6},{6,4},{5,7},{7,5},{8,10},{10,8},{9,1... | collective-permute-start | bytes 3080 | tf_op jit(solution)/shard_map/ppermute | solution.py:29
  88.6 3.9 %collective-permute-start.6 = (f32[2,128]{1,0:T(2,128)S(1)}, f32[2,128]{1,0:T(2,128)S(1)}, u32[]{:S(2)}, u32[]{:S(2)}) collective-permute-start(f32[2,128]{1,0:T(2,128)S(1)} %add_select_fusion.4), channel_id=1, source_target_pairs={{0,16},{16,0},{1,17},{17,1},{2,18},{18,2},{3,19},{19,3},{4,20},{20... | collective-permute-start | bytes 3080 | tf_op jit(solution)/shard_map/ppermute | solution.py:29
  98.8 4.3 %collective-permute-start.7 = (f32[4,264,128]{2,1,0:T(8,128)S(1)}, f32[4,264,128]{2,1,0:T(8,128)S(1)}, u32[]{:S(2)}, u32[]{:S(2)}) collective-permute-start(f32[4,264,128]{2,1,0:T(8,128)S(1)} %get-tuple-element.23), channel_id=1, source_target_pairs={{0,1},{1,0},{2,3},{3,2},{4,5},{5,4},{6,7},{7,6},{8,9},{9,8},{10,11... | collective-permute-start | bytes 1622024 | tf_op jit(solution)/shard_map/ppermute | solution.py:29
  129.6 4.0 %collective-permute-start.11 = (f32[4,264,128]{2,1,0:T(8,128)S(1)}, f32[4,264,128]{2,1,0:T(8,128)S(1)}, u32[]{:S(2)}, u32[]{:S(2)}) collective-permute-start(f32[4,264,128]{2,1,0:T(8,128)S(1)} %all_to_all.33.g0), channel_id=1, source_target_pairs={{0,1},{1,0},{2,3},{3,2},{4,5},{5,4},{6,7},{7,6},{8,9},{9,8},{10,11... | collective-permute-start | bytes 1622024 | tf_op jit(solution)/shard_map/ppermute | solution.py:29
  133.6 45.7 %copy-start = (f32[32,1024]{1,0:T(8,128)S(1)}, f32[32,1024]{1,0:T(8,128)}, u32[]{:S(2)}) copy-start(f32[32,1024]{1,0:T(8,128)} %f_ref.1) | copy-start | bytes 393220
  164.1 2.7 %collective-permute-start.12 = (f32[2,128]{1,0:T(2,128)S(1)}, f32[2,128]{1,0:T(2,128)S(1)}, u32[]{:S(2)}, u32[]{:S(2)}) collective-permute-start(f32[2,128]{1,0:T(2,128)S(1)} %get-tuple-element.30), channel_id=1, source_target_pairs={{0,1},{1,0},{2,3},{3,2},{4,5},{5,4},{6,7},{7,6},{8,9},{9,8},{10,11... | collective-permute-start | bytes 3080 | tf_op jit(solution)/shard_map/ppermute | solution.py:29
  166.9 2.4 %collective-permute-start.13 = (f32[2,128]{1,0:T(2,128)S(1)}, f32[2,128]{1,0:T(2,128)S(1)}, u32[]{:S(2)}, u32[]{:S(2)}) collective-permute-start(f32[2,128]{1,0:T(2,128)S(1)} %add_select_fusion.2), channel_id=1, source_target_pairs={{0,2},{2,0},{1,3},{3,1},{4,6},{6,4},{5,7},{7,5},{8,10},{10,8},{9,1... | collective-permute-start | bytes 3080 | tf_op jit(solution)/shard_map/ppermute | solution.py:29
  169.4 6.7 %collective-permute-start.14 = (f32[2,128]{1,0:T(2,128)S(1)}, f32[2,128]{1,0:T(2,128)S(1)}, u32[]{:S(2)}, u32[]{:S(2)}) collective-permute-start(f32[2,128]{1,0:T(2,128)S(1)} %add_select_fusion.1), channel_id=1, source_target_pairs={{0,16},{16,0},{1,17},{17,1},{2,18},{18,2},{3,19},{19,3},{4,20},{20... | collective-permute-start | bytes 3080 | tf_op jit(solution)/shard_map/ppermute | solution.py:29
  169.7 6.5 %collective-permute-start.8 = (f32[40,256]{1,0:T(8,128)S(1)}, f32[40,256]{1,0:T(8,128)S(1)}, u32[]{:S(2)}, u32[]{:S(2)}) collective-permute-start(f32[40,256]{1,0:T(8,128)S(1)} %get-tuple-element.25), channel_id=1, source_target_pairs={{0,4},{4,8},{8,12},{12,0},{1,5},{5,9},{9,13},{13,1},{2,6},{6,10},{... | collective-permute-start | bytes 122888 | tf_op jit(solution)/shard_map/ppermute | solution.py:359
  172.5 6.8 %collective-permute-start.9 = (f32[40,256]{1,0:T(8,128)S(1)}, f32[40,256]{1,0:T(8,128)S(1)}, u32[]{:S(2)}, u32[]{:S(2)}) collective-permute-start(f32[40,256]{1,0:T(8,128)S(1)} %get-tuple-element.26), channel_id=1, source_target_pairs={{0,8},{4,12},{8,0},{12,4},{1,9},{5,13},{9,1},{13,5},{2,10},{6,14},... | collective-permute-start | bytes 122888 | tf_op jit(solution)/shard_map/ppermute | solution.py:359
  172.9 6.4 %collective-permute-start.10 = (f32[40,256]{1,0:T(8,128)S(1)}, f32[40,256]{1,0:T(8,128)S(1)}, u32[]{:S(2)}, u32[]{:S(2)}) collective-permute-start(f32[40,256]{1,0:T(8,128)S(1)} %get-tuple-element.27), channel_id=1, source_target_pairs={{0,12},{4,0},{8,4},{12,8},{1,13},{5,1},{9,5},{13,9},{2,14},{6,2},{... | collective-permute-start | bytes 122888 | tf_op jit(solution)/shard_map/ppermute | solution.py:359

commit v4 on v3

--- a/solution.py
+++ b/solution.py
@@ -11,7 +11,6 @@
 
 GRP = ("xl", "y")
 SMP = ("xh", "zh", "zl", "c")
-SUM = ("zh", "xl", "y")
 QUAD = ("xh", "zl")
 SWAP = [(0, 1), (1, 0)]
 LAM = 0.01
@@ -190,6 +189,21 @@
     st_ref[1:2, :] = total((v - mean) ** 2)
 
 
+def over_chain_kernel(got_ref, all_ref):
+    x = got_ref[0]
+    for k in range(1, got_ref.shape[0]):
+        x = x + got_ref[k]
+    for k in range(all_ref.shape[0]):
+        all_ref[k] = x
+
+
+def over_groups(partial):
+    got = to_all(partial, "zh", lax.axis_size("zh"))
+    size = lax.axis_size(GRP)
+    (x,) = call(over_chain_kernel, [VMEM], [jax.ShapeDtypeStruct((size, *partial.shape), F32)])(got)
+    return lax.all_to_all(x, GRP, 0, 0, tiled=True)
+
+
 def first_sum_kernel(got_ref, v_ref, st_ref, norm_ref):
     x = got_ref[0]
     for k in range(1, got_ref.shape[0]):
@@ -328,7 +342,6 @@
 def body(spins_packed, weight, hidden_bias, force_w, force_b):
     xh, zh, zl, c = (lax.axis_index(a) for a in SMP)
     parts = lax.axis_size("zh")
-    summed = lax.axis_size(SUM)
     units = weight.shape[1] // parts
     samples = spins_packed.shape[1] * lax.axis_size(SMP)
     hb = hidden_bias.reshape(-1, 128)
@@ -349,18 +362,20 @@
     packed = to_all(spins_packed, "zh", parts)
     spins, hidden = hidden_pass(pos, packed, weight, hb, units)
     partial = first_pass(pos, spins, hidden, f, fb)
-    values, st, norm = first_sum(to_all(partial, SUM, summed))
+    values, st, norm = first_sum(over_groups(partial))
     n = values.size
     st0 = over_sets(st, n)
 
     keep, send = image_pass(samples, pos, spins, hidden, values, st0)
     g = keep + swap(send, "c")
     g, *rows = image_sum(pos, lax.all_to_all(g, QUAD, 0, 0, tiled=True), units)
-    rows = [rows[0]] + [lax.ppermute(rows[d], "zh", [(i, (i + d) % 4) for i in range(4)]) for d in (1, 2, 3)]
+    for d in (1, 2, 3):
+        rows[d] = lax.ppermute(rows[d], "zh", [(i, (i + d) % 4) for i in range(4)])
     g = lax.all_to_all(g, QUAD, 0, 0, tiled=True)
 
-    partial = second_pass(samples, pos, spins, hidden, f, fb, g, swap(g, "c"), st0, norm)
-    st, norms = second_sum(to_all(partial, SUM, summed), values, norm)
+    g_far = swap(g, "c")
+    partial = second_pass(samples, pos, spins, hidden, f, fb, g, g_far, st0, norm)
+    st, norms = second_sum(over_groups(partial), values, norm)
     st1 = over_sets(st, n)
     out_w, out_b = update_pass(samples, pos, force_w, fb, rows, st0, norm, st1, norms)
     return out_w, out_b.reshape(-1)

time: 183 us -> 173 us (0.945)
  blocking collectives: 92.6 us -> 82.1 us
    all_to_all x2, blocking collectives: 50.7 us -> 22.4 us  [to_all(): lax.all_to_all(jnp.broadcast_to(x[None], (size, *x.shape)), axes, 0, 0, t...]
    all_to_all x0 -> x2, blocking collectives: none -> 18.3 us  [over_groups(): return lax.all_to_all(x, GRP, 0, 0, tiled=True)]
    ppermute x12, starting transfers between devices: 23.9 us -> 26.3 us  [swap(): return lax.ppermute(x, axis, SWAP)]
    ppermute x3, starting transfers between devices: 6.38 us -> 3.98 us  [body(): rows[d] = lax.ppermute(rows[d], 'zh', [(i, (i + d) % 4) for i in range(4)])]
  transfers between devices with their start and end apart: 16 -> 16, of which waited for: 10 -> 12; matrix products, arithmetic and copies ran while one was open for 0% -> 0% of each run, Pallas kernels for 2% -> 3%
where the time goes in v4:
time: 173 us; the launch traced here: 171 us
  blocking collectives  82.1 us (47%)
  starting transfers between devices  33.8 us (20%)
  Pallas kernels  25.9 us (15%)
  waiting for transfers between devices  23.1 us (13%)
  local copies, waits for them, and re-layouts  4.98 us (3%)
    ppermute x12, starting transfers between devices, swap(): return lax.ppermute(x, axis, SWAP)  26.3 us
    all_to_all x2, blocking collectives, to_all(): lax.all_to_all(jnp.broadcast_to(x[None], (size, *x.shape)), axes, 0, 0, t...  22.4 us
    ppermute x12, waiting for transfers between devices, swap(): return lax.ppermute(x, axis, SWAP)  18.6 us
    all_to_all x2, blocking collectives, over_groups(): return lax.all_to_all(x, GRP, 0, 0, tiled=True)  18.3 us
    all_to_all x1, blocking collectives, body(): lax.all_to_all(f_cols, 'zh', 0, 0, tiled=True).reshape(parts * ROWS, units)  16 us
    all_to_all x1, blocking collectives, body(): g, *rows = image_sum(pos, lax.all_to_all(g, QUAD, 0, 0, tiled=True), units)  13.9 us
    all_to_all x1, blocking collectives, body(): g = lax.all_to_all(g, QUAD, 0, 0, tiled=True)  11.4 us
    pallas_call x1, Pallas kernels, second_pass(): call(functools.partial(second_kernel, samples), [SMEM] + [VMEM] * 11, [ja...  6.57 us
  transfers between devices with their start and end apart: 16, of which 12 were waited for; matrix products, arithmetic and copies ran while one was open for 0% of the time, Pallas kernels for 3%

profile of v4, /device:TPU:1, one launch (start us, length us, event | category | flops | bytes accessed | tf_op | source)
XLA Modules:
  0.0 171.3 jit_solution(8364820202424138053)
XLA Ops:
  0.6 0.8 slice_bitcast_fusion.3
  1.5 16.0 %all_to_all.40 = f32[4,32,256]{2,1,0:T(8,128)S(1)} all-to-all(f32[4,32,256]{2,1,0:T(8,128)S(1)} %pad_maximum_fusion.1), channel_id=1, replica_groups=mesh['xl'=2,'y'=4,'xh'=2,'zh'=4,'zl'=2,'c'=2] {'zh'}, dimensions={0} | all-to-all | bytes 262144 | tf_op jit(solution)/shard_map/all_to_all | solution.py:357
  17.5 1.8 %broadcast_in_dim.8 = s32[4,32,1024]{2,1,0:T(8,128)} broadcast(s32[32,1024]{1,0:T(8,128)} %param.5), dimensions={1,2} | broadcast | bytes 655360 | tf_op jit(solution)/shard_map/broadcast_in_dim | solution.py:32
  19.3 3.5 %all-to-all-start = ((s32[4,32,1024]{2,1,0:T(8,128)}), s32[4,32,1024]{2,1,0:T(8,128)S(1)}, u32[]{:S(2)}, u32[]{:S(2)}) async-start(s32[4,32,1024]{2,1,0:T(8,128)} %broadcast_in_dim.8), calls=%async_computation | async-start | bytes 1048576 | tf_op jit(solution)/shard_map/all_to_all | solution.py:32
  22.7 0.1 copy.8
  22.8 2.8 %collective-permute-start = (f32[1,256,128]{2,1,0:T(8,128)S(1)}, f32[1,256,128]{2,1,0:T(8,128)S(1)}, u32[]{:S(2)}, u32[]{:S(2)}) collective-permute-start(f32[1,256,128]{2,1,0:T(8,128)S(1)} %bitcast.33), channel_id=1, source_target_pairs={{0,16},{16,0},{1,17},{17,1},{2,18},{18,2},{3,19},{19,3},{4,20},{20... | collective-permute-start | bytes 393224 | tf_op jit(solution)/shard_map/ppermute | solution.py:28
  25.7 2.6 %collective-permute-done = f32[1,256,128]{2,1,0:T(8,128)S(1)} collective-permute-done((f32[1,256,128]{2,1,0:T(8,128)S(1)}, f32[1,256,128]{2,1,0:T(8,128)S(1)}, u32[]{:S(2)}, u32[]{:S(2)}) %collective-permute-start) | collective-permute-done | bytes 131104 | tf_op jit(solution)/shard_map/ppermute | solution.py:28
  28.3 0.8 collective-permute-start.1
  29.2 4.4 %collective-permute-start.2 = (f32[2,256,128]{2,1,0:T(8,128)S(1)}, f32[2,256,128]{2,1,0:T(8,128)S(1)}, u32[]{:S(2)}, u32[]{:S(2)}) collective-permute-start(f32[2,256,128]{2,1,0:T(8,128)S(1)} %pad_maximum_fusion.f0), channel_id=1, source_target_pairs={{0,1},{1,0},{2,3},{3,2},{4,5},{5,4},{6,7},{7,6},{8,9},{9,8},{10,11... | collective-permute-start | bytes 786440 | tf_op jit(solution)/shard_map/ppermute | solution.py:28
  33.6 6.2 %collective-permute-done.1.f1 = f32[2,256,128]{2,1,0:T(8,128)S(1)} collective-permute-done((f32[2,256,128]{2,1,0:T(8,128)S(1)}, f32[2,256,128]{2,1,0:T(8,128)S(1)}, u32[]{:S(2)}, u32[]{:S(2)}) %collective-permute-start.1) | collective-permute-done | bytes 262176 | tf_op jit(solution)/shard_map/ppermute | solution.py:28
  39.8 2.4 %collective-permute-start.3 = (f32[2,256,128]{2,1,0:T(8,128)S(1)}, f32[2,256,128]{2,1,0:T(8,128)S(1)}, u32[]{:S(2)}, u32[]{:S(2)}) collective-permute-start(f32[2,256,128]{2,1,0:T(8,128)S(1)} %collective-permute-done.1.f1), channel_id=1, source_target_pairs={{0,1},{1,0},{2,3},{3,2},{4,5},{5,4},{6,7},{7,6},{8,9},{9,8},{10,11... | collective-permute-start | bytes 786440 | tf_op jit(solution)/shard_map/ppermute | solution.py:28
  42.2 1.6 copy-done.2
  43.8 0.7 copy-done.3
  44.5 4.4 %shard_map.68 = (bf16[1024,4096]{1,0:T(8,128)(2,1)S(1)}, f32[256,4096]{1,0:T(8,128)S(1)}) custom-call(s32[37]{0:T(128)S(1)} %pad_add_fusion.pos_ref, s32[4,32,1024]{2,1,0:T(8,128)S(1)} %all-to-all-done.packed_ref, bf16[1024,1024]{1,0:T(8,128)(2,1)S(1)} %copy-done.2, f32[8,128]{1,0:T(8,128)S(1)} %bitcast.31), custom_call_target="tpu_custom_call" | custom-call | flops 4000000000 | bytes 1048576 | tf_op jit(solution)/shard_map/pallas_call | solution.py:94
  49.0 6.2 %shard_map.69 = f32[4,1152]{1,0:T(4,128)S(1)} custom-call(s32[37]{0:T(128)S(1)} %pad_add_fusion.pos_ref, bf16[1024,4096]{1,0:T(8,128)(2,1)S(1)} %get-tuple-element.18.s_ref, f32[256,4096]{1,0:T(8,128)S(1)} %get-tuple-element.19.h_ref, f32[2,256,128]{2,1,0:T(8,128)S(1)} %pad_maximum_fusion.f0, f32[2,256,128]{2,1,0:T(8,128)S(1)} %collective-permute-done.1.f1, ...), custom_call_target="tpu_custom_call" | custom-call | flops 4000000000 | bytes 1048576 | tf_op jit(solution)/shard_map/pallas_call | solution.py:141
  55.2 13.0 %all_to_all.41.got_ref = f32[4,4,1152]{2,1,0:T(4,128)S(1)} all-to-all(f32[4,4,1152]{2,1,0:T(4,128)S(1)} %broadcast_in_dim.10), channel_id=1, replica_groups=mesh['xl'=2,'y'=4,'xh'=2,'zh'=4,'zl'=2,'c'=2] {'zh'}, dimensions={0} | all-to-all | bytes 147456 | tf_op jit(solution)/shard_map/all_to_all | solution.py:32
  68.2 10.4 %all_to_all.42.got_ref = f32[8,4,1152]{2,1,0:T(4,128)S(1)} all-to-all(f32[8,4,1152]{2,1,0:T(4,128)S(1)} %shard_map.70), channel_id=1, replica_groups=mesh['xl'=2,'y'=4,'xh'=2,'zh'=4,'zl'=2,'c'=2] {'xl','y'}, dimensions={0} | all-to-all | bytes 294912 | tf_op jit(solution)/shard_map/all_to_all | solution.py:204
  78.6 0.3 shard_map.71
  78.9 3.3 %collective-permute-start.4 = (f32[2,128]{1,0:T(2,128)S(1)}, f32[2,128]{1,0:T(2,128)S(1)}, u32[]{:S(2)}, u32[]{:S(2)}) collective-permute-start(f32[2,128]{1,0:T(2,128)S(1)} %get-tuple-element.21), channel_id=1, source_target_pairs={{0,1},{1,0},{2,3},{3,2},{4,5},{5,4},{6,7},{7,6},{8,9},{9,8},{10,11... | collective-permute-start | bytes 3080 | tf_op jit(solution)/shard_map/ppermute | solution.py:28
  82.2 0.8 collective-permute-done.4
  83.1 0.8 collective-permute-start.5
  83.8 1.7 collective-permute-done.5
  85.6 2.5 %collective-permute-start.6 = (f32[2,128]{1,0:T(2,128)S(1)}, f32[2,128]{1,0:T(2,128)S(1)}, u32[]{:S(2)}, u32[]{:S(2)}) collective-permute-start(f32[2,128]{1,0:T(2,128)S(1)} %add_select_fusion.4), channel_id=1, source_target_pairs={{0,16},{16,0},{1,17},{17,1},{2,18},{18,2},{3,19},{19,3},{4,20},{20... | collective-permute-start | bytes 3080 | tf_op jit(solution)/shard_map/ppermute | solution.py:28
  88.1 1.5 collective-permute-done.6
  89.6 6.2 %shard_map.72 = (f32[4,264,128]{2,1,0:T(8,128)S(1)}, f32[4,264,128]{2,1,0:T(8,128)S(1)}) custom-call(s32[37]{0:T(128)S(1)} %pad_add_fusion.pos_ref, bf16[1024,4096]{1,0:T(8,128)(2,1)S(1)} %get-tuple-element.18.s_ref, f32[256,4096]{1,0:T(8,128)S(1)} %get-tuple-element.19.h_ref, f32[4,1024]{1,0:T(4,128)S(1)} %get-tuple-element.20.v_ref, ...), custom_call_target="tpu_custom_call" | custom-call | flops 4000000000 | bytes 1048576 | tf_op jit(solution)/shard_map/pallas_call | solution.py:282
  95.8 2.7 %collective-permute-start.7 = (f32[4,264,128]{2,1,0:T(8,128)S(1)}, f32[4,264,128]{2,1,0:T(8,128)S(1)}, u32[]{:S(2)}, u32[]{:S(2)}) collective-permute-start(f32[4,264,128]{2,1,0:T(8,128)S(1)} %get-tuple-element.23), channel_id=1, source_target_pairs={{0,1},{1,0},{2,3},{3,2},{4,5},{5,4},{6,7},{7,6},{8,9},{9,8},{10,11... | collective-permute-start | bytes 1622024 | tf_op jit(solution)/shard_map/ppermute | solution.py:28
  98.5 1.6 collective-permute-done.7
  100.1 13.9 %all_to_all.43.got_ref = f32[4,264,128]{2,1,0:T(8,128)S(1)} all-to-all(f32[4,264,128]{2,1,0:T(8,128)S(1)} %add.115), channel_id=1, replica_groups=mesh['xl'=2,'y'=4,'xh'=2,'zh'=4,'zl'=2,'c'=2] {'xh','zl'}, dimensions={0} | all-to-all | bytes 1081344 | tf_op jit(solution)/shard_map/all_to_all | solution.py:371
  114.0 0.7 shard_map.73
  114.7 11.4 %all_to_all.44.g0 = f32[4,264,128]{2,1,0:T(8,128)S(1)} all-to-all(f32[4,264,128]{2,1,0:T(8,128)S(1)} %get-tuple-element.29), channel_id=1, replica_groups=mesh['xl'=2,'y'=4,'xh'=2,'zh'=4,'zl'=2,'c'=2] {'xh','zl'}, dimensions={0} | all-to-all | bytes 1081344 | tf_op jit(solution)/shard_map/all_to_all | solution.py:374
  126.1 2.5 %collective-permute-start.11 = (f32[4,264,128]{2,1,0:T(8,128)S(1)}, f32[4,264,128]{2,1,0:T(8,128)S(1)}, u32[]{:S(2)}, u32[]{:S(2)}) collective-permute-start(f32[4,264,128]{2,1,0:T(8,128)S(1)} %all_to_all.44.g0), channel_id=1, source_target_pairs={{0,1},{1,0},{2,3},{3,2},{4,5},{5,4},{6,7},{7,6},{8,9},{9,8},{10,11... | collective-permute-start | bytes 1622024 | tf_op jit(solution)/shard_map/ppermute | solution.py:28
  128.5 1.6 collective-permute-done.11.g1
  130.1 6.6 %shard_map.74 = f32[4,1152]{1,0:T(4,128)S(1)} custom-call(s32[37]{0:T(128)S(1)} %pad_add_fusion.pos_ref, bf16[1024,4096]{1,0:T(8,128)(2,1)S(1)} %get-tuple-element.18.s_ref, f32[256,4096]{1,0:T(8,128)S(1)} %get-tuple-element.19.h_ref, f32[2,256,128]{2,1,0:T(8,128)S(1)} %pad_maximum_fusion.f0, f32[2,256,128]{2,1,0:T(8,128)S(1)} %collective-permute-done.1.f1, ...), custom_call_target="tpu_custom_call" | custom-call | flops 4000000000 | bytes 1048576 | tf_op jit(solution)/shard_map/pallas_call | solution.py:177
  136.7 9.4 %all_to_all.45.got_ref = f32[4,4,1152]{2,1,0:T(4,128)S(1)} all-to-all(f32[4,4,1152]{2,1,0:T(4,128)S(1)} %broadcast_in_dim.11), channel_id=1, replica_groups=mesh['xl'=2,'y'=4,'xh'=2,'zh'=4,'zl'=2,'c'=2] {'zh'}, dimensions={0} | all-to-all | bytes 147456 | tf_op jit(solution)/shard_map/all_to_all | solution.py:32
  146.1 7.9 %all_to_all.46.got_ref = f32[8,4,1152]{2,1,0:T(4,128)S(1)} all-to-all(f32[8,4,1152]{2,1,0:T(4,128)S(1)} %shard_map.75), channel_id=1, replica_groups=mesh['xl'=2,'y'=4,'xh'=2,'zh'=4,'zl'=2,'c'=2] {'xl','y'}, dimensions={0} | all-to-all | bytes 294912 | tf_op jit(solution)/shard_map/all_to_all | solution.py:204
  154.1 0.3 shard_map.76
  154.4 3.1 %collective-permute-start.12 = (f32[2,128]{1,0:T(2,128)S(1)}, f32[2,128]{1,0:T(2,128)S(1)}, u32[]{:S(2)}, u32[]{:S(2)}) collective-permute-start(f32[2,128]{1,0:T(2,128)S(1)} %get-tuple-element.30), channel_id=1, source_target_pairs={{0,1},{1,0},{2,3},{3,2},{4,5},{5,4},{6,7},{7,6},{8,9},{9,8},{10,11... | collective-permute-start | bytes 3080 | tf_op jit(solution)/shard_map/ppermute | solution.py:28
  157.4 0.8 collective-permute-done.12
  158.3 0.6 collective-permute-start.13
  158.9 1.9 %collective-permute-done.13 = f32[2,128]{1,0:T(2,128)S(1)} collective-permute-done((f32[2,128]{1,0:T(2,128)S(1)}, f32[2,128]{1,0:T(2,128)S(1)}, u32[]{:S(2)}, u32[]{:S(2)}) %collective-permute-start.13) | collective-permute-done | bytes 1056 | tf_op jit(solution)/shard_map/ppermute | solution.py:28
  160.8 0.5 collective-permute-start.14
  161.3 0.4 collective-permute-start.8
  161.7 1.7 collective-permute-start.9
  163.4 1.9 %collective-permute-start.10 = (f32[40,256]{1,0:T(8,128)S(1)}, f32[40,256]{1,0:T(8,128)S(1)}, u32[]{:S(2)}, u32[]{:S(2)}) collective-permute-start(f32[40,256]{1,0:T(8,128)S(1)} %get-tuple-element.27), channel_id=1, source_target_pairs={{0,12},{4,0},{8,4},{12,8},{1,13},{5,1},{9,5},{13,9},{2,14},{6,2},{... | collective-permute-start | bytes 122888 | tf_op jit(solution)/shard_map/ppermute | solution.py:373
  165.4 1.6 collective-permute-done.8.g1
  167.0 1.8 %collective-permute-done.9.g2 = f32[40,256]{1,0:T(8,128)S(1)} collective-permute-done((f32[40,256]{1,0:T(8,128)S(1)}, f32[40,256]{1,0:T(8,128)S(1)}, u32[]{:S(2)}, u32[]{:S(2)}) %collective-permute-start.9) | collective-permute-done | bytes 40992 | tf_op jit(solution)/shard_map/ppermute | solution.py:373
  168.9 1.1 collective-permute-done.10.g3
  170.0 1.3 shard_map.77
  (33 shorter events, 0.7 us)
Async XLA Ops:
  19.3 22.9 %all-to-all-start = ((s32[4,32,1024]{2,1,0:T(8,128)}), s32[4,32,1024]{2,1,0:T(8,128)S(1)}, u32[]{:S(2)}, u32[]{:S(2)}) async-start(s32[4,32,1024]{2,1,0:T(8,128)} %broadcast_in_dim.8), calls=%async_computation | async-start | bytes 1048576 | tf_op jit(solution)/shard_map/all_to_all | solution.py:32
  22.8 5.4 %collective-permute-start = (f32[1,256,128]{2,1,0:T(8,128)S(1)}, f32[1,256,128]{2,1,0:T(8,128)S(1)}, u32[]{:S(2)}, u32[]{:S(2)}) collective-permute-start(f32[1,256,128]{2,1,0:T(8,128)S(1)} %bitcast.33), channel_id=1, source_target_pairs={{0,16},{16,0},{1,17},{17,1},{2,18},{18,2},{3,19},{19,3},{4,20},{20... | collective-permute-start | bytes 393224 | tf_op jit(solution)/shard_map/ppermute | solution.py:28
  28.3 11.5 %collective-permute-start.1 = (f32[2,256,128]{2,1,0:T(8,128)S(1)}, f32[2,256,128]{2,1,0:T(8,128)S(1)}, u32[]{:S(2)}, u32[]{:S(2)}) collective-permute-start(f32[2,256,128]{2,1,0:T(8,128)S(1)} %pad_maximum_fusion.f0), channel_id=1, source_target_pairs={{0,2},{2,0},{1,3},{3,1},{4,6},{6,4},{5,7},{7,5},{8,10},{10,8},{9,1... | collective-permute-start | bytes 786440 | tf_op jit(solution)/shard_map/ppermute | solution.py:28
  29.2 19.7 %collective-permute-start.2 = (f32[2,256,128]{2,1,0:T(8,128)S(1)}, f32[2,256,128]{2,1,0:T(8,128)S(1)}, u32[]{:S(2)}, u32[]{:S(2)}) collective-permute-start(f32[2,256,128]{2,1,0:T(8,128)S(1)} %pad_maximum_fusion.f0), channel_id=1, source_target_pairs={{0,1},{1,0},{2,3},{3,2},{4,5},{5,4},{6,7},{7,6},{8,9},{9,8},{10,11... | collective-permute-start | bytes 786440 | tf_op jit(solution)/shard_map/ppermute | solution.py:28
  39.8 9.2 %collective-permute-start.3 = (f32[2,256,128]{2,1,0:T(8,128)S(1)}, f32[2,256,128]{2,1,0:T(8,128)S(1)}, u32[]{:S(2)}, u32[]{:S(2)}) collective-permute-start(f32[2,256,128]{2,1,0:T(8,128)S(1)} %collective-permute-done.1.f1), channel_id=1, source_target_pairs={{0,1},{1,0},{2,3},{3,2},{4,5},{5,4},{6,7},{7,6},{8,9},{9,8},{10,11... | collective-permute-start | bytes 786440 | tf_op jit(solution)/shard_map/ppermute | solution.py:28
  42.2 1.6 copy-start.2
  43.8 0.7 copy-start.3
  44.5 4.4 %copy-start.1 = (f32[1024]{0:T(1024)S(1)}, f32[1024]{0:T(1024)}, u32[]{:S(2)}) copy-start(f32[1024]{0:T(1024)} %param.9) | copy-start | bytes 12292
  78.9 4.1 %collective-permute-start.4 = (f32[2,128]{1,0:T(2,128)S(1)}, f32[2,128]{1,0:T(2,128)S(1)}, u32[]{:S(2)}, u32[]{:S(2)}) collective-permute-start(f32[2,128]{1,0:T(2,128)S(1)} %get-tuple-element.21), channel_id=1, source_target_pairs={{0,1},{1,0},{2,3},{3,2},{4,5},{5,4},{6,7},{7,6},{8,9},{9,8},{10,11... | collective-permute-start | bytes 3080 | tf_op jit(solution)/shard_map/ppermute | solution.py:28
  83.1 2.4 %collective-permute-start.5 = (f32[2,128]{1,0:T(2,128)S(1)}, f32[2,128]{1,0:T(2,128)S(1)}, u32[]{:S(2)}, u32[]{:S(2)}) collective-permute-start(f32[2,128]{1,0:T(2,128)S(1)} %add_select_fusion.5), channel_id=1, source_target_pairs={{0,2},{2,0},{1,3},{3,1},{4,6},{6,4},{5,7},{7,5},{8,10},{10,8},{9,1... | collective-permute-start | bytes 3080 | tf_op jit(solution)/shard_map/ppermute | solution.py:28
  85.6 3.9 %collective-permute-start.6 = (f32[2,128]{1,0:T(2,128)S(1)}, f32[2,128]{1,0:T(2,128)S(1)}, u32[]{:S(2)}, u32[]{:S(2)}) collective-permute-start(f32[2,128]{1,0:T(2,128)S(1)} %add_select_fusion.4), channel_id=1, source_target_pairs={{0,16},{16,0},{1,17},{17,1},{2,18},{18,2},{3,19},{19,3},{4,20},{20... | collective-permute-start | bytes 3080 | tf_op jit(solution)/shard_map/ppermute | solution.py:28
  95.8 4.3 %collective-permute-start.7 = (f32[4,264,128]{2,1,0:T(8,128)S(1)}, f32[4,264,128]{2,1,0:T(8,128)S(1)}, u32[]{:S(2)}, u32[]{:S(2)}) collective-permute-start(f32[4,264,128]{2,1,0:T(8,128)S(1)} %get-tuple-element.23), channel_id=1, source_target_pairs={{0,1},{1,0},{2,3},{3,2},{4,5},{5,4},{6,7},{7,6},{8,9},{9,8},{10,11... | collective-permute-start | bytes 1622024 | tf_op jit(solution)/shard_map/ppermute | solution.py:28
  126.1 4.0 %collective-permute-start.11 = (f32[4,264,128]{2,1,0:T(8,128)S(1)}, f32[4,264,128]{2,1,0:T(8,128)S(1)}, u32[]{:S(2)}, u32[]{:S(2)}) collective-permute-start(f32[4,264,128]{2,1,0:T(8,128)S(1)} %all_to_all.44.g0), channel_id=1, source_target_pairs={{0,1},{1,0},{2,3},{3,2},{4,5},{5,4},{6,7},{7,6},{8,9},{9,8},{10,11... | collective-permute-start | bytes 1622024 | tf_op jit(solution)/shard_map/ppermute | solution.py:28
  130.1 39.9 %copy-start = (f32[32,1024]{1,0:T(8,128)S(1)}, f32[32,1024]{1,0:T(8,128)}, u32[]{:S(2)}) copy-start(f32[32,1024]{1,0:T(8,128)} %f_ref.1) | copy-start | bytes 393220
  154.4 3.9 %collective-permute-start.12 = (f32[2,128]{1,0:T(2,128)S(1)}, f32[2,128]{1,0:T(2,128)S(1)}, u32[]{:S(2)}, u32[]{:S(2)}) collective-permute-start(f32[2,128]{1,0:T(2,128)S(1)} %get-tuple-element.30), channel_id=1, source_target_pairs={{0,1},{1,0},{2,3},{3,2},{4,5},{5,4},{6,7},{7,6},{8,9},{9,8},{10,11... | collective-permute-start | bytes 3080 | tf_op jit(solution)/shard_map/ppermute | solution.py:28
  158.3 2.4 %collective-permute-start.13 = (f32[2,128]{1,0:T(2,128)S(1)}, f32[2,128]{1,0:T(2,128)S(1)}, u32[]{:S(2)}, u32[]{:S(2)}) collective-permute-start(f32[2,128]{1,0:T(2,128)S(1)} %add_select_fusion.2), channel_id=1, source_target_pairs={{0,2},{2,0},{1,3},{3,1},{4,6},{6,4},{5,7},{7,5},{8,10},{10,8},{9,1... | collective-permute-start | bytes 3080 | tf_op jit(solution)/shard_map/ppermute | solution.py:28
  160.8 4.5 %collective-permute-start.14 = (f32[2,128]{1,0:T(2,128)S(1)}, f32[2,128]{1,0:T(2,128)S(1)}, u32[]{:S(2)}, u32[]{:S(2)}) collective-permute-start(f32[2,128]{1,0:T(2,128)S(1)} %add_select_fusion.1), channel_id=1, source_target_pairs={{0,16},{16,0},{1,17},{17,1},{2,18},{18,2},{3,19},{19,3},{4,20},{20... | collective-permute-start | bytes 3080 | tf_op jit(solution)/shard_map/ppermute | solution.py:28
  161.3 5.7 %collective-permute-start.8 = (f32[40,256]{1,0:T(8,128)S(1)}, f32[40,256]{1,0:T(8,128)S(1)}, u32[]{:S(2)}, u32[]{:S(2)}) collective-permute-start(f32[40,256]{1,0:T(8,128)S(1)} %get-tuple-element.25), channel_id=1, source_target_pairs={{0,4},{4,8},{8,12},{12,0},{1,5},{5,9},{9,13},{13,1},{2,6},{6,10},{... | collective-permute-start | bytes 122888 | tf_op jit(solution)/shard_map/ppermute | solution.py:373
  161.7 7.1 %collective-permute-start.9 = (f32[40,256]{1,0:T(8,128)S(1)}, f32[40,256]{1,0:T(8,128)S(1)}, u32[]{:S(2)}, u32[]{:S(2)}) collective-permute-start(f32[40,256]{1,0:T(8,128)S(1)} %get-tuple-element.26), channel_id=1, source_target_pairs={{0,8},{4,12},{8,0},{12,4},{1,9},{5,13},{9,1},{13,5},{2,10},{6,14},... | collective-permute-start | bytes 122888 | tf_op jit(solution)/shard_map/ppermute | solution.py:373
  163.4 6.6 %collective-permute-start.10 = (f32[40,256]{1,0:T(8,128)S(1)}, f32[40,256]{1,0:T(8,128)S(1)}, u32[]{:S(2)}, u32[]{:S(2)}) collective-permute-start(f32[40,256]{1,0:T(8,128)S(1)} %get-tuple-element.27), channel_id=1, source_target_pairs={{0,12},{4,0},{8,4},{12,8},{1,13},{5,1},{9,5},{13,9},{2,14},{6,2},{... | collective-permute-start | bytes 122888 | tf_op jit(solution)/shard_map/ppermute | solution.py:373

commit v5 on v3

--- a/solution.py
+++ b/solution.py
@@ -11,7 +11,6 @@
 
 GRP = ("xl", "y")
 SMP = ("xh", "zh", "zl", "c")
-SUM = ("zh", "xl", "y")
 QUAD = ("xh", "zl")
 SWAP = [(0, 1), (1, 0)]
 LAM = 0.01
@@ -19,7 +18,8 @@
 NB = 8
 TILE = 1024
 LIMIT = 14
-EXTRA = 128
+SUB = TILE // 128
+EXTRA = 8
 F32, BF16 = jnp.float32, jnp.bfloat16
 VMEM = pl.BlockSpec(memory_space=pltpu.VMEM)
 SMEM = pl.BlockSpec(memory_space=pltpu.SMEM)
@@ -65,14 +65,25 @@
 
 
 def total(x):
-    return jnp.full((1, EXTRA), jnp.sum(x), F32)
+    return jnp.full((1, 128), jnp.sum(x), F32)
+
+
+def to_rows(line):
+    return jnp.concatenate([line[:, k * 128 : (k + 1) * 128] for k in range(line.shape[1] // 128)], axis=0)
+
+
+def to_line(rows):
+    return jnp.concatenate([rows[k : k + 1, :] for k in range(rows.shape[0])], axis=1)
+
+
+def sub(t):
+    return pl.ds(pl.multiple_of(t * SUB, SUB), SUB)
 
 
 def hidden_kernel(pos_ref, packed_ref, w_ref, hb_ref, s_ref, h_ref, wt):
     units = wt.shape[0]
-    mine = pl.ds(pl.multiple_of(pos_ref[32] * units, units), units)
     for b in range(NB):
-        rows = [w_ref[pl.ds(pl.multiple_of(pos_ref[4 * b + k] * ROWS, ROWS), ROWS), mine] for k in range(4)]
+        rows = [w_ref[pl.ds(pl.multiple_of(pos_ref[4 * b + k] * ROWS, ROWS), ROWS), :] for k in range(4)]
         block = jnp.concatenate(rows, axis=0).astype(F32)
         wt[:, b * 128 : (b + 1) * 128] = block.T.astype(BF16)
     shifts = 31 - lax.broadcasted_iota(jnp.int32, (ROWS, TILE), 0)
@@ -107,7 +118,7 @@
     def step(t, carry):
         out = jnp.dot(lhs[...], s_ref[:, cols(t)], preferred_element_type=F32)
         proj = out[:units] + out[units:] + bias
-        p_ref[pl.ds(t, 1), :TILE] = jnp.sum(h_ref[:, cols(t)] * proj, axis=0, keepdims=True)
+        p_ref[sub(t), :] = to_rows(jnp.sum(h_ref[:, cols(t)] * proj, axis=0, keepdims=True))
         return carry
 
     lax.fori_loop(0, s_ref.shape[1] // TILE, step, 0)
@@ -132,8 +143,9 @@
         set_block(lhs, b, x)
         norm = norm + x * x
     fb = my_rows(pos_ref, fb_ref, units)
-    p_ref[:, TILE:] = jnp.zeros((p_ref.shape[0], EXTRA), F32)
-    p_ref[0:1, TILE:] = total(norm) + total(fb * fb)
+    n = p_ref.shape[0] - EXTRA
+    p_ref[n:, :] = jnp.zeros((EXTRA, 128), F32)
+    p_ref[n : n + 1, :] = total(norm) + total(fb * fb)
     project(s_ref, h_ref, lhs, rows_to_column(fb), p_ref)
 
 
@@ -142,7 +154,7 @@
     return call(
         first_kernel,
         [SMEM] + [VMEM] * 7,
-        [jax.ShapeDtypeStruct((n // TILE, TILE + EXTRA), F32)],
+        [jax.ShapeDtypeStruct((n // 128 + EXTRA, 128), F32)],
         [pltpu.VMEM((2 * units, NB * 128), BF16)],
         flops=4 * 10**9,
     )(pos, resident(spins), resident(hidden), *f, fb)[0]
@@ -152,7 +164,7 @@
     return norm / (spread / samples + LAM * length)
 
 
-def second_kernel(samples, pos_ref, s_ref, h_ref, f0, f1, f2, f3, fb_ref, g0, g1, st_ref, norm_ref, p_ref, lhs):
+def second_kernel(samples, pos_ref, s_ref, h_ref, f0, f1, f2, f3, fb_ref, g0, g1, mine_ref, st_ref, norm_ref, out_ref, lhs):
     units = h_ref.shape[0]
     norm0 = norm_ref[0:1, :]
     a = step_of(norm0, st_ref[1:2, :], samples, norm0)
@@ -167,21 +179,31 @@
         rf = rf + r * f
     fb = my_rows(pos_ref, fb_ref, units)
     rb = fb - a * (g0[0, units : units + units // 128, :] + LAM * fb)
-    p_ref[:, TILE:] = jnp.zeros((p_ref.shape[0], EXTRA), F32)
-    p_ref[0:1, TILE:] = total(rr) + total(rb * rb)
-    p_ref[1:2, TILE:] = total(rf) + total(rb * fb)
+    n = h_ref.shape[1] // 128
+    p_ref = out_ref.at[0]
+    p_ref[n : n + EXTRA, :] = jnp.zeros((EXTRA, 128), F32)
+    p_ref[n : n + 1, :] = total(rr) + total(rb * rb)
+    p_ref[n + 1 : n + 2, :] = total(rf) + total(rb * fb)
+    p_ref[n + 2 : n + 2 + units // 128, :] = g0[0, units : units + units // 128, :]
     project(s_ref, h_ref, lhs, rows_to_column(rb), p_ref)
-
-
-def second_pass(samples, pos, spins, hidden, f, fb, g0, g1, st, norm):
+    for k in range(1, out_ref.shape[0]):
+        out_ref[k, : n + EXTRA, :] = out_ref[0, : n + EXTRA, :]
+    for k in range(out_ref.shape[0]):
+        for h in range(units // 128):
+            at = n + EXTRA + h * ROWS
+            out_ref[k, at : at + ROWS, :] = mine_ref[k * ROWS : (k + 1) * ROWS, h * 128 : (h + 1) * 128]
+
+
+def second_pass(samples, pos, spins, hidden, f, fb, g0, g1, mine, st, norm):
     units, n = hidden.shape
+    parts = mine.shape[0] // ROWS
     return call(
         functools.partial(second_kernel, samples),
-        [SMEM] + [VMEM] * 11,
-        [jax.ShapeDtypeStruct((n // TILE, TILE + EXTRA), F32)],
+        [SMEM] + [VMEM] * 12,
+        [jax.ShapeDtypeStruct((parts, n // 128 + EXTRA + units // 128 * ROWS, 128), F32)],
         [pltpu.VMEM((2 * units, NB * 128), BF16)],
         flops=4 * 10**9,
-    )(pos, resident(spins), resident(hidden), *f, fb, g0, g1, st, norm)[0]
+    )(pos, resident(spins), resident(hidden), *f, fb, g0, g1, mine, st, norm)[0]
 
 
 def put_stats(v, st_ref):
@@ -190,34 +212,52 @@
     st_ref[1:2, :] = total((v - mean) ** 2)
 
 
-def first_sum_kernel(got_ref, v_ref, st_ref, norm_ref):
+def over_chain_kernel(got_ref, all_ref):
+    rows = all_ref.shape[1]
+    x = got_ref[0, :rows, :]
+    for k in range(1, got_ref.shape[0]):
+        x = x + got_ref[k, :rows, :]
+    for k in range(all_ref.shape[0]):
+        all_ref[k] = x
+
+
+def over_groups(got, rows):
+    (x,) = call(over_chain_kernel, [VMEM], [jax.ShapeDtypeStruct((lax.axis_size(GRP), rows, 128), F32)])(got)
+    return lax.all_to_all(x, GRP, 0, 0, tiled=True)
+
+
+def summed(got_ref):
     x = got_ref[0]
     for k in range(1, got_ref.shape[0]):
         x = x + got_ref[k]
-    v = x[:, :TILE]
+    n = x.shape[0] - EXTRA
+    return x[:n], x[n:]
+
+
+def first_sum_kernel(got_ref, v_ref, st_ref, norm_ref):
+    v, extra = summed(got_ref)
     v_ref[...] = v
-    norm_ref[...] = x[:, TILE:]
+    norm_ref[...] = extra
     put_stats(v, st_ref)
 
 
 def first_sum(got):
-    parts = got.shape[1]
     shape = lambda *s: jax.ShapeDtypeStruct(s, F32)
-    return call(first_sum_kernel, [VMEM], [shape(parts, TILE), shape(2, 128), shape(parts, EXTRA)])(got)
+    return call(first_sum_kernel, [VMEM], [shape(got.shape[1] - EXTRA, 128), shape(2, 128), shape(EXTRA, 128)])(got)
 
 
 def second_sum_kernel(got_ref, v_ref, norm_ref, st_ref, next_ref):
-    x = got_ref[0]
-    for k in range(1, got_ref.shape[0]):
-        x = x + got_ref[k]
-    next_ref[...] = x[:, TILE:]
-    beta = x[0:1, TILE : TILE + 1] / norm_ref[0:1, 0:1]
-    put_stats(x[:, :TILE] + beta * v_ref[...], st_ref)
+    u, extra = summed(got_ref)
+    next_ref[...] = extra
+    beta = extra[0:1, 0:1] / norm_ref[0:1, 0:1]
+    put_stats(u + beta * v_ref[...], st_ref)
 
 
 def second_sum(got, values, norm):
     shape = lambda *s: jax.ShapeDtypeStruct(s, F32)
-    return call(second_sum_kernel, [VMEM] * 3, [shape(2, 128), shape(got.shape[1], EXTRA)])(got, values, norm)
+    return call(second_sum_kernel, [VMEM] * 3, [shape(2, 128), shape(EXTRA, 128)])(
+        got, values, norm
+    )
 
 
 def merged(st, count, axis):
@@ -241,7 +281,7 @@
     lanes[...] = jnp.zeros(lanes.shape, F32)
 
     def step(t, carry):
-        r = h_ref[:, cols(t)] * ((v_ref[pl.ds(t, 1), :] - mean) * (1.0 / samples))
+        r = h_ref[:, cols(t)] * to_line((v_ref[sub(t), :] - mean) * (1.0 / samples))
         both = jnp.concatenate(split_terms(r), axis=0)
         out = lax.dot_general(both, s_ref[:, cols(t)], (((1,), (1,)), ((), ())), preferred_element_type=F32)
         acc[...] += out[:units] + out[units:]
@@ -274,30 +314,20 @@
     )(pos, resident(spins), resident(hidden), values, st)
 
 
-def image_sum_kernel(pos_ref, got_ref, all_ref, r0, r1, r2, r3, turned):
-    units = r0.shape[1]
+def image_sum_kernel(got_ref, all_ref, mine_ref):
+    units = mine_ref.shape[1]
     x = got_ref[0] + got_ref[1] + (got_ref[2] + got_ref[3])
     for k in range(4):
         all_ref[k] = x
-    turned[...] = x[:units].T
-    bias = jnp.concatenate([x[units + k : units + k + 1, :] for k in range(units // 128)], axis=1)
-    for d, ref in enumerate((r0, r1, r2, r3)):
-        to = (pos_ref[32] + d) % 4
-        ref[:ROWS, :] = turned[pl.ds(pl.multiple_of(to * ROWS, ROWS), ROWS), :]
-        ref[ROWS:, :] = jnp.broadcast_to(bias, (ref.shape[0] - ROWS, units))
-
-
-def image_sum(pos, got, units):
+    mine_ref[...] = x[:units].T
+
+
+def image_sum(got, units):
     shape = lambda *s: jax.ShapeDtypeStruct(s, F32)
-    return call(
-        image_sum_kernel,
-        [SMEM, VMEM],
-        [shape(*got.shape)] + [shape(ROWS + 8, units)] * 4,
-        [pltpu.VMEM((128, units), F32)],
-    )(pos, got)
-
-
-def update_kernel(samples, pos_ref, f_ref, fb_ref, g0, g1, g2, g3, st0_ref, norm_ref, st1_ref, next_ref, w_ref, b_ref):
+    return call(image_sum_kernel, [VMEM], [shape(*got.shape), shape(128, units)])(got)
+
+
+def update_kernel(samples, f_ref, fb_ref, got_ref, st0_ref, norm_ref, st1_ref, next_ref, w_ref, b_ref):
     norm0, norm1 = norm_ref[0:1, 0:1], next_ref[0:1, 0:1]
     cross = next_ref[1:2, 0:1]
     beta = norm1 / norm0
@@ -308,27 +338,27 @@
         r = f - step0 * (g + LAM * f)
         return step0 * f + step1 * (r + beta * f)
 
-    units = g0.shape[1]
-    for d, g_ref in enumerate((g0, g1, g2, g3)):
-        source = (pos_ref[32] + 4 - d) % 4
-        at = pl.ds(pl.multiple_of(source * units, units), units)
-        w_ref[:, at] = update(f_ref[:, at], g_ref[:ROWS, :])
-        for h in range(units // 128):
-            row = pl.ds(source * (units // 128) + h, 1)
-            b_ref[row, :] = update(fb_ref[row, :], g_ref[ROWS : ROWS + 1, h * 128 : (h + 1) * 128])
-
-
-def update_pass(samples, pos, f, fb, g, st0, norm, st1, norms):
+    parts = got_ref.shape[0]
+    per = f_ref.shape[1] // 128 // parts
+    n = got_ref.shape[1] - EXTRA - per * ROWS
+    for k in range(parts):
+        for h in range(per):
+            b = k * per + h
+            at = n + EXTRA + h * ROWS
+            w_ref[:, b * 128 : (b + 1) * 128] = update(f_ref[:, b * 128 : (b + 1) * 128], got_ref[k, at : at + ROWS, :])
+            b_ref[b : b + 1, :] = update(fb_ref[b : b + 1, :], got_ref[k, n + 2 + h : n + 3 + h, :])
+
+
+def update_pass(samples, f, fb, got, st0, norm, st1, norms):
     shape = lambda s: jax.ShapeDtypeStruct(s, F32)
     return call(
-        functools.partial(update_kernel, samples), [SMEM] + [VMEM] * 10, [shape(f.shape), shape(fb.shape)]
-    )(pos, f, fb, *g, st0, norm, st1, norms)
+        functools.partial(update_kernel, samples), [VMEM] * 7, [shape(f.shape), shape(fb.shape)]
+    )(f, fb, got, st0, norm, st1, norms)
 
 
 def body(spins_packed, weight, hidden_bias, force_w, force_b):
     xh, zh, zl, c = (lax.axis_index(a) for a in SMP)
     parts = lax.axis_size("zh")
-    summed = lax.axis_size(SUM)
     units = weight.shape[1] // parts
     samples = spins_packed.shape[1] * lax.axis_size(SMP)
     hb = hidden_bias.reshape(-1, 128)
@@ -341,28 +371,32 @@
     pos = jnp.concatenate([words, zh.reshape(1), blocks])
 
     f_cols = jnp.stack([force_w[:, k * units : (k + 1) * units] for k in range(parts)])
-    f = lax.all_to_all(f_cols, "zh", 0, 0, tiled=True).reshape(parts * ROWS, units).T[None]
-    f = jnp.concatenate([f, swap(f, "xh")], axis=0)
+    f = lax.all_to_all(f_cols, "zh", 0, 0, tiled=True)
+    f = f.reshape(parts * ROWS, units).T[None]
+    f_xh = swap(f, "xh")
+    f = jnp.concatenate([f, f_xh], axis=0)
     f_zl = swap(f, "zl")
     f = (f, f_zl, swap(f, "c"), swap(f_zl, "c"))
 
     packed = to_all(spins_packed, "zh", parts)
-    spins, hidden = hidden_pass(pos, packed, weight, hb, units)
+    w = lax.dynamic_slice_in_dim(weight, zh * units, units, 1)
+    spins, hidden = hidden_pass(pos, packed, w, hb, units)
     partial = first_pass(pos, spins, hidden, f, fb)
-    values, st, norm = first_sum(to_all(partial, SUM, summed))
+    rows = partial.shape[0]
+    values, st, norm = first_sum(over_groups(to_all(partial, "zh", parts), rows))
     n = values.size
     st0 = over_sets(st, n)
 
     keep, send = image_pass(samples, pos, spins, hidden, values, st0)
     g = keep + swap(send, "c")
-    g, *rows = image_sum(pos, lax.all_to_all(g, QUAD, 0, 0, tiled=True), units)
-    rows = [rows[0]] + [lax.ppermute(rows[d], "zh", [(i, (i + d) % 4) for i in range(4)]) for d in (1, 2, 3)]
+    g, mine = image_sum(lax.all_to_all(g, QUAD, 0, 0, tiled=True), units)
     g = lax.all_to_all(g, QUAD, 0, 0, tiled=True)
 
-    partial = second_pass(samples, pos, spins, hidden, f, fb, g, swap(g, "c"), st0, norm)
-    st, norms = second_sum(to_all(partial, SUM, summed), values, norm)
+    partial = second_pass(samples, pos, spins, hidden, f, fb, g, swap(g, "c"), mine, st0, norm)
+    got = lax.all_to_all(partial, "zh", 0, 0, tiled=True)
+    st, norms = second_sum(over_groups(got, rows), values, norm)
     st1 = over_sets(st, n)
-    out_w, out_b = update_pass(samples, pos, force_w, fb, rows, st0, norm, st1, norms)
+    out_w, out_b = update_pass(samples, force_w, fb, got, st0, norm, st1, norms)
     return out_w, out_b.reshape(-1)
 
 

time: 183 us -> 167 us (0.913)
  blocking collectives: 92.6 us -> 83.9 us
  starting transfers between devices: 33.7 us -> 30.5 us
  local copies, waits for them, and re-layouts: 5.12 us -> 2.91 us
    all_to_all x2 -> x1, blocking collectives: 50.7 us -> 12.9 us  [to_all(): lax.all_to_all(jnp.broadcast_to(x[None], (size, *x.shape)), axes, 0, 0, t...]
    all_to_all x2 -> x5, blocking collectives: 30.5 us -> 59.6 us  [the longest x2 18.5 us: over_groups(): return lax.all_to_all(x, GRP, 0, 0, tiled=True)]
    ppermute x3 -> x0, starting transfers between devices: 6.38 us -> none  [body(): lax.ppermute(rows[d], 'zh', [(i, (i + d) % 4) for i in range(4)])]
    ppermute x12, starting transfers between devices: 23.9 us -> 27 us  [swap(): return lax.ppermute(x, axis, SWAP)]
    ppermute x3 -> x0, waiting for transfers between devices: 3.1 us -> none  [body(): lax.ppermute(rows[d], 'zh', [(i, (i + d) % 4) for i in range(4)])]
    ppermute x12, waiting for transfers between devices: 18.6 us -> 21.5 us  [swap(): return lax.ppermute(x, axis, SWAP)]
    unnamed x8, local copies, waits for them, and re-layouts: 2.29 us -> 0.02 us
    pallas_call x6 -> x8, Pallas kernels: 15.3 us -> 15.2 us  [the longest x1 7.08 us: second_pass(): call(functools.partial(second_kernel, samples), [SMEM] + [VMEM] * 12, [ja...]
  transfers between devices with their start and end apart: 16 -> 13, of which waited for: 10 -> 10; matrix products, arithmetic and copies ran while one was open for 0% -> 0% of each run, Pallas kernels for 2% -> 3%
where the time goes in v5:
time: 167 us; the launch traced here: 166 us
  blocking collectives  83.9 us (50%)
  starting transfers between devices  30.5 us (18%)
  Pallas kernels  25.8 us (15%)
  waiting for transfers between devices  21.5 us (13%)
  local copies, waits for them, and re-layouts  2.91 us (2%)
    ppermute x12, starting transfers between devices, swap(): return lax.ppermute(x, axis, SWAP)  27 us
    ppermute x12, waiting for transfers between devices, swap(): return lax.ppermute(x, axis, SWAP)  21.5 us
    all_to_all x2, blocking collectives, over_groups(): return lax.all_to_all(x, GRP, 0, 0, tiled=True)  18.5 us
    all_to_all x1, blocking collectives, body(): f = lax.all_to_all(f_cols, 'zh', 0, 0, tiled=True)  16 us
    all_to_all x1, blocking collectives, body(): g, mine = image_sum(lax.all_to_all(g, QUAD, 0, 0, tiled=True), units)  13.9 us
    all_to_all x1, blocking collectives, to_all(): lax.all_to_all(jnp.broadcast_to(x[None], (size, *x.shape)), axes, 0, 0, t...  12.9 us
    all_to_all x1, blocking collectives, body(): g = lax.all_to_all(g, QUAD, 0, 0, tiled=True)  11.4 us
    all_to_all x1, blocking collectives, body(): got = lax.all_to_all(partial, 'zh', 0, 0, tiled=True)  11.2 us
  transfers between devices with their start and end apart: 13, of which 10 were waited for; matrix products, arithmetic and copies ran while one was open for 0% of the time, Pallas kernels for 3%

profile of v5, /device:TPU:1, one launch (start us, length us, event | category | flops | bytes accessed | tf_op | source)
XLA Modules:
  0.0 166.1 jit_solution(6009932980965533381)
XLA Ops:
  0.7 1.0 slice_bitcast_fusion.3
  1.6 16.0 %all_to_all.40 = f32[4,32,256]{2,1,0:T(8,128)S(1)} all-to-all(f32[4,32,256]{2,1,0:T(8,128)S(1)} %pad_maximum_fusion.1), channel_id=1, replica_groups=mesh['xl'=2,'y'=4,'xh'=2,'zh'=4,'zl'=2,'c'=2] {'zh'}, dimensions={0} | all-to-all | bytes 262144 | tf_op jit(solution)/shard_map/all_to_all | solution.py:374
  17.7 1.8 %broadcast_in_dim.6 = s32[4,32,1024]{2,1,0:T(8,128)} broadcast(s32[32,1024]{1,0:T(8,128)} %param.5), dimensions={1,2} | broadcast | bytes 655360 | tf_op jit(solution)/shard_map/broadcast_in_dim | solution.py:33
  19.4 3.5 %all-to-all-start = ((s32[4,32,1024]{2,1,0:T(8,128)}), s32[4,32,1024]{2,1,0:T(8,128)S(1)}, u32[]{:S(2)}, u32[]{:S(2)}) async-start(s32[4,32,1024]{2,1,0:T(8,128)} %broadcast_in_dim.6), calls=%async_computation | async-start | bytes 1048576 | tf_op jit(solution)/shard_map/all_to_all | solution.py:33
  22.9 0.1 copy.8
  23.0 2.8 %collective-permute-start = (f32[1,256,128]{2,1,0:T(8,128)S(1)}, f32[1,256,128]{2,1,0:T(8,128)S(1)}, u32[]{:S(2)}, u32[]{:S(2)}) collective-permute-start(f32[1,256,128]{2,1,0:T(8,128)S(1)} %bitcast.33), channel_id=1, source_target_pairs={{0,16},{16,0},{1,17},{17,1},{2,18},{18,2},{3,19},{19,3},{4,20},{20... | collective-permute-start | bytes 393224 | tf_op jit(solution)/shard_map/ppermute | solution.py:29
  25.8 2.6 %collective-permute-done = f32[1,256,128]{2,1,0:T(8,128)S(1)} collective-permute-done((f32[1,256,128]{2,1,0:T(8,128)S(1)}, f32[1,256,128]{2,1,0:T(8,128)S(1)}, u32[]{:S(2)}, u32[]{:S(2)}) %collective-permute-start) | collective-permute-done | bytes 131104 | tf_op jit(solution)/shard_map/ppermute | solution.py:29
  28.4 0.8 collective-permute-start.1
  29.3 0.1 pad_add_fusion.pos_ref
  29.4 4.5 %collective-permute-start.2 = (f32[2,256,128]{2,1,0:T(8,128)S(1)}, f32[2,256,128]{2,1,0:T(8,128)}, u32[]{:S(2)}, u32[]{:S(2)}) collective-permute-start(f32[2,256,128]{2,1,0:T(8,128)S(1)} %pad_maximum_fusion.f0), channel_id=1, source_target_pairs={{0,1},{1,0},{2,3},{3,2},{4,5},{5,4},{6,7},{7,6},{8,9},{9,8},{10,11... | collective-permute-start | bytes 786440 | tf_op jit(solution)/shard_map/ppermute | solution.py:29
  33.9 6.2 %collective-permute-done.1.f1 = f32[2,256,128]{2,1,0:T(8,128)} collective-permute-done((f32[2,256,128]{2,1,0:T(8,128)S(1)}, f32[2,256,128]{2,1,0:T(8,128)}, u32[]{:S(2)}, u32[]{:S(2)}) %collective-permute-start.1) | collective-permute-done | bytes 262176 | tf_op jit(solution)/shard_map/ppermute | solution.py:29
  40.1 2.4 %collective-permute-start.3 = (f32[2,256,128]{2,1,0:T(8,128)}, f32[2,256,128]{2,1,0:T(8,128)}, u32[]{:S(2)}, u32[]{:S(2)}) collective-permute-start(f32[2,256,128]{2,1,0:T(8,128)} %collective-permute-done.1.f1), channel_id=1, source_target_pairs={{0,1},{1,0},{2,3},{3,2},{4,5},{5,4},{6,7},{7,6},{8,9},{9,8},{10,11... | collective-permute-start | bytes 786440 | tf_op jit(solution)/shard_map/ppermute | solution.py:29
  42.5 4.4 %shard_map.68 = (bf16[1024,4096]{1,0:T(8,128)(2,1)S(1)}, f32[256,4096]{1,0:T(8,128)S(1)}) custom-call(s32[37]{0:T(128)S(1)} %pad_add_fusion.pos_ref, s32[4,32,1024]{2,1,0:T(8,128)S(1)} %all-to-all-done.packed_ref, bf16[1024,256]{1,0:T(8,128)(2,1)S(1)} %constant_dynamic-slice_fusion.w_ref, f32[8,128]{1,0:T(8,128)S(1)} %bitcast.31), custom_call_target="tpu_custom_call" | custom-call | flops 4000000000 | bytes 1048576 | tf_op jit(solution)/shard_map/pallas_call | solution.py:106
  47.0 6.7 %shard_map.69 = f32[40,128]{1,0:T(8,128)S(1)} custom-call(s32[37]{0:T(128)S(1)} %pad_add_fusion.pos_ref, bf16[1024,4096]{1,0:T(8,128)(2,1)S(1)} %get-tuple-element.15.s_ref, f32[256,4096]{1,0:T(8,128)S(1)} %get-tuple-element.16.h_ref, f32[2,256,128]{2,1,0:T(8,128)S(1)} %pad_maximum_fusion.f0, f32[2,256,128]{2,1,0:T(8,128)} %collective-permute-done.1.f1, ...), custom_call_target="tpu_custom_call" | custom-call | flops 4000000000 | bytes 1048576 | tf_op jit(solution)/shard_map/pallas_call | solution.py:154
  53.7 12.9 %all_to_all.41.got_ref = f32[4,40,128]{2,1,0:T(8,128)S(1)} all-to-all(f32[4,40,128]{2,1,0:T(8,128)S(1)} %broadcast_in_dim.8), channel_id=1, replica_groups=mesh['xl'=2,'y'=4,'xh'=2,'zh'=4,'zl'=2,'c'=2] {'zh'}, dimensions={0} | all-to-all | bytes 163840 | tf_op jit(solution)/shard_map/all_to_all | solution.py:33
  66.6 10.5 %all_to_all.42.got_ref = f32[8,40,128]{2,1,0:T(8,128)S(1)} all-to-all(f32[8,40,128]{2,1,0:T(8,128)S(1)} %shard_map.70), channel_id=1, replica_groups=mesh['xl'=2,'y'=4,'xh'=2,'zh'=4,'zl'=2,'c'=2] {'xl','y'}, dimensions={0} | all-to-all | bytes 327680 | tf_op jit(solution)/shard_map/all_to_all | solution.py:226
  77.1 0.2 shard_map.71
  77.4 3.5 %collective-permute-start.4 = (f32[2,128]{1,0:T(2,128)S(1)}, f32[2,128]{1,0:T(2,128)S(1)}, u32[]{:S(2)}, u32[]{:S(2)}) collective-permute-start(f32[2,128]{1,0:T(2,128)S(1)} %get-tuple-element.18), channel_id=1, source_target_pairs={{0,1},{1,0},{2,3},{3,2},{4,5},{5,4},{6,7},{7,6},{8,9},{9,8},{10,11... | collective-permute-start | bytes 3080 | tf_op jit(solution)/shard_map/ppermute | solution.py:29
  80.9 0.8 collective-permute-done.4
  81.7 0.1 add_select_fusion.5
  81.8 0.8 collective-permute-start.5
  82.6 1.7 %collective-permute-done.5 = f32[2,128]{1,0:T(2,128)S(1)} collective-permute-done((f32[2,128]{1,0:T(2,128)S(1)}, f32[2,128]{1,0:T(2,128)S(1)}, u32[]{:S(2)}, u32[]{:S(2)}) %collective-permute-start.5) | collective-permute-done | bytes 1056 | tf_op jit(solution)/shard_map/ppermute | solution.py:29
  84.3 0.1 add_select_fusion.4
  84.3 2.5 %collective-permute-start.6 = (f32[2,128]{1,0:T(2,128)S(1)}, f32[2,128]{1,0:T(2,128)S(1)}, u32[]{:S(2)}, u32[]{:S(2)}) collective-permute-start(f32[2,128]{1,0:T(2,128)S(1)} %add_select_fusion.4), channel_id=1, source_target_pairs={{0,16},{16,0},{1,17},{17,1},{2,18},{18,2},{3,19},{19,3},{4,20},{20... | collective-permute-start | bytes 3080 | tf_op jit(solution)/shard_map/ppermute | solution.py:29
  86.8 1.5 collective-permute-done.6
  88.3 0.1 add_select_fusion.3.st_ref.st0_ref
  88.4 6.2 %shard_map.72 = (f32[4,264,128]{2,1,0:T(8,128)S(1)}, f32[4,264,128]{2,1,0:T(8,128)S(1)}) custom-call(s32[37]{0:T(128)S(1)} %pad_add_fusion.pos_ref, bf16[1024,4096]{1,0:T(8,128)(2,1)S(1)} %get-tuple-element.15.s_ref, f32[256,4096]{1,0:T(8,128)S(1)} %get-tuple-element.16.h_ref, f32[32,128]{1,0:T(8,128)S(1)} %get-tuple-element.17.v_ref, ...), custom_call_target="tpu_custom_call" | custom-call | flops 4000000000 | bytes 1048576 | tf_op jit(solution)/shard_map/pallas_call | solution.py:308
  94.5 2.7 %collective-permute-start.7 = (f32[4,264,128]{2,1,0:T(8,128)S(1)}, f32[4,264,128]{2,1,0:T(8,128)S(1)}, u32[]{:S(2)}, u32[]{:S(2)}) collective-permute-start(f32[4,264,128]{2,1,0:T(8,128)S(1)} %get-tuple-element.20), channel_id=1, source_target_pairs={{0,1},{1,0},{2,3},{3,2},{4,5},{5,4},{6,7},{7,6},{8,9},{9,8},{10,11... | collective-permute-start | bytes 1622024 | tf_op jit(solution)/shard_map/ppermute | solution.py:29
  97.2 1.6 collective-permute-done.7
  98.9 13.9 %all_to_all.43.got_ref = f32[4,264,128]{2,1,0:T(8,128)S(1)} all-to-all(f32[4,264,128]{2,1,0:T(8,128)S(1)} %add.119), channel_id=1, replica_groups=mesh['xl'=2,'y'=4,'xh'=2,'zh'=4,'zl'=2,'c'=2] {'xh','zl'}, dimensions={0} | all-to-all | bytes 1081344 | tf_op jit(solution)/shard_map/all_to_all | solution.py:392
  112.8 0.1 shard_map.73
  112.9 11.4 %all_to_all.44.g0 = f32[4,264,128]{2,1,0:T(8,128)S(1)} all-to-all(f32[4,264,128]{2,1,0:T(8,128)S(1)} %get-tuple-element.21), channel_id=1, replica_groups=mesh['xl'=2,'y'=4,'xh'=2,'zh'=4,'zl'=2,'c'=2] {'xh','zl'}, dimensions={0} | all-to-all | bytes 1081344 | tf_op jit(solution)/shard_map/all_to_all | solution.py:393
  124.2 2.5 %collective-permute-start.8 = (f32[4,264,128]{2,1,0:T(8,128)S(1)}, f32[4,264,128]{2,1,0:T(8,128)S(1)}, u32[]{:S(2)}, u32[]{:S(2)}) collective-permute-start(f32[4,264,128]{2,1,0:T(8,128)S(1)} %all_to_all.44.g0), channel_id=1, source_target_pairs={{0,1},{1,0},{2,3},{3,2},{4,5},{5,4},{6,7},{7,6},{8,9},{9,8},{10,11... | collective-permute-start | bytes 1622024 | tf_op jit(solution)/shard_map/ppermute | solution.py:29
  126.7 1.6 collective-permute-done.8.g1
  128.3 7.1 %shard_map.74 = f32[4,104,128]{2,1,0:T(8,128)S(1)} custom-call(s32[37]{0:T(128)S(1)} %pad_add_fusion.pos_ref, bf16[1024,4096]{1,0:T(8,128)(2,1)S(1)} %get-tuple-element.15.s_ref, f32[256,4096]{1,0:T(8,128)S(1)} %get-tuple-element.16.h_ref, f32[2,256,128]{2,1,0:T(8,128)S(1)} %pad_maximum_fusion.f0, f32[2,256,128]{2,1,0:T(8,128)} %collective-permute-done.1.f1, ...), custom_call_target="tpu_custom_call" | custom-call | flops 4000000000 | bytes 1048576 | tf_op jit(solution)/shard_map/pallas_call | solution.py:200
  135.3 11.2 %all_to_all.45.got_ref = f32[4,104,128]{2,1,0:T(8,128)S(1)} all-to-all(f32[4,104,128]{2,1,0:T(8,128)S(1)} %shard_map.74), channel_id=1, replica_groups=mesh['xl'=2,'y'=4,'xh'=2,'zh'=4,'zl'=2,'c'=2] {'zh'}, dimensions={0} | all-to-all | bytes 425984 | tf_op jit(solution)/shard_map/all_to_all | solution.py:396
  146.6 8.0 %all_to_all.46.got_ref = f32[8,40,128]{2,1,0:T(8,128)S(1)} all-to-all(f32[8,40,128]{2,1,0:T(8,128)S(1)} %shard_map.75), channel_id=1, replica_groups=mesh['xl'=2,'y'=4,'xh'=2,'zh'=4,'zl'=2,'c'=2] {'xl','y'}, dimensions={0} | all-to-all | bytes 327680 | tf_op jit(solution)/shard_map/all_to_all | solution.py:226
  154.6 0.3 shard_map.76
  154.9 3.1 %collective-permute-start.9 = (f32[2,128]{1,0:T(2,128)S(1)}, f32[2,128]{1,0:T(2,128)S(1)}, u32[]{:S(2)}, u32[]{:S(2)}) collective-permute-start(f32[2,128]{1,0:T(2,128)S(1)} %get-tuple-element.24), channel_id=1, source_target_pairs={{0,1},{1,0},{2,3},{3,2},{4,5},{5,4},{6,7},{7,6},{8,9},{9,8},{10,11... | collective-permute-start | bytes 3080 | tf_op jit(solution)/shard_map/ppermute | solution.py:29
  157.9 0.8 collective-permute-done.9
  158.7 0.1 add_select_fusion.2
  158.8 1.1 collective-permute-start.10
  159.9 1.4 collective-permute-done.10
  161.3 0.1 add_select_fusion.1
  161.3 0.4 collective-permute-start.11
  161.8 3.5 %collective-permute-done.11 = f32[2,128]{1,0:T(2,128)S(1)} collective-permute-done((f32[2,128]{1,0:T(2,128)S(1)}, f32[2,128]{1,0:T(2,128)S(1)}, u32[]{:S(2)}, u32[]{:S(2)}) %collective-permute-start.11) | collective-permute-done | bytes 1056 | tf_op jit(solution)/shard_map/ppermute | solution.py:29
  165.3 0.1 add_select_fusion.st1_ref
  165.4 0.7 shard_map.77
  (27 shorter events, 0.3 us)
Async XLA Ops:
  0.6 28.7 %copy-start = (bf16[1024,1024]{1,0:T(8,128)(2,1)S(1)}, bf16[1024,1024]{1,0:T(8,128)(2,1)}, u32[]{:S(2)}) copy-start(bf16[1024,1024]{1,0:T(8,128)(2,1)} %param.6) | copy-start | bytes 6291460
  0.6 41.8 %copy-start.3 = (f32[1024]{0:T(1024)S(1)}, f32[1024]{0:T(1024)}, u32[]{:S(2)}) copy-start(f32[1024]{0:T(1024)} %param.7) | copy-start | bytes 12292
  19.4 23.1 %all-to-all-start = ((s32[4,32,1024]{2,1,0:T(8,128)}), s32[4,32,1024]{2,1,0:T(8,128)S(1)}, u32[]{:S(2)}, u32[]{:S(2)}) async-start(s32[4,32,1024]{2,1,0:T(8,128)} %broadcast_in_dim.6), calls=%async_computation | async-start | bytes 1048576 | tf_op jit(solution)/shard_map/all_to_all | solution.py:33
  23.0 5.4 %collective-permute-start = (f32[1,256,128]{2,1,0:T(8,128)S(1)}, f32[1,256,128]{2,1,0:T(8,128)S(1)}, u32[]{:S(2)}, u32[]{:S(2)}) collective-permute-start(f32[1,256,128]{2,1,0:T(8,128)S(1)} %bitcast.33), channel_id=1, source_target_pairs={{0,16},{16,0},{1,17},{17,1},{2,18},{18,2},{3,19},{19,3},{4,20},{20... | collective-permute-start | bytes 393224 | tf_op jit(solution)/shard_map/ppermute | solution.py:29
  28.4 11.6 %collective-permute-start.1 = (f32[2,256,128]{2,1,0:T(8,128)S(1)}, f32[2,256,128]{2,1,0:T(8,128)}, u32[]{:S(2)}, u32[]{:S(2)}) collective-permute-start(f32[2,256,128]{2,1,0:T(8,128)S(1)} %pad_maximum_fusion.f0), channel_id=1, source_target_pairs={{0,2},{2,0},{1,3},{3,1},{4,6},{6,4},{5,7},{7,5},{8,10},{10,8},{9,1... | collective-permute-start | bytes 786440 | tf_op jit(solution)/shard_map/ppermute | solution.py:29
  29.4 17.5 %collective-permute-start.2 = (f32[2,256,128]{2,1,0:T(8,128)S(1)}, f32[2,256,128]{2,1,0:T(8,128)}, u32[]{:S(2)}, u32[]{:S(2)}) collective-permute-start(f32[2,256,128]{2,1,0:T(8,128)S(1)} %pad_maximum_fusion.f0), channel_id=1, source_target_pairs={{0,1},{1,0},{2,3},{3,2},{4,5},{5,4},{6,7},{7,6},{8,9},{9,8},{10,11... | collective-permute-start | bytes 786440 | tf_op jit(solution)/shard_map/ppermute | solution.py:29
  40.1 6.9 %collective-permute-start.3 = (f32[2,256,128]{2,1,0:T(8,128)}, f32[2,256,128]{2,1,0:T(8,128)}, u32[]{:S(2)}, u32[]{:S(2)}) collective-permute-start(f32[2,256,128]{2,1,0:T(8,128)} %collective-permute-done.1.f1), channel_id=1, source_target_pairs={{0,1},{1,0},{2,3},{3,2},{4,5},{5,4},{6,7},{7,6},{8,9},{9,8},{10,11... | collective-permute-start | bytes 786440 | tf_op jit(solution)/shard_map/ppermute | solution.py:29
  42.5 4.5 %copy-start.2 = (f32[1024]{0:T(1024)S(1)}, f32[1024]{0:T(1024)}, u32[]{:S(2)}) copy-start(f32[1024]{0:T(1024)} %param.9) | copy-start | bytes 12292
  77.4 4.3 %collective-permute-start.4 = (f32[2,128]{1,0:T(2,128)S(1)}, f32[2,128]{1,0:T(2,128)S(1)}, u32[]{:S(2)}, u32[]{:S(2)}) collective-permute-start(f32[2,128]{1,0:T(2,128)S(1)} %get-tuple-element.18), channel_id=1, source_target_pairs={{0,1},{1,0},{2,3},{3,2},{4,5},{5,4},{6,7},{7,6},{8,9},{9,8},{10,11... | collective-permute-start | bytes 3080 | tf_op jit(solution)/shard_map/ppermute | solution.py:29
  81.8 2.4 %collective-permute-start.5 = (f32[2,128]{1,0:T(2,128)S(1)}, f32[2,128]{1,0:T(2,128)S(1)}, u32[]{:S(2)}, u32[]{:S(2)}) collective-permute-start(f32[2,128]{1,0:T(2,128)S(1)} %add_select_fusion.5), channel_id=1, source_target_pairs={{0,2},{2,0},{1,3},{3,1},{4,6},{6,4},{5,7},{7,5},{8,10},{10,8},{9,1... | collective-permute-start | bytes 3080 | tf_op jit(solution)/shard_map/ppermute | solution.py:29
  84.3 3.9 %collective-permute-start.6 = (f32[2,128]{1,0:T(2,128)S(1)}, f32[2,128]{1,0:T(2,128)S(1)}, u32[]{:S(2)}, u32[]{:S(2)}) collective-permute-start(f32[2,128]{1,0:T(2,128)S(1)} %add_select_fusion.4), channel_id=1, source_target_pairs={{0,16},{16,0},{1,17},{17,1},{2,18},{18,2},{3,19},{19,3},{4,20},{20... | collective-permute-start | bytes 3080 | tf_op jit(solution)/shard_map/ppermute | solution.py:29
  94.5 4.3 %collective-permute-start.7 = (f32[4,264,128]{2,1,0:T(8,128)S(1)}, f32[4,264,128]{2,1,0:T(8,128)S(1)}, u32[]{:S(2)}, u32[]{:S(2)}) collective-permute-start(f32[4,264,128]{2,1,0:T(8,128)S(1)} %get-tuple-element.20), channel_id=1, source_target_pairs={{0,1},{1,0},{2,3},{3,2},{4,5},{5,4},{6,7},{7,6},{8,9},{9,8},{10,11... | collective-permute-start | bytes 1622024 | tf_op jit(solution)/shard_map/ppermute | solution.py:29
  124.2 4.0 %collective-permute-start.8 = (f32[4,264,128]{2,1,0:T(8,128)S(1)}, f32[4,264,128]{2,1,0:T(8,128)S(1)}, u32[]{:S(2)}, u32[]{:S(2)}) collective-permute-start(f32[4,264,128]{2,1,0:T(8,128)S(1)} %all_to_all.44.g0), channel_id=1, source_target_pairs={{0,1},{1,0},{2,3},{3,2},{4,5},{5,4},{6,7},{7,6},{8,9},{9,8},{10,11... | collective-permute-start | bytes 1622024 | tf_op jit(solution)/shard_map/ppermute | solution.py:29
  128.3 37.1 %copy-start.1 = (f32[32,1024]{1,0:T(8,128)S(1)}, f32[32,1024]{1,0:T(8,128)}, u32[]{:S(2)}) copy-start(f32[32,1024]{1,0:T(8,128)} %f_ref.1) | copy-start | bytes 393220
  154.9 3.9 %collective-permute-start.9 = (f32[2,128]{1,0:T(2,128)S(1)}, f32[2,128]{1,0:T(2,128)S(1)}, u32[]{:S(2)}, u32[]{:S(2)}) collective-permute-start(f32[2,128]{1,0:T(2,128)S(1)} %get-tuple-element.24), channel_id=1, source_target_pairs={{0,1},{1,0},{2,3},{3,2},{4,5},{5,4},{6,7},{7,6},{8,9},{9,8},{10,11... | collective-permute-start | bytes 3080 | tf_op jit(solution)/shard_map/ppermute | solution.py:29
  158.8 2.4 %collective-permute-start.10 = (f32[2,128]{1,0:T(2,128)S(1)}, f32[2,128]{1,0:T(2,128)S(1)}, u32[]{:S(2)}, u32[]{:S(2)}) collective-permute-start(f32[2,128]{1,0:T(2,128)S(1)} %add_select_fusion.2), channel_id=1, source_target_pairs={{0,2},{2,0},{1,3},{3,1},{4,6},{6,4},{5,7},{7,5},{8,10},{10,8},{9,1... | collective-permute-start | bytes 3080 | tf_op jit(solution)/shard_map/ppermute | solution.py:29
  161.3 3.9 %collective-permute-start.11 = (f32[2,128]{1,0:T(2,128)S(1)}, f32[2,128]{1,0:T(2,128)S(1)}, u32[]{:S(2)}, u32[]{:S(2)}) collective-permute-start(f32[2,128]{1,0:T(2,128)S(1)} %add_select_fusion.1), channel_id=1, source_target_pairs={{0,16},{16,0},{1,17},{17,1},{2,18},{18,2},{3,19},{19,3},{4,20},{20... | collective-permute-start | bytes 3080 | tf_op jit(solution)/shard_map/ppermute | solution.py:29

commit v6 on v5

--- a/solution.py
+++ b/solution.py
@@ -12,6 +12,7 @@
 GRP = ("xl", "y")
 SMP = ("xh", "zh", "zl", "c")
 QUAD = ("xh", "zl")
+SETS = ("xh", "zl", "c")
 SWAP = [(0, 1), (1, 0)]
 LAM = 0.01
 ROWS = 32
@@ -167,7 +168,7 @@
 def second_kernel(samples, pos_ref, s_ref, h_ref, f0, f1, f2, f3, fb_ref, g0, g1, mine_ref, st_ref, norm_ref, out_ref, lhs):
     units = h_ref.shape[0]
     norm0 = norm_ref[0:1, :]
-    a = step_of(norm0, st_ref[1:2, :], samples, norm0)
+    a = step_of(norm0, joined(st_ref, h_ref.shape[1])[1], samples, norm0)
     rr = jnp.zeros((units, 128), F32)
     rf = jnp.zeros((units, 128), F32)
     for b in range(NB):
@@ -210,6 +211,7 @@
     mean = jnp.sum(v) / v.size
     st_ref[0:1, :] = jnp.full((1, 128), mean, F32)
     st_ref[1:2, :] = total((v - mean) ** 2)
+    st_ref[2:, :] = jnp.zeros((st_ref.shape[0] - 2, 128), F32)
 
 
 def over_chain_kernel(got_ref, all_ref):
@@ -243,7 +245,7 @@
 
 def first_sum(got):
     shape = lambda *s: jax.ShapeDtypeStruct(s, F32)
-    return call(first_sum_kernel, [VMEM], [shape(got.shape[1] - EXTRA, 128), shape(2, 128), shape(EXTRA, 128)])(got)
+    return call(first_sum_kernel, [VMEM], [shape(got.shape[1] - EXTRA, 128), shape(8, 128), shape(EXTRA, 128)])(got)
 
 
 def second_sum_kernel(got_ref, v_ref, norm_ref, st_ref, next_ref):
@@ -255,28 +257,31 @@
 
 def second_sum(got, values, norm):
     shape = lambda *s: jax.ShapeDtypeStruct(s, F32)
-    return call(second_sum_kernel, [VMEM] * 3, [shape(2, 128), shape(EXTRA, 128)])(
+    return call(second_sum_kernel, [VMEM] * 3, [shape(8, 128), shape(EXTRA, 128)])(
         got, values, norm
     )
 
 
-def merged(st, count, axis):
-    got = swap(st, axis)
-    delta = got[0:1] - st[0:1]
-    first = lax.broadcasted_iota(jnp.int32, st.shape, 0) == 0
-    return jnp.where(first, 0.5 * (st + got), st + got + (0.5 * count) * delta * delta)
-
-
-def over_sets(st, count):
-    for axis in ("c", "zl", "xh"):
-        st = merged(st, count, axis)
-        count *= 2
-    return st
+def of_sets(st):
+    return to_all(st, SETS, lax.axis_size(SETS))
+
+
+def joined(st_ref, count):
+    sets = st_ref.shape[0]
+    mean = st_ref[0, 0:1, :]
+    for k in range(1, sets):
+        mean = mean + st_ref[k, 0:1, :]
+    mean = mean * (1.0 / sets)
+    spread = jnp.zeros_like(mean)
+    for k in range(sets):
+        off = st_ref[k, 0:1, :] - mean
+        spread = spread + (st_ref[k, 1:2, :] + count * (off * off))
+    return mean, spread
 
 
 def image_kernel(samples, pos_ref, s_ref, h_ref, v_ref, st_ref, keep_ref, send_ref, acc, lanes):
     units = h_ref.shape[0]
-    mean = st_ref[0:1, 0:1]
+    mean = joined(st_ref, h_ref.shape[1])[0][:, 0:1]
     acc[...] = jnp.zeros(acc.shape, F32)
     lanes[...] = jnp.zeros(lanes.shape, F32)
 
@@ -328,11 +333,12 @@
 
 
 def update_kernel(samples, f_ref, fb_ref, got_ref, st0_ref, norm_ref, st1_ref, next_ref, w_ref, b_ref):
+    count = samples // st0_ref.shape[0]
     norm0, norm1 = norm_ref[0:1, 0:1], next_ref[0:1, 0:1]
     cross = next_ref[1:2, 0:1]
     beta = norm1 / norm0
-    step0 = step_of(norm0, st0_ref[1:2, 0:1], samples, norm0)
-    step1 = step_of(norm1, st1_ref[1:2, 0:1], samples, norm1 + 2.0 * beta * cross + beta * beta * norm0)
+    step0 = step_of(norm0, joined(st0_ref, count)[1][:, 0:1], samples, norm0)
+    step1 = step_of(norm1, joined(st1_ref, count)[1][:, 0:1], samples, norm1 + 2.0 * beta * cross + beta * beta * norm0)
 
     def update(f, g):
         r = f - step0 * (g + LAM * f)
@@ -384,8 +390,7 @@
     partial = first_pass(pos, spins, hidden, f, fb)
     rows = partial.shape[0]
     values, st, norm = first_sum(over_groups(to_all(partial, "zh", parts), rows))
-    n = values.size
-    st0 = over_sets(st, n)
+    st0 = of_sets(st)
 
     keep, send = image_pass(samples, pos, spins, hidden, values, st0)
     g = keep + swap(send, "c")
@@ -395,7 +400,7 @@
     partial = second_pass(samples, pos, spins, hidden, f, fb, g, swap(g, "c"), mine, st0, norm)
     got = lax.all_to_all(partial, "zh", 0, 0, tiled=True)
     st, norms = second_sum(over_groups(got, rows), values, norm)
-    st1 = over_sets(st, n)
+    st1 = of_sets(st)
     out_w, out_b = update_pass(samples, force_w, fb, got, st0, norm, st1, norms)
     return out_w, out_b.reshape(-1)
 

time: 167 us -> 166 us (level)
  blocking collectives: 83.9 us -> 107 us
  starting transfers between devices: 30.5 us -> 17.4 us
  waiting for transfers between devices: 21.5 us -> 11.9 us
    all_to_all x1 -> x3, blocking collectives: 12.9 us -> 37.4 us  [to_all(): lax.all_to_all(jnp.broadcast_to(x[None], (size, *x.shape)), axes, 0, 0, t...]
    ppermute x12 -> x6, starting transfers between devices: 27 us -> 13.9 us  [swap(): return lax.ppermute(x, axis, SWAP)]
    ppermute x12 -> x6, waiting for transfers between devices: 21.5 us -> 11.9 us  [swap(): return lax.ppermute(x, axis, SWAP)]
  transfers between devices with their start and end apart: 13 -> 7, of which waited for: 10 -> 4; matrix products, arithmetic and copies ran while one was open for 0% -> 0% of each run, Pallas kernels for 3% -> 3%
where the time goes in v6:
time: 166 us
  blocking collectives  107 us (64%)
  Pallas kernels  26 us (16%)
  starting transfers between devices  17.4 us (10%)
  waiting for transfers between devices  11.9 us (7%)
  local copies, waits for them, and re-layouts  2.92 us (2%)
    all_to_all x3, blocking collectives, to_all(): lax.all_to_all(jnp.broadcast_to(x[None], (size, *x.shape)), axes, 0, 0, t...  37.4 us
    all_to_all x2, blocking collectives, over_groups(): return lax.all_to_all(x, GRP, 0, 0, tiled=True)  18.5 us
    all_to_all x1, blocking collectives, body(): f = lax.all_to_all(f_cols, 'zh', 0, 0, tiled=True)  16 us
    ppermute x6, starting transfers between devices, swap(): return lax.ppermute(x, axis, SWAP)  13.9 us
    all_to_all x1, blocking collectives, body(): g, mine = image_sum(lax.all_to_all(g, QUAD, 0, 0, tiled=True), units)  12.3 us
    ppermute x6, waiting for transfers between devices, swap(): return lax.ppermute(x, axis, SWAP)  11.9 us
    all_to_all x1, blocking collectives, body(): g = lax.all_to_all(g, QUAD, 0, 0, tiled=True)  11.4 us
    all_to_all x1, blocking collectives, body(): got = lax.all_to_all(partial, 'zh', 0, 0, tiled=True)  11.2 us
  transfers between devices with their start and end apart: 7, of which 4 were waited for; matrix products, arithmetic and copies ran while one was open for 0% of the time, Pallas kernels for 3%

profile of v6, /device:TPU:1, one launch (start us, length us, event | category | flops | bytes accessed | tf_op | source)
XLA Modules:
  0.0 165.8 jit_solution(563221215957726201)
XLA Ops:
  0.6 0.0 copy-start
  0.6 0.0 copy-start.3
  0.7 1.0 slice_bitcast_fusion.3
  1.6 16.0 %all_to_all.50 = f32[4,32,256]{2,1,0:T(8,128)S(1)} all-to-all(f32[4,32,256]{2,1,0:T(8,128)S(1)} %pad_maximum_fusion.1), channel_id=1, replica_groups=mesh['xl'=2,'y'=4,'xh'=2,'zh'=4,'zl'=2,'c'=2] {'zh'}, dimensions={0} | all-to-all | bytes 262144 | tf_op jit(solution)/shard_map/all_to_all | solution.py:380
  17.7 1.8 %broadcast_in_dim.10 = s32[4,32,1024]{2,1,0:T(8,128)} broadcast(s32[32,1024]{1,0:T(8,128)} %param.5), dimensions={1,2} | broadcast | bytes 655360 | tf_op jit(solution)/shard_map/broadcast_in_dim | solution.py:34
  19.4 3.5 %all-to-all-start = ((s32[4,32,1024]{2,1,0:T(8,128)}), s32[4,32,1024]{2,1,0:T(8,128)S(1)}, u32[]{:S(2)}, u32[]{:S(2)}) async-start(s32[4,32,1024]{2,1,0:T(8,128)} %broadcast_in_dim.10), calls=%async_computation | async-start | bytes 1048576 | tf_op jit(solution)/shard_map/all_to_all | solution.py:34
  22.9 0.1 copy.8
  23.0 2.8 %collective-permute-start = (f32[1,256,128]{2,1,0:T(8,128)S(1)}, f32[1,256,128]{2,1,0:T(8,128)S(1)}, u32[]{:S(2)}, u32[]{:S(2)}) collective-permute-start(f32[1,256,128]{2,1,0:T(8,128)S(1)} %bitcast.21), channel_id=1, source_target_pairs={{0,16},{16,0},{1,17},{17,1},{2,18},{18,2},{3,19},{19,3},{4,20},{20... | collective-permute-start | bytes 393224 | tf_op jit(solution)/shard_map/ppermute | solution.py:30
  25.8 2.6 %collective-permute-done = f32[1,256,128]{2,1,0:T(8,128)S(1)} collective-permute-done((f32[1,256,128]{2,1,0:T(8,128)S(1)}, f32[1,256,128]{2,1,0:T(8,128)S(1)}, u32[]{:S(2)}, u32[]{:S(2)}) %collective-permute-start) | collective-permute-done | bytes 131104 | tf_op jit(solution)/shard_map/ppermute | solution.py:30
  28.4 0.8 collective-permute-start.1
  29.3 0.1 pad_add_fusion.pos_ref
  29.4 0.0 copy-done
  29.4 0.1 constant_dynamic-slice_fusion.w_ref
  29.4 4.5 %collective-permute-start.2 = (f32[2,256,128]{2,1,0:T(8,128)S(1)}, f32[2,256,128]{2,1,0:T(8,128)}, u32[]{:S(2)}, u32[]{:S(2)}) collective-permute-start(f32[2,256,128]{2,1,0:T(8,128)S(1)} %pad_maximum_fusion.f0), channel_id=1, source_target_pairs={{0,1},{1,0},{2,3},{3,2},{4,5},{5,4},{6,7},{7,6},{8,9},{9,8},{10,11... | collective-permute-start | bytes 786440 | tf_op jit(solution)/shard_map/ppermute | solution.py:30
  33.9 6.2 %collective-permute-done.1.f1 = f32[2,256,128]{2,1,0:T(8,128)} collective-permute-done((f32[2,256,128]{2,1,0:T(8,128)S(1)}, f32[2,256,128]{2,1,0:T(8,128)}, u32[]{:S(2)}, u32[]{:S(2)}) %collective-permute-start.1) | collective-permute-done | bytes 262176 | tf_op jit(solution)/shard_map/ppermute | solution.py:30
  40.1 2.4 %collective-permute-start.3 = (f32[2,256,128]{2,1,0:T(8,128)}, f32[2,256,128]{2,1,0:T(8,128)}, u32[]{:S(2)}, u32[]{:S(2)}) collective-permute-start(f32[2,256,128]{2,1,0:T(8,128)} %collective-permute-done.1.f1), channel_id=1, source_target_pairs={{0,1},{1,0},{2,3},{3,2},{4,5},{5,4},{6,7},{7,6},{8,9},{9,8},{10,11... | collective-permute-start | bytes 786440 | tf_op jit(solution)/shard_map/ppermute | solution.py:30
  42.5 0.0 all-to-all-done.packed_ref
  42.5 0.0 copy-done.3
  42.5 0.0 copy-start.2
  42.5 4.4 %shard_map.68 = (bf16[1024,4096]{1,0:T(8,128)(2,1)S(1)}, f32[256,4096]{1,0:T(8,128)S(1)}) custom-call(s32[37]{0:T(128)S(1)} %pad_add_fusion.pos_ref, s32[4,32,1024]{2,1,0:T(8,128)S(1)} %all-to-all-done.packed_ref, bf16[1024,256]{1,0:T(8,128)(2,1)S(1)} %constant_dynamic-slice_fusion.w_ref, f32[8,128]{1,0:T(8,128)S(1)} %bitcast.19), custom_call_target="tpu_custom_call" | custom-call | flops 4000000000 | bytes 1048576 | tf_op jit(solution)/shard_map/pallas_call | solution.py:107
  46.9 0.0 collective-permute-done.2.f2
  46.9 0.0 collective-permute-done.3.f3
  46.9 0.0 copy-done.2
  47.0 6.8 %shard_map.69 = f32[40,128]{1,0:T(8,128)S(1)} custom-call(s32[37]{0:T(128)S(1)} %pad_add_fusion.pos_ref, bf16[1024,4096]{1,0:T(8,128)(2,1)S(1)} %get-tuple-element.15.s_ref, f32[256,4096]{1,0:T(8,128)S(1)} %get-tuple-element.16.h_ref, f32[2,256,128]{2,1,0:T(8,128)S(1)} %pad_maximum_fusion.f0, f32[2,256,128]{2,1,0:T(8,128)} %collective-permute-done.1.f1, ...), custom_call_target="tpu_custom_call" | custom-call | flops 4000000000 | bytes 1048576 | tf_op jit(solution)/shard_map/pallas_call | solution.py:155
  53.8 12.9 %all_to_all.51.got_ref = f32[4,40,128]{2,1,0:T(8,128)S(1)} all-to-all(f32[4,40,128]{2,1,0:T(8,128)S(1)} %broadcast_in_dim.12), channel_id=1, replica_groups=mesh['xl'=2,'y'=4,'xh'=2,'zh'=4,'zl'=2,'c'=2] {'zh'}, dimensions={0} | all-to-all | bytes 163840 | tf_op jit(solution)/shard_map/all_to_all | solution.py:34
  66.7 10.5 %all_to_all.52.got_ref = f32[8,40,128]{2,1,0:T(8,128)S(1)} all-to-all(f32[8,40,128]{2,1,0:T(8,128)S(1)} %shard_map.70), channel_id=1, replica_groups=mesh['xl'=2,'y'=4,'xh'=2,'zh'=4,'zl'=2,'c'=2] {'xl','y'}, dimensions={0} | all-to-all | bytes 327680 | tf_op jit(solution)/shard_map/all_to_all | solution.py:228
  77.2 0.2 shard_map.71
  77.5 13.2 %all_to_all.53.st_ref.st0_ref = f32[8,8,128]{2,1,0:T(8,128)S(1)} all-to-all(f32[8,8,128]{2,1,0:T(8,128)S(1)} %broadcast_in_dim.13), channel_id=1, replica_groups=mesh['xl'=2,'y'=4,'xh'=2,'zh'=4,'zl'=2,'c'=2] {'xh','zl','c'}, dimensions={0} | all-to-all | bytes 65536 | tf_op jit(solution)/shard_map/all_to_all | solution.py:34
  90.7 6.2 %shard_map.72 = (f32[4,264,128]{2,1,0:T(8,128)S(1)}, f32[4,264,128]{2,1,0:T(8,128)S(1)}) custom-call(s32[37]{0:T(128)S(1)} %pad_add_fusion.pos_ref, bf16[1024,4096]{1,0:T(8,128)(2,1)S(1)} %get-tuple-element.15.s_ref, f32[256,4096]{1,0:T(8,128)S(1)} %get-tuple-element.16.h_ref, f32[32,128]{1,0:T(8,128)S(1)} %get-tuple-element.17.v_ref, ...), custom_call_target="tpu_custom_call" | custom-call | flops 4000000000 | bytes 1048576 | tf_op jit(solution)/shard_map/pallas_call | solution.py:313
  96.9 0.9 collective-permute-start.4
  97.8 1.6 collective-permute-done.4
  99.3 0.1 add.23
  99.4 12.3 %all_to_all.54.got_ref = f32[4,264,128]{2,1,0:T(8,128)S(1)} all-to-all(f32[4,264,128]{2,1,0:T(8,128)S(1)} %add.23), channel_id=1, replica_groups=mesh['xl'=2,'y'=4,'xh'=2,'zh'=4,'zl'=2,'c'=2] {'xh','zl'}, dimensions={0} | all-to-all | bytes 1081344 | tf_op jit(solution)/shard_map/all_to_all | solution.py:397
  111.7 0.1 shard_map.73
  111.8 11.4 %all_to_all.55.g0 = f32[4,264,128]{2,1,0:T(8,128)S(1)} all-to-all(f32[4,264,128]{2,1,0:T(8,128)S(1)} %get-tuple-element.21), channel_id=1, replica_groups=mesh['xl'=2,'y'=4,'xh'=2,'zh'=4,'zl'=2,'c'=2] {'xh','zl'}, dimensions={0} | all-to-all | bytes 1081344 | tf_op jit(solution)/shard_map/all_to_all | solution.py:398
  123.1 2.5 %collective-permute-start.5 = (f32[4,264,128]{2,1,0:T(8,128)S(1)}, f32[4,264,128]{2,1,0:T(8,128)S(1)}, u32[]{:S(2)}, u32[]{:S(2)}) collective-permute-start(f32[4,264,128]{2,1,0:T(8,128)S(1)} %all_to_all.55.g0), channel_id=1, source_target_pairs={{0,1},{1,0},{2,3},{3,2},{4,5},{5,4},{6,7},{7,6},{8,9},{9,8},{10,11... | collective-permute-start | bytes 1622024 | tf_op jit(solution)/shard_map/ppermute | solution.py:30
  125.6 1.6 collective-permute-done.5.g1
  127.2 0.0 copy-start.1
  127.2 7.2 %shard_map.74 = f32[4,104,128]{2,1,0:T(8,128)S(1)} custom-call(s32[37]{0:T(128)S(1)} %pad_add_fusion.pos_ref, bf16[1024,4096]{1,0:T(8,128)(2,1)S(1)} %get-tuple-element.15.s_ref, f32[256,4096]{1,0:T(8,128)S(1)} %get-tuple-element.16.h_ref, f32[2,256,128]{2,1,0:T(8,128)S(1)} %pad_maximum_fusion.f0, f32[2,256,128]{2,1,0:T(8,128)} %collective-permute-done.1.f1, ...), custom_call_target="tpu_custom_call" | custom-call | flops 4000000000 | bytes 1048576 | tf_op jit(solution)/shard_map/pallas_call | solution.py:201
  134.3 11.2 %all_to_all.56.got_ref = f32[4,104,128]{2,1,0:T(8,128)S(1)} all-to-all(f32[4,104,128]{2,1,0:T(8,128)S(1)} %shard_map.74), channel_id=1, replica_groups=mesh['xl'=2,'y'=4,'xh'=2,'zh'=4,'zl'=2,'c'=2] {'zh'}, dimensions={0} | all-to-all | bytes 425984 | tf_op jit(solution)/shard_map/all_to_all | solution.py:401
  145.5 8.0 %all_to_all.57.got_ref = f32[8,40,128]{2,1,0:T(8,128)S(1)} all-to-all(f32[8,40,128]{2,1,0:T(8,128)S(1)} %shard_map.75), channel_id=1, replica_groups=mesh['xl'=2,'y'=4,'xh'=2,'zh'=4,'zl'=2,'c'=2] {'xl','y'}, dimensions={0} | all-to-all | bytes 327680 | tf_op jit(solution)/shard_map/all_to_all | solution.py:228
  153.5 0.3 shard_map.76
  153.8 11.2 %all_to_all.58.st1_ref = f32[8,8,128]{2,1,0:T(8,128)S(1)} all-to-all(f32[8,8,128]{2,1,0:T(8,128)S(1)} %broadcast_in_dim.14), channel_id=1, replica_groups=mesh['xl'=2,'y'=4,'xh'=2,'zh'=4,'zl'=2,'c'=2] {'xh','zl','c'}, dimensions={0} | all-to-all | bytes 65536 | tf_op jit(solution)/shard_map/all_to_all | solution.py:34
  165.1 0.0 copy-done.1
  165.1 0.8 shard_map.77
  (9 shorter events, 0.1 us)
Async XLA Ops:
  0.6 28.7 %copy-start = (bf16[1024,1024]{1,0:T(8,128)(2,1)S(1)}, bf16[1024,1024]{1,0:T(8,128)(2,1)}, u32[]{:S(2)}) copy-start(bf16[1024,1024]{1,0:T(8,128)(2,1)} %param.6) | copy-start | bytes 6291460
  0.6 41.8 %copy-start.3 = (f32[1024]{0:T(1024)S(1)}, f32[1024]{0:T(1024)}, u32[]{:S(2)}) copy-start(f32[1024]{0:T(1024)} %param.7) | copy-start | bytes 12292
  19.4 23.1 %all-to-all-start = ((s32[4,32,1024]{2,1,0:T(8,128)}), s32[4,32,1024]{2,1,0:T(8,128)S(1)}, u32[]{:S(2)}, u32[]{:S(2)}) async-start(s32[4,32,1024]{2,1,0:T(8,128)} %broadcast_in_dim.10), calls=%async_computation | async-start | bytes 1048576 | tf_op jit(solution)/shard_map/all_to_all | solution.py:34
  23.0 5.4 %collective-permute-start = (f32[1,256,128]{2,1,0:T(8,128)S(1)}, f32[1,256,128]{2,1,0:T(8,128)S(1)}, u32[]{:S(2)}, u32[]{:S(2)}) collective-permute-start(f32[1,256,128]{2,1,0:T(8,128)S(1)} %bitcast.21), channel_id=1, source_target_pairs={{0,16},{16,0},{1,17},{17,1},{2,18},{18,2},{3,19},{19,3},{4,20},{20... | collective-permute-start | bytes 393224 | tf_op jit(solution)/shard_map/ppermute | solution.py:30
  28.4 11.6 %collective-permute-start.1 = (f32[2,256,128]{2,1,0:T(8,128)S(1)}, f32[2,256,128]{2,1,0:T(8,128)}, u32[]{:S(2)}, u32[]{:S(2)}) collective-permute-start(f32[2,256,128]{2,1,0:T(8,128)S(1)} %pad_maximum_fusion.f0), channel_id=1, source_target_pairs={{0,2},{2,0},{1,3},{3,1},{4,6},{6,4},{5,7},{7,5},{8,10},{10,8},{9,1... | collective-permute-start | bytes 786440 | tf_op jit(solution)/shard_map/ppermute | solution.py:30
  29.4 17.5 %collective-permute-start.2 = (f32[2,256,128]{2,1,0:T(8,128)S(1)}, f32[2,256,128]{2,1,0:T(8,128)}, u32[]{:S(2)}, u32[]{:S(2)}) collective-permute-start(f32[2,256,128]{2,1,0:T(8,128)S(1)} %pad_maximum_fusion.f0), channel_id=1, source_target_pairs={{0,1},{1,0},{2,3},{3,2},{4,5},{5,4},{6,7},{7,6},{8,9},{9,8},{10,11... | collective-permute-start | bytes 786440 | tf_op jit(solution)/shard_map/ppermute | solution.py:30
  40.1 6.9 %collective-permute-start.3 = (f32[2,256,128]{2,1,0:T(8,128)}, f32[2,256,128]{2,1,0:T(8,128)}, u32[]{:S(2)}, u32[]{:S(2)}) collective-permute-start(f32[2,256,128]{2,1,0:T(8,128)} %collective-permute-done.1.f1), channel_id=1, source_target_pairs={{0,1},{1,0},{2,3},{3,2},{4,5},{5,4},{6,7},{7,6},{8,9},{9,8},{10,11... | collective-permute-start | bytes 786440 | tf_op jit(solution)/shard_map/ppermute | solution.py:30
  42.5 4.5 %copy-start.2 = (f32[1024]{0:T(1024)S(1)}, f32[1024]{0:T(1024)}, u32[]{:S(2)}) copy-start(f32[1024]{0:T(1024)} %param.9) | copy-start | bytes 12292
  96.9 2.4 %collective-permute-start.4 = (f32[4,264,128]{2,1,0:T(8,128)S(1)}, f32[4,264,128]{2,1,0:T(8,128)S(1)}, u32[]{:S(2)}, u32[]{:S(2)}) collective-permute-start(f32[4,264,128]{2,1,0:T(8,128)S(1)} %get-tuple-element.20), channel_id=1, source_target_pairs={{0,1},{1,0},{2,3},{3,2},{4,5},{5,4},{6,7},{7,6},{8,9},{9,8},{10,11... | collective-permute-start | bytes 1622024 | tf_op jit(solution)/shard_map/ppermute | solution.py:30
  123.1 4.0 %collective-permute-start.5 = (f32[4,264,128]{2,1,0:T(8,128)S(1)}, f32[4,264,128]{2,1,0:T(8,128)S(1)}, u32[]{:S(2)}, u32[]{:S(2)}) collective-permute-start(f32[4,264,128]{2,1,0:T(8,128)S(1)} %all_to_all.55.g0), channel_id=1, source_target_pairs={{0,1},{1,0},{2,3},{3,2},{4,5},{5,4},{6,7},{7,6},{8,9},{9,8},{10,11... | collective-permute-start | bytes 1622024 | tf_op jit(solution)/shard_map/ppermute | solution.py:30
  127.2 37.9 %copy-start.1 = (f32[32,1024]{1,0:T(8,128)S(1)}, f32[32,1024]{1,0:T(8,128)}, u32[]{:S(2)}) copy-start(f32[32,1024]{1,0:T(8,128)} %f_ref.1) | copy-start | bytes 393220

commit v7 on v6

--- a/solution.py
+++ b/solution.py
@@ -148,6 +148,7 @@
     p_ref[n:, :] = jnp.zeros((EXTRA, 128), F32)
     p_ref[n : n + 1, :] = total(norm) + total(fb * fb)
     project(s_ref, h_ref, lhs, rows_to_column(fb), p_ref)
+    p_ref[n + 1 : n + 2, :] = total(p_ref[:n, :])
 
 
 def first_pass(pos, spins, hidden, f, fb):
@@ -165,10 +166,11 @@
     return norm / (spread / samples + LAM * length)
 
 
-def second_kernel(samples, pos_ref, s_ref, h_ref, f0, f1, f2, f3, fb_ref, g0, g1, mine_ref, st_ref, norm_ref, out_ref, lhs):
+def second_kernel(samples, pos_ref, s_ref, h_ref, f0, f1, f2, f3, fb_ref, g0, g1, mine_ref, norm_ref, out_ref, lhs):
     units = h_ref.shape[0]
     norm0 = norm_ref[0:1, :]
-    a = step_of(norm0, joined(st_ref, h_ref.shape[1])[1], samples, norm0)
+    spread = g0[0, units + units // 128 : units + units // 128 + 1, :]
+    a = step_of(norm0, spread, samples, norm0)
     rr = jnp.zeros((units, 128), F32)
     rf = jnp.zeros((units, 128), F32)
     for b in range(NB):
@@ -186,6 +188,7 @@
     p_ref[n : n + 1, :] = total(rr) + total(rb * rb)
     p_ref[n + 1 : n + 2, :] = total(rf) + total(rb * fb)
     p_ref[n + 2 : n + 2 + units // 128, :] = g0[0, units : units + units // 128, :]
+    p_ref[n + 2 + units // 128 : n + 3 + units // 128, :] = spread
     project(s_ref, h_ref, lhs, rows_to_column(rb), p_ref)
     for k in range(1, out_ref.shape[0]):
         out_ref[k, : n + EXTRA, :] = out_ref[0, : n + EXTRA, :]
@@ -195,16 +198,16 @@
             out_ref[k, at : at + ROWS, :] = mine_ref[k * ROWS : (k + 1) * ROWS, h * 128 : (h + 1) * 128]
 
 
-def second_pass(samples, pos, spins, hidden, f, fb, g0, g1, mine, st, norm):
+def second_pass(samples, pos, spins, hidden, f, fb, g0, g1, mine, norm):
     units, n = hidden.shape
     parts = mine.shape[0] // ROWS
     return call(
         functools.partial(second_kernel, samples),
-        [SMEM] + [VMEM] * 12,
+        [SMEM] + [VMEM] * 11,
         [jax.ShapeDtypeStruct((parts, n // 128 + EXTRA + units // 128 * ROWS, 128), F32)],
         [pltpu.VMEM((2 * units, NB * 128), BF16)],
         flops=4 * 10**9,
-    )(pos, resident(spins), resident(hidden), *f, fb, g0, g1, mine, st, norm)[0]
+    )(pos, resident(spins), resident(hidden), *f, fb, g0, g1, mine, norm)[0]
 
 
 def put_stats(v, st_ref):
@@ -236,16 +239,40 @@
     return x[:n], x[n:]
 
 
-def first_sum_kernel(got_ref, v_ref, st_ref, norm_ref):
-    v, extra = summed(got_ref)
-    v_ref[...] = v
-    norm_ref[...] = extra
-    put_stats(v, st_ref)
-
-
-def first_sum(got):
+def sum_of_set(got_ref, mine, stride, count):
+    x = got_ref[mine]
+    for k in range(1, count):
+        x = x + got_ref[mine + k * stride]
+    n = x.shape[0] - EXTRA
+    everyone = got_ref[0, n + 1 : n + 2, :]
+    for k in range(1, got_ref.shape[0]):
+        everyone = everyone + got_ref[k, n + 1 : n + 2, :]
+    return x, everyone, n
+
+
+def first_chain_kernel(pos_ref, got_ref, all_ref):
+    x, everyone, n = sum_of_set(got_ref, pos_ref[37], 2, got_ref.shape[0] // 2)
+    for k in range(all_ref.shape[0]):
+        all_ref[k] = x
+        all_ref[k, n + 1 : n + 2, :] = everyone
+
+
+def first_sum_kernel(pos_ref, got_ref, v_ref, extra_ref):
+    peers = got_ref.shape[0] // 2
+    x, everyone, n = sum_of_set(got_ref, pos_ref[38] * peers, 1, peers)
+    v_ref[...] = x[:n]
+    extra_ref[...] = x[n:]
+    extra_ref[1:2, :] = everyone
+
+
+def first_sum(pos, partial):
     shape = lambda *s: jax.ShapeDtypeStruct(s, F32)
-    return call(first_sum_kernel, [VMEM], [shape(got.shape[1] - EXTRA, 128), shape(8, 128), shape(EXTRA, 128)])(got)
+    rows = partial.shape[0]
+    chain, plane = ("zh", "zl"), ("xh", *GRP)
+    got = to_all(partial, chain, lax.axis_size(chain))
+    (x,) = call(first_chain_kernel, [SMEM, VMEM], [shape(lax.axis_size(plane), rows, 128)])(pos, got)
+    got = lax.all_to_all(x, plane, 0, 0, tiled=True)
+    return call(first_sum_kernel, [SMEM, VMEM], [shape(rows - EXTRA, 128), shape(EXTRA, 128)])(pos, got)
 
 
 def second_sum_kernel(got_ref, v_ref, norm_ref, st_ref, next_ref):
@@ -279,9 +306,10 @@
     return mean, spread
 
 
-def image_kernel(samples, pos_ref, s_ref, h_ref, v_ref, st_ref, keep_ref, send_ref, acc, lanes):
+def image_kernel(samples, pos_ref, s_ref, h_ref, v_ref, near_ref, far_ref, keep_ref, send_ref, acc, lanes):
     units = h_ref.shape[0]
-    mean = joined(st_ref, h_ref.shape[1])[0][:, 0:1]
+    mean = (near_ref[1:2, 0:1] + far_ref[1:2, 0:1]) * (1.0 / samples)
+    spread = total((v_ref[...] - mean) ** 2)
     acc[...] = jnp.zeros(acc.shape, F32)
     lanes[...] = jnp.zeros(lanes.shape, F32)
 
@@ -299,7 +327,7 @@
     lax.fori_loop(0, s_ref.shape[1] // TILE, step, 0)
     bias = [
         jnp.sum(lanes[k * 128 : (k + 1) * 128, :].T, axis=0, keepdims=True) for k in range(units // 128)
-    ] + [jnp.zeros((8 - units // 128, 128), F32)]
+    ] + [spread, jnp.zeros((7 - units // 128, 128), F32)]
     bias = jnp.concatenate(bias, axis=0)
     for b in range(NB):
         ref = (keep_ref, send_ref)[b // 4]
@@ -308,15 +336,15 @@
         ref[at, units:, :] = bias
 
 
-def image_pass(samples, pos, spins, hidden, values, st):
+def image_pass(samples, pos, spins, hidden, values, near, far):
     units = hidden.shape[0]
     return call(
         functools.partial(image_kernel, samples),
-        [SMEM] + [VMEM] * 4,
+        [SMEM] + [VMEM] * 5,
         [jax.ShapeDtypeStruct((4, units + 8, 128), F32)] * 2,
         [pltpu.VMEM((units, NB * 128), F32), pltpu.VMEM((units, 128), F32)],
         flops=4 * 10**9,
-    )(pos, resident(spins), resident(hidden), values, st)
+    )(pos, resident(spins), resident(hidden), values, near, far)
 
 
 def image_sum_kernel(got_ref, all_ref, mine_ref):
@@ -332,21 +360,21 @@
     return call(image_sum_kernel, [VMEM], [shape(*got.shape), shape(128, units)])(got)
 
 
-def update_kernel(samples, f_ref, fb_ref, got_ref, st0_ref, norm_ref, st1_ref, next_ref, w_ref, b_ref):
-    count = samples // st0_ref.shape[0]
+def update_kernel(samples, f_ref, fb_ref, got_ref, norm_ref, st1_ref, next_ref, w_ref, b_ref):
+    parts = got_ref.shape[0]
+    per = f_ref.shape[1] // 128 // parts
+    n = got_ref.shape[1] - EXTRA - per * ROWS
+    count = samples // st1_ref.shape[0]
     norm0, norm1 = norm_ref[0:1, 0:1], next_ref[0:1, 0:1]
     cross = next_ref[1:2, 0:1]
     beta = norm1 / norm0
-    step0 = step_of(norm0, joined(st0_ref, count)[1][:, 0:1], samples, norm0)
+    step0 = step_of(norm0, got_ref[0, n + 2 + per : n + 3 + per, 0:1], samples, norm0)
     step1 = step_of(norm1, joined(st1_ref, count)[1][:, 0:1], samples, norm1 + 2.0 * beta * cross + beta * beta * norm0)
 
     def update(f, g):
         r = f - step0 * (g + LAM * f)
         return step0 * f + step1 * (r + beta * f)
 
-    parts = got_ref.shape[0]
-    per = f_ref.shape[1] // 128 // parts
-    n = got_ref.shape[1] - EXTRA - per * ROWS
     for k in range(parts):
         for h in range(per):
             b = k * per + h
@@ -355,11 +383,11 @@
             b_ref[b : b + 1, :] = update(fb_ref[b : b + 1, :], got_ref[k, n + 2 + h : n + 3 + h, :])
 
 
-def update_pass(samples, f, fb, got, st0, norm, st1, norms):
+def update_pass(samples, f, fb, got, norm, st1, norms):
     shape = lambda s: jax.ShapeDtypeStruct(s, F32)
     return call(
-        functools.partial(update_kernel, samples), [VMEM] * 7, [shape(f.shape), shape(fb.shape)]
-    )(f, fb, got, st0, norm, st1, norms)
+        functools.partial(update_kernel, samples), [VMEM] * 6, [shape(f.shape), shape(fb.shape)]
+    )(f, fb, got, norm, st1, norms)
 
 
 def body(spins_packed, weight, hidden_bias, force_w, force_b):
@@ -374,7 +402,7 @@
     words = (((q >> 2) & 1) ^ xh) * 16 + (q & 3) * 4 + (((q >> 3) & 1) ^ zl) * 2 + ((q >> 4) ^ c)
     k = jnp.arange(4, dtype=jnp.int32)
     blocks = ((k & 1) ^ xh) * 2 + ((k >> 1) ^ zl)
-    pos = jnp.concatenate([words, zh.reshape(1), blocks])
+    pos = jnp.concatenate([words, zh.reshape(1), blocks, zl.reshape(1), xh.reshape(1)])
 
     f_cols = jnp.stack([force_w[:, k * units : (k + 1) * units] for k in range(parts)])
     f = lax.all_to_all(f_cols, "zh", 0, 0, tiled=True)
@@ -389,19 +417,19 @@
     spins, hidden = hidden_pass(pos, packed, w, hb, units)
     partial = first_pass(pos, spins, hidden, f, fb)
     rows = partial.shape[0]
-    values, st, norm = first_sum(over_groups(to_all(partial, "zh", parts), rows))
-    st0 = of_sets(st)
-
-    keep, send = image_pass(samples, pos, spins, hidden, values, st0)
+    values, norm = first_sum(pos, partial)
+    norm_far = swap(norm, "c")
+
+    keep, send = image_pass(samples, pos, spins, hidden, values, norm, norm_far)
     g = keep + swap(send, "c")
     g, mine = image_sum(lax.all_to_all(g, QUAD, 0, 0, tiled=True), units)
     g = lax.all_to_all(g, QUAD, 0, 0, tiled=True)
 
-    partial = second_pass(samples, pos, spins, hidden, f, fb, g, swap(g, "c"), mine, st0, norm)
+    partial = second_pass(samples, pos, spins, hidden, f, fb, g, swap(g, "c"), mine, norm)
     got = lax.all_to_all(partial, "zh", 0, 0, tiled=True)
     st, norms = second_sum(over_groups(got, rows), values, norm)
     st1 = of_sets(st)
-    out_w, out_b = update_pass(samples, force_w, fb, got, st0, norm, st1, norms)
+    out_w, out_b = update_pass(samples, force_w, fb, got, norm, st1, norms)
     return out_w, out_b.reshape(-1)
 
 

time: 166 us -> 164 us (0.988)
  blocking collectives: 107 us -> 99.8 us
  starting transfers between devices: 17.4 us -> 19.9 us
    all_to_all x0 -> x1, blocking collectives: none -> 14.2 us  [first_sum(): got = lax.all_to_all(x, plane, 0, 0, tiled=True)]
    all_to_all x3 -> x2, blocking collectives: 37.4 us -> 26.7 us  [to_all(): lax.all_to_all(jnp.broadcast_to(x[None], (size, *x.shape)), axes, 0, 0, t...]
    all_to_all x2 -> x1, blocking collectives: 18.5 us -> 8.01 us  [over_groups(): return lax.all_to_all(x, GRP, 0, 0, tiled=True)]
    ppermute x6 -> x7, starting transfers between devices: 13.9 us -> 16.5 us  [swap(): return lax.ppermute(x, axis, SWAP)]
    ppermute x6 -> x7, waiting for transfers between devices: 11.9 us -> 12.7 us  [swap(): return lax.ppermute(x, axis, SWAP)]
    pallas_call x4 -> x5, Pallas kernels: 14.3 us -> 15.1 us  [the longest x1 7.14 us: second_pass(): call(functools.partial(second_kernel, samples), [SMEM] + [VMEM] * 11, [ja...]
  transfers between devices with their start and end apart: 7 -> 8, of which waited for: 4 -> 5; matrix products, arithmetic and copies ran while one was open for 0% -> 0% of each run, Pallas kernels for 3% -> 3%
where the time goes in v7:
time: 164 us; the launch traced here: 163 us
  blocking collectives  99.8 us (61%)
  Pallas kernels  26.8 us (16%)
  starting transfers between devices  19.9 us (12%)
  waiting for transfers between devices  12.7 us (8%)
  local copies, waits for them, and re-layouts  3 us (2%)
    all_to_all x2, blocking collectives, to_all(): lax.all_to_all(jnp.broadcast_to(x[None], (size, *x.shape)), axes, 0, 0, t...  26.7 us
    ppermute x7, starting transfers between devices, swap(): return lax.ppermute(x, axis, SWAP)  16.5 us
    all_to_all x1, blocking collectives, body(): f = lax.all_to_all(f_cols, 'zh', 0, 0, tiled=True)  16 us
    all_to_all x1, blocking collectives, first_sum(): got = lax.all_to_all(x, plane, 0, 0, tiled=True)  14.2 us
    ppermute x7, waiting for transfers between devices, swap(): return lax.ppermute(x, axis, SWAP)  12.7 us
    all_to_all x1, blocking collectives, body(): g, mine = image_sum(lax.all_to_all(g, QUAD, 0, 0, tiled=True), units)  12.3 us
    all_to_all x1, blocking collectives, body(): g = lax.all_to_all(g, QUAD, 0, 0, tiled=True)  11.4 us
    all_to_all x1, blocking collectives, body(): got = lax.all_to_all(partial, 'zh', 0, 0, tiled=True)  11.2 us
  transfers between devices with their start and end apart: 8, of which 5 were waited for; matrix products, arithmetic and copies ran while one was open for 0% of the time, Pallas kernels for 3%

profile of v7, /device:TPU:1, one launch (start us, length us, event | category | flops | bytes accessed | tf_op | source)
XLA Modules:
  0.0 163.2 jit_solution(10826000159930636725)
XLA Ops:
  0.6 0.0 copy-start
  0.6 0.0 copy-start.3
  0.7 1.0 slice_bitcast_fusion.3
  1.6 16.0 %all_to_all.45 = f32[4,32,256]{2,1,0:T(8,128)S(1)} all-to-all(f32[4,32,256]{2,1,0:T(8,128)S(1)} %pad_maximum_fusion.1), channel_id=1, replica_groups=mesh['xl'=2,'y'=4,'xh'=2,'zh'=4,'zl'=2,'c'=2] {'zh'}, dimensions={0} | all-to-all | bytes 262144 | tf_op jit(solution)/shard_map/all_to_all | solution.py:408
  17.7 1.8 %broadcast_in_dim.8 = s32[4,32,1024]{2,1,0:T(8,128)} broadcast(s32[32,1024]{1,0:T(8,128)} %param.5), dimensions={1,2} | broadcast | bytes 655360 | tf_op jit(solution)/shard_map/broadcast_in_dim | solution.py:34
  19.4 3.5 %all-to-all-start = ((s32[4,32,1024]{2,1,0:T(8,128)}), s32[4,32,1024]{2,1,0:T(8,128)S(1)}, u32[]{:S(2)}, u32[]{:S(2)}) async-start(s32[4,32,1024]{2,1,0:T(8,128)} %broadcast_in_dim.8), calls=%async_computation | async-start | bytes 1048576 | tf_op jit(solution)/shard_map/all_to_all | solution.py:34
  22.9 0.1 copy.8
  23.0 2.8 %collective-permute-start = (f32[1,256,128]{2,1,0:T(8,128)S(1)}, f32[1,256,128]{2,1,0:T(8,128)S(1)}, u32[]{:S(2)}, u32[]{:S(2)}) collective-permute-start(f32[1,256,128]{2,1,0:T(8,128)S(1)} %bitcast.23), channel_id=1, source_target_pairs={{0,16},{16,0},{1,17},{17,1},{2,18},{18,2},{3,19},{19,3},{4,20},{20... | collective-permute-start | bytes 393224 | tf_op jit(solution)/shard_map/ppermute | solution.py:30
  25.8 2.6 %collective-permute-done = f32[1,256,128]{2,1,0:T(8,128)S(1)} collective-permute-done((f32[1,256,128]{2,1,0:T(8,128)S(1)}, f32[1,256,128]{2,1,0:T(8,128)S(1)}, u32[]{:S(2)}, u32[]{:S(2)}) %collective-permute-start) | collective-permute-done | bytes 131104 | tf_op jit(solution)/shard_map/ppermute | solution.py:30
  28.4 0.8 collective-permute-start.1
  29.3 0.1 concatenate.6.pos_ref
  29.4 0.0 copy-done
  29.4 0.1 constant_dynamic-slice_fusion.w_ref
  29.4 4.5 %collective-permute-start.2 = (f32[2,256,128]{2,1,0:T(8,128)S(1)}, f32[2,256,128]{2,1,0:T(8,128)}, u32[]{:S(2)}, u32[]{:S(2)}) collective-permute-start(f32[2,256,128]{2,1,0:T(8,128)S(1)} %pad_maximum_fusion.f0), channel_id=1, source_target_pairs={{0,1},{1,0},{2,3},{3,2},{4,5},{5,4},{6,7},{7,6},{8,9},{9,8},{10,11... | collective-permute-start | bytes 786440 | tf_op jit(solution)/shard_map/ppermute | solution.py:30
  33.9 6.1 %collective-permute-done.1.f1 = f32[2,256,128]{2,1,0:T(8,128)} collective-permute-done((f32[2,256,128]{2,1,0:T(8,128)S(1)}, f32[2,256,128]{2,1,0:T(8,128)}, u32[]{:S(2)}, u32[]{:S(2)}) %collective-permute-start.1) | collective-permute-done | bytes 262176 | tf_op jit(solution)/shard_map/ppermute | solution.py:30
  40.0 2.4 %collective-permute-start.3 = (f32[2,256,128]{2,1,0:T(8,128)}, f32[2,256,128]{2,1,0:T(8,128)}, u32[]{:S(2)}, u32[]{:S(2)}) collective-permute-start(f32[2,256,128]{2,1,0:T(8,128)} %collective-permute-done.1.f1), channel_id=1, source_target_pairs={{0,1},{1,0},{2,3},{3,2},{4,5},{5,4},{6,7},{7,6},{8,9},{9,8},{10,11... | collective-permute-start | bytes 786440 | tf_op jit(solution)/shard_map/ppermute | solution.py:30
  42.5 0.0 all-to-all-done.packed_ref
  42.5 0.0 copy-done.3
  42.5 0.0 copy-start.2
  42.5 4.4 %shard_map.68 = (bf16[1024,4096]{1,0:T(8,128)(2,1)S(1)}, f32[256,4096]{1,0:T(8,128)S(1)}) custom-call(s32[39]{0:T(128)S(1)} %concatenate.6.pos_ref, s32[4,32,1024]{2,1,0:T(8,128)S(1)} %all-to-all-done.packed_ref, bf16[1024,256]{1,0:T(8,128)(2,1)S(1)} %constant_dynamic-slice_fusion.w_ref, f32[8,128]{1,0:T(8,128)S(1)} %bitcast.21), custom_call_target="tpu_custom_call" | custom-call | flops 4000000000 | bytes 1048576 | tf_op jit(solution)/shard_map/pallas_call | solution.py:107
  46.9 0.0 collective-permute-done.2.f2
  46.9 0.0 collective-permute-done.3.f3
  46.9 0.0 copy-done.2
  46.9 6.9 %shard_map.69 = f32[40,128]{1,0:T(8,128)S(1)} custom-call(s32[39]{0:T(128)S(1)} %concatenate.6.pos_ref, bf16[1024,4096]{1,0:T(8,128)(2,1)S(1)} %get-tuple-element.14.s_ref, f32[256,4096]{1,0:T(8,128)S(1)} %get-tuple-element.15.h_ref, f32[2,256,128]{2,1,0:T(8,128)S(1)} %pad_maximum_fusion.f0, f32[2,256,128]{2,1,0:T(8,128)} %collective-permute-done.1.f1, ...), custom_call_target="tpu_custom_call" | custom-call | flops 4000000000 | bytes 1048576 | tf_op jit(solution)/shard_map/pallas_call | solution.py:156
  53.9 15.1 %all_to_all.46.got_ref = f32[8,40,128]{2,1,0:T(8,128)S(1)} all-to-all(f32[8,40,128]{2,1,0:T(8,128)S(1)} %broadcast_in_dim.10), channel_id=1, replica_groups=mesh['xl'=2,'y'=4,'xh'=2,'zh'=4,'zl'=2,'c'=2] {'zh','zl'}, dimensions={0} | all-to-all | bytes 327680 | tf_op jit(solution)/shard_map/all_to_all | solution.py:34
  69.0 0.6 shard_map.70
  69.6 14.2 %all_to_all.47.got_ref = f32[16,40,128]{2,1,0:T(8,128)S(1)} all-to-all(f32[16,40,128]{2,1,0:T(8,128)S(1)} %shard_map.70), channel_id=1, replica_groups=mesh['xl'=2,'y'=4,'xh'=2,'zh'=4,'zl'=2,'c'=2] {'xh','xl','y'}, dimensions={0} | all-to-all | bytes 655360 | tf_op jit(solution)/shard_map/all_to_all | solution.py:274
  83.8 0.6 shard_map.71
  84.4 3.0 %collective-permute-start.4 = (f32[8,128]{1,0:T(8,128)S(1)}, f32[8,128]{1,0:T(8,128)S(1)}, u32[]{:S(2)}, u32[]{:S(2)}) collective-permute-start(f32[8,128]{1,0:T(8,128)S(1)} %get-tuple-element.17.near_ref.norm_ref), channel_id=1, source_target_pairs={{0,1},{1,0},{2,3},{3,2},{4,5},{5,4},{6,7},{7,6},{8,9},{9,8},{10,11... | collective-permute-start | bytes 12296 | tf_op jit(solution)/shard_map/ppermute | solution.py:30
  87.4 0.8 collective-permute-done.4.far_ref
  88.3 6.1 %shard_map.72 = (f32[4,264,128]{2,1,0:T(8,128)S(1)}, f32[4,264,128]{2,1,0:T(8,128)S(1)}) custom-call(s32[39]{0:T(128)S(1)} %concatenate.6.pos_ref, bf16[1024,4096]{1,0:T(8,128)(2,1)S(1)} %get-tuple-element.14.s_ref, f32[256,4096]{1,0:T(8,128)S(1)} %get-tuple-element.15.h_ref, f32[32,128]{1,0:T(8,128)S(1)} %get-tuple-element.16.v_ref, ...), custom_call_target="tpu_custom_call" | custom-call | flops 4000000000 | bytes 1048576 | tf_op jit(solution)/shard_map/pallas_call | solution.py:341
  94.4 0.4 collective-permute-start.5
  94.8 1.6 collective-permute-done.5
  96.4 0.1 add.23
  96.5 12.3 %all_to_all.48.got_ref = f32[4,264,128]{2,1,0:T(8,128)S(1)} all-to-all(f32[4,264,128]{2,1,0:T(8,128)S(1)} %add.23), channel_id=1, replica_groups=mesh['xl'=2,'y'=4,'xh'=2,'zh'=4,'zl'=2,'c'=2] {'xh','zl'}, dimensions={0} | all-to-all | bytes 1081344 | tf_op jit(solution)/shard_map/all_to_all | solution.py:425
  108.7 0.1 shard_map.73
  108.8 11.4 %all_to_all.49.g0 = f32[4,264,128]{2,1,0:T(8,128)S(1)} all-to-all(f32[4,264,128]{2,1,0:T(8,128)S(1)} %get-tuple-element.20), channel_id=1, replica_groups=mesh['xl'=2,'y'=4,'xh'=2,'zh'=4,'zl'=2,'c'=2] {'xh','zl'}, dimensions={0} | all-to-all | bytes 1081344 | tf_op jit(solution)/shard_map/all_to_all | solution.py:426
  120.2 2.4 %collective-permute-start.6 = (f32[4,264,128]{2,1,0:T(8,128)S(1)}, f32[4,264,128]{2,1,0:T(8,128)S(1)}, u32[]{:S(2)}, u32[]{:S(2)}) collective-permute-start(f32[4,264,128]{2,1,0:T(8,128)S(1)} %all_to_all.49.g0), channel_id=1, source_target_pairs={{0,1},{1,0},{2,3},{3,2},{4,5},{5,4},{6,7},{7,6},{8,9},{9,8},{10,11... | collective-permute-start | bytes 1622024 | tf_op jit(solution)/shard_map/ppermute | solution.py:30
  122.7 1.6 collective-permute-done.6.g1
  124.2 0.0 copy-start.1
  124.2 7.1 %shard_map.74 = f32[4,104,128]{2,1,0:T(8,128)S(1)} custom-call(s32[39]{0:T(128)S(1)} %concatenate.6.pos_ref, bf16[1024,4096]{1,0:T(8,128)(2,1)S(1)} %get-tuple-element.14.s_ref, f32[256,4096]{1,0:T(8,128)S(1)} %get-tuple-element.15.h_ref, f32[2,256,128]{2,1,0:T(8,128)S(1)} %pad_maximum_fusion.f0, f32[2,256,128]{2,1,0:T(8,128)} %collective-permute-done.1.f1, ...), custom_call_target="tpu_custom_call" | custom-call | flops 4000000000 | bytes 1048576 | tf_op jit(solution)/shard_map/pallas_call | solution.py:204
  131.4 11.2 %all_to_all.50.got_ref = f32[4,104,128]{2,1,0:T(8,128)S(1)} all-to-all(f32[4,104,128]{2,1,0:T(8,128)S(1)} %shard_map.74), channel_id=1, replica_groups=mesh['xl'=2,'y'=4,'xh'=2,'zh'=4,'zl'=2,'c'=2] {'zh'}, dimensions={0} | all-to-all | bytes 425984 | tf_op jit(solution)/shard_map/all_to_all | solution.py:429
  142.6 8.0 %all_to_all.51.got_ref = f32[8,40,128]{2,1,0:T(8,128)S(1)} all-to-all(f32[8,40,128]{2,1,0:T(8,128)S(1)} %shard_map.75), channel_id=1, replica_groups=mesh['xl'=2,'y'=4,'xh'=2,'zh'=4,'zl'=2,'c'=2] {'xl','y'}, dimensions={0} | all-to-all | bytes 327680 | tf_op jit(solution)/shard_map/all_to_all | solution.py:231
  150.6 0.3 shard_map.76
  150.9 11.6 %all_to_all.52.st1_ref = f32[8,8,128]{2,1,0:T(8,128)S(1)} all-to-all(f32[8,8,128]{2,1,0:T(8,128)S(1)} %broadcast_in_dim.11), channel_id=1, replica_groups=mesh['xl'=2,'y'=4,'xh'=2,'zh'=4,'zl'=2,'c'=2] {'xh','zl','c'}, dimensions={0} | all-to-all | bytes 65536 | tf_op jit(solution)/shard_map/all_to_all | solution.py:34
  162.5 0.0 copy-done.1
  162.5 0.7 shard_map.77
  (7 shorter events, 0.1 us)
Async XLA Ops:
  0.6 28.7 %copy-start = (bf16[1024,1024]{1,0:T(8,128)(2,1)S(1)}, bf16[1024,1024]{1,0:T(8,128)(2,1)}, u32[]{:S(2)}) copy-start(bf16[1024,1024]{1,0:T(8,128)(2,1)} %param.6) | copy-start | bytes 6291460
  0.6 41.8 %copy-start.3 = (f32[1024]{0:T(1024)S(1)}, f32[1024]{0:T(1024)}, u32[]{:S(2)}) copy-start(f32[1024]{0:T(1024)} %param.7) | copy-start | bytes 12292
  19.4 23.1 %all-to-all-start = ((s32[4,32,1024]{2,1,0:T(8,128)}), s32[4,32,1024]{2,1,0:T(8,128)S(1)}, u32[]{:S(2)}, u32[]{:S(2)}) async-start(s32[4,32,1024]{2,1,0:T(8,128)} %broadcast_in_dim.8), calls=%async_computation | async-start | bytes 1048576 | tf_op jit(solution)/shard_map/all_to_all | solution.py:34
  23.0 5.4 %collective-permute-start = (f32[1,256,128]{2,1,0:T(8,128)S(1)}, f32[1,256,128]{2,1,0:T(8,128)S(1)}, u32[]{:S(2)}, u32[]{:S(2)}) collective-permute-start(f32[1,256,128]{2,1,0:T(8,128)S(1)} %bitcast.23), channel_id=1, source_target_pairs={{0,16},{16,0},{1,17},{17,1},{2,18},{18,2},{3,19},{19,3},{4,20},{20... | collective-permute-start | bytes 393224 | tf_op jit(solution)/shard_map/ppermute | solution.py:30
  28.4 11.6 %collective-permute-start.1 = (f32[2,256,128]{2,1,0:T(8,128)S(1)}, f32[2,256,128]{2,1,0:T(8,128)}, u32[]{:S(2)}, u32[]{:S(2)}) collective-permute-start(f32[2,256,128]{2,1,0:T(8,128)S(1)} %pad_maximum_fusion.f0), channel_id=1, source_target_pairs={{0,2},{2,0},{1,3},{3,1},{4,6},{6,4},{5,7},{7,5},{8,10},{10,8},{9,1... | collective-permute-start | bytes 786440 | tf_op jit(solution)/shard_map/ppermute | solution.py:30
  29.4 17.5 %collective-permute-start.2 = (f32[2,256,128]{2,1,0:T(8,128)S(1)}, f32[2,256,128]{2,1,0:T(8,128)}, u32[]{:S(2)}, u32[]{:S(2)}) collective-permute-start(f32[2,256,128]{2,1,0:T(8,128)S(1)} %pad_maximum_fusion.f0), channel_id=1, source_target_pairs={{0,1},{1,0},{2,3},{3,2},{4,5},{5,4},{6,7},{7,6},{8,9},{9,8},{10,11... | collective-permute-start | bytes 786440 | tf_op jit(solution)/shard_map/ppermute | solution.py:30
  40.0 6.9 %collective-permute-start.3 = (f32[2,256,128]{2,1,0:T(8,128)}, f32[2,256,128]{2,1,0:T(8,128)}, u32[]{:S(2)}, u32[]{:S(2)}) collective-permute-start(f32[2,256,128]{2,1,0:T(8,128)} %collective-permute-done.1.f1), channel_id=1, source_target_pairs={{0,1},{1,0},{2,3},{3,2},{4,5},{5,4},{6,7},{7,6},{8,9},{9,8},{10,11... | collective-permute-start | bytes 786440 | tf_op jit(solution)/shard_map/ppermute | solution.py:30
  42.5 4.5 %copy-start.2 = (f32[1024]{0:T(1024)S(1)}, f32[1024]{0:T(1024)}, u32[]{:S(2)}) copy-start(f32[1024]{0:T(1024)} %param.9) | copy-start | bytes 12292
  84.4 3.8 %collective-permute-start.4 = (f32[8,128]{1,0:T(8,128)S(1)}, f32[8,128]{1,0:T(8,128)S(1)}, u32[]{:S(2)}, u32[]{:S(2)}) collective-permute-start(f32[8,128]{1,0:T(8,128)S(1)} %get-tuple-element.17.near_ref.norm_ref), channel_id=1, source_target_pairs={{0,1},{1,0},{2,3},{3,2},{4,5},{5,4},{6,7},{7,6},{8,9},{9,8},{10,11... | collective-permute-start | bytes 12296 | tf_op jit(solution)/shard_map/ppermute | solution.py:30
  94.4 2.0 %collective-permute-start.5 = (f32[4,264,128]{2,1,0:T(8,128)S(1)}, f32[4,264,128]{2,1,0:T(8,128)S(1)}, u32[]{:S(2)}, u32[]{:S(2)}) collective-permute-start(f32[4,264,128]{2,1,0:T(8,128)S(1)} %get-tuple-element.19), channel_id=1, source_target_pairs={{0,1},{1,0},{2,3},{3,2},{4,5},{5,4},{6,7},{7,6},{8,9},{9,8},{10,11... | collective-permute-start | bytes 1622024 | tf_op jit(solution)/shard_map/ppermute | solution.py:30
  120.2 4.0 %collective-permute-start.6 = (f32[4,264,128]{2,1,0:T(8,128)S(1)}, f32[4,264,128]{2,1,0:T(8,128)S(1)}, u32[]{:S(2)}, u32[]{:S(2)}) collective-permute-start(f32[4,264,128]{2,1,0:T(8,128)S(1)} %all_to_all.49.g0), channel_id=1, source_target_pairs={{0,1},{1,0},{2,3},{3,2},{4,5},{5,4},{6,7},{7,6},{8,9},{9,8},{10,11... | collective-permute-start | bytes 1622024 | tf_op jit(solution)/shard_map/ppermute | solution.py:30
  124.2 38.2 %copy-start.1 = (f32[32,1024]{1,0:T(8,128)S(1)}, f32[32,1024]{1,0:T(8,128)}, u32[]{:S(2)}) copy-start(f32[32,1024]{1,0:T(8,128)} %f_ref.1) | copy-start | bytes 393220

commit v8 on v7

--- a/solution.py
+++ b/solution.py
@@ -81,8 +81,10 @@
     return pl.ds(pl.multiple_of(t * SUB, SUB), SUB)
 
 
-def hidden_kernel(pos_ref, packed_ref, w_ref, hb_ref, s_ref, h_ref, wt):
+def hidden_kernel(pos_ref, x0, x1, x2, x3, w_ref, hb_ref, s_ref, h_ref, wt, packed_ref):
     units = wt.shape[0]
+    for d, x in enumerate((x0, x1, x2, x3)):
+        packed_ref[(pos_ref[32] + 4 - d) % 4] = x[...]
     for b in range(NB):
         rows = [w_ref[pl.ds(pl.multiple_of(pos_ref[4 * b + k] * ROWS, ROWS), ROWS), :] for k in range(4)]
         block = jnp.concatenate(rows, axis=0).astype(F32)
@@ -103,14 +105,14 @@
 
 
 def hidden_pass(pos, packed, w, hb, units):
-    n = packed.shape[0] * TILE
+    n = len(packed) * TILE
     return call(
         hidden_kernel,
-        [SMEM, VMEM, VMEM, VMEM],
+        [SMEM] + [VMEM] * 6,
         [pltpu.VMEM((NB * 128, n), BF16), pltpu.VMEM((units, n), F32)],
-        [pltpu.VMEM((units, NB * 128), BF16)],
+        [pltpu.VMEM((units, NB * 128), BF16), pltpu.VMEM((len(packed), *packed[0].shape), jnp.int32)],
         flops=4 * 10**9,
-    )(pos, packed, w, hb)
+    )(pos, *packed, w, hb)
 
 
 def project(s_ref, h_ref, lhs, bias, p_ref):
@@ -404,6 +406,10 @@
     blocks = ((k & 1) ^ xh) * 2 + ((k >> 1) ^ zl)
     pos = jnp.concatenate([words, zh.reshape(1), blocks, zl.reshape(1), xh.reshape(1)])
 
+    packed = [spins_packed]
+    for d in (1, 2, 3):
+        packed.append(lax.ppermute(spins_packed, "zh", [(i, (i + d) % 4) for i in range(4)]))
+
     f_cols = jnp.stack([force_w[:, k * units : (k + 1) * units] for k in range(parts)])
     f = lax.all_to_all(f_cols, "zh", 0, 0, tiled=True)
     f = f.reshape(parts * ROWS, units).T[None]
@@ -412,7 +418,6 @@
     f_zl = swap(f, "zl")
     f = (f, f_zl, swap(f, "c"), swap(f_zl, "c"))
 
-    packed = to_all(spins_packed, "zh", parts)
     w = lax.dynamic_slice_in_dim(weight, zh * units, units, 1)
     spins, hidden = hidden_pass(pos, packed, w, hb, units)
     partial = first_pass(pos, spins, hidden, f, fb)

time: 164 us -> 161 us (0.982)
  blocking collectives: 99.8 us -> 97.6 us
    ppermute x0 -> x3, starting transfers between devices: none -> 4.5 us  [body(): lax.ppermute(spins_packed, 'zh', [(i, (i + d) % 4) for i in range(4)])]
    all_to_all x1 -> x0, starting transfers between devices: 3.47 us -> none  [to_all(): lax.all_to_all(jnp.broadcast_to(x[None], (size, *x.shape)), axes, 0, 0, t...]
    all_to_all x1, blocking collectives: 14.2 us -> 12.3 us  [first_sum(): got = lax.all_to_all(x, plane, 0, 0, tiled=True)]
    broadcast_in_dim x3 -> x2, local copies, waits for them, and re-layouts: 1.77 us -> 0.02 us  [to_all(): jnp.broadcast_to(x[None], (size, *x.shape))]
  transfers between devices with their start and end apart: 8 -> 10, of which waited for: 5 -> 4; matrix products, arithmetic and copies ran while one was open for 0% -> 0% of each run, Pallas kernels for 3% -> 3%
where the time goes in v8:
time: 161 us; the launch traced here: 160 us
  blocking collectives  97.6 us (61%)
  Pallas kernels  25.7 us (16%)
  starting transfers between devices  20.2 us (13%)
  waiting for transfers between devices  13.2 us (8%)
  local copies, waits for them, and re-layouts  2.83 us (2%)
    all_to_all x2, blocking collectives, to_all(): lax.all_to_all(jnp.broadcast_to(x[None], (size, *x.shape)), axes, 0, 0, t...  26.3 us
    all_to_all x1, blocking collectives, body(): f = lax.all_to_all(f_cols, 'zh', 0, 0, tiled=True)  16 us
    ppermute x7, starting transfers between devices, swap(): return lax.ppermute(x, axis, SWAP)  15.7 us
    ppermute x7, waiting for transfers between devices, swap(): return lax.ppermute(x, axis, SWAP)  13.2 us
    all_to_all x1, blocking collectives, first_sum(): got = lax.all_to_all(x, plane, 0, 0, tiled=True)  12.3 us
    all_to_all x1, blocking collectives, body(): g, mine = image_sum(lax.all_to_all(g, QUAD, 0, 0, tiled=True), units)  12.3 us
    all_to_all x1, blocking collectives, body(): g = lax.all_to_all(g, QUAD, 0, 0, tiled=True)  11.4 us
    all_to_all x1, blocking collectives, body(): got = lax.all_to_all(partial, 'zh', 0, 0, tiled=True)  11.2 us
  transfers between devices with their start and end apart: 10, of which 4 were waited for; matrix products, arithmetic and copies ran while one was open for 0% of the time, Pallas kernels for 3%

profile of v8, /device:TPU:1, one launch (start us, length us, event | category | flops | bytes accessed | tf_op | source)
XLA Modules:
  0.0 160.4 jit_solution(17794703862225625245)
XLA Ops:
  0.6 0.0 copy-start
  0.6 1.0 slice_bitcast_fusion.3
  1.6 16.0 %all_to_all.40 = f32[4,32,256]{2,1,0:T(8,128)S(1)} all-to-all(f32[4,32,256]{2,1,0:T(8,128)S(1)} %pad_maximum_fusion.1), channel_id=1, replica_groups=mesh['xl'=2,'y'=4,'xh'=2,'zh'=4,'zl'=2,'c'=2] {'zh'}, dimensions={0} | all-to-all | bytes 262144 | tf_op jit(solution)/shard_map/all_to_all | solution.py:414
  17.7 0.1 copy.8
  17.8 2.8 %collective-permute-start.3 = (f32[1,256,128]{2,1,0:T(8,128)S(1)}, f32[1,256,128]{2,1,0:T(8,128)S(1)}, u32[]{:S(2)}, u32[]{:S(2)}) collective-permute-start(f32[1,256,128]{2,1,0:T(8,128)S(1)} %bitcast.23), channel_id=1, source_target_pairs={{0,16},{16,0},{1,17},{17,1},{2,18},{18,2},{3,19},{19,3},{4,20},{20... | collective-permute-start | bytes 393224 | tf_op jit(solution)/shard_map/ppermute | solution.py:30
  20.6 0.9 collective-permute-start.1
  21.5 2.8 %collective-permute-start = (s32[32,1024]{1,0:T(8,128)}, s32[32,1024]{1,0:T(8,128)S(1)}, u32[]{:S(2)}, u32[]{:S(2)}) collective-permute-start(s32[32,1024]{1,0:T(8,128)} %x0.1), channel_id=1, source_target_pairs={{0,4},{4,8},{8,12},{12,0},{1,5},{5,9},{9,13},{13,1},{2,6},{6,10},{... | collective-permute-start | bytes 393224 | tf_op jit(solution)/shard_map/ppermute | solution.py:411
  24.3 0.8 collective-permute-start.2
  25.1 0.0 collective-permute-done.3
  25.1 1.2 collective-permute-start.4
  26.4 0.1 concatenate.6.pos_ref
  26.5 0.0 copy-done
  26.5 0.1 constant_dynamic-slice_fusion.w_ref
  26.5 3.7 %collective-permute-start.5 = (f32[2,256,128]{2,1,0:T(8,128)S(1)}, f32[2,256,128]{2,1,0:T(8,128)S(1)}, u32[]{:S(2)}, u32[]{:S(2)}) collective-permute-start(f32[2,256,128]{2,1,0:T(8,128)S(1)} %pad_maximum_fusion.f0), channel_id=1, source_target_pairs={{0,1},{1,0},{2,3},{3,2},{4,5},{5,4},{6,7},{7,6},{8,9},{9,8},{10,11... | collective-permute-start | bytes 786440 | tf_op jit(solution)/shard_map/ppermute | solution.py:30
  30.2 9.2 %collective-permute-done.4.f1 = f32[2,256,128]{2,1,0:T(8,128)S(1)} collective-permute-done((f32[2,256,128]{2,1,0:T(8,128)S(1)}, f32[2,256,128]{2,1,0:T(8,128)S(1)}, u32[]{:S(2)}, u32[]{:S(2)}) %collective-permute-start.4) | collective-permute-done | bytes 262176 | tf_op jit(solution)/shard_map/ppermute | solution.py:30
  39.5 2.1 %collective-permute-start.6 = (f32[2,256,128]{2,1,0:T(8,128)S(1)}, f32[2,256,128]{2,1,0:T(8,128)S(1)}, u32[]{:S(2)}, u32[]{:S(2)}) collective-permute-start(f32[2,256,128]{2,1,0:T(8,128)S(1)} %collective-permute-done.4.f1), channel_id=1, source_target_pairs={{0,1},{1,0},{2,3},{3,2},{4,5},{5,4},{6,7},{7,6},{8,9},{9,8},{10,11... | collective-permute-start | bytes 786440 | tf_op jit(solution)/shard_map/ppermute | solution.py:30
  41.5 0.0 collective-permute-done.1.x2
  41.5 0.0 collective-permute-done.x1
  41.5 0.0 collective-permute-done.2.x3
  41.5 0.0 copy-start.3
  41.6 0.9 copy-done.3
  42.5 0.7 copy-done.4
  43.1 4.4 %shard_map.68 = (bf16[1024,4096]{1,0:T(8,128)(2,1)S(1)}, f32[256,4096]{1,0:T(8,128)S(1)}) custom-call(s32[39]{0:T(128)S(1)} %concatenate.6.pos_ref, s32[32,1024]{1,0:T(8,128)S(1)} %copy-done.3, s32[32,1024]{1,0:T(8,128)S(1)} %collective-permute-done.x1, s32[32,1024]{1,0:T(8,128)S(1)} %collective-permute-done.1.x2, s32[32,1024]{1,0:T(8,128)S(1)} %collective-permute-done.2.x3, ...), custom_call_target="tpu_custom_call" | custom-call | flops 4000000000 | bytes 1048576 | tf_op jit(solution)/shard_map/pallas_call | solution.py:109
  47.6 0.0 collective-permute-done.5.f2
  47.6 0.0 collective-permute-done.6.f3
  47.6 0.0 copy-done.2
  47.6 6.3 %shard_map.69 = f32[40,128]{1,0:T(8,128)S(1)} custom-call(s32[39]{0:T(128)S(1)} %concatenate.6.pos_ref, bf16[1024,4096]{1,0:T(8,128)(2,1)S(1)} %get-tuple-element.14.s_ref, f32[256,4096]{1,0:T(8,128)S(1)} %get-tuple-element.15.h_ref, f32[2,256,128]{2,1,0:T(8,128)S(1)} %pad_maximum_fusion.f0, f32[2,256,128]{2,1,0:T(8,128)S(1)} %collective-permute-done.4.f1, ...), custom_call_target="tpu_custom_call" | custom-call | flops 4000000000 | bytes 1048576 | tf_op jit(solution)/shard_map/pallas_call | solution.py:158
  54.0 14.8 %all_to_all.41.got_ref = f32[8,40,128]{2,1,0:T(8,128)S(1)} all-to-all(f32[8,40,128]{2,1,0:T(8,128)S(1)} %broadcast_in_dim.7), channel_id=1, replica_groups=mesh['xl'=2,'y'=4,'xh'=2,'zh'=4,'zl'=2,'c'=2] {'zh','zl'}, dimensions={0} | all-to-all | bytes 327680 | tf_op jit(solution)/shard_map/all_to_all | solution.py:34
  68.8 0.6 shard_map.70
  69.3 12.3 %all_to_all.42.got_ref = f32[16,40,128]{2,1,0:T(8,128)S(1)} all-to-all(f32[16,40,128]{2,1,0:T(8,128)S(1)} %shard_map.70), channel_id=1, replica_groups=mesh['xl'=2,'y'=4,'xh'=2,'zh'=4,'zl'=2,'c'=2] {'xh','xl','y'}, dimensions={0} | all-to-all | bytes 655360 | tf_op jit(solution)/shard_map/all_to_all | solution.py:276
  81.7 0.6 shard_map.71
  82.2 3.0 %collective-permute-start.7 = (f32[8,128]{1,0:T(8,128)S(1)}, f32[8,128]{1,0:T(8,128)S(1)}, u32[]{:S(2)}, u32[]{:S(2)}) collective-permute-start(f32[8,128]{1,0:T(8,128)S(1)} %get-tuple-element.17.near_ref.norm_ref), channel_id=1, source_target_pairs={{0,1},{1,0},{2,3},{3,2},{4,5},{5,4},{6,7},{7,6},{8,9},{9,8},{10,11... | collective-permute-start | bytes 12296 | tf_op jit(solution)/shard_map/ppermute | solution.py:30
  85.2 0.8 collective-permute-done.7.far_ref
  86.0 6.1 %shard_map.72 = (f32[4,264,128]{2,1,0:T(8,128)S(1)}, f32[4,264,128]{2,1,0:T(8,128)S(1)}) custom-call(s32[39]{0:T(128)S(1)} %concatenate.6.pos_ref, bf16[1024,4096]{1,0:T(8,128)(2,1)S(1)} %get-tuple-element.14.s_ref, f32[256,4096]{1,0:T(8,128)S(1)} %get-tuple-element.15.h_ref, f32[32,128]{1,0:T(8,128)S(1)} %get-tuple-element.16.v_ref, ...), custom_call_target="tpu_custom_call" | custom-call | flops 4000000000 | bytes 1048576 | tf_op jit(solution)/shard_map/pallas_call | solution.py:343
  92.2 0.4 collective-permute-start.8
  92.6 1.6 collective-permute-done.8
  94.2 0.1 add.23
  94.2 12.3 %all_to_all.43.got_ref = f32[4,264,128]{2,1,0:T(8,128)S(1)} all-to-all(f32[4,264,128]{2,1,0:T(8,128)S(1)} %add.23), channel_id=1, replica_groups=mesh['xl'=2,'y'=4,'xh'=2,'zh'=4,'zl'=2,'c'=2] {'xh','zl'}, dimensions={0} | all-to-all | bytes 1081344 | tf_op jit(solution)/shard_map/all_to_all | solution.py:430
  106.5 0.1 shard_map.73
  106.7 11.4 %all_to_all.44.g0 = f32[4,264,128]{2,1,0:T(8,128)S(1)} all-to-all(f32[4,264,128]{2,1,0:T(8,128)S(1)} %get-tuple-element.20), channel_id=1, replica_groups=mesh['xl'=2,'y'=4,'xh'=2,'zh'=4,'zl'=2,'c'=2] {'xh','zl'}, dimensions={0} | all-to-all | bytes 1081344 | tf_op jit(solution)/shard_map/all_to_all | solution.py:431
  118.1 2.4 %collective-permute-start.9 = (f32[4,264,128]{2,1,0:T(8,128)S(1)}, f32[4,264,128]{2,1,0:T(8,128)S(1)}, u32[]{:S(2)}, u32[]{:S(2)}) collective-permute-start(f32[4,264,128]{2,1,0:T(8,128)S(1)} %all_to_all.44.g0), channel_id=1, source_target_pairs={{0,1},{1,0},{2,3},{3,2},{4,5},{5,4},{6,7},{7,6},{8,9},{9,8},{10,11... | collective-permute-start | bytes 1622024 | tf_op jit(solution)/shard_map/ppermute | solution.py:30
  120.5 1.6 collective-permute-done.9.g1
  122.0 6.5 %shard_map.74 = f32[4,104,128]{2,1,0:T(8,128)S(1)} custom-call(s32[39]{0:T(128)S(1)} %concatenate.6.pos_ref, bf16[1024,4096]{1,0:T(8,128)(2,1)S(1)} %get-tuple-element.14.s_ref, f32[256,4096]{1,0:T(8,128)S(1)} %get-tuple-element.15.h_ref, f32[2,256,128]{2,1,0:T(8,128)S(1)} %pad_maximum_fusion.f0, f32[2,256,128]{2,1,0:T(8,128)S(1)} %collective-permute-done.4.f1, ...), custom_call_target="tpu_custom_call" | custom-call | flops 4000000000 | bytes 1048576 | tf_op jit(solution)/shard_map/pallas_call | solution.py:206
  128.6 11.2 %all_to_all.45.got_ref = f32[4,104,128]{2,1,0:T(8,128)S(1)} all-to-all(f32[4,104,128]{2,1,0:T(8,128)S(1)} %shard_map.74), channel_id=1, replica_groups=mesh['xl'=2,'y'=4,'xh'=2,'zh'=4,'zl'=2,'c'=2] {'zh'}, dimensions={0} | all-to-all | bytes 425984 | tf_op jit(solution)/shard_map/all_to_all | solution.py:434
  139.8 8.0 %all_to_all.46.got_ref = f32[8,40,128]{2,1,0:T(8,128)S(1)} all-to-all(f32[8,40,128]{2,1,0:T(8,128)S(1)} %shard_map.75), channel_id=1, replica_groups=mesh['xl'=2,'y'=4,'xh'=2,'zh'=4,'zl'=2,'c'=2] {'xl','y'}, dimensions={0} | all-to-all | bytes 327680 | tf_op jit(solution)/shard_map/all_to_all | solution.py:233
  147.8 0.3 shard_map.76
  148.1 11.5 %all_to_all.47.st1_ref = f32[8,8,128]{2,1,0:T(8,128)S(1)} all-to-all(f32[8,8,128]{2,1,0:T(8,128)S(1)} %broadcast_in_dim.8), channel_id=1, replica_groups=mesh['xl'=2,'y'=4,'xh'=2,'zh'=4,'zl'=2,'c'=2] {'xh','zl','c'}, dimensions={0} | all-to-all | bytes 65536 | tf_op jit(solution)/shard_map/all_to_all | solution.py:34
  159.7 0.7 shard_map.77
  (11 shorter events, 0.1 us)
Async XLA Ops:
  0.6 25.8 %copy-start = (bf16[1024,1024]{1,0:T(8,128)(2,1)S(1)}, bf16[1024,1024]{1,0:T(8,128)(2,1)}, u32[]{:S(2)}) copy-start(bf16[1024,1024]{1,0:T(8,128)(2,1)} %param.6) | copy-start | bytes 6291460
  17.8 7.3 %collective-permute-start.3 = (f32[1,256,128]{2,1,0:T(8,128)S(1)}, f32[1,256,128]{2,1,0:T(8,128)S(1)}, u32[]{:S(2)}, u32[]{:S(2)}) collective-permute-start(f32[1,256,128]{2,1,0:T(8,128)S(1)} %bitcast.23), channel_id=1, source_target_pairs={{0,16},{16,0},{1,17},{17,1},{2,18},{18,2},{3,19},{19,3},{4,20},{20... | collective-permute-start | bytes 393224 | tf_op jit(solution)/shard_map/ppermute | solution.py:30
  20.6 20.9 %collective-permute-start.1 = (s32[32,1024]{1,0:T(8,128)}, s32[32,1024]{1,0:T(8,128)S(1)}, u32[]{:S(2)}, u32[]{:S(2)}) collective-permute-start(s32[32,1024]{1,0:T(8,128)} %x0.1), channel_id=1, source_target_pairs={{0,8},{4,12},{8,0},{12,4},{1,9},{5,13},{9,1},{13,5},{2,10},{6,14},... | collective-permute-start | bytes 393224 | tf_op jit(solution)/shard_map/ppermute | solution.py:411
  21.5 20.0 %collective-permute-start = (s32[32,1024]{1,0:T(8,128)}, s32[32,1024]{1,0:T(8,128)S(1)}, u32[]{:S(2)}, u32[]{:S(2)}) collective-permute-start(s32[32,1024]{1,0:T(8,128)} %x0.1), channel_id=1, source_target_pairs={{0,4},{4,8},{8,12},{12,0},{1,5},{5,9},{9,13},{13,1},{2,6},{6,10},{... | collective-permute-start | bytes 393224 | tf_op jit(solution)/shard_map/ppermute | solution.py:411
  24.3 17.2 %collective-permute-start.2 = (s32[32,1024]{1,0:T(8,128)}, s32[32,1024]{1,0:T(8,128)S(1)}, u32[]{:S(2)}, u32[]{:S(2)}) collective-permute-start(s32[32,1024]{1,0:T(8,128)} %x0.1), channel_id=1, source_target_pairs={{0,12},{4,0},{8,4},{12,8},{1,13},{5,1},{9,5},{13,9},{2,14},{6,2},{... | collective-permute-start | bytes 393224 | tf_op jit(solution)/shard_map/ppermute | solution.py:411
  25.1 14.3 %collective-permute-start.4 = (f32[2,256,128]{2,1,0:T(8,128)S(1)}, f32[2,256,128]{2,1,0:T(8,128)S(1)}, u32[]{:S(2)}, u32[]{:S(2)}) collective-permute-start(f32[2,256,128]{2,1,0:T(8,128)S(1)} %pad_maximum_fusion.f0), channel_id=1, source_target_pairs={{0,2},{2,0},{1,3},{3,1},{4,6},{6,4},{5,7},{7,5},{8,10},{10,8},{9,1... | collective-permute-start | bytes 786440 | tf_op jit(solution)/shard_map/ppermute | solution.py:30
  26.5 21.0 %collective-permute-start.5 = (f32[2,256,128]{2,1,0:T(8,128)S(1)}, f32[2,256,128]{2,1,0:T(8,128)S(1)}, u32[]{:S(2)}, u32[]{:S(2)}) collective-permute-start(f32[2,256,128]{2,1,0:T(8,128)S(1)} %pad_maximum_fusion.f0), channel_id=1, source_target_pairs={{0,1},{1,0},{2,3},{3,2},{4,5},{5,4},{6,7},{7,6},{8,9},{9,8},{10,11... | collective-permute-start | bytes 786440 | tf_op jit(solution)/shard_map/ppermute | solution.py:30
  39.5 8.1 %collective-permute-start.6 = (f32[2,256,128]{2,1,0:T(8,128)S(1)}, f32[2,256,128]{2,1,0:T(8,128)S(1)}, u32[]{:S(2)}, u32[]{:S(2)}) collective-permute-start(f32[2,256,128]{2,1,0:T(8,128)S(1)} %collective-permute-done.4.f1), channel_id=1, source_target_pairs={{0,1},{1,0},{2,3},{3,2},{4,5},{5,4},{6,7},{7,6},{8,9},{9,8},{10,11... | collective-permute-start | bytes 786440 | tf_op jit(solution)/shard_map/ppermute | solution.py:30
  41.5 0.9 copy-start.3
  42.4 0.7 copy-start.4
  43.1 4.5 %copy-start.2 = (f32[1024]{0:T(1024)S(1)}, f32[1024]{0:T(1024)}, u32[]{:S(2)}) copy-start(f32[1024]{0:T(1024)} %param.9) | copy-start | bytes 12292
  82.2 3.8 %collective-permute-start.7 = (f32[8,128]{1,0:T(8,128)S(1)}, f32[8,128]{1,0:T(8,128)S(1)}, u32[]{:S(2)}, u32[]{:S(2)}) collective-permute-start(f32[8,128]{1,0:T(8,128)S(1)} %get-tuple-element.17.near_ref.norm_ref), channel_id=1, source_target_pairs={{0,1},{1,0},{2,3},{3,2},{4,5},{5,4},{6,7},{7,6},{8,9},{9,8},{10,11... | collective-permute-start | bytes 12296 | tf_op jit(solution)/shard_map/ppermute | solution.py:30
  92.2 2.0 %collective-permute-start.8 = (f32[4,264,128]{2,1,0:T(8,128)S(1)}, f32[4,264,128]{2,1,0:T(8,128)S(1)}, u32[]{:S(2)}, u32[]{:S(2)}) collective-permute-start(f32[4,264,128]{2,1,0:T(8,128)S(1)} %get-tuple-element.19), channel_id=1, source_target_pairs={{0,1},{1,0},{2,3},{3,2},{4,5},{5,4},{6,7},{7,6},{8,9},{9,8},{10,11... | collective-permute-start | bytes 1622024 | tf_op jit(solution)/shard_map/ppermute | solution.py:30
  118.1 4.0 %collective-permute-start.9 = (f32[4,264,128]{2,1,0:T(8,128)S(1)}, f32[4,264,128]{2,1,0:T(8,128)S(1)}, u32[]{:S(2)}, u32[]{:S(2)}) collective-permute-start(f32[4,264,128]{2,1,0:T(8,128)S(1)} %all_to_all.44.g0), channel_id=1, source_target_pairs={{0,1},{1,0},{2,3},{3,2},{4,5},{5,4},{6,7},{7,6},{8,9},{9,8},{10,11... | collective-permute-start | bytes 1622024 | tf_op jit(solution)/shard_map/ppermute | solution.py:30
  122.0 37.6 %copy-start.1 = (f32[32,1024]{1,0:T(8,128)S(1)}, f32[32,1024]{1,0:T(8,128)}, u32[]{:S(2)}) copy-start(f32[32,1024]{1,0:T(8,128)} %f_ref.1) | copy-start | bytes 393220

commit v9 on v8

--- a/solution.py
+++ b/solution.py
@@ -195,9 +195,10 @@
     for k in range(1, out_ref.shape[0]):
         out_ref[k, : n + EXTRA, :] = out_ref[0, : n + EXTRA, :]
     for k in range(out_ref.shape[0]):
+        to = (pos_ref[32] + 4 - k) % 4
         for h in range(units // 128):
             at = n + EXTRA + h * ROWS
-            out_ref[k, at : at + ROWS, :] = mine_ref[k * ROWS : (k + 1) * ROWS, h * 128 : (h + 1) * 128]
+            out_ref[to, at : at + ROWS, :] = mine_ref[k * ROWS : (k + 1) * ROWS, h * 128 : (h + 1) * 128]
 
 
 def second_pass(samples, pos, spins, hidden, f, fb, g0, g1, mine, norm):
@@ -308,6 +309,28 @@
     return mean, spread
 
 
+def columns_kernel(pos_ref, f_ref, o0, o1, o2, o3):
+    units = o0.shape[1]
+    for d, out in enumerate((o0, o1, o2, o3)):
+        to = (pos_ref[32] + d) % 4
+        out[...] = f_ref[:, pl.ds(pl.multiple_of(to * units, units), units)]
+
+
+def columns_of(pos, f, units):
+    out = jax.ShapeDtypeStruct((f.shape[0], units), F32)
+    return call(columns_kernel, [SMEM, VMEM], [out] * 4)(pos, f)
+
+
+def turned_kernel(f0, f1, f2, f3, out_ref):
+    out_ref[0] = jnp.concatenate([f0[...], f1[...], f2[...], f3[...]], axis=0).T
+
+
+def turned(f):
+    rows, units = f[0].shape
+    out = jax.ShapeDtypeStruct((1, units, rows * 4), F32)
+    return call(turned_kernel, [VMEM] * 4, [out])(*f)[0]
+
+
 def image_kernel(samples, pos_ref, s_ref, h_ref, v_ref, near_ref, far_ref, keep_ref, send_ref, acc, lanes):
     units = h_ref.shape[0]
     mean = (near_ref[1:2, 0:1] + far_ref[1:2, 0:1]) * (1.0 / samples)
@@ -401,18 +424,21 @@
     fb = force_b.reshape(-1, 128)
 
     q = jnp.arange(32, dtype=jnp.int32)
-    words = (((q >> 2) & 1) ^ xh) * 16 + (q & 3) * 4 + (((q >> 3) & 1) ^ zl) * 2 + ((q >> 4) ^ c)
+    words = (((q >> 2) & 1) ^ xh) * 16 + ((zh - q) & 3) * 4 + (((q >> 3) & 1) ^ zl) * 2 + ((q >> 4) ^ c)
     k = jnp.arange(4, dtype=jnp.int32)
     blocks = ((k & 1) ^ xh) * 2 + ((k >> 1) ^ zl)
     pos = jnp.concatenate([words, zh.reshape(1), blocks, zl.reshape(1), xh.reshape(1)])
 
+    turn = lambda x, d: lax.ppermute(x, "zh", [(i, (i + d) % parts) for i in range(parts)])
+    f = list(columns_of(pos, force_w, units))
+    for d in (1, 2, 3):
+        f[d] = turn(f[d], d)
+
     packed = [spins_packed]
     for d in (1, 2, 3):
-        packed.append(lax.ppermute(spins_packed, "zh", [(i, (i + d) % 4) for i in range(4)]))
-
-    f_cols = jnp.stack([force_w[:, k * units : (k + 1) * units] for k in range(parts)])
-    f = lax.all_to_all(f_cols, "zh", 0, 0, tiled=True)
-    f = f.reshape(parts * ROWS, units).T[None]
+        packed.append(turn(spins_packed, d))
+
+    f = turned(f)
     f_xh = swap(f, "xh")
     f = jnp.concatenate([f, f_xh], axis=0)
     f_zl = swap(f, "zl")

time: 161 us -> 162 us (level)
  starting transfers between devices: 20.2 us -> 38.2 us
  blocking collectives: 97.6 us -> 80.7 us
    all_to_all x1 -> x0, blocking collectives: 16 us -> none  [body(): f = lax.all_to_all(f_cols, 'zh', 0, 0, tiled=True)]
    ppermute x3 -> x6, starting transfers between devices: 4.5 us -> 17.5 us  [body(): lax.ppermute(x, 'zh', [(i, (i + d) % parts) for i in range(parts)])]
    ppermute x7, waiting for transfers between devices: 13.2 us -> 6.56 us  [swap(): return lax.ppermute(x, axis, SWAP)]
    ppermute x3 -> x6, waiting for transfers between devices: 0.01 us -> 5.84 us  [body(): lax.ppermute(x, 'zh', [(i, (i + d) % parts) for i in range(parts)])]
    ppermute x7, starting transfers between devices: 15.7 us -> 20.7 us  [swap(): return lax.ppermute(x, axis, SWAP)]
    all_to_all x2, blocking collectives: 26.3 us -> 23.4 us  [to_all(): lax.all_to_all(jnp.broadcast_to(x[None], (size, *x.shape)), axes, 0, 0, t...]
    all_to_all x1, blocking collectives: 12.3 us -> 14.2 us  [first_sum(): got = lax.all_to_all(x, plane, 0, 0, tiled=True)]
  transfers between devices with their start and end apart: 10 -> 13, of which waited for: 4 -> 6; matrix products, arithmetic and copies ran while one was open for 0% -> 0% of each run, Pallas kernels for 3% -> 3%
where the time goes in v9:
time: 162 us; the launch traced here: 161 us
  blocking collectives  80.7 us (50%)
  starting transfers between devices  38.2 us (24%)
  Pallas kernels  26.3 us (16%)
  waiting for transfers between devices  12.4 us (8%)
  local copies, waits for them, and re-layouts  2.81 us (2%)
    all_to_all x2, blocking collectives, to_all(): lax.all_to_all(jnp.broadcast_to(x[None], (size, *x.shape)), axes, 0, 0, t...  23.4 us
    ppermute x7, starting transfers between devices, swap(): return lax.ppermute(x, axis, SWAP)  20.7 us
    ppermute x6, starting transfers between devices, body(): lax.ppermute(x, 'zh', [(i, (i + d) % parts) for i in range(parts)])  17.5 us
    all_to_all x1, blocking collectives, first_sum(): got = lax.all_to_all(x, plane, 0, 0, tiled=True)  14.2 us
    all_to_all x1, blocking collectives, body(): g, mine = image_sum(lax.all_to_all(g, QUAD, 0, 0, tiled=True), units)  12.3 us
    all_to_all x1, blocking collectives, body(): g = lax.all_to_all(g, QUAD, 0, 0, tiled=True)  11.6 us
    all_to_all x1, blocking collectives, body(): got = lax.all_to_all(partial, 'zh', 0, 0, tiled=True)  11.2 us
    all_to_all x1, blocking collectives, over_groups(): return lax.all_to_all(x, GRP, 0, 0, tiled=True)  8.01 us
  transfers between devices with their start and end apart: 13, of which 6 were waited for; matrix products, arithmetic and copies ran while one was open for 0% of the time, Pallas kernels for 3%

profile of v9, /device:TPU:1, one launch (start us, length us, event | category | flops | bytes accessed | tf_op | source)
XLA Modules:
  0.0 161.4 jit_solution(16688091685996019008)
XLA Ops:
  0.6 0.0 copy-start
  0.7 0.1 concatenate.6.pos_ref
  0.8 1.0 copy-done.1
  1.8 0.6 shard_map.69
  2.4 3.9 %collective-permute-start.3 = (f32[32,256]{1,0:T(8,128)S(1)}, f32[32,256]{1,0:T(8,128)S(1)}, u32[]{:S(2)}, u32[]{:S(2)}) collective-permute-start(f32[32,256]{1,0:T(8,128)S(1)} %get-tuple-element.21), channel_id=1, source_target_pairs={{0,4},{4,8},{8,12},{12,0},{1,5},{5,9},{9,13},{13,1},{2,6},{6,10},{... | collective-permute-start | bytes 98312 | tf_op jit(solution)/shard_map/ppermute | solution.py:432
  6.3 5.1 %collective-permute-start.4 = (f32[32,256]{1,0:T(8,128)S(1)}, f32[32,256]{1,0:T(8,128)S(1)}, u32[]{:S(2)}, u32[]{:S(2)}) collective-permute-start(f32[32,256]{1,0:T(8,128)S(1)} %get-tuple-element.22), channel_id=1, source_target_pairs={{0,8},{4,12},{8,0},{12,4},{1,9},{5,13},{9,1},{13,5},{2,10},{6,14},... | collective-permute-start | bytes 98312 | tf_op jit(solution)/shard_map/ppermute | solution.py:432
  11.4 2.4 %collective-permute-start.5 = (f32[32,256]{1,0:T(8,128)S(1)}, f32[32,256]{1,0:T(8,128)S(1)}, u32[]{:S(2)}, u32[]{:S(2)}) collective-permute-start(f32[32,256]{1,0:T(8,128)S(1)} %get-tuple-element.23), channel_id=1, source_target_pairs={{0,12},{4,0},{8,4},{12,8},{1,13},{5,1},{9,5},{13,9},{2,14},{6,2},{... | collective-permute-start | bytes 98312 | tf_op jit(solution)/shard_map/ppermute | solution.py:432
  13.8 1.3 collective-permute-done.5.f3
  15.1 0.1 shard_map.70
  15.2 2.8 %collective-permute-start.6 = (f32[1,256,128]{2,1,0:T(8,128)S(1)}, f32[1,256,128]{2,1,0:T(8,128)S(1)}, u32[]{:S(2)}, u32[]{:S(2)}) collective-permute-start(f32[1,256,128]{2,1,0:T(8,128)S(1)} %shard_map.70), channel_id=1, source_target_pairs={{0,16},{16,0},{1,17},{17,1},{2,18},{18,2},{3,19},{19,3},{4,20},{20... | collective-permute-start | bytes 393224 | tf_op jit(solution)/shard_map/ppermute | solution.py:30
  18.0 2.6 %collective-permute-done.6 = f32[1,256,128]{2,1,0:T(8,128)S(1)} collective-permute-done((f32[1,256,128]{2,1,0:T(8,128)S(1)}, f32[1,256,128]{2,1,0:T(8,128)S(1)}, u32[]{:S(2)}, u32[]{:S(2)}) %collective-permute-start.6) | collective-permute-done | bytes 131104 | tf_op jit(solution)/shard_map/ppermute | solution.py:30
  20.6 1.5 collective-permute-start.7
  22.1 2.6 %collective-permute-start.1 = (s32[32,1024]{1,0:T(8,128)}, s32[32,1024]{1,0:T(8,128)S(1)}, u32[]{:S(2)}, u32[]{:S(2)}) collective-permute-start(s32[32,1024]{1,0:T(8,128)} %x0.1), channel_id=1, source_target_pairs={{0,8},{4,12},{8,0},{12,4},{1,9},{5,13},{9,1},{13,5},{2,10},{6,14},... | collective-permute-start | bytes 393224 | tf_op jit(solution)/shard_map/ppermute | solution.py:432
  24.7 2.4 %collective-permute-start = (s32[32,1024]{1,0:T(8,128)}, s32[32,1024]{1,0:T(8,128)S(1)}, u32[]{:S(2)}, u32[]{:S(2)}) collective-permute-start(s32[32,1024]{1,0:T(8,128)} %x0.1), channel_id=1, source_target_pairs={{0,4},{4,8},{8,12},{12,0},{1,5},{5,9},{9,13},{13,1},{2,6},{6,10},{... | collective-permute-start | bytes 393224 | tf_op jit(solution)/shard_map/ppermute | solution.py:432
  27.1 1.2 collective-permute-start.2
  28.2 0.1 constant_dynamic-slice_fusion.w_ref
  28.3 4.8 %collective-permute-start.8 = (f32[2,256,128]{2,1,0:T(8,128)S(1)}, f32[2,256,128]{2,1,0:T(8,128)S(1)}, u32[]{:S(2)}, u32[]{:S(2)}) collective-permute-start(f32[2,256,128]{2,1,0:T(8,128)S(1)} %pad_maximum_fusion.f0), channel_id=1, source_target_pairs={{0,1},{1,0},{2,3},{3,2},{4,5},{5,4},{6,7},{7,6},{8,9},{9,8},{10,11... | collective-permute-start | bytes 786440 | tf_op jit(solution)/shard_map/ppermute | solution.py:30
  33.1 0.0 collective-permute-done.7.f1
  33.1 2.5 %collective-permute-start.9 = (f32[2,256,128]{2,1,0:T(8,128)S(1)}, f32[2,256,128]{2,1,0:T(8,128)S(1)}, u32[]{:S(2)}, u32[]{:S(2)}) collective-permute-start(f32[2,256,128]{2,1,0:T(8,128)S(1)} %collective-permute-done.7.f1), channel_id=1, source_target_pairs={{0,1},{1,0},{2,3},{3,2},{4,5},{5,4},{6,7},{7,6},{8,9},{9,8},{10,11... | collective-permute-start | bytes 786440 | tf_op jit(solution)/shard_map/ppermute | solution.py:30
  35.6 0.0 collective-permute-done.1.x2
  35.6 4.5 %collective-permute-done.x1 = s32[32,1024]{1,0:T(8,128)S(1)} collective-permute-done((s32[32,1024]{1,0:T(8,128)}, s32[32,1024]{1,0:T(8,128)S(1)}, u32[]{:S(2)}, u32[]{:S(2)}) %collective-permute-start) | collective-permute-done | bytes 131104 | tf_op jit(solution)/shard_map/ppermute | solution.py:432
  40.1 0.0 collective-permute-done.2.x3
  40.2 0.9 copy-done.4
  41.1 0.7 copy-done.5
  41.7 4.4 %shard_map.68 = (bf16[1024,4096]{1,0:T(8,128)(2,1)S(1)}, f32[256,4096]{1,0:T(8,128)S(1)}) custom-call(s32[39]{0:T(128)S(1)} %concatenate.6.pos_ref, s32[32,1024]{1,0:T(8,128)S(1)} %copy-done.4, s32[32,1024]{1,0:T(8,128)S(1)} %collective-permute-done.x1, s32[32,1024]{1,0:T(8,128)S(1)} %collective-permute-done.1.x2, s32[32,1024]{1,0:T(8,128)S(1)} %collective-permute-done.2.x3, ...), custom_call_target="tpu_custom_call" | custom-call | flops 4000000000 | bytes 1048576 | tf_op jit(solution)/shard_map/pallas_call | solution.py:109
  46.2 0.0 collective-permute-done.8.f2
  46.2 6.3 %shard_map.71 = f32[40,128]{1,0:T(8,128)S(1)} custom-call(s32[39]{0:T(128)S(1)} %concatenate.6.pos_ref, bf16[1024,4096]{1,0:T(8,128)(2,1)S(1)} %get-tuple-element.18.s_ref, f32[256,4096]{1,0:T(8,128)S(1)} %get-tuple-element.19.h_ref, f32[2,256,128]{2,1,0:T(8,128)S(1)} %pad_maximum_fusion.f0, f32[2,256,128]{2,1,0:T(8,128)S(1)} %collective-permute-done.7.f1, ...), custom_call_target="tpu_custom_call" | custom-call | flops 4000000000 | bytes 1048576 | tf_op jit(solution)/shard_map/pallas_call | solution.py:158
  52.6 11.9 %all_to_all.35.got_ref = f32[8,40,128]{2,1,0:T(8,128)S(1)} all-to-all(f32[8,40,128]{2,1,0:T(8,128)S(1)} %broadcast_in_dim.4), channel_id=1, replica_groups=mesh['xl'=2,'y'=4,'xh'=2,'zh'=4,'zl'=2,'c'=2] {'zh','zl'}, dimensions={0} | all-to-all | bytes 327680 | tf_op jit(solution)/shard_map/all_to_all | solution.py:34
  64.5 0.6 shard_map.72
  65.0 14.2 %all_to_all.36.got_ref = f32[16,40,128]{2,1,0:T(8,128)S(1)} all-to-all(f32[16,40,128]{2,1,0:T(8,128)S(1)} %shard_map.72), channel_id=1, replica_groups=mesh['xl'=2,'y'=4,'xh'=2,'zh'=4,'zl'=2,'c'=2] {'xh','xl','y'}, dimensions={0} | all-to-all | bytes 655360 | tf_op jit(solution)/shard_map/all_to_all | solution.py:277
  79.3 0.6 shard_map.73
  79.8 6.2 %collective-permute-start.10 = (f32[8,128]{1,0:T(8,128)S(1)}, f32[8,128]{1,0:T(8,128)S(1)}, u32[]{:S(2)}, u32[]{:S(2)}) collective-permute-start(f32[8,128]{1,0:T(8,128)S(1)} %get-tuple-element.25.near_ref.norm_ref), channel_id=1, source_target_pairs={{0,1},{1,0},{2,3},{3,2},{4,5},{5,4},{6,7},{7,6},{8,9},{9,8},{10,11... | collective-permute-start | bytes 12296 | tf_op jit(solution)/shard_map/ppermute | solution.py:30
  86.1 0.8 collective-permute-done.10.far_ref
  86.9 6.1 %shard_map.74 = (f32[4,264,128]{2,1,0:T(8,128)S(1)}, f32[4,264,128]{2,1,0:T(8,128)S(1)}) custom-call(s32[39]{0:T(128)S(1)} %concatenate.6.pos_ref, bf16[1024,4096]{1,0:T(8,128)(2,1)S(1)} %get-tuple-element.18.s_ref, f32[256,4096]{1,0:T(8,128)S(1)} %get-tuple-element.19.h_ref, f32[32,128]{1,0:T(8,128)S(1)} %get-tuple-element.24.v_ref, ...), custom_call_target="tpu_custom_call" | custom-call | flops 4000000000 | bytes 1048576 | tf_op jit(solution)/shard_map/pallas_call | solution.py:366
  93.0 0.4 collective-permute-start.11
  93.4 1.6 collective-permute-done.11
  95.0 0.1 add.23
  95.1 12.3 %all_to_all.37.got_ref = f32[4,264,128]{2,1,0:T(8,128)S(1)} all-to-all(f32[4,264,128]{2,1,0:T(8,128)S(1)} %add.23), channel_id=1, replica_groups=mesh['xl'=2,'y'=4,'xh'=2,'zh'=4,'zl'=2,'c'=2] {'xh','zl'}, dimensions={0} | all-to-all | bytes 1081344 | tf_op jit(solution)/shard_map/all_to_all | solution.py:456
  107.4 0.1 shard_map.75
  107.5 11.6 %all_to_all.38.g0 = f32[4,264,128]{2,1,0:T(8,128)S(1)} all-to-all(f32[4,264,128]{2,1,0:T(8,128)S(1)} %get-tuple-element.28), channel_id=1, replica_groups=mesh['xl'=2,'y'=4,'xh'=2,'zh'=4,'zl'=2,'c'=2] {'xh','zl'}, dimensions={0} | all-to-all | bytes 1081344 | tf_op jit(solution)/shard_map/all_to_all | solution.py:457
  119.0 2.4 %collective-permute-start.12 = (f32[4,264,128]{2,1,0:T(8,128)S(1)}, f32[4,264,128]{2,1,0:T(8,128)S(1)}, u32[]{:S(2)}, u32[]{:S(2)}) collective-permute-start(f32[4,264,128]{2,1,0:T(8,128)S(1)} %all_to_all.38.g0), channel_id=1, source_target_pairs={{0,1},{1,0},{2,3},{3,2},{4,5},{5,4},{6,7},{7,6},{8,9},{9,8},{10,11... | collective-permute-start | bytes 1622024 | tf_op jit(solution)/shard_map/ppermute | solution.py:30
  121.5 1.6 collective-permute-done.12.g1
  123.0 6.5 %shard_map.76 = f32[4,104,128]{2,1,0:T(8,128)S(1)} custom-call(s32[39]{0:T(128)S(1)} %concatenate.6.pos_ref, bf16[1024,4096]{1,0:T(8,128)(2,1)S(1)} %get-tuple-element.18.s_ref, f32[256,4096]{1,0:T(8,128)S(1)} %get-tuple-element.19.h_ref, f32[2,256,128]{2,1,0:T(8,128)S(1)} %pad_maximum_fusion.f0, f32[2,256,128]{2,1,0:T(8,128)S(1)} %collective-permute-done.7.f1, ...), custom_call_target="tpu_custom_call" | custom-call | flops 4000000000 | bytes 1048576 | tf_op jit(solution)/shard_map/pallas_call | solution.py:207
  129.6 11.2 %all_to_all.39.got_ref = f32[4,104,128]{2,1,0:T(8,128)S(1)} all-to-all(f32[4,104,128]{2,1,0:T(8,128)S(1)} %shard_map.76), channel_id=1, replica_groups=mesh['xl'=2,'y'=4,'xh'=2,'zh'=4,'zl'=2,'c'=2] {'zh'}, dimensions={0} | all-to-all | bytes 425984 | tf_op jit(solution)/shard_map/all_to_all | solution.py:460
  140.8 8.0 %all_to_all.40.got_ref = f32[8,40,128]{2,1,0:T(8,128)S(1)} all-to-all(f32[8,40,128]{2,1,0:T(8,128)S(1)} %shard_map.77), channel_id=1, replica_groups=mesh['xl'=2,'y'=4,'xh'=2,'zh'=4,'zl'=2,'c'=2] {'xl','y'}, dimensions={0} | all-to-all | bytes 327680 | tf_op jit(solution)/shard_map/all_to_all | solution.py:234
  148.8 0.3 shard_map.78
  149.1 11.5 %all_to_all.41.st1_ref = f32[8,8,128]{2,1,0:T(8,128)S(1)} all-to-all(f32[8,8,128]{2,1,0:T(8,128)S(1)} %broadcast_in_dim.5), channel_id=1, replica_groups=mesh['xl'=2,'y'=4,'xh'=2,'zh'=4,'zl'=2,'c'=2] {'xh','zl','c'}, dimensions={0} | all-to-all | bytes 65536 | tf_op jit(solution)/shard_map/all_to_all | solution.py:34
  160.7 0.7 shard_map.79
  (17 shorter events, 0.1 us)
Async XLA Ops:
  0.6 27.6 %copy-start = (bf16[1024,1024]{1,0:T(8,128)(2,1)S(1)}, bf16[1024,1024]{1,0:T(8,128)(2,1)}, u32[]{:S(2)}) copy-start(bf16[1024,1024]{1,0:T(8,128)(2,1)} %param.6) | copy-start | bytes 6291460
  0.8 1.0 copy-start.1
  2.4 11.4 %collective-permute-start.3 = (f32[32,256]{1,0:T(8,128)S(1)}, f32[32,256]{1,0:T(8,128)S(1)}, u32[]{:S(2)}, u32[]{:S(2)}) collective-permute-start(f32[32,256]{1,0:T(8,128)S(1)} %get-tuple-element.21), channel_id=1, source_target_pairs={{0,4},{4,8},{8,12},{12,0},{1,5},{5,9},{9,13},{13,1},{2,6},{6,10},{... | collective-permute-start | bytes 98312 | tf_op jit(solution)/shard_map/ppermute | solution.py:432
  6.3 7.5 %collective-permute-start.4 = (f32[32,256]{1,0:T(8,128)S(1)}, f32[32,256]{1,0:T(8,128)S(1)}, u32[]{:S(2)}, u32[]{:S(2)}) collective-permute-start(f32[32,256]{1,0:T(8,128)S(1)} %get-tuple-element.22), channel_id=1, source_target_pairs={{0,8},{4,12},{8,0},{12,4},{1,9},{5,13},{9,1},{13,5},{2,10},{6,14},... | collective-permute-start | bytes 98312 | tf_op jit(solution)/shard_map/ppermute | solution.py:432
  11.4 3.7 %collective-permute-start.5 = (f32[32,256]{1,0:T(8,128)S(1)}, f32[32,256]{1,0:T(8,128)S(1)}, u32[]{:S(2)}, u32[]{:S(2)}) collective-permute-start(f32[32,256]{1,0:T(8,128)S(1)} %get-tuple-element.23), channel_id=1, source_target_pairs={{0,12},{4,0},{8,4},{12,8},{1,13},{5,1},{9,5},{13,9},{2,14},{6,2},{... | collective-permute-start | bytes 98312 | tf_op jit(solution)/shard_map/ppermute | solution.py:432
  15.2 5.4 %collective-permute-start.6 = (f32[1,256,128]{2,1,0:T(8,128)S(1)}, f32[1,256,128]{2,1,0:T(8,128)S(1)}, u32[]{:S(2)}, u32[]{:S(2)}) collective-permute-start(f32[1,256,128]{2,1,0:T(8,128)S(1)} %shard_map.70), channel_id=1, source_target_pairs={{0,16},{16,0},{1,17},{17,1},{2,18},{18,2},{3,19},{19,3},{4,20},{20... | collective-permute-start | bytes 393224 | tf_op jit(solution)/shard_map/ppermute | solution.py:30
  20.6 12.5 %collective-permute-start.7 = (f32[2,256,128]{2,1,0:T(8,128)S(1)}, f32[2,256,128]{2,1,0:T(8,128)S(1)}, u32[]{:S(2)}, u32[]{:S(2)}) collective-permute-start(f32[2,256,128]{2,1,0:T(8,128)S(1)} %pad_maximum_fusion.f0), channel_id=1, source_target_pairs={{0,2},{2,0},{1,3},{3,1},{4,6},{6,4},{5,7},{7,5},{8,10},{10,8},{9,1... | collective-permute-start | bytes 786440 | tf_op jit(solution)/shard_map/ppermute | solution.py:30
  22.1 13.5 %collective-permute-start.1 = (s32[32,1024]{1,0:T(8,128)}, s32[32,1024]{1,0:T(8,128)S(1)}, u32[]{:S(2)}, u32[]{:S(2)}) collective-permute-start(s32[32,1024]{1,0:T(8,128)} %x0.1), channel_id=1, source_target_pairs={{0,8},{4,12},{8,0},{12,4},{1,9},{5,13},{9,1},{13,5},{2,10},{6,14},... | collective-permute-start | bytes 393224 | tf_op jit(solution)/shard_map/ppermute | solution.py:432
  24.7 15.5 %collective-permute-start = (s32[32,1024]{1,0:T(8,128)}, s32[32,1024]{1,0:T(8,128)S(1)}, u32[]{:S(2)}, u32[]{:S(2)}) collective-permute-start(s32[32,1024]{1,0:T(8,128)} %x0.1), channel_id=1, source_target_pairs={{0,4},{4,8},{8,12},{12,0},{1,5},{5,9},{9,13},{13,1},{2,6},{6,10},{... | collective-permute-start | bytes 393224 | tf_op jit(solution)/shard_map/ppermute | solution.py:432
  27.1 13.1 %collective-permute-start.2 = (s32[32,1024]{1,0:T(8,128)}, s32[32,1024]{1,0:T(8,128)S(1)}, u32[]{:S(2)}, u32[]{:S(2)}) collective-permute-start(s32[32,1024]{1,0:T(8,128)} %x0.1), channel_id=1, source_target_pairs={{0,12},{4,0},{8,4},{12,8},{1,13},{5,1},{9,5},{13,9},{2,14},{6,2},{... | collective-permute-start | bytes 393224 | tf_op jit(solution)/shard_map/ppermute | solution.py:432
  28.3 17.9 %collective-permute-start.8 = (f32[2,256,128]{2,1,0:T(8,128)S(1)}, f32[2,256,128]{2,1,0:T(8,128)S(1)}, u32[]{:S(2)}, u32[]{:S(2)}) collective-permute-start(f32[2,256,128]{2,1,0:T(8,128)S(1)} %pad_maximum_fusion.f0), channel_id=1, source_target_pairs={{0,1},{1,0},{2,3},{3,2},{4,5},{5,4},{6,7},{7,6},{8,9},{9,8},{10,11... | collective-permute-start | bytes 786440 | tf_op jit(solution)/shard_map/ppermute | solution.py:30
  33.1 13.1 %collective-permute-start.9 = (f32[2,256,128]{2,1,0:T(8,128)S(1)}, f32[2,256,128]{2,1,0:T(8,128)S(1)}, u32[]{:S(2)}, u32[]{:S(2)}) collective-permute-start(f32[2,256,128]{2,1,0:T(8,128)S(1)} %collective-permute-done.7.f1), channel_id=1, source_target_pairs={{0,1},{1,0},{2,3},{3,2},{4,5},{5,4},{6,7},{7,6},{8,9},{9,8},{10,11... | collective-permute-start | bytes 786440 | tf_op jit(solution)/shard_map/ppermute | solution.py:30
  40.1 0.9 copy-start.4
  41.1 0.7 copy-start.5
  41.7 4.5 %copy-start.3 = (f32[1024]{0:T(1024)S(1)}, f32[1024]{0:T(1024)}, u32[]{:S(2)}) copy-start(f32[1024]{0:T(1024)} %param.9) | copy-start | bytes 12292
  79.8 7.0 %collective-permute-start.10 = (f32[8,128]{1,0:T(8,128)S(1)}, f32[8,128]{1,0:T(8,128)S(1)}, u32[]{:S(2)}, u32[]{:S(2)}) collective-permute-start(f32[8,128]{1,0:T(8,128)S(1)} %get-tuple-element.25.near_ref.norm_ref), channel_id=1, source_target_pairs={{0,1},{1,0},{2,3},{3,2},{4,5},{5,4},{6,7},{7,6},{8,9},{9,8},{10,11... | collective-permute-start | bytes 12296 | tf_op jit(solution)/shard_map/ppermute | solution.py:30
  93.0 2.0 %collective-permute-start.11 = (f32[4,264,128]{2,1,0:T(8,128)S(1)}, f32[4,264,128]{2,1,0:T(8,128)S(1)}, u32[]{:S(2)}, u32[]{:S(2)}) collective-permute-start(f32[4,264,128]{2,1,0:T(8,128)S(1)} %get-tuple-element.27), channel_id=1, source_target_pairs={{0,1},{1,0},{2,3},{3,2},{4,5},{5,4},{6,7},{7,6},{8,9},{9,8},{10,11... | collective-permute-start | bytes 1622024 | tf_op jit(solution)/shard_map/ppermute | solution.py:30
  119.0 4.0 %collective-permute-start.12 = (f32[4,264,128]{2,1,0:T(8,128)S(1)}, f32[4,264,128]{2,1,0:T(8,128)S(1)}, u32[]{:S(2)}, u32[]{:S(2)}) collective-permute-start(f32[4,264,128]{2,1,0:T(8,128)S(1)} %all_to_all.38.g0), channel_id=1, source_target_pairs={{0,1},{1,0},{2,3},{3,2},{4,5},{5,4},{6,7},{7,6},{8,9},{9,8},{10,11... | collective-permute-start | bytes 1622024 | tf_op jit(solution)/shard_map/ppermute | solution.py:30
  123.0 37.6 %copy-start.2 = (f32[32,1024]{1,0:T(8,128)S(1)}, f32[32,1024]{1,0:T(8,128)}, u32[]{:S(2)}) copy-start(f32[32,1024]{1,0:T(8,128)} %f_ref.3) | copy-start | bytes 393220

commit v10 on v9

--- a/solution.py
+++ b/solution.py
@@ -168,28 +168,28 @@
     return norm / (spread / samples + LAM * length)
 
 
-def second_kernel(samples, pos_ref, s_ref, h_ref, f0, f1, f2, f3, fb_ref, g0, g1, mine_ref, norm_ref, out_ref, lhs):
+def second_kernel(samples, pos_ref, s_ref, h_ref, f0, f1, f2, f3, fb_ref, *refs):
+    *g, mine_ref, norm_ref, out_ref, lhs = refs
     units = h_ref.shape[0]
     norm0 = norm_ref[0:1, :]
-    spread = g0[0, units + units // 128 : units + units // 128 + 1, :]
+    spread = g[0][units + units // 128 : units + units // 128 + 1, :]
     a = step_of(norm0, spread, samples, norm0)
     rr = jnp.zeros((units, 128), F32)
     rf = jnp.zeros((units, 128), F32)
     for b in range(NB):
         f = (f0, f1, f2, f3)[b // 2][b % 2]
-        g = (g0, g1)[b // 4][pos_ref[33 + b % 4], :units, :]
-        r = f - a * (g + LAM * f)
+        r = f - a * (g[b][:units, :] + LAM * f)
         set_block(lhs, b, r)
         rr = rr + r * r
         rf = rf + r * f
     fb = my_rows(pos_ref, fb_ref, units)
-    rb = fb - a * (g0[0, units : units + units // 128, :] + LAM * fb)
+    rb = fb - a * (g[0][units : units + units // 128, :] + LAM * fb)
     n = h_ref.shape[1] // 128
     p_ref = out_ref.at[0]
     p_ref[n : n + EXTRA, :] = jnp.zeros((EXTRA, 128), F32)
     p_ref[n : n + 1, :] = total(rr) + total(rb * rb)
     p_ref[n + 1 : n + 2, :] = total(rf) + total(rb * fb)
-    p_ref[n + 2 : n + 2 + units // 128, :] = g0[0, units : units + units // 128, :]
+    p_ref[n + 2 : n + 2 + units // 128, :] = g[0][units : units + units // 128, :]
     p_ref[n + 2 + units // 128 : n + 3 + units // 128, :] = spread
     project(s_ref, h_ref, lhs, rows_to_column(rb), p_ref)
     for k in range(1, out_ref.shape[0]):
@@ -201,16 +201,16 @@
             out_ref[to, at : at + ROWS, :] = mine_ref[k * ROWS : (k + 1) * ROWS, h * 128 : (h + 1) * 128]
 
 
-def second_pass(samples, pos, spins, hidden, f, fb, g0, g1, mine, norm):
+def second_pass(samples, pos, spins, hidden, f, fb, g, mine, norm):
     units, n = hidden.shape
     parts = mine.shape[0] // ROWS
     return call(
         functools.partial(second_kernel, samples),
-        [SMEM] + [VMEM] * 11,
+        [SMEM] + [VMEM] * (9 + NB),
         [jax.ShapeDtypeStruct((parts, n // 128 + EXTRA + units // 128 * ROWS, 128), F32)],
         [pltpu.VMEM((2 * units, NB * 128), BF16)],
         flops=4 * 10**9,
-    )(pos, resident(spins), resident(hidden), *f, fb, g0, g1, mine, norm)[0]
+    )(pos, resident(spins), resident(hidden), *f, fb, *g, mine, norm)[0]
 
 
 def put_stats(v, st_ref):
@@ -356,7 +356,7 @@
     bias = jnp.concatenate(bias, axis=0)
     for b in range(NB):
         ref = (keep_ref, send_ref)[b // 4]
-        at = pos_ref[33 + b % 4]
+        at = b % 4
         ref[at, :units, :] = acc[:, b * 128 : (b + 1) * 128]
         ref[at, units:, :] = bias
 
@@ -372,17 +372,34 @@
     )(pos, resident(spins), resident(hidden), values, near, far)
 
 
-def image_sum_kernel(got_ref, all_ref, mine_ref):
+def halves_kernel(keep_ref, got_ref, o0, o1, o2, o3):
+    for k, out in enumerate((o0, o1, o2, o3)):
+        out[...] = keep_ref[k] + got_ref[k]
+
+
+def halves(keep, got):
+    return call(halves_kernel, [VMEM] * 2, [jax.ShapeDtypeStruct(keep.shape[1:], F32)] * 4)(keep, got)
+
+
+def image_sum_kernel(g0, g1, g2, g3, all_ref, mine_ref):
     units = mine_ref.shape[1]
-    x = got_ref[0] + got_ref[1] + (got_ref[2] + got_ref[3])
-    for k in range(4):
-        all_ref[k] = x
+    x = g0[...] + g1[...] + (g2[...] + g3[...])
+    all_ref[...] = x
     mine_ref[...] = x[:units].T
 
 
-def image_sum(got, units):
+def image_sum(g, units):
     shape = lambda *s: jax.ShapeDtypeStruct(s, F32)
-    return call(image_sum_kernel, [VMEM], [shape(*got.shape), shape(128, units)])(got)
+    return call(image_sum_kernel, [VMEM] * 4, [shape(*g[0].shape), shape(128, units)])(*g)
+
+
+def to_quad(blocks):
+    return [
+        blocks[0],
+        swap(blocks[1], "xh"),
+        swap(blocks[2], "zl"),
+        lax.ppermute(blocks[3], QUAD, [(i, i ^ 3) for i in range(4)]),
+    ]
 
 
 def update_kernel(samples, f_ref, fb_ref, got_ref, norm_ref, st1_ref, next_ref, w_ref, b_ref):
@@ -452,11 +469,11 @@
     norm_far = swap(norm, "c")
 
     keep, send = image_pass(samples, pos, spins, hidden, values, norm, norm_far)
-    g = keep + swap(send, "c")
-    g, mine = image_sum(lax.all_to_all(g, QUAD, 0, 0, tiled=True), units)
-    g = lax.all_to_all(g, QUAD, 0, 0, tiled=True)
-
-    partial = second_pass(samples, pos, spins, hidden, f, fb, g, swap(g, "c"), mine, norm)
+    g, mine = image_sum(to_quad(halves(keep, swap(send, "c"))), units)
+    g = to_quad([g] * 4)
+    g += [swap(x, "c") for x in g]
+
+    partial = second_pass(samples, pos, spins, hidden, f, fb, g, mine, norm)
     got = lax.all_to_all(partial, "zh", 0, 0, tiled=True)
     st, norms = second_sum(over_groups(got, rows), values, norm)
     st1 = of_sets(st)

time: 162 us -> 158 us (0.975)
  blocking collectives: 80.7 us -> 58.4 us
  starting transfers between devices: 38.2 us -> 51.6 us
  waiting for transfers between devices: 12.4 us -> 17.8 us
    all_to_all x2 -> x0, blocking collectives: 23.9 us -> none  [the longest x1 12.3 us: body(): g, mine = image_sum(lax.all_to_all(g, QUAD, 0, 0, tiled=True), units)]
    ppermute x7 -> x14, starting transfers between devices: 20.7 us -> 30.4 us  [swap(): return lax.ppermute(x, axis, SWAP)]
    ppermute x0 -> x2, waiting for transfers between devices: none -> 3.8 us  [to_quad(): lax.ppermute(blocks[3], QUAD, [(i, i ^ 3) for i in range(4)])]
    ppermute x0 -> x2, starting transfers between devices: none -> 3.73 us  [to_quad(): lax.ppermute(blocks[3], QUAD, [(i, i ^ 3) for i in range(4)])]
    ppermute x7 -> x14, waiting for transfers between devices: 6.56 us -> 8.12 us  [swap(): return lax.ppermute(x, axis, SWAP)]
    pallas_call x2 -> x3, Pallas kernels: 6.65 us -> 6.72 us  [the longest x1 6.52 us: second_pass(): call(functools.partial(second_kernel, samples), [SMEM] + [VMEM] * (9 + NB...]
  transfers between devices with their start and end apart: 13 -> 22, of which waited for: 6 -> 8; matrix products, arithmetic and copies ran while one was open for 0% -> 0% of each run, Pallas kernels for 3% -> 3%
where the time goes in v10:
time: 158 us
  blocking collectives  58.4 us (37%)
  starting transfers between devices  51.6 us (33%)
  Pallas kernels  26.3 us (17%)
  waiting for transfers between devices  17.8 us (11%)
  local copies, waits for them, and re-layouts  2.81 us (2%)
    ppermute x14, starting transfers between devices, swap(): return lax.ppermute(x, axis, SWAP)  30.4 us
    all_to_all x2, blocking collectives, to_all(): lax.all_to_all(jnp.broadcast_to(x[None], (size, *x.shape)), axes, 0, 0, t...  25 us
    ppermute x6, starting transfers between devices, body(): lax.ppermute(x, 'zh', [(i, (i + d) % parts) for i in range(parts)])  17.5 us
    all_to_all x1, blocking collectives, first_sum(): got = lax.all_to_all(x, plane, 0, 0, tiled=True)  14.2 us
    all_to_all x1, blocking collectives, body(): got = lax.all_to_all(partial, 'zh', 0, 0, tiled=True)  11.2 us
    ppermute x14, waiting for transfers between devices, swap(): return lax.ppermute(x, axis, SWAP)  8.12 us
    all_to_all x1, blocking collectives, over_groups(): return lax.all_to_all(x, GRP, 0, 0, tiled=True)  8.01 us
    pallas_call x1, Pallas kernels, second_pass(): call(functools.partial(second_kernel, samples), [SMEM] + [VMEM] * (9 + NB...  6.52 us
  transfers between devices with their start and end apart: 22, of which 8 were waited for; matrix products, arithmetic and copies ran while one was open for 0% of the time, Pallas kernels for 3%

profile of v10, /device:TPU:1, one launch (start us, length us, event | category | flops | bytes accessed | tf_op | source)
XLA Modules:
  0.0 157.7 jit_solution(271988291983568661)
XLA Ops:
  0.8 1.0 copy-done.1
  1.8 0.6 shard_map.69
  2.4 3.9 %collective-permute-start.3 = (f32[32,256]{1,0:T(8,128)S(1)}, f32[32,256]{1,0:T(8,128)S(1)}, u32[]{:S(2)}, u32[]{:S(2)}) collective-permute-start(f32[32,256]{1,0:T(8,128)S(1)} %get-tuple-element.25), channel_id=1, source_target_pairs={{0,4},{4,8},{8,12},{12,0},{1,5},{5,9},{9,13},{13,1},{2,6},{6,10},{... | collective-permute-start | bytes 98312 | tf_op jit(solution)/shard_map/ppermute | solution.py:449
  6.3 5.1 %collective-permute-start.4 = (f32[32,256]{1,0:T(8,128)S(1)}, f32[32,256]{1,0:T(8,128)S(1)}, u32[]{:S(2)}, u32[]{:S(2)}) collective-permute-start(f32[32,256]{1,0:T(8,128)S(1)} %get-tuple-element.26), channel_id=1, source_target_pairs={{0,8},{4,12},{8,0},{12,4},{1,9},{5,13},{9,1},{13,5},{2,10},{6,14},... | collective-permute-start | bytes 98312 | tf_op jit(solution)/shard_map/ppermute | solution.py:449
  11.4 2.4 %collective-permute-start.5 = (f32[32,256]{1,0:T(8,128)S(1)}, f32[32,256]{1,0:T(8,128)S(1)}, u32[]{:S(2)}, u32[]{:S(2)}) collective-permute-start(f32[32,256]{1,0:T(8,128)S(1)} %get-tuple-element.27), channel_id=1, source_target_pairs={{0,12},{4,0},{8,4},{12,8},{1,13},{5,1},{9,5},{13,9},{2,14},{6,2},{... | collective-permute-start | bytes 98312 | tf_op jit(solution)/shard_map/ppermute | solution.py:449
  13.8 1.3 collective-permute-done.5.f3
  15.1 0.1 shard_map.70
  15.2 2.8 %collective-permute-start.6 = (f32[1,256,128]{2,1,0:T(8,128)S(1)}, f32[1,256,128]{2,1,0:T(8,128)S(1)}, u32[]{:S(2)}, u32[]{:S(2)}) collective-permute-start(f32[1,256,128]{2,1,0:T(8,128)S(1)} %shard_map.70), channel_id=1, source_target_pairs={{0,16},{16,0},{1,17},{17,1},{2,18},{18,2},{3,19},{19,3},{4,20},{20... | collective-permute-start | bytes 393224 | tf_op jit(solution)/shard_map/ppermute | solution.py:30
  18.0 2.6 %collective-permute-done.6 = f32[1,256,128]{2,1,0:T(8,128)S(1)} collective-permute-done((f32[1,256,128]{2,1,0:T(8,128)S(1)}, f32[1,256,128]{2,1,0:T(8,128)S(1)}, u32[]{:S(2)}, u32[]{:S(2)}) %collective-permute-start.6) | collective-permute-done | bytes 131104 | tf_op jit(solution)/shard_map/ppermute | solution.py:30
  20.6 1.5 collective-permute-start.7
  22.1 2.6 %collective-permute-start.1 = (s32[32,1024]{1,0:T(8,128)}, s32[32,1024]{1,0:T(8,128)S(1)}, u32[]{:S(2)}, u32[]{:S(2)}) collective-permute-start(s32[32,1024]{1,0:T(8,128)} %x0.1), channel_id=1, source_target_pairs={{0,8},{4,12},{8,0},{12,4},{1,9},{5,13},{9,1},{13,5},{2,10},{6,14},... | collective-permute-start | bytes 393224 | tf_op jit(solution)/shard_map/ppermute | solution.py:449
  24.7 2.4 %collective-permute-start = (s32[32,1024]{1,0:T(8,128)}, s32[32,1024]{1,0:T(8,128)S(1)}, u32[]{:S(2)}, u32[]{:S(2)}) collective-permute-start(s32[32,1024]{1,0:T(8,128)} %x0.1), channel_id=1, source_target_pairs={{0,4},{4,8},{8,12},{12,0},{1,5},{5,9},{9,13},{13,1},{2,6},{6,10},{... | collective-permute-start | bytes 393224 | tf_op jit(solution)/shard_map/ppermute | solution.py:449
  27.1 1.2 collective-permute-start.2
  28.3 4.8 %collective-permute-start.8 = (f32[2,256,128]{2,1,0:T(8,128)S(1)}, f32[2,256,128]{2,1,0:T(8,128)S(1)}, u32[]{:S(2)}, u32[]{:S(2)}) collective-permute-start(f32[2,256,128]{2,1,0:T(8,128)S(1)} %pad_maximum_fusion.f0), channel_id=1, source_target_pairs={{0,1},{1,0},{2,3},{3,2},{4,5},{5,4},{6,7},{7,6},{8,9},{9,8},{10,11... | collective-permute-start | bytes 786440 | tf_op jit(solution)/shard_map/ppermute | solution.py:30
  33.1 2.5 %collective-permute-start.9 = (f32[2,256,128]{2,1,0:T(8,128)S(1)}, f32[2,256,128]{2,1,0:T(8,128)S(1)}, u32[]{:S(2)}, u32[]{:S(2)}) collective-permute-start(f32[2,256,128]{2,1,0:T(8,128)S(1)} %collective-permute-done.7.f1), channel_id=1, source_target_pairs={{0,1},{1,0},{2,3},{3,2},{4,5},{5,4},{6,7},{7,6},{8,9},{9,8},{10,11... | collective-permute-start | bytes 786440 | tf_op jit(solution)/shard_map/ppermute | solution.py:30
  35.6 4.5 %collective-permute-done.x1 = s32[32,1024]{1,0:T(8,128)S(1)} collective-permute-done((s32[32,1024]{1,0:T(8,128)}, s32[32,1024]{1,0:T(8,128)S(1)}, u32[]{:S(2)}, u32[]{:S(2)}) %collective-permute-start) | collective-permute-done | bytes 131104 | tf_op jit(solution)/shard_map/ppermute | solution.py:449
  40.2 0.9 copy-done.4
  41.1 0.7 copy-done.5
  41.7 4.4 %shard_map.68 = (bf16[1024,4096]{1,0:T(8,128)(2,1)S(1)}, f32[256,4096]{1,0:T(8,128)S(1)}) custom-call(s32[39]{0:T(128)S(1)} %concatenate.6.pos_ref, s32[32,1024]{1,0:T(8,128)S(1)} %copy-done.4, s32[32,1024]{1,0:T(8,128)S(1)} %collective-permute-done.x1, s32[32,1024]{1,0:T(8,128)S(1)} %collective-permute-done.1.x2, s32[32,1024]{1,0:T(8,128)S(1)} %collective-permute-done.2.x3, ...), custom_call_target="tpu_custom_call" | custom-call | flops 4000000000 | bytes 1048576 | tf_op jit(solution)/shard_map/pallas_call | solution.py:109
  46.2 6.3 %shard_map.71 = f32[40,128]{1,0:T(8,128)S(1)} custom-call(s32[39]{0:T(128)S(1)} %concatenate.6.pos_ref, bf16[1024,4096]{1,0:T(8,128)(2,1)S(1)} %get-tuple-element.22.s_ref, f32[256,4096]{1,0:T(8,128)S(1)} %get-tuple-element.23.h_ref, f32[2,256,128]{2,1,0:T(8,128)S(1)} %pad_maximum_fusion.f0, f32[2,256,128]{2,1,0:T(8,128)S(1)} %collective-permute-done.7.f1, ...), custom_call_target="tpu_custom_call" | custom-call | flops 4000000000 | bytes 1048576 | tf_op jit(solution)/shard_map/pallas_call | solution.py:158
  52.6 11.9 %all_to_all.25.got_ref = f32[8,40,128]{2,1,0:T(8,128)S(1)} all-to-all(f32[8,40,128]{2,1,0:T(8,128)S(1)} %broadcast_in_dim.4), channel_id=1, replica_groups=mesh['xl'=2,'y'=4,'xh'=2,'zh'=4,'zl'=2,'c'=2] {'zh','zl'}, dimensions={0} | all-to-all | bytes 327680 | tf_op jit(solution)/shard_map/all_to_all | solution.py:34
  64.5 0.6 shard_map.72
  65.0 14.2 %all_to_all.26.got_ref = f32[16,40,128]{2,1,0:T(8,128)S(1)} all-to-all(f32[16,40,128]{2,1,0:T(8,128)S(1)} %shard_map.72), channel_id=1, replica_groups=mesh['xl'=2,'y'=4,'xh'=2,'zh'=4,'zl'=2,'c'=2] {'xh','xl','y'}, dimensions={0} | all-to-all | bytes 655360 | tf_op jit(solution)/shard_map/all_to_all | solution.py:277
  79.3 0.6 shard_map.73
  79.8 6.2 %collective-permute-start.10 = (f32[8,128]{1,0:T(8,128)S(1)}, f32[8,128]{1,0:T(8,128)S(1)}, u32[]{:S(2)}, u32[]{:S(2)}) collective-permute-start(f32[8,128]{1,0:T(8,128)S(1)} %get-tuple-element.29.near_ref.refs_9_.norm_ref), channel_id=1, source_target_pairs={{0,1},{1,0},{2,3},{3,2},{4,5},{5,4},{6,7},{7,6},{8,9},{9,8},{10,11... | collective-permute-start | bytes 12296 | tf_op jit(solution)/shard_map/ppermute | solution.py:30
  86.1 0.8 collective-permute-done.10.far_ref
  86.9 6.0 %shard_map.74 = (f32[4,264,128]{2,1,0:T(8,128)S(1)}, f32[4,264,128]{2,1,0:T(8,128)S(1)}) custom-call(s32[39]{0:T(128)S(1)} %concatenate.6.pos_ref, bf16[1024,4096]{1,0:T(8,128)(2,1)S(1)} %get-tuple-element.22.s_ref, f32[256,4096]{1,0:T(8,128)S(1)} %get-tuple-element.23.h_ref, f32[32,128]{1,0:T(8,128)S(1)} %get-tuple-element.28.v_ref, ...), custom_call_target="tpu_custom_call" | custom-call | flops 4000000000 | bytes 1048576 | tf_op jit(solution)/shard_map/pallas_call | solution.py:366
  92.9 0.4 collective-permute-start.11
  93.3 1.6 %collective-permute-done.11.got_ref = f32[4,264,128]{2,1,0:T(8,128)S(1)} collective-permute-done((f32[4,264,128]{2,1,0:T(8,128)S(1)}, f32[4,264,128]{2,1,0:T(8,128)S(1)}, u32[]{:S(2)}, u32[]{:S(2)}) %collective-permute-start.11) | collective-permute-done | bytes 540704 | tf_op jit(solution)/shard_map/ppermute | solution.py:30
  95.0 1.3 collective-permute-start.12
  96.3 0.3 collective-permute-start.13
  96.6 2.8 %collective-permute-start.14 = (f32[264,128]{1,0:T(8,128)S(1)}, f32[264,128]{1,0:T(8,128)S(1)}, u32[]{:S(2)}, u32[]{:S(2)}) collective-permute-start(f32[264,128]{1,0:T(8,128)S(1)} %get-tuple-element.35), channel_id=1, source_target_pairs={{0,18},{2,16},{16,2},{18,0},{1,19},{3,17},{17,3},{19,1},{4,22},{6,... | collective-permute-start | bytes 405512 | tf_op jit(solution)/shard_map/ppermute | solution.py:401
  99.4 2.1 %collective-permute-done.12.g1 = f32[264,128]{1,0:T(8,128)S(1)} collective-permute-done((f32[264,128]{1,0:T(8,128)S(1)}, f32[264,128]{1,0:T(8,128)S(1)}, u32[]{:S(2)}, u32[]{:S(2)}) %collective-permute-start.12) | collective-permute-done | bytes 135200 | tf_op jit(solution)/shard_map/ppermute | solution.py:30
  101.5 3.8 %collective-permute-done.14.g3 = f32[264,128]{1,0:T(8,128)S(1)} collective-permute-done((f32[264,128]{1,0:T(8,128)S(1)}, f32[264,128]{1,0:T(8,128)S(1)}, u32[]{:S(2)}, u32[]{:S(2)}) %collective-permute-start.14) | collective-permute-done | bytes 135200 | tf_op jit(solution)/shard_map/ppermute | solution.py:401
  105.3 0.1 shard_map.76
  105.5 0.9 collective-permute-start.17
  106.3 1.6 collective-permute-start.16
  107.9 1.8 %collective-permute-start.15 = (f32[264,128]{1,0:T(8,128)S(1)}, f32[264,128]{1,0:T(8,128)S(1)}, u32[]{:S(2)}, u32[]{:S(2)}) collective-permute-start(f32[264,128]{1,0:T(8,128)S(1)} %get-tuple-element.36.refs_0_), channel_id=1, source_target_pairs={{0,16},{16,0},{1,17},{17,1},{2,18},{18,2},{3,19},{19,3},{4,20},{20... | collective-permute-start | bytes 405512 | tf_op jit(solution)/shard_map/ppermute | solution.py:30
  109.7 2.3 %collective-permute-start.18 = (f32[264,128]{1,0:T(8,128)S(1)}, f32[264,128]{1,0:T(8,128)S(1)}, u32[]{:S(2)}, u32[]{:S(2)}) collective-permute-start(f32[264,128]{1,0:T(8,128)S(1)} %get-tuple-element.36.refs_0_), channel_id=1, source_target_pairs={{0,1},{1,0},{2,3},{3,2},{4,5},{5,4},{6,7},{7,6},{8,9},{9,8},{10,11... | collective-permute-start | bytes 405512 | tf_op jit(solution)/shard_map/ppermute | solution.py:30
  112.0 3.5 %collective-permute-start.21 = (f32[264,128]{1,0:T(8,128)S(1)}, f32[264,128]{1,0:T(8,128)S(1)}, u32[]{:S(2)}, u32[]{:S(2)}) collective-permute-start(f32[264,128]{1,0:T(8,128)S(1)} %collective-permute-done.17.refs_3_), channel_id=1, source_target_pairs={{0,1},{1,0},{2,3},{3,2},{4,5},{5,4},{6,7},{7,6},{8,9},{9,8},{10,11... | collective-permute-start | bytes 405512 | tf_op jit(solution)/shard_map/ppermute | solution.py:30
  115.5 1.4 collective-permute-start.19
  116.9 1.0 collective-permute-done.19.refs_5_
  117.9 6.5 %shard_map.77 = f32[4,104,128]{2,1,0:T(8,128)S(1)} custom-call(s32[39]{0:T(128)S(1)} %concatenate.6.pos_ref, bf16[1024,4096]{1,0:T(8,128)(2,1)S(1)} %get-tuple-element.22.s_ref, f32[256,4096]{1,0:T(8,128)S(1)} %get-tuple-element.23.h_ref, f32[2,256,128]{2,1,0:T(8,128)S(1)} %pad_maximum_fusion.f0, f32[2,256,128]{2,1,0:T(8,128)S(1)} %collective-permute-done.7.f1, ...), custom_call_target="tpu_custom_call" | custom-call | flops 4000000000 | bytes 1048576 | tf_op jit(solution)/shard_map/pallas_call | solution.py:207
  124.4 11.2 %all_to_all.27.got_ref = f32[4,104,128]{2,1,0:T(8,128)S(1)} all-to-all(f32[4,104,128]{2,1,0:T(8,128)S(1)} %shard_map.77), channel_id=1, replica_groups=mesh['xl'=2,'y'=4,'xh'=2,'zh'=4,'zl'=2,'c'=2] {'zh'}, dimensions={0} | all-to-all | bytes 425984 | tf_op jit(solution)/shard_map/all_to_all | solution.py:477
  135.6 8.0 %all_to_all.28.got_ref = f32[8,40,128]{2,1,0:T(8,128)S(1)} all-to-all(f32[8,40,128]{2,1,0:T(8,128)S(1)} %shard_map.78), channel_id=1, replica_groups=mesh['xl'=2,'y'=4,'xh'=2,'zh'=4,'zl'=2,'c'=2] {'xl','y'}, dimensions={0} | all-to-all | bytes 327680 | tf_op jit(solution)/shard_map/all_to_all | solution.py:234
  143.6 0.3 shard_map.79
  143.9 13.1 %all_to_all.29.st1_ref = f32[8,8,128]{2,1,0:T(8,128)S(1)} all-to-all(f32[8,8,128]{2,1,0:T(8,128)S(1)} %broadcast_in_dim.5), channel_id=1, replica_groups=mesh['xl'=2,'y'=4,'xh'=2,'zh'=4,'zl'=2,'c'=2] {'xh','zl','c'}, dimensions={0} | all-to-all | bytes 65536 | tf_op jit(solution)/shard_map/all_to_all | solution.py:34
  157.0 0.7 shard_map.80
  (33 shorter events, 0.4 us)
Async XLA Ops:
  0.6 27.6 %copy-start = (bf16[1024,1024]{1,0:T(8,128)(2,1)S(1)}, bf16[1024,1024]{1,0:T(8,128)(2,1)}, u32[]{:S(2)}) copy-start(bf16[1024,1024]{1,0:T(8,128)(2,1)} %param.6) | copy-start | bytes 6291460
  0.8 1.0 copy-start.1
  2.4 11.4 %collective-permute-start.3 = (f32[32,256]{1,0:T(8,128)S(1)}, f32[32,256]{1,0:T(8,128)S(1)}, u32[]{:S(2)}, u32[]{:S(2)}) collective-permute-start(f32[32,256]{1,0:T(8,128)S(1)} %get-tuple-element.25), channel_id=1, source_target_pairs={{0,4},{4,8},{8,12},{12,0},{1,5},{5,9},{9,13},{13,1},{2,6},{6,10},{... | collective-permute-start | bytes 98312 | tf_op jit(solution)/shard_map/ppermute | solution.py:449
  6.3 7.5 %collective-permute-start.4 = (f32[32,256]{1,0:T(8,128)S(1)}, f32[32,256]{1,0:T(8,128)S(1)}, u32[]{:S(2)}, u32[]{:S(2)}) collective-permute-start(f32[32,256]{1,0:T(8,128)S(1)} %get-tuple-element.26), channel_id=1, source_target_pairs={{0,8},{4,12},{8,0},{12,4},{1,9},{5,13},{9,1},{13,5},{2,10},{6,14},... | collective-permute-start | bytes 98312 | tf_op jit(solution)/shard_map/ppermute | solution.py:449
  11.4 3.7 %collective-permute-start.5 = (f32[32,256]{1,0:T(8,128)S(1)}, f32[32,256]{1,0:T(8,128)S(1)}, u32[]{:S(2)}, u32[]{:S(2)}) collective-permute-start(f32[32,256]{1,0:T(8,128)S(1)} %get-tuple-element.27), channel_id=1, source_target_pairs={{0,12},{4,0},{8,4},{12,8},{1,13},{5,1},{9,5},{13,9},{2,14},{6,2},{... | collective-permute-start | bytes 98312 | tf_op jit(solution)/shard_map/ppermute | solution.py:449
  15.2 5.4 %collective-permute-start.6 = (f32[1,256,128]{2,1,0:T(8,128)S(1)}, f32[1,256,128]{2,1,0:T(8,128)S(1)}, u32[]{:S(2)}, u32[]{:S(2)}) collective-permute-start(f32[1,256,128]{2,1,0:T(8,128)S(1)} %shard_map.70), channel_id=1, source_target_pairs={{0,16},{16,0},{1,17},{17,1},{2,18},{18,2},{3,19},{19,3},{4,20},{20... | collective-permute-start | bytes 393224 | tf_op jit(solution)/shard_map/ppermute | solution.py:30
  20.6 12.5 %collective-permute-start.7 = (f32[2,256,128]{2,1,0:T(8,128)S(1)}, f32[2,256,128]{2,1,0:T(8,128)S(1)}, u32[]{:S(2)}, u32[]{:S(2)}) collective-permute-start(f32[2,256,128]{2,1,0:T(8,128)S(1)} %pad_maximum_fusion.f0), channel_id=1, source_target_pairs={{0,2},{2,0},{1,3},{3,1},{4,6},{6,4},{5,7},{7,5},{8,10},{10,8},{9,1... | collective-permute-start | bytes 786440 | tf_op jit(solution)/shard_map/ppermute | solution.py:30
  22.1 13.5 %collective-permute-start.1 = (s32[32,1024]{1,0:T(8,128)}, s32[32,1024]{1,0:T(8,128)S(1)}, u32[]{:S(2)}, u32[]{:S(2)}) collective-permute-start(s32[32,1024]{1,0:T(8,128)} %x0.1), channel_id=1, source_target_pairs={{0,8},{4,12},{8,0},{12,4},{1,9},{5,13},{9,1},{13,5},{2,10},{6,14},... | collective-permute-start | bytes 393224 | tf_op jit(solution)/shard_map/ppermute | solution.py:449
  24.7 15.5 %collective-permute-start = (s32[32,1024]{1,0:T(8,128)}, s32[32,1024]{1,0:T(8,128)S(1)}, u32[]{:S(2)}, u32[]{:S(2)}) collective-permute-start(s32[32,1024]{1,0:T(8,128)} %x0.1), channel_id=1, source_target_pairs={{0,4},{4,8},{8,12},{12,0},{1,5},{5,9},{9,13},{13,1},{2,6},{6,10},{... | collective-permute-start | bytes 393224 | tf_op jit(solution)/shard_map/ppermute | solution.py:449
  27.1 13.1 %collective-permute-start.2 = (s32[32,1024]{1,0:T(8,128)}, s32[32,1024]{1,0:T(8,128)S(1)}, u32[]{:S(2)}, u32[]{:S(2)}) collective-permute-start(s32[32,1024]{1,0:T(8,128)} %x0.1), channel_id=1, source_target_pairs={{0,12},{4,0},{8,4},{12,8},{1,13},{5,1},{9,5},{13,9},{2,14},{6,2},{... | collective-permute-start | bytes 393224 | tf_op jit(solution)/shard_map/ppermute | solution.py:449
  28.3 17.9 %collective-permute-start.8 = (f32[2,256,128]{2,1,0:T(8,128)S(1)}, f32[2,256,128]{2,1,0:T(8,128)S(1)}, u32[]{:S(2)}, u32[]{:S(2)}) collective-permute-start(f32[2,256,128]{2,1,0:T(8,128)S(1)} %pad_maximum_fusion.f0), channel_id=1, source_target_pairs={{0,1},{1,0},{2,3},{3,2},{4,5},{5,4},{6,7},{7,6},{8,9},{9,8},{10,11... | collective-permute-start | bytes 786440 | tf_op jit(solution)/shard_map/ppermute | solution.py:30
  33.1 13.1 %collective-permute-start.9 = (f32[2,256,128]{2,1,0:T(8,128)S(1)}, f32[2,256,128]{2,1,0:T(8,128)S(1)}, u32[]{:S(2)}, u32[]{:S(2)}) collective-permute-start(f32[2,256,128]{2,1,0:T(8,128)S(1)} %collective-permute-done.7.f1), channel_id=1, source_target_pairs={{0,1},{1,0},{2,3},{3,2},{4,5},{5,4},{6,7},{7,6},{8,9},{9,8},{10,11... | collective-permute-start | bytes 786440 | tf_op jit(solution)/shard_map/ppermute | solution.py:30
  40.1 0.9 copy-start.4
  41.1 0.7 copy-start.5
  41.7 4.5 %copy-start.3 = (f32[1024]{0:T(1024)S(1)}, f32[1024]{0:T(1024)}, u32[]{:S(2)}) copy-start(f32[1024]{0:T(1024)} %param.9) | copy-start | bytes 12292
  79.8 7.0 %collective-permute-start.10 = (f32[8,128]{1,0:T(8,128)S(1)}, f32[8,128]{1,0:T(8,128)S(1)}, u32[]{:S(2)}, u32[]{:S(2)}) collective-permute-start(f32[8,128]{1,0:T(8,128)S(1)} %get-tuple-element.29.near_ref.refs_9_.norm_ref), channel_id=1, source_target_pairs={{0,1},{1,0},{2,3},{3,2},{4,5},{5,4},{6,7},{7,6},{8,9},{9,8},{10,11... | collective-permute-start | bytes 12296 | tf_op jit(solution)/shard_map/ppermute | solution.py:30
  92.9 2.0 %collective-permute-start.11 = (f32[4,264,128]{2,1,0:T(8,128)S(1)}, f32[4,264,128]{2,1,0:T(8,128)S(1)}, u32[]{:S(2)}, u32[]{:S(2)}) collective-permute-start(f32[4,264,128]{2,1,0:T(8,128)S(1)} %get-tuple-element.31), channel_id=1, source_target_pairs={{0,1},{1,0},{2,3},{3,2},{4,5},{5,4},{6,7},{7,6},{8,9},{9,8},{10,11... | collective-permute-start | bytes 1622024 | tf_op jit(solution)/shard_map/ppermute | solution.py:30
  95.0 6.6 %collective-permute-start.12 = (f32[264,128]{1,0:T(8,128)S(1)}, f32[264,128]{1,0:T(8,128)S(1)}, u32[]{:S(2)}, u32[]{:S(2)}) collective-permute-start(f32[264,128]{1,0:T(8,128)S(1)} %get-tuple-element.33), channel_id=1, source_target_pairs={{0,16},{16,0},{1,17},{17,1},{2,18},{18,2},{3,19},{19,3},{4,20},{20... | collective-permute-start | bytes 405512 | tf_op jit(solution)/shard_map/ppermute | solution.py:30
  96.3 5.3 %collective-permute-start.13 = (f32[264,128]{1,0:T(8,128)S(1)}, f32[264,128]{1,0:T(8,128)S(1)}, u32[]{:S(2)}, u32[]{:S(2)}) collective-permute-start(f32[264,128]{1,0:T(8,128)S(1)} %get-tuple-element.34), channel_id=1, source_target_pairs={{0,2},{2,0},{1,3},{3,1},{4,6},{6,4},{5,7},{7,5},{8,10},{10,8},{9,1... | collective-permute-start | bytes 405512 | tf_op jit(solution)/shard_map/ppermute | solution.py:30
  96.6 8.8 %collective-permute-start.14 = (f32[264,128]{1,0:T(8,128)S(1)}, f32[264,128]{1,0:T(8,128)S(1)}, u32[]{:S(2)}, u32[]{:S(2)}) collective-permute-start(f32[264,128]{1,0:T(8,128)S(1)} %get-tuple-element.35), channel_id=1, source_target_pairs={{0,18},{2,16},{16,2},{18,0},{1,19},{3,17},{17,3},{19,1},{4,22},{6,... | collective-permute-start | bytes 405512 | tf_op jit(solution)/shard_map/ppermute | solution.py:401
  105.5 6.6 %collective-permute-start.17 = (f32[264,128]{1,0:T(8,128)S(1)}, f32[264,128]{1,0:T(8,128)S(1)}, u32[]{:S(2)}, u32[]{:S(2)}) collective-permute-start(f32[264,128]{1,0:T(8,128)S(1)} %get-tuple-element.36.refs_0_), channel_id=1, source_target_pairs={{0,18},{2,16},{16,2},{18,0},{1,19},{3,17},{17,3},{19,1},{4,22},{6,... | collective-permute-start | bytes 405512 | tf_op jit(solution)/shard_map/ppermute | solution.py:401
  106.3 9.2 %collective-permute-start.16 = (f32[264,128]{1,0:T(8,128)S(1)}, f32[264,128]{1,0:T(8,128)S(1)}, u32[]{:S(2)}, u32[]{:S(2)}) collective-permute-start(f32[264,128]{1,0:T(8,128)S(1)} %get-tuple-element.36.refs_0_), channel_id=1, source_target_pairs={{0,2},{2,0},{1,3},{3,1},{4,6},{6,4},{5,7},{7,5},{8,10},{10,8},{9,1... | collective-permute-start | bytes 405512 | tf_op jit(solution)/shard_map/ppermute | solution.py:30
  107.9 7.6 %collective-permute-start.15 = (f32[264,128]{1,0:T(8,128)S(1)}, f32[264,128]{1,0:T(8,128)S(1)}, u32[]{:S(2)}, u32[]{:S(2)}) collective-permute-start(f32[264,128]{1,0:T(8,128)S(1)} %get-tuple-element.36.refs_0_), channel_id=1, source_target_pairs={{0,16},{16,0},{1,17},{17,1},{2,18},{18,2},{3,19},{19,3},{4,20},{20... | collective-permute-start | bytes 405512 | tf_op jit(solution)/shard_map/ppermute | solution.py:30
  109.7 7.2 %collective-permute-start.18 = (f32[264,128]{1,0:T(8,128)S(1)}, f32[264,128]{1,0:T(8,128)S(1)}, u32[]{:S(2)}, u32[]{:S(2)}) collective-permute-start(f32[264,128]{1,0:T(8,128)S(1)} %get-tuple-element.36.refs_0_), channel_id=1, source_target_pairs={{0,1},{1,0},{2,3},{3,2},{4,5},{5,4},{6,7},{7,6},{8,9},{9,8},{10,11... | collective-permute-start | bytes 405512 | tf_op jit(solution)/shard_map/ppermute | solution.py:30
  112.0 4.8 %collective-permute-start.21 = (f32[264,128]{1,0:T(8,128)S(1)}, f32[264,128]{1,0:T(8,128)S(1)}, u32[]{:S(2)}, u32[]{:S(2)}) collective-permute-start(f32[264,128]{1,0:T(8,128)S(1)} %collective-permute-done.17.refs_3_), channel_id=1, source_target_pairs={{0,1},{1,0},{2,3},{3,2},{4,5},{5,4},{6,7},{7,6},{8,9},{9,8},{10,11... | collective-permute-start | bytes 405512 | tf_op jit(solution)/shard_map/ppermute | solution.py:30
  115.5 1.4 collective-permute-start.20
  115.5 2.3 %collective-permute-start.19 = (f32[264,128]{1,0:T(8,128)S(1)}, f32[264,128]{1,0:T(8,128)S(1)}, u32[]{:S(2)}, u32[]{:S(2)}) collective-permute-start(f32[264,128]{1,0:T(8,128)S(1)} %collective-permute-done.15.refs_1_), channel_id=1, source_target_pairs={{0,1},{1,0},{2,3},{3,2},{4,5},{5,4},{6,7},{7,6},{8,9},{9,8},{10,11... | collective-permute-start | bytes 405512 | tf_op jit(solution)/shard_map/ppermute | solution.py:30
  117.9 39.1 %copy-start.2 = (f32[32,1024]{1,0:T(8,128)S(1)}, f32[32,1024]{1,0:T(8,128)}, u32[]{:S(2)}) copy-start(f32[32,1024]{1,0:T(8,128)} %f_ref.3) | copy-start | bytes 393220

commit v11 on v10

--- a/solution.py
+++ b/solution.py
@@ -12,7 +12,6 @@
 GRP = ("xl", "y")
 SMP = ("xh", "zh", "zl", "c")
 QUAD = ("xh", "zl")
-SETS = ("xh", "zl", "c")
 SWAP = [(0, 1), (1, 0)]
 LAM = 0.01
 ROWS = 32
@@ -169,7 +168,7 @@
 
 
 def second_kernel(samples, pos_ref, s_ref, h_ref, f0, f1, f2, f3, fb_ref, *refs):
-    *g, mine_ref, norm_ref, out_ref, lhs = refs
+    g, (mine_ref, norm_ref, *outs, lhs) = refs[:NB], refs[NB:]
     units = h_ref.shape[0]
     norm0 = norm_ref[0:1, :]
     spread = g[0][units + units // 128 : units + units // 128 + 1, :]
@@ -185,20 +184,20 @@
     fb = my_rows(pos_ref, fb_ref, units)
     rb = fb - a * (g[0][units : units + units // 128, :] + LAM * fb)
     n = h_ref.shape[1] // 128
-    p_ref = out_ref.at[0]
+    p_ref = outs[0]
     p_ref[n : n + EXTRA, :] = jnp.zeros((EXTRA, 128), F32)
     p_ref[n : n + 1, :] = total(rr) + total(rb * rb)
     p_ref[n + 1 : n + 2, :] = total(rf) + total(rb * fb)
     p_ref[n + 2 : n + 2 + units // 128, :] = g[0][units : units + units // 128, :]
     p_ref[n + 2 + units // 128 : n + 3 + units // 128, :] = spread
     project(s_ref, h_ref, lhs, rows_to_column(rb), p_ref)
-    for k in range(1, out_ref.shape[0]):
-        out_ref[k, : n + EXTRA, :] = out_ref[0, : n + EXTRA, :]
-    for k in range(out_ref.shape[0]):
-        to = (pos_ref[32] + 4 - k) % 4
+    for k, out in enumerate(outs):
+        if k:
+            out[: n + EXTRA, :] = p_ref[: n + EXTRA, :]
+        place = -k % len(outs)
         for h in range(units // 128):
             at = n + EXTRA + h * ROWS
-            out_ref[to, at : at + ROWS, :] = mine_ref[k * ROWS : (k + 1) * ROWS, h * 128 : (h + 1) * 128]
+            out[at : at + ROWS, :] = mine_ref[place * ROWS : (place + 1) * ROWS, h * 128 : (h + 1) * 128]
 
 
 def second_pass(samples, pos, spins, hidden, f, fb, g, mine, norm):
@@ -207,10 +206,10 @@
     return call(
         functools.partial(second_kernel, samples),
         [SMEM] + [VMEM] * (9 + NB),
-        [jax.ShapeDtypeStruct((parts, n // 128 + EXTRA + units // 128 * ROWS, 128), F32)],
+        [jax.ShapeDtypeStruct((n // 128 + EXTRA + units // 128 * ROWS, 128), F32)] * parts,
         [pltpu.VMEM((2 * units, NB * 128), BF16)],
         flops=4 * 10**9,
-    )(pos, resident(spins), resident(hidden), *f, fb, *g, mine, norm)[0]
+    )(pos, resident(spins), resident(hidden), *f, fb, *g, mine, norm)
 
 
 def put_stats(v, st_ref):
@@ -220,7 +219,9 @@
     st_ref[2:, :] = jnp.zeros((st_ref.shape[0] - 2, 128), F32)
 
 
-def over_chain_kernel(got_ref, all_ref):
+def over_chain_kernel(pos_ref, x0, x1, x2, x3, all_ref, got_ref):
+    for d, x in enumerate((x0, x1, x2, x3)):
+        got_ref[(pos_ref[32] + 4 - d) % 4] = x[...]
     rows = all_ref.shape[1]
     x = got_ref[0, :rows, :]
     for k in range(1, got_ref.shape[0]):
@@ -229,9 +230,14 @@
         all_ref[k] = x
 
 
-def over_groups(got, rows):
-    (x,) = call(over_chain_kernel, [VMEM], [jax.ShapeDtypeStruct((lax.axis_size(GRP), rows, 128), F32)])(got)
-    return lax.all_to_all(x, GRP, 0, 0, tiled=True)
+def over_groups(pos, parts, rows):
+    shape = lambda *s: jax.ShapeDtypeStruct(s, F32)
+    x, got = call(
+        over_chain_kernel,
+        [SMEM] + [VMEM] * 4,
+        [shape(lax.axis_size(GRP), rows, 128), shape(len(parts), *parts[0].shape)],
+    )(pos, *parts)
+    return lax.all_to_all(x, GRP, 0, 0, tiled=True), got
 
 
 def summed(got_ref):
@@ -292,21 +298,25 @@
     )
 
 
-def of_sets(st):
-    return to_all(st, SETS, lax.axis_size(SETS))
-
-
-def joined(st_ref, count):
-    sets = st_ref.shape[0]
-    mean = st_ref[0, 0:1, :]
-    for k in range(1, sets):
-        mean = mean + st_ref[k, 0:1, :]
-    mean = mean * (1.0 / sets)
-    spread = jnp.zeros_like(mean)
-    for k in range(sets):
-        off = st_ref[k, 0:1, :] - mean
-        spread = spread + (st_ref[k, 1:2, :] + count * (off * off))
-    return mean, spread
+def pair_kernel(count, st_ref, got_ref, out_ref):
+    delta = got_ref[0:1, :] - st_ref[0:1, :]
+    out_ref[...] = st_ref[...] + got_ref[...]
+    out_ref[0:1, :] = 0.5 * (st_ref[0:1, :] + got_ref[0:1, :])
+    out_ref[1:2, :] = st_ref[1:2, :] + got_ref[1:2, :] + (0.5 * count) * delta * delta
+
+
+def of_chips(st, count):
+    (st,) = call(
+        functools.partial(pair_kernel, count), [VMEM] * 2, [jax.ShapeDtypeStruct(st.shape, F32)]
+    )(st, swap(st, "c"))
+    return to_quad([st] * 4)
+
+
+def joined_spread(refs, count):
+    a, b, c, d = (ref[0:1, :] for ref in refs)
+    mean = 0.25 * ((a + b) + (c + d))
+    a, b, c, d = (ref[1:2, :] + count * (ref[0:1, :] - mean) ** 2 for ref in refs)
+    return (a + b) + (c + d)
 
 
 def columns_kernel(pos_ref, f_ref, o0, o1, o2, o3):
@@ -402,16 +412,16 @@
     ]
 
 
-def update_kernel(samples, f_ref, fb_ref, got_ref, norm_ref, st1_ref, next_ref, w_ref, b_ref):
+def update_kernel(samples, f_ref, fb_ref, got_ref, norm_ref, next_ref, *refs):
+    *st_refs, w_ref, b_ref = refs
     parts = got_ref.shape[0]
     per = f_ref.shape[1] // 128 // parts
     n = got_ref.shape[1] - EXTRA - per * ROWS
-    count = samples // st1_ref.shape[0]
     norm0, norm1 = norm_ref[0:1, 0:1], next_ref[0:1, 0:1]
     cross = next_ref[1:2, 0:1]
     beta = norm1 / norm0
     step0 = step_of(norm0, got_ref[0, n + 2 + per : n + 3 + per, 0:1], samples, norm0)
-    step1 = step_of(norm1, joined(st1_ref, count)[1][:, 0:1], samples, norm1 + 2.0 * beta * cross + beta * beta * norm0)
+    step1 = step_of(norm1, joined_spread(st_refs, samples // 4)[:, 0:1], samples, norm1 + 2.0 * beta * cross + beta * beta * norm0)
 
     def update(f, g):
         r = f - step0 * (g + LAM * f)
@@ -428,8 +438,8 @@
 def update_pass(samples, f, fb, got, norm, st1, norms):
     shape = lambda s: jax.ShapeDtypeStruct(s, F32)
     return call(
-        functools.partial(update_kernel, samples), [VMEM] * 6, [shape(f.shape), shape(fb.shape)]
-    )(f, fb, got, norm, st1, norms)
+        functools.partial(update_kernel, samples), [VMEM] * 9, [shape(f.shape), shape(fb.shape)]
+    )(f, fb, got, norm, norms, *st1)
 
 
 def body(spins_packed, weight, hidden_bias, force_w, force_b):
@@ -473,10 +483,10 @@
     g = to_quad([g] * 4)
     g += [swap(x, "c") for x in g]
 
-    partial = second_pass(samples, pos, spins, hidden, f, fb, g, mine, norm)
-    got = lax.all_to_all(partial, "zh", 0, 0, tiled=True)
-    st, norms = second_sum(over_groups(got, rows), values, norm)
-    st1 = of_sets(st)
+    partials = second_pass(samples, pos, spins, hidden, f, fb, g, mine, norm)
+    sums, got = over_groups(pos, [turn(x, d) if d else x for d, x in enumerate(partials)], rows)
+    st, norms = second_sum(sums, values, norm)
+    st1 = of_chips(st, values.size)
     out_w, out_b = update_pass(samples, force_w, fb, got, norm, st1, norms)
     return out_w, out_b.reshape(-1)
 

time: 158 us -> 156 us (0.987)
  blocking collectives: 58.4 us -> 34.2 us
  waiting for transfers between devices: 17.8 us -> 29 us
  starting transfers between devices: 51.6 us -> 61.7 us
    all_to_all x2 -> x1, blocking collectives: 25 us -> 11.9 us  [to_all(): lax.all_to_all(jnp.broadcast_to(x[None], (size, *x.shape)), axes, 0, 0, t...]
    all_to_all x2 -> x1, blocking collectives: 19.2 us -> 8.09 us  [over_groups(): return (lax.all_to_all(x, GRP, 0, 0, tiled=True), got)]
    ppermute x6 -> x9, waiting for transfers between devices: 5.84 us -> 13.2 us  [body(): lax.ppermute(x, 'zh', [(i, (i + d) % parts) for i in range(parts)])]
    ppermute x14 -> x17, starting transfers between devices: 30.4 us -> 35.1 us  [swap(): return lax.ppermute(x, axis, SWAP)]
    ppermute x6 -> x9, starting transfers between devices: 17.5 us -> 21.5 us  [body(): lax.ppermute(x, 'zh', [(i, (i + d) % parts) for i in range(parts)])]
    ppermute x14 -> x17, waiting for transfers between devices: 8.12 us -> 11.3 us  [swap(): return lax.ppermute(x, axis, SWAP)]
    ppermute x2 -> x3, starting transfers between devices: 3.73 us -> 5 us  [to_quad(): lax.ppermute(blocks[3], QUAD, [(i, i ^ 3) for i in range(4)])]
    ppermute x2 -> x3, waiting for transfers between devices: 3.8 us -> 4.51 us  [to_quad(): lax.ppermute(blocks[3], QUAD, [(i, i ^ 3) for i in range(4)])]
  transfers between devices with their start and end apart: 22 -> 29, of which waited for: 8 -> 14; matrix products, arithmetic and copies ran while one was open for 0% -> 0% of each run, Pallas kernels for 3% -> 3%
where the time goes in v11:
time: 156 us; the launch traced here: 155 us
  starting transfers between devices  61.7 us (40%)
  blocking collectives  34.2 us (22%)
  waiting for transfers between devices  29 us (19%)
  Pallas kernels  26.8 us (17%)
  local copies, waits for them, and re-layouts  2.8 us (2%)
    ppermute x17, starting transfers between devices, swap(): return lax.ppermute(x, axis, SWAP)  35.1 us
    ppermute x9, starting transfers between devices, body(): lax.ppermute(x, 'zh', [(i, (i + d) % parts) for i in range(parts)])  21.5 us
    all_to_all x1, blocking collectives, first_sum(): got = lax.all_to_all(x, plane, 0, 0, tiled=True)  14.2 us
    ppermute x9, waiting for transfers between devices, body(): lax.ppermute(x, 'zh', [(i, (i + d) % parts) for i in range(parts)])  13.2 us
    all_to_all x1, blocking collectives, to_all(): lax.all_to_all(jnp.broadcast_to(x[None], (size, *x.shape)), axes, 0, 0, t...  11.9 us
    ppermute x17, waiting for transfers between devices, swap(): return lax.ppermute(x, axis, SWAP)  11.3 us
    all_to_all x1, blocking collectives, over_groups(): return (lax.all_to_all(x, GRP, 0, 0, tiled=True), got)  8.09 us
    pallas_call x1, Pallas kernels, second_pass(): call(functools.partial(second_kernel, samples), [SMEM] + [VMEM] * (9 + NB...  6.51 us
  transfers between devices with their start and end apart: 29, of which 14 were waited for; matrix products, arithmetic and copies ran while one was open for 0% of the time, Pallas kernels for 3%

profile of v11, /device:TPU:1, one launch (start us, length us, event | category | flops | bytes accessed | tf_op | source)
XLA Modules:
  0.0 155.4 jit_solution(5625881965385958738)
XLA Ops:
  0.8 1.0 copy-done.1
  2.4 3.9 %collective-permute-start.3 = (f32[32,256]{1,0:T(8,128)S(1)}, f32[32,256]{1,0:T(8,128)S(1)}, u32[]{:S(2)}, u32[]{:S(2)}) collective-permute-start(f32[32,256]{1,0:T(8,128)S(1)} %get-tuple-element.31), channel_id=1, source_target_pairs={{0,4},{4,8},{8,12},{12,0},{1,5},{5,9},{9,13},{13,1},{2,6},{6,10},{... | collective-permute-start | bytes 98312 | tf_op jit(solution)/shard_map/ppermute | solution.py:459
  6.3 5.1 %collective-permute-start.4 = (f32[32,256]{1,0:T(8,128)S(1)}, f32[32,256]{1,0:T(8,128)S(1)}, u32[]{:S(2)}, u32[]{:S(2)}) collective-permute-start(f32[32,256]{1,0:T(8,128)S(1)} %get-tuple-element.32), channel_id=1, source_target_pairs={{0,8},{4,12},{8,0},{12,4},{1,9},{5,13},{9,1},{13,5},{2,10},{6,14},... | collective-permute-start | bytes 98312 | tf_op jit(solution)/shard_map/ppermute | solution.py:459
  11.4 2.4 %collective-permute-start.5 = (f32[32,256]{1,0:T(8,128)S(1)}, f32[32,256]{1,0:T(8,128)S(1)}, u32[]{:S(2)}, u32[]{:S(2)}) collective-permute-start(f32[32,256]{1,0:T(8,128)S(1)} %get-tuple-element.33), channel_id=1, source_target_pairs={{0,12},{4,0},{8,4},{12,8},{1,13},{5,1},{9,5},{13,9},{2,14},{6,2},{... | collective-permute-start | bytes 98312 | tf_op jit(solution)/shard_map/ppermute | solution.py:459
  13.8 1.3 collective-permute-done.5.f3
  15.2 2.8 %collective-permute-start.6 = (f32[1,256,128]{2,1,0:T(8,128)S(1)}, f32[1,256,128]{2,1,0:T(8,128)S(1)}, u32[]{:S(2)}, u32[]{:S(2)}) collective-permute-start(f32[1,256,128]{2,1,0:T(8,128)S(1)} %shard_map.70), channel_id=1, source_target_pairs={{0,16},{16,0},{1,17},{17,1},{2,18},{18,2},{3,19},{19,3},{4,20},{20... | collective-permute-start | bytes 393224 | tf_op jit(solution)/shard_map/ppermute | solution.py:29
  18.0 2.6 %collective-permute-done.6 = f32[1,256,128]{2,1,0:T(8,128)S(1)} collective-permute-done((f32[1,256,128]{2,1,0:T(8,128)S(1)}, f32[1,256,128]{2,1,0:T(8,128)S(1)}, u32[]{:S(2)}, u32[]{:S(2)}) %collective-permute-start.6) | collective-permute-done | bytes 131104 | tf_op jit(solution)/shard_map/ppermute | solution.py:29
  20.6 1.5 collective-permute-start.7
  22.1 2.6 %collective-permute-start.1 = (s32[32,1024]{1,0:T(8,128)}, s32[32,1024]{1,0:T(8,128)S(1)}, u32[]{:S(2)}, u32[]{:S(2)}) collective-permute-start(s32[32,1024]{1,0:T(8,128)} %x0.1), channel_id=1, source_target_pairs={{0,8},{4,12},{8,0},{12,4},{1,9},{5,13},{9,1},{13,5},{2,10},{6,14},... | collective-permute-start | bytes 393224 | tf_op jit(solution)/shard_map/ppermute | solution.py:459
  24.7 2.4 %collective-permute-start = (s32[32,1024]{1,0:T(8,128)}, s32[32,1024]{1,0:T(8,128)S(1)}, u32[]{:S(2)}, u32[]{:S(2)}) collective-permute-start(s32[32,1024]{1,0:T(8,128)} %x0.1), channel_id=1, source_target_pairs={{0,4},{4,8},{8,12},{12,0},{1,5},{5,9},{9,13},{13,1},{2,6},{6,10},{... | collective-permute-start | bytes 393224 | tf_op jit(solution)/shard_map/ppermute | solution.py:459
  27.1 1.2 collective-permute-start.2
  28.3 4.8 %collective-permute-start.8 = (f32[2,256,128]{2,1,0:T(8,128)S(1)}, f32[2,256,128]{2,1,0:T(8,128)S(1)}, u32[]{:S(2)}, u32[]{:S(2)}) collective-permute-start(f32[2,256,128]{2,1,0:T(8,128)S(1)} %pad_maximum_fusion.f0), channel_id=1, source_target_pairs={{0,1},{1,0},{2,3},{3,2},{4,5},{5,4},{6,7},{7,6},{8,9},{9,8},{10,11... | collective-permute-start | bytes 786440 | tf_op jit(solution)/shard_map/ppermute | solution.py:29
  33.1 2.5 %collective-permute-start.9 = (f32[2,256,128]{2,1,0:T(8,128)S(1)}, f32[2,256,128]{2,1,0:T(8,128)S(1)}, u32[]{:S(2)}, u32[]{:S(2)}) collective-permute-start(f32[2,256,128]{2,1,0:T(8,128)S(1)} %collective-permute-done.7.f1), channel_id=1, source_target_pairs={{0,1},{1,0},{2,3},{3,2},{4,5},{5,4},{6,7},{7,6},{8,9},{9,8},{10,11... | collective-permute-start | bytes 786440 | tf_op jit(solution)/shard_map/ppermute | solution.py:29
  35.6 4.5 %collective-permute-done.x1 = s32[32,1024]{1,0:T(8,128)S(1)} collective-permute-done((s32[32,1024]{1,0:T(8,128)}, s32[32,1024]{1,0:T(8,128)S(1)}, u32[]{:S(2)}, u32[]{:S(2)}) %collective-permute-start) | collective-permute-done | bytes 131104 | tf_op jit(solution)/shard_map/ppermute | solution.py:459
  40.2 0.9 copy-done.4
  41.7 4.4 %shard_map.68 = (bf16[1024,4096]{1,0:T(8,128)(2,1)S(1)}, f32[256,4096]{1,0:T(8,128)S(1)}) custom-call(s32[39]{0:T(128)S(1)} %concatenate.6.pos_ref, s32[32,1024]{1,0:T(8,128)S(1)} %copy-done.4, s32[32,1024]{1,0:T(8,128)S(1)} %collective-permute-done.x1, s32[32,1024]{1,0:T(8,128)S(1)} %collective-permute-done.1.x2, s32[32,1024]{1,0:T(8,128)S(1)} %collective-permute-done.2.x3, ...), custom_call_target="tpu_custom_call" | custom-call | flops 4000000000 | bytes 1048576 | tf_op jit(solution)/shard_map/pallas_call | solution.py:108
  46.2 6.3 %shard_map.71 = f32[40,128]{1,0:T(8,128)S(1)} custom-call(s32[39]{0:T(128)S(1)} %concatenate.6.pos_ref, bf16[1024,4096]{1,0:T(8,128)(2,1)S(1)} %get-tuple-element.28.s_ref, f32[256,4096]{1,0:T(8,128)S(1)} %get-tuple-element.29.h_ref, f32[2,256,128]{2,1,0:T(8,128)S(1)} %pad_maximum_fusion.f0, f32[2,256,128]{2,1,0:T(8,128)S(1)} %collective-permute-done.7.f1, ...), custom_call_target="tpu_custom_call" | custom-call | flops 4000000000 | bytes 1048576 | tf_op jit(solution)/shard_map/pallas_call | solution.py:157
  52.6 11.9 %all_to_all.15.got_ref = f32[8,40,128]{2,1,0:T(8,128)S(1)} all-to-all(f32[8,40,128]{2,1,0:T(8,128)S(1)} %broadcast_in_dim.2), channel_id=1, replica_groups=mesh['xl'=2,'y'=4,'xh'=2,'zh'=4,'zl'=2,'c'=2] {'zh','zl'}, dimensions={0} | all-to-all | bytes 327680 | tf_op jit(solution)/shard_map/all_to_all | solution.py:33
  65.0 14.2 %all_to_all.16.got_ref = f32[16,40,128]{2,1,0:T(8,128)S(1)} all-to-all(f32[16,40,128]{2,1,0:T(8,128)S(1)} %shard_map.72), channel_id=1, replica_groups=mesh['xl'=2,'y'=4,'xh'=2,'zh'=4,'zl'=2,'c'=2] {'xh','xl','y'}, dimensions={0} | all-to-all | bytes 655360 | tf_op jit(solution)/shard_map/all_to_all | solution.py:283
  79.8 6.2 %collective-permute-start.10 = (f32[8,128]{1,0:T(8,128)S(1)}, f32[8,128]{1,0:T(8,128)S(1)}, u32[]{:S(2)}, u32[]{:S(2)}) collective-permute-start(f32[8,128]{1,0:T(8,128)S(1)} %get-tuple-element.35.near_ref.refs_9_.norm_ref), channel_id=1, source_target_pairs={{0,1},{1,0},{2,3},{3,2},{4,5},{5,4},{6,7},{7,6},{8,9},{9,8},{10,11... | collective-permute-start | bytes 12296 | tf_op jit(solution)/shard_map/ppermute | solution.py:29
  86.1 0.8 collective-permute-done.10.far_ref
  86.9 6.0 %shard_map.74 = (f32[4,264,128]{2,1,0:T(8,128)S(1)}, f32[4,264,128]{2,1,0:T(8,128)S(1)}) custom-call(s32[39]{0:T(128)S(1)} %concatenate.6.pos_ref, bf16[1024,4096]{1,0:T(8,128)(2,1)S(1)} %get-tuple-element.28.s_ref, f32[256,4096]{1,0:T(8,128)S(1)} %get-tuple-element.29.h_ref, f32[32,128]{1,0:T(8,128)S(1)} %get-tuple-element.34.v_ref, ...), custom_call_target="tpu_custom_call" | custom-call | flops 4000000000 | bytes 1048576 | tf_op jit(solution)/shard_map/pallas_call | solution.py:376
  93.3 1.6 %collective-permute-done.11.got_ref = f32[4,264,128]{2,1,0:T(8,128)S(1)} collective-permute-done((f32[4,264,128]{2,1,0:T(8,128)S(1)}, f32[4,264,128]{2,1,0:T(8,128)S(1)}, u32[]{:S(2)}, u32[]{:S(2)}) %collective-permute-start.11) | collective-permute-done | bytes 540704 | tf_op jit(solution)/shard_map/ppermute | solution.py:29
  95.0 1.3 collective-permute-start.12
  96.6 2.8 %collective-permute-start.14 = (f32[264,128]{1,0:T(8,128)S(1)}, f32[264,128]{1,0:T(8,128)S(1)}, u32[]{:S(2)}, u32[]{:S(2)}) collective-permute-start(f32[264,128]{1,0:T(8,128)S(1)} %get-tuple-element.41), channel_id=1, source_target_pairs={{0,18},{2,16},{16,2},{18,0},{1,19},{3,17},{17,3},{19,1},{4,22},{6,... | collective-permute-start | bytes 405512 | tf_op jit(solution)/shard_map/ppermute | solution.py:411
  99.4 2.1 %collective-permute-done.12.g1 = f32[264,128]{1,0:T(8,128)S(1)} collective-permute-done((f32[264,128]{1,0:T(8,128)S(1)}, f32[264,128]{1,0:T(8,128)S(1)}, u32[]{:S(2)}, u32[]{:S(2)}) %collective-permute-start.12) | collective-permute-done | bytes 135200 | tf_op jit(solution)/shard_map/ppermute | solution.py:29
  101.5 3.8 %collective-permute-done.14.g3 = f32[264,128]{1,0:T(8,128)S(1)} collective-permute-done((f32[264,128]{1,0:T(8,128)S(1)}, f32[264,128]{1,0:T(8,128)S(1)}, u32[]{:S(2)}, u32[]{:S(2)}) %collective-permute-start.14) | collective-permute-done | bytes 135200 | tf_op jit(solution)/shard_map/ppermute | solution.py:411
  105.4 0.9 collective-permute-start.17
  106.3 1.6 %collective-permute-start.16 = (f32[264,128]{1,0:T(8,128)S(1)}, f32[264,128]{1,0:T(8,128)S(1)}, u32[]{:S(2)}, u32[]{:S(2)}) collective-permute-start(f32[264,128]{1,0:T(8,128)S(1)} %get-tuple-element.42.refs_0_), channel_id=1, source_target_pairs={{0,2},{2,0},{1,3},{3,1},{4,6},{6,4},{5,7},{7,5},{8,10},{10,8},{9,1... | collective-permute-start | bytes 405512 | tf_op jit(solution)/shard_map/ppermute | solution.py:29
  107.9 1.8 %collective-permute-start.15 = (f32[264,128]{1,0:T(8,128)S(1)}, f32[264,128]{1,0:T(8,128)S(1)}, u32[]{:S(2)}, u32[]{:S(2)}) collective-permute-start(f32[264,128]{1,0:T(8,128)S(1)} %get-tuple-element.42.refs_0_), channel_id=1, source_target_pairs={{0,16},{16,0},{1,17},{17,1},{2,18},{18,2},{3,19},{19,3},{4,20},{20... | collective-permute-start | bytes 405512 | tf_op jit(solution)/shard_map/ppermute | solution.py:29
  109.7 2.3 %collective-permute-start.18 = (f32[264,128]{1,0:T(8,128)S(1)}, f32[264,128]{1,0:T(8,128)S(1)}, u32[]{:S(2)}, u32[]{:S(2)}) collective-permute-start(f32[264,128]{1,0:T(8,128)S(1)} %get-tuple-element.42.refs_0_), channel_id=1, source_target_pairs={{0,1},{1,0},{2,3},{3,2},{4,5},{5,4},{6,7},{7,6},{8,9},{9,8},{10,11... | collective-permute-start | bytes 405512 | tf_op jit(solution)/shard_map/ppermute | solution.py:29
  112.0 3.5 %collective-permute-start.21 = (f32[264,128]{1,0:T(8,128)S(1)}, f32[264,128]{1,0:T(8,128)S(1)}, u32[]{:S(2)}, u32[]{:S(2)}) collective-permute-start(f32[264,128]{1,0:T(8,128)S(1)} %collective-permute-done.17.refs_3_), channel_id=1, source_target_pairs={{0,1},{1,0},{2,3},{3,2},{4,5},{5,4},{6,7},{7,6},{8,9},{9,8},{10,11... | collective-permute-start | bytes 405512 | tf_op jit(solution)/shard_map/ppermute | solution.py:29
  115.5 1.4 collective-permute-start.19
  116.9 1.0 collective-permute-done.19.refs_5_
  117.8 6.5 %shard_map.77 = (f32[104,128]{1,0:T(8,128)S(1)}, f32[104,128]{1,0:T(8,128)S(1)}, f32[104,128]{1,0:T(8,128)S(1)}, f32[104,128]{1,0:T(8,128)S(1)}) custom-call(s32[39]{0:T(128)S(1)} %concatenate.6.pos_ref, bf16[1024,4096]{1,0:T(8,128)(2,1)S(1)} %get-tuple-element.28.s_ref, f32[256,4096]{1,0:T(8,128)S(1)} %get-tuple-element.29.h_ref, ...), custom_call_target="tpu_custom_call" | custom-call | flops 4000000000 | bytes 1048576 | tf_op jit(solution)/shard_map/pallas_call | solution.py:206
  124.5 2.3 %collective-permute-start.23 = (f32[104,128]{1,0:T(8,128)S(1)}, f32[104,128]{1,0:T(8,128)S(1)}, u32[]{:S(2)}, u32[]{:S(2)}) collective-permute-start(f32[104,128]{1,0:T(8,128)S(1)} %get-tuple-element.46), channel_id=1, source_target_pairs={{0,8},{4,12},{8,0},{12,4},{1,9},{5,13},{9,1},{13,5},{2,10},{6,14},... | collective-permute-start | bytes 159752 | tf_op jit(solution)/shard_map/ppermute | solution.py:459
  126.8 1.5 collective-permute-start.24
  128.4 1.2 collective-permute-done.22.x1
  129.6 2.0 %collective-permute-done.23.x2 = f32[104,128]{1,0:T(8,128)S(1)} collective-permute-done((f32[104,128]{1,0:T(8,128)S(1)}, f32[104,128]{1,0:T(8,128)S(1)}, u32[]{:S(2)}, u32[]{:S(2)}) %collective-permute-start.23) | collective-permute-done | bytes 53280 | tf_op jit(solution)/shard_map/ppermute | solution.py:459
  131.6 4.1 %collective-permute-done.24.x3 = f32[104,128]{1,0:T(8,128)S(1)} collective-permute-done((f32[104,128]{1,0:T(8,128)S(1)}, f32[104,128]{1,0:T(8,128)S(1)}, u32[]{:S(2)}, u32[]{:S(2)}) %collective-permute-start.24) | collective-permute-done | bytes 53280 | tf_op jit(solution)/shard_map/ppermute | solution.py:459
  136.3 8.1 %all_to_all.17.got_ref = f32[8,40,128]{2,1,0:T(8,128)S(1)} all-to-all(f32[8,40,128]{2,1,0:T(8,128)S(1)} %get-tuple-element.49), channel_id=1, replica_groups=mesh['xl'=2,'y'=4,'xh'=2,'zh'=4,'zl'=2,'c'=2] {'xl','y'}, dimensions={0} | all-to-all | bytes 327680 | tf_op jit(solution)/shard_map/all_to_all | solution.py:240
  144.7 1.9 %collective-permute-start.25 = (f32[8,128]{1,0:T(8,128)S(1)}, f32[8,128]{1,0:T(8,128)S(1)}, u32[]{:S(2)}, u32[]{:S(2)}) collective-permute-start(f32[8,128]{1,0:T(8,128)S(1)} %get-tuple-element.51.st_ref), channel_id=1, source_target_pairs={{0,1},{1,0},{2,3},{3,2},{4,5},{5,4},{6,7},{7,6},{8,9},{9,8},{10,11... | collective-permute-start | bytes 12296 | tf_op jit(solution)/shard_map/ppermute | solution.py:29
  146.6 0.8 collective-permute-done.25.got_ref
  147.4 1.3 collective-permute-start.28
  148.7 2.0 %collective-permute-start.27 = (f32[8,128]{1,0:T(8,128)S(1)}, f32[8,128]{1,0:T(8,128)S(1)}, u32[]{:S(2)}, u32[]{:S(2)}) collective-permute-start(f32[8,128]{1,0:T(8,128)S(1)} %shard_map.80.refs_0_), channel_id=1, source_target_pairs={{0,2},{2,0},{1,3},{3,1},{4,6},{6,4},{5,7},{7,5},{8,10},{10,8},{9,1... | collective-permute-start | bytes 12296 | tf_op jit(solution)/shard_map/ppermute | solution.py:29
  150.7 0.9 collective-permute-start.26
  152.3 2.4 %collective-permute-done.26.refs_1_ = f32[8,128]{1,0:T(8,128)S(1)} collective-permute-done((f32[8,128]{1,0:T(8,128)S(1)}, f32[8,128]{1,0:T(8,128)S(1)}, u32[]{:S(2)}, u32[]{:S(2)}) %collective-permute-start.26) | collective-permute-done | bytes 4128 | tf_op jit(solution)/shard_map/ppermute | solution.py:29
  154.7 0.7 shard_map.81
  (45 shorter events, 5.4 us)
Async XLA Ops:
  0.6 27.6 %copy-start = (bf16[1024,1024]{1,0:T(8,128)(2,1)S(1)}, bf16[1024,1024]{1,0:T(8,128)(2,1)}, u32[]{:S(2)}) copy-start(bf16[1024,1024]{1,0:T(8,128)(2,1)} %param.6) | copy-start | bytes 6291460
  0.8 1.0 copy-start.1
  2.4 11.4 %collective-permute-start.3 = (f32[32,256]{1,0:T(8,128)S(1)}, f32[32,256]{1,0:T(8,128)S(1)}, u32[]{:S(2)}, u32[]{:S(2)}) collective-permute-start(f32[32,256]{1,0:T(8,128)S(1)} %get-tuple-element.31), channel_id=1, source_target_pairs={{0,4},{4,8},{8,12},{12,0},{1,5},{5,9},{9,13},{13,1},{2,6},{6,10},{... | collective-permute-start | bytes 98312 | tf_op jit(solution)/shard_map/ppermute | solution.py:459
  6.3 7.5 %collective-permute-start.4 = (f32[32,256]{1,0:T(8,128)S(1)}, f32[32,256]{1,0:T(8,128)S(1)}, u32[]{:S(2)}, u32[]{:S(2)}) collective-permute-start(f32[32,256]{1,0:T(8,128)S(1)} %get-tuple-element.32), channel_id=1, source_target_pairs={{0,8},{4,12},{8,0},{12,4},{1,9},{5,13},{9,1},{13,5},{2,10},{6,14},... | collective-permute-start | bytes 98312 | tf_op jit(solution)/shard_map/ppermute | solution.py:459
  11.4 3.7 %collective-permute-start.5 = (f32[32,256]{1,0:T(8,128)S(1)}, f32[32,256]{1,0:T(8,128)S(1)}, u32[]{:S(2)}, u32[]{:S(2)}) collective-permute-start(f32[32,256]{1,0:T(8,128)S(1)} %get-tuple-element.33), channel_id=1, source_target_pairs={{0,12},{4,0},{8,4},{12,8},{1,13},{5,1},{9,5},{13,9},{2,14},{6,2},{... | collective-permute-start | bytes 98312 | tf_op jit(solution)/shard_map/ppermute | solution.py:459
  15.2 5.4 %collective-permute-start.6 = (f32[1,256,128]{2,1,0:T(8,128)S(1)}, f32[1,256,128]{2,1,0:T(8,128)S(1)}, u32[]{:S(2)}, u32[]{:S(2)}) collective-permute-start(f32[1,256,128]{2,1,0:T(8,128)S(1)} %shard_map.70), channel_id=1, source_target_pairs={{0,16},{16,0},{1,17},{17,1},{2,18},{18,2},{3,19},{19,3},{4,20},{20... | collective-permute-start | bytes 393224 | tf_op jit(solution)/shard_map/ppermute | solution.py:29
  20.6 12.5 %collective-permute-start.7 = (f32[2,256,128]{2,1,0:T(8,128)S(1)}, f32[2,256,128]{2,1,0:T(8,128)S(1)}, u32[]{:S(2)}, u32[]{:S(2)}) collective-permute-start(f32[2,256,128]{2,1,0:T(8,128)S(1)} %pad_maximum_fusion.f0), channel_id=1, source_target_pairs={{0,2},{2,0},{1,3},{3,1},{4,6},{6,4},{5,7},{7,5},{8,10},{10,8},{9,1... | collective-permute-start | bytes 786440 | tf_op jit(solution)/shard_map/ppermute | solution.py:29
  22.1 13.5 %collective-permute-start.1 = (s32[32,1024]{1,0:T(8,128)}, s32[32,1024]{1,0:T(8,128)S(1)}, u32[]{:S(2)}, u32[]{:S(2)}) collective-permute-start(s32[32,1024]{1,0:T(8,128)} %x0.1), channel_id=1, source_target_pairs={{0,8},{4,12},{8,0},{12,4},{1,9},{5,13},{9,1},{13,5},{2,10},{6,14},... | collective-permute-start | bytes 393224 | tf_op jit(solution)/shard_map/ppermute | solution.py:459
  24.7 15.5 %collective-permute-start = (s32[32,1024]{1,0:T(8,128)}, s32[32,1024]{1,0:T(8,128)S(1)}, u32[]{:S(2)}, u32[]{:S(2)}) collective-permute-start(s32[32,1024]{1,0:T(8,128)} %x0.1), channel_id=1, source_target_pairs={{0,4},{4,8},{8,12},{12,0},{1,5},{5,9},{9,13},{13,1},{2,6},{6,10},{... | collective-permute-start | bytes 393224 | tf_op jit(solution)/shard_map/ppermute | solution.py:459
  27.1 13.1 %collective-permute-start.2 = (s32[32,1024]{1,0:T(8,128)}, s32[32,1024]{1,0:T(8,128)S(1)}, u32[]{:S(2)}, u32[]{:S(2)}) collective-permute-start(s32[32,1024]{1,0:T(8,128)} %x0.1), channel_id=1, source_target_pairs={{0,12},{4,0},{8,4},{12,8},{1,13},{5,1},{9,5},{13,9},{2,14},{6,2},{... | collective-permute-start | bytes 393224 | tf_op jit(solution)/shard_map/ppermute | solution.py:459
  28.3 17.9 %collective-permute-start.8 = (f32[2,256,128]{2,1,0:T(8,128)S(1)}, f32[2,256,128]{2,1,0:T(8,128)S(1)}, u32[]{:S(2)}, u32[]{:S(2)}) collective-permute-start(f32[2,256,128]{2,1,0:T(8,128)S(1)} %pad_maximum_fusion.f0), channel_id=1, source_target_pairs={{0,1},{1,0},{2,3},{3,2},{4,5},{5,4},{6,7},{7,6},{8,9},{9,8},{10,11... | collective-permute-start | bytes 786440 | tf_op jit(solution)/shard_map/ppermute | solution.py:29
  33.1 13.1 %collective-permute-start.9 = (f32[2,256,128]{2,1,0:T(8,128)S(1)}, f32[2,256,128]{2,1,0:T(8,128)S(1)}, u32[]{:S(2)}, u32[]{:S(2)}) collective-permute-start(f32[2,256,128]{2,1,0:T(8,128)S(1)} %collective-permute-done.7.f1), channel_id=1, source_target_pairs={{0,1},{1,0},{2,3},{3,2},{4,5},{5,4},{6,7},{7,6},{8,9},{9,8},{10,11... | collective-permute-start | bytes 786440 | tf_op jit(solution)/shard_map/ppermute | solution.py:29
  40.1 0.9 copy-start.4
  41.1 0.7 copy-start.5
  41.7 4.5 %copy-start.3 = (f32[1024]{0:T(1024)S(1)}, f32[1024]{0:T(1024)}, u32[]{:S(2)}) copy-start(f32[1024]{0:T(1024)} %param.9) | copy-start | bytes 12292
  79.8 7.0 %collective-permute-start.10 = (f32[8,128]{1,0:T(8,128)S(1)}, f32[8,128]{1,0:T(8,128)S(1)}, u32[]{:S(2)}, u32[]{:S(2)}) collective-permute-start(f32[8,128]{1,0:T(8,128)S(1)} %get-tuple-element.35.near_ref.refs_9_.norm_ref), channel_id=1, source_target_pairs={{0,1},{1,0},{2,3},{3,2},{4,5},{5,4},{6,7},{7,6},{8,9},{9,8},{10,11... | collective-permute-start | bytes 12296 | tf_op jit(solution)/shard_map/ppermute | solution.py:29
  92.9 2.0 %collective-permute-start.11 = (f32[4,264,128]{2,1,0:T(8,128)S(1)}, f32[4,264,128]{2,1,0:T(8,128)S(1)}, u32[]{:S(2)}, u32[]{:S(2)}) collective-permute-start(f32[4,264,128]{2,1,0:T(8,128)S(1)} %get-tuple-element.37), channel_id=1, source_target_pairs={{0,1},{1,0},{2,3},{3,2},{4,5},{5,4},{6,7},{7,6},{8,9},{9,8},{10,11... | collective-permute-start | bytes 1622024 | tf_op jit(solution)/shard_map/ppermute | solution.py:29
  95.0 6.6 %collective-permute-start.12 = (f32[264,128]{1,0:T(8,128)S(1)}, f32[264,128]{1,0:T(8,128)S(1)}, u32[]{:S(2)}, u32[]{:S(2)}) collective-permute-start(f32[264,128]{1,0:T(8,128)S(1)} %get-tuple-element.39), channel_id=1, source_target_pairs={{0,16},{16,0},{1,17},{17,1},{2,18},{18,2},{3,19},{19,3},{4,20},{20... | collective-permute-start | bytes 405512 | tf_op jit(solution)/shard_map/ppermute | solution.py:29
  96.3 5.3 %collective-permute-start.13 = (f32[264,128]{1,0:T(8,128)S(1)}, f32[264,128]{1,0:T(8,128)S(1)}, u32[]{:S(2)}, u32[]{:S(2)}) collective-permute-start(f32[264,128]{1,0:T(8,128)S(1)} %get-tuple-element.40), channel_id=1, source_target_pairs={{0,2},{2,0},{1,3},{3,1},{4,6},{6,4},{5,7},{7,5},{8,10},{10,8},{9,1... | collective-permute-start | bytes 405512 | tf_op jit(solution)/shard_map/ppermute | solution.py:29
  96.6 8.8 %collective-permute-start.14 = (f32[264,128]{1,0:T(8,128)S(1)}, f32[264,128]{1,0:T(8,128)S(1)}, u32[]{:S(2)}, u32[]{:S(2)}) collective-permute-start(f32[264,128]{1,0:T(8,128)S(1)} %get-tuple-element.41), channel_id=1, source_target_pairs={{0,18},{2,16},{16,2},{18,0},{1,19},{3,17},{17,3},{19,1},{4,22},{6,... | collective-permute-start | bytes 405512 | tf_op jit(solution)/shard_map/ppermute | solution.py:411
  105.4 6.6 %collective-permute-start.17 = (f32[264,128]{1,0:T(8,128)S(1)}, f32[264,128]{1,0:T(8,128)S(1)}, u32[]{:S(2)}, u32[]{:S(2)}) collective-permute-start(f32[264,128]{1,0:T(8,128)S(1)} %get-tuple-element.42.refs_0_), channel_id=1, source_target_pairs={{0,18},{2,16},{16,2},{18,0},{1,19},{3,17},{17,3},{19,1},{4,22},{6,... | collective-permute-start | bytes 405512 | tf_op jit(solution)/shard_map/ppermute | solution.py:411
  106.3 9.2 %collective-permute-start.16 = (f32[264,128]{1,0:T(8,128)S(1)}, f32[264,128]{1,0:T(8,128)S(1)}, u32[]{:S(2)}, u32[]{:S(2)}) collective-permute-start(f32[264,128]{1,0:T(8,128)S(1)} %get-tuple-element.42.refs_0_), channel_id=1, source_target_pairs={{0,2},{2,0},{1,3},{3,1},{4,6},{6,4},{5,7},{7,5},{8,10},{10,8},{9,1... | collective-permute-start | bytes 405512 | tf_op jit(solution)/shard_map/ppermute | solution.py:29
  107.9 7.6 %collective-permute-start.15 = (f32[264,128]{1,0:T(8,128)S(1)}, f32[264,128]{1,0:T(8,128)S(1)}, u32[]{:S(2)}, u32[]{:S(2)}) collective-permute-start(f32[264,128]{1,0:T(8,128)S(1)} %get-tuple-element.42.refs_0_), channel_id=1, source_target_pairs={{0,16},{16,0},{1,17},{17,1},{2,18},{18,2},{3,19},{19,3},{4,20},{20... | collective-permute-start | bytes 405512 | tf_op jit(solution)/shard_map/ppermute | solution.py:29
  109.7 7.2 %collective-permute-start.18 = (f32[264,128]{1,0:T(8,128)S(1)}, f32[264,128]{1,0:T(8,128)S(1)}, u32[]{:S(2)}, u32[]{:S(2)}) collective-permute-start(f32[264,128]{1,0:T(8,128)S(1)} %get-tuple-element.42.refs_0_), channel_id=1, source_target_pairs={{0,1},{1,0},{2,3},{3,2},{4,5},{5,4},{6,7},{7,6},{8,9},{9,8},{10,11... | collective-permute-start | bytes 405512 | tf_op jit(solution)/shard_map/ppermute | solution.py:29
  112.0 4.8 %collective-permute-start.21 = (f32[264,128]{1,0:T(8,128)S(1)}, f32[264,128]{1,0:T(8,128)S(1)}, u32[]{:S(2)}, u32[]{:S(2)}) collective-permute-start(f32[264,128]{1,0:T(8,128)S(1)} %collective-permute-done.17.refs_3_), channel_id=1, source_target_pairs={{0,1},{1,0},{2,3},{3,2},{4,5},{5,4},{6,7},{7,6},{8,9},{9,8},{10,11... | collective-permute-start | bytes 405512 | tf_op jit(solution)/shard_map/ppermute | solution.py:29
  115.5 1.4 collective-permute-start.20
  115.5 2.3 %collective-permute-start.19 = (f32[264,128]{1,0:T(8,128)S(1)}, f32[264,128]{1,0:T(8,128)S(1)}, u32[]{:S(2)}, u32[]{:S(2)}) collective-permute-start(f32[264,128]{1,0:T(8,128)S(1)} %collective-permute-done.15.refs_1_), channel_id=1, source_target_pairs={{0,1},{1,0},{2,3},{3,2},{4,5},{5,4},{6,7},{7,6},{8,9},{9,8},{10,11... | collective-permute-start | bytes 405512 | tf_op jit(solution)/shard_map/ppermute | solution.py:29
  117.8 36.8 %copy-start.2 = (f32[32,1024]{1,0:T(8,128)S(1)}, f32[32,1024]{1,0:T(8,128)}, u32[]{:S(2)}) copy-start(f32[32,1024]{1,0:T(8,128)} %f_ref.3) | copy-start | bytes 393220
  124.4 5.2 %collective-permute-start.22 = (f32[104,128]{1,0:T(8,128)S(1)}, f32[104,128]{1,0:T(8,128)S(1)}, u32[]{:S(2)}, u32[]{:S(2)}) collective-permute-start(f32[104,128]{1,0:T(8,128)S(1)} %get-tuple-element.45), channel_id=1, source_target_pairs={{0,4},{4,8},{8,12},{12,0},{1,5},{5,9},{9,13},{13,1},{2,6},{6,10},{... | collective-permute-start | bytes 159752 | tf_op jit(solution)/shard_map/ppermute | solution.py:459
  124.5 7.1 %collective-permute-start.23 = (f32[104,128]{1,0:T(8,128)S(1)}, f32[104,128]{1,0:T(8,128)S(1)}, u32[]{:S(2)}, u32[]{:S(2)}) collective-permute-start(f32[104,128]{1,0:T(8,128)S(1)} %get-tuple-element.46), channel_id=1, source_target_pairs={{0,8},{4,12},{8,0},{12,4},{1,9},{5,13},{9,1},{13,5},{2,10},{6,14},... | collective-permute-start | bytes 159752 | tf_op jit(solution)/shard_map/ppermute | solution.py:459
  126.8 8.9 %collective-permute-start.24 = (f32[104,128]{1,0:T(8,128)S(1)}, f32[104,128]{1,0:T(8,128)S(1)}, u32[]{:S(2)}, u32[]{:S(2)}) collective-permute-start(f32[104,128]{1,0:T(8,128)S(1)} %get-tuple-element.47), channel_id=1, source_target_pairs={{0,12},{4,0},{8,4},{12,8},{1,13},{5,1},{9,5},{13,9},{2,14},{6,2},{... | collective-permute-start | bytes 159752 | tf_op jit(solution)/shard_map/ppermute | solution.py:459
  144.7 2.7 %collective-permute-start.25 = (f32[8,128]{1,0:T(8,128)S(1)}, f32[8,128]{1,0:T(8,128)S(1)}, u32[]{:S(2)}, u32[]{:S(2)}) collective-permute-start(f32[8,128]{1,0:T(8,128)S(1)} %get-tuple-element.51.st_ref), channel_id=1, source_target_pairs={{0,1},{1,0},{2,3},{3,2},{4,5},{5,4},{6,7},{7,6},{8,9},{9,8},{10,11... | collective-permute-start | bytes 12296 | tf_op jit(solution)/shard_map/ppermute | solution.py:29
  147.4 4.9 %collective-permute-start.28 = (f32[8,128]{1,0:T(8,128)S(1)}, f32[8,128]{1,0:T(8,128)S(1)}, u32[]{:S(2)}, u32[]{:S(2)}) collective-permute-start(f32[8,128]{1,0:T(8,128)S(1)} %shard_map.80.refs_0_), channel_id=1, source_target_pairs={{0,18},{2,16},{16,2},{18,0},{1,19},{3,17},{17,3},{19,1},{4,22},{6,... | collective-permute-start | bytes 12296 | tf_op jit(solution)/shard_map/ppermute | solution.py:411
  148.7 3.6 %collective-permute-start.27 = (f32[8,128]{1,0:T(8,128)S(1)}, f32[8,128]{1,0:T(8,128)S(1)}, u32[]{:S(2)}, u32[]{:S(2)}) collective-permute-start(f32[8,128]{1,0:T(8,128)S(1)} %shard_map.80.refs_0_), channel_id=1, source_target_pairs={{0,2},{2,0},{1,3},{3,1},{4,6},{6,4},{5,7},{7,5},{8,10},{10,8},{9,1... | collective-permute-start | bytes 12296 | tf_op jit(solution)/shard_map/ppermute | solution.py:29
  150.7 4.0 %collective-permute-start.26 = (f32[8,128]{1,0:T(8,128)S(1)}, f32[8,128]{1,0:T(8,128)S(1)}, u32[]{:S(2)}, u32[]{:S(2)}) collective-permute-start(f32[8,128]{1,0:T(8,128)S(1)} %shard_map.80.refs_0_), channel_id=1, source_target_pairs={{0,16},{16,0},{1,17},{17,1},{2,18},{18,2},{3,19},{19,3},{4,20},{20... | collective-permute-start | bytes 12296 | tf_op jit(solution)/shard_map/ppermute | solution.py:29

commit v12 on v11

--- a/solution.py
+++ b/solution.py
@@ -17,8 +17,8 @@
 ROWS = 32
 NB = 8
 TILE = 1024
-LIMIT = 14
-SUB = TILE // 128
+LIMIT = 36
+WIDE = 4096
 EXTRA = 8
 F32, BF16 = jnp.float32, jnp.bfloat16
 VMEM = pl.BlockSpec(memory_space=pltpu.VMEM)
@@ -54,8 +54,8 @@
     )
 
 
-def cols(t):
-    return pl.ds(pl.multiple_of(t * TILE, TILE), TILE)
+def cols(t, width=TILE):
+    return pl.ds(pl.multiple_of(t * width, width), width)
 
 
 def rows_to_column(rows):
@@ -77,7 +77,7 @@
 
 
 def sub(t):
-    return pl.ds(pl.multiple_of(t * SUB, SUB), SUB)
+    return cols(t, WIDE // 128)
 
 
 def hidden_kernel(pos_ref, x0, x1, x2, x3, w_ref, hb_ref, s_ref, h_ref, wt, packed_ref):
@@ -118,12 +118,12 @@
     units = h_ref.shape[0]
 
     def step(t, carry):
-        out = jnp.dot(lhs[...], s_ref[:, cols(t)], preferred_element_type=F32)
+        out = jnp.dot(lhs[...], s_ref[:, cols(t, WIDE)], preferred_element_type=F32)
         proj = out[:units] + out[units:] + bias
-        p_ref[sub(t), :] = to_rows(jnp.sum(h_ref[:, cols(t)] * proj, axis=0, keepdims=True))
+        p_ref[sub(t), :] = to_rows(jnp.sum(h_ref[:, cols(t, WIDE)] * proj, axis=0, keepdims=True))
         return carry
 
-    lax.fori_loop(0, s_ref.shape[1] // TILE, step, 0)
+    lax.fori_loop(0, s_ref.shape[1] // WIDE, step, 0)
 
 
 def set_block(lhs, b, x):
@@ -349,17 +349,17 @@
     lanes[...] = jnp.zeros(lanes.shape, F32)
 
     def step(t, carry):
-        r = h_ref[:, cols(t)] * to_line((v_ref[sub(t), :] - mean) * (1.0 / samples))
+        r = h_ref[:, cols(t, WIDE)] * to_line((v_ref[sub(t), :] - mean) * (1.0 / samples))
         both = jnp.concatenate(split_terms(r), axis=0)
-        out = lax.dot_general(both, s_ref[:, cols(t)], (((1,), (1,)), ((), ())), preferred_element_type=F32)
+        out = lax.dot_general(both, s_ref[:, cols(t, WIDE)], (((1,), (1,)), ((), ())), preferred_element_type=F32)
         acc[...] += out[:units] + out[units:]
         part = r[:, :128]
-        for k in range(1, TILE // 128):
+        for k in range(1, WIDE // 128):
             part = part + r[:, k * 128 : (k + 1) * 128]
         lanes[...] += part
         return carry
 
-    lax.fori_loop(0, s_ref.shape[1] // TILE, step, 0)
+    lax.fori_loop(0, s_ref.shape[1] // WIDE, step, 0)
     bias = [
         jnp.sum(lanes[k * 128 : (k + 1) * 128, :].T, axis=0, keepdims=True) for k in range(units // 128)
     ] + [spread, jnp.zeros((7 - units // 128, 128), F32)]

time: 156 us -> 153 us (0.981)
  Pallas kernels: 26.8 us -> 24 us
where the time goes in v12:
time: 153 us
  starting transfers between devices  61.5 us (40%)
  blocking collectives  34.2 us (22%)
  waiting for transfers between devices  29.1 us (19%)
  Pallas kernels  24 us (16%)
  local copies, waits for them, and re-layouts  2.8 us (2%)
    ppermute x17, starting transfers between devices, swap(): return lax.ppermute(x, axis, SWAP)  35 us
    ppermute x9, starting transfers between devices, body(): lax.ppermute(x, 'zh', [(i, (i + d) % parts) for i in range(parts)])  21.5 us
    all_to_all x1, blocking collectives, first_sum(): got = lax.all_to_all(x, plane, 0, 0, tiled=True)  14.2 us
    ppermute x9, waiting for transfers between devices, body(): lax.ppermute(x, 'zh', [(i, (i + d) % parts) for i in range(parts)])  13.3 us
    all_to_all x1, blocking collectives, to_all(): lax.all_to_all(jnp.broadcast_to(x[None], (size, *x.shape)), axes, 0, 0, t...  11.9 us
    ppermute x17, waiting for transfers between devices, swap(): return lax.ppermute(x, axis, SWAP)  11.4 us
    all_to_all x1, blocking collectives, over_groups(): return (lax.all_to_all(x, GRP, 0, 0, tiled=True), got)  8.11 us
    pallas_call x1, Pallas kernels, image_pass(): call(functools.partial(image_kernel, samples), [SMEM] + [VMEM] * 5, [jax....  5.37 us
  transfers between devices with their start and end apart: 29, of which 14 were waited for; matrix products, arithmetic and copies ran while one was open for 0% of the time, Pallas kernels for 3%

profile of v12, /device:TPU:1, one launch (start us, length us, event | category | flops | bytes accessed | tf_op | source)
XLA Modules:
  0.0 152.5 jit_solution(17723003920735668765)
XLA Ops:
  0.8 1.0 copy-done.1
  2.4 3.9 %collective-permute-start.3 = (f32[32,256]{1,0:T(8,128)S(1)}, f32[32,256]{1,0:T(8,128)S(1)}, u32[]{:S(2)}, u32[]{:S(2)}) collective-permute-start(f32[32,256]{1,0:T(8,128)S(1)} %get-tuple-element.31), channel_id=1, source_target_pairs={{0,4},{4,8},{8,12},{12,0},{1,5},{5,9},{9,13},{13,1},{2,6},{6,10},{... | collective-permute-start | bytes 98312 | tf_op jit(solution)/shard_map/ppermute | solution.py:459
  6.3 5.1 %collective-permute-start.4 = (f32[32,256]{1,0:T(8,128)S(1)}, f32[32,256]{1,0:T(8,128)S(1)}, u32[]{:S(2)}, u32[]{:S(2)}) collective-permute-start(f32[32,256]{1,0:T(8,128)S(1)} %get-tuple-element.32), channel_id=1, source_target_pairs={{0,8},{4,12},{8,0},{12,4},{1,9},{5,13},{9,1},{13,5},{2,10},{6,14},... | collective-permute-start | bytes 98312 | tf_op jit(solution)/shard_map/ppermute | solution.py:459
  11.4 2.4 %collective-permute-start.5 = (f32[32,256]{1,0:T(8,128)S(1)}, f32[32,256]{1,0:T(8,128)S(1)}, u32[]{:S(2)}, u32[]{:S(2)}) collective-permute-start(f32[32,256]{1,0:T(8,128)S(1)} %get-tuple-element.33), channel_id=1, source_target_pairs={{0,12},{4,0},{8,4},{12,8},{1,13},{5,1},{9,5},{13,9},{2,14},{6,2},{... | collective-permute-start | bytes 98312 | tf_op jit(solution)/shard_map/ppermute | solution.py:459
  13.8 1.3 collective-permute-done.5.f3
  15.2 2.8 %collective-permute-start.6 = (f32[1,256,128]{2,1,0:T(8,128)S(1)}, f32[1,256,128]{2,1,0:T(8,128)S(1)}, u32[]{:S(2)}, u32[]{:S(2)}) collective-permute-start(f32[1,256,128]{2,1,0:T(8,128)S(1)} %shard_map.70), channel_id=1, source_target_pairs={{0,16},{16,0},{1,17},{17,1},{2,18},{18,2},{3,19},{19,3},{4,20},{20... | collective-permute-start | bytes 393224 | tf_op jit(solution)/shard_map/ppermute | solution.py:29
  18.0 2.6 %collective-permute-done.6 = f32[1,256,128]{2,1,0:T(8,128)S(1)} collective-permute-done((f32[1,256,128]{2,1,0:T(8,128)S(1)}, f32[1,256,128]{2,1,0:T(8,128)S(1)}, u32[]{:S(2)}, u32[]{:S(2)}) %collective-permute-start.6) | collective-permute-done | bytes 131104 | tf_op jit(solution)/shard_map/ppermute | solution.py:29
  20.6 1.5 collective-permute-start.7
  22.1 2.6 %collective-permute-start.1 = (s32[32,1024]{1,0:T(8,128)}, s32[32,1024]{1,0:T(8,128)S(1)}, u32[]{:S(2)}, u32[]{:S(2)}) collective-permute-start(s32[32,1024]{1,0:T(8,128)} %x0.1), channel_id=1, source_target_pairs={{0,8},{4,12},{8,0},{12,4},{1,9},{5,13},{9,1},{13,5},{2,10},{6,14},... | collective-permute-start | bytes 393224 | tf_op jit(solution)/shard_map/ppermute | solution.py:459
  24.7 2.4 %collective-permute-start = (s32[32,1024]{1,0:T(8,128)}, s32[32,1024]{1,0:T(8,128)S(1)}, u32[]{:S(2)}, u32[]{:S(2)}) collective-permute-start(s32[32,1024]{1,0:T(8,128)} %x0.1), channel_id=1, source_target_pairs={{0,4},{4,8},{8,12},{12,0},{1,5},{5,9},{9,13},{13,1},{2,6},{6,10},{... | collective-permute-start | bytes 393224 | tf_op jit(solution)/shard_map/ppermute | solution.py:459
  27.1 1.2 collective-permute-start.2
  28.3 4.8 %collective-permute-start.8 = (f32[2,256,128]{2,1,0:T(8,128)S(1)}, f32[2,256,128]{2,1,0:T(8,128)S(1)}, u32[]{:S(2)}, u32[]{:S(2)}) collective-permute-start(f32[2,256,128]{2,1,0:T(8,128)S(1)} %pad_maximum_fusion.f0), channel_id=1, source_target_pairs={{0,1},{1,0},{2,3},{3,2},{4,5},{5,4},{6,7},{7,6},{8,9},{9,8},{10,11... | collective-permute-start | bytes 786440 | tf_op jit(solution)/shard_map/ppermute | solution.py:29
  33.1 2.5 %collective-permute-start.9 = (f32[2,256,128]{2,1,0:T(8,128)S(1)}, f32[2,256,128]{2,1,0:T(8,128)S(1)}, u32[]{:S(2)}, u32[]{:S(2)}) collective-permute-start(f32[2,256,128]{2,1,0:T(8,128)S(1)} %collective-permute-done.7.f1), channel_id=1, source_target_pairs={{0,1},{1,0},{2,3},{3,2},{4,5},{5,4},{6,7},{7,6},{8,9},{9,8},{10,11... | collective-permute-start | bytes 786440 | tf_op jit(solution)/shard_map/ppermute | solution.py:29
  35.6 4.5 %collective-permute-done.x1 = s32[32,1024]{1,0:T(8,128)S(1)} collective-permute-done((s32[32,1024]{1,0:T(8,128)}, s32[32,1024]{1,0:T(8,128)S(1)}, u32[]{:S(2)}, u32[]{:S(2)}) %collective-permute-start) | collective-permute-done | bytes 131104 | tf_op jit(solution)/shard_map/ppermute | solution.py:459
  40.2 0.9 copy-done.4
  41.7 4.4 %shard_map.68 = (bf16[1024,4096]{1,0:T(8,128)(2,1)S(1)}, f32[256,4096]{1,0:T(8,128)S(1)}) custom-call(s32[39]{0:T(128)S(1)} %concatenate.6.pos_ref, s32[32,1024]{1,0:T(8,128)S(1)} %copy-done.4, s32[32,1024]{1,0:T(8,128)S(1)} %collective-permute-done.x1, s32[32,1024]{1,0:T(8,128)S(1)} %collective-permute-done.1.x2, s32[32,1024]{1,0:T(8,128)S(1)} %collective-permute-done.2.x3, ...), custom_call_target="tpu_custom_call" | custom-call | flops 4000000000 | bytes 1048576 | tf_op jit(solution)/shard_map/pallas_call | solution.py:108
  46.2 5.3 %shard_map.71 = f32[40,128]{1,0:T(8,128)S(1)} custom-call(s32[39]{0:T(128)S(1)} %concatenate.6.pos_ref, bf16[1024,4096]{1,0:T(8,128)(2,1)S(1)} %get-tuple-element.28.s_ref, f32[256,4096]{1,0:T(8,128)S(1)} %get-tuple-element.29.h_ref, f32[2,256,128]{2,1,0:T(8,128)S(1)} %pad_maximum_fusion.f0, f32[2,256,128]{2,1,0:T(8,128)S(1)} %collective-permute-done.7.f1, ...), custom_call_target="tpu_custom_call" | custom-call | flops 4000000000 | bytes 1048576 | tf_op jit(solution)/shard_map/pallas_call | solution.py:157
  51.5 11.9 %all_to_all.15.got_ref = f32[8,40,128]{2,1,0:T(8,128)S(1)} all-to-all(f32[8,40,128]{2,1,0:T(8,128)S(1)} %broadcast_in_dim.2), channel_id=1, replica_groups=mesh['xl'=2,'y'=4,'xh'=2,'zh'=4,'zl'=2,'c'=2] {'zh','zl'}, dimensions={0} | all-to-all | bytes 327680 | tf_op jit(solution)/shard_map/all_to_all | solution.py:33
  64.0 14.2 %all_to_all.16.got_ref = f32[16,40,128]{2,1,0:T(8,128)S(1)} all-to-all(f32[16,40,128]{2,1,0:T(8,128)S(1)} %shard_map.72), channel_id=1, replica_groups=mesh['xl'=2,'y'=4,'xh'=2,'zh'=4,'zl'=2,'c'=2] {'xh','xl','y'}, dimensions={0} | all-to-all | bytes 655360 | tf_op jit(solution)/shard_map/all_to_all | solution.py:283
  78.8 6.4 %collective-permute-start.10 = (f32[8,128]{1,0:T(8,128)S(1)}, f32[8,128]{1,0:T(8,128)S(1)}, u32[]{:S(2)}, u32[]{:S(2)}) collective-permute-start(f32[8,128]{1,0:T(8,128)S(1)} %get-tuple-element.35.near_ref.refs_9_.norm_ref), channel_id=1, source_target_pairs={{0,1},{1,0},{2,3},{3,2},{4,5},{5,4},{6,7},{7,6},{8,9},{9,8},{10,11... | collective-permute-start | bytes 12296 | tf_op jit(solution)/shard_map/ppermute | solution.py:29
  85.2 0.8 collective-permute-done.10.far_ref
  86.0 5.4 %shard_map.74 = (f32[4,264,128]{2,1,0:T(8,128)S(1)}, f32[4,264,128]{2,1,0:T(8,128)S(1)}) custom-call(s32[39]{0:T(128)S(1)} %concatenate.6.pos_ref, bf16[1024,4096]{1,0:T(8,128)(2,1)S(1)} %get-tuple-element.28.s_ref, f32[256,4096]{1,0:T(8,128)S(1)} %get-tuple-element.29.h_ref, f32[32,128]{1,0:T(8,128)S(1)} %get-tuple-element.34.v_ref, ...), custom_call_target="tpu_custom_call" | custom-call | flops 4000000000 | bytes 1048576 | tf_op jit(solution)/shard_map/pallas_call | solution.py:376
  91.8 1.6 %collective-permute-done.11.got_ref = f32[4,264,128]{2,1,0:T(8,128)S(1)} collective-permute-done((f32[4,264,128]{2,1,0:T(8,128)S(1)}, f32[4,264,128]{2,1,0:T(8,128)S(1)}, u32[]{:S(2)}, u32[]{:S(2)}) %collective-permute-start.11) | collective-permute-done | bytes 540704 | tf_op jit(solution)/shard_map/ppermute | solution.py:29
  93.5 1.1 collective-permute-start.12
  94.9 2.9 %collective-permute-start.14 = (f32[264,128]{1,0:T(8,128)S(1)}, f32[264,128]{1,0:T(8,128)S(1)}, u32[]{:S(2)}, u32[]{:S(2)}) collective-permute-start(f32[264,128]{1,0:T(8,128)S(1)} %get-tuple-element.41), channel_id=1, source_target_pairs={{0,18},{2,16},{16,2},{18,0},{1,19},{3,17},{17,3},{19,1},{4,22},{6,... | collective-permute-start | bytes 405512 | tf_op jit(solution)/shard_map/ppermute | solution.py:411
  97.7 2.1 %collective-permute-done.12.g1 = f32[264,128]{1,0:T(8,128)S(1)} collective-permute-done((f32[264,128]{1,0:T(8,128)S(1)}, f32[264,128]{1,0:T(8,128)S(1)}, u32[]{:S(2)}, u32[]{:S(2)}) %collective-permute-start.12) | collective-permute-done | bytes 135200 | tf_op jit(solution)/shard_map/ppermute | solution.py:29
  99.9 3.8 %collective-permute-done.14.g3 = f32[264,128]{1,0:T(8,128)S(1)} collective-permute-done((f32[264,128]{1,0:T(8,128)S(1)}, f32[264,128]{1,0:T(8,128)S(1)}, u32[]{:S(2)}, u32[]{:S(2)}) %collective-permute-start.14) | collective-permute-done | bytes 135200 | tf_op jit(solution)/shard_map/ppermute | solution.py:411
  103.8 0.9 collective-permute-start.17
  104.6 1.6 %collective-permute-start.16 = (f32[264,128]{1,0:T(8,128)S(1)}, f32[264,128]{1,0:T(8,128)S(1)}, u32[]{:S(2)}, u32[]{:S(2)}) collective-permute-start(f32[264,128]{1,0:T(8,128)S(1)} %get-tuple-element.42.refs_0_), channel_id=1, source_target_pairs={{0,2},{2,0},{1,3},{3,1},{4,6},{6,4},{5,7},{7,5},{8,10},{10,8},{9,1... | collective-permute-start | bytes 405512 | tf_op jit(solution)/shard_map/ppermute | solution.py:29
  106.2 1.8 %collective-permute-start.15 = (f32[264,128]{1,0:T(8,128)S(1)}, f32[264,128]{1,0:T(8,128)S(1)}, u32[]{:S(2)}, u32[]{:S(2)}) collective-permute-start(f32[264,128]{1,0:T(8,128)S(1)} %get-tuple-element.42.refs_0_), channel_id=1, source_target_pairs={{0,16},{16,0},{1,17},{17,1},{2,18},{18,2},{3,19},{19,3},{4,20},{20... | collective-permute-start | bytes 405512 | tf_op jit(solution)/shard_map/ppermute | solution.py:29
  108.0 2.3 %collective-permute-start.18 = (f32[264,128]{1,0:T(8,128)S(1)}, f32[264,128]{1,0:T(8,128)S(1)}, u32[]{:S(2)}, u32[]{:S(2)}) collective-permute-start(f32[264,128]{1,0:T(8,128)S(1)} %get-tuple-element.42.refs_0_), channel_id=1, source_target_pairs={{0,1},{1,0},{2,3},{3,2},{4,5},{5,4},{6,7},{7,6},{8,9},{9,8},{10,11... | collective-permute-start | bytes 405512 | tf_op jit(solution)/shard_map/ppermute | solution.py:29
  110.3 3.5 %collective-permute-start.21 = (f32[264,128]{1,0:T(8,128)S(1)}, f32[264,128]{1,0:T(8,128)S(1)}, u32[]{:S(2)}, u32[]{:S(2)}) collective-permute-start(f32[264,128]{1,0:T(8,128)S(1)} %collective-permute-done.17.refs_3_), channel_id=1, source_target_pairs={{0,1},{1,0},{2,3},{3,2},{4,5},{5,4},{6,7},{7,6},{8,9},{9,8},{10,11... | collective-permute-start | bytes 405512 | tf_op jit(solution)/shard_map/ppermute | solution.py:29
  113.8 1.3 collective-permute-start.19
  115.2 1.0 collective-permute-done.19.refs_5_
  116.2 5.3 %shard_map.77 = (f32[104,128]{1,0:T(8,128)S(1)}, f32[104,128]{1,0:T(8,128)S(1)}, f32[104,128]{1,0:T(8,128)S(1)}, f32[104,128]{1,0:T(8,128)S(1)}) custom-call(s32[39]{0:T(128)S(1)} %concatenate.6.pos_ref, bf16[1024,4096]{1,0:T(8,128)(2,1)S(1)} %get-tuple-element.28.s_ref, f32[256,4096]{1,0:T(8,128)S(1)} %get-tuple-element.29.h_ref, ...), custom_call_target="tpu_custom_call" | custom-call | flops 4000000000 | bytes 1048576 | tf_op jit(solution)/shard_map/pallas_call | solution.py:206
  121.6 2.4 %collective-permute-start.23 = (f32[104,128]{1,0:T(8,128)S(1)}, f32[104,128]{1,0:T(8,128)S(1)}, u32[]{:S(2)}, u32[]{:S(2)}) collective-permute-start(f32[104,128]{1,0:T(8,128)S(1)} %get-tuple-element.46), channel_id=1, source_target_pairs={{0,8},{4,12},{8,0},{12,4},{1,9},{5,13},{9,1},{13,5},{2,10},{6,14},... | collective-permute-start | bytes 159752 | tf_op jit(solution)/shard_map/ppermute | solution.py:459
  123.9 1.5 %collective-permute-start.24 = (f32[104,128]{1,0:T(8,128)S(1)}, f32[104,128]{1,0:T(8,128)S(1)}, u32[]{:S(2)}, u32[]{:S(2)}) collective-permute-start(f32[104,128]{1,0:T(8,128)S(1)} %get-tuple-element.47), channel_id=1, source_target_pairs={{0,12},{4,0},{8,4},{12,8},{1,13},{5,1},{9,5},{13,9},{2,14},{6,2},{... | collective-permute-start | bytes 159752 | tf_op jit(solution)/shard_map/ppermute | solution.py:459
  125.5 1.2 collective-permute-done.22.x1
  126.7 2.0 %collective-permute-done.23.x2 = f32[104,128]{1,0:T(8,128)S(1)} collective-permute-done((f32[104,128]{1,0:T(8,128)S(1)}, f32[104,128]{1,0:T(8,128)S(1)}, u32[]{:S(2)}, u32[]{:S(2)}) %collective-permute-start.23) | collective-permute-done | bytes 53280 | tf_op jit(solution)/shard_map/ppermute | solution.py:459
  128.7 4.2 %collective-permute-done.24.x3 = f32[104,128]{1,0:T(8,128)S(1)} collective-permute-done((f32[104,128]{1,0:T(8,128)S(1)}, f32[104,128]{1,0:T(8,128)S(1)}, u32[]{:S(2)}, u32[]{:S(2)}) %collective-permute-start.24) | collective-permute-done | bytes 53280 | tf_op jit(solution)/shard_map/ppermute | solution.py:459
  133.5 8.1 %all_to_all.17.got_ref = f32[8,40,128]{2,1,0:T(8,128)S(1)} all-to-all(f32[8,40,128]{2,1,0:T(8,128)S(1)} %get-tuple-element.49), channel_id=1, replica_groups=mesh['xl'=2,'y'=4,'xh'=2,'zh'=4,'zl'=2,'c'=2] {'xl','y'}, dimensions={0} | all-to-all | bytes 327680 | tf_op jit(solution)/shard_map/all_to_all | solution.py:240
  141.9 1.8 %collective-permute-start.25 = (f32[8,128]{1,0:T(8,128)S(1)}, f32[8,128]{1,0:T(8,128)S(1)}, u32[]{:S(2)}, u32[]{:S(2)}) collective-permute-start(f32[8,128]{1,0:T(8,128)S(1)} %get-tuple-element.51.st_ref), channel_id=1, source_target_pairs={{0,1},{1,0},{2,3},{3,2},{4,5},{5,4},{6,7},{7,6},{8,9},{9,8},{10,11... | collective-permute-start | bytes 12296 | tf_op jit(solution)/shard_map/ppermute | solution.py:29
  143.7 0.8 collective-permute-done.25.got_ref
  144.5 1.3 collective-permute-start.28
  145.8 2.0 %collective-permute-start.27 = (f32[8,128]{1,0:T(8,128)S(1)}, f32[8,128]{1,0:T(8,128)S(1)}, u32[]{:S(2)}, u32[]{:S(2)}) collective-permute-start(f32[8,128]{1,0:T(8,128)S(1)} %shard_map.80.refs_0_), channel_id=1, source_target_pairs={{0,2},{2,0},{1,3},{3,1},{4,6},{6,4},{5,7},{7,5},{8,10},{10,8},{9,1... | collective-permute-start | bytes 12296 | tf_op jit(solution)/shard_map/ppermute | solution.py:29
  147.8 0.8 collective-permute-start.26
  149.4 2.4 %collective-permute-done.26.refs_1_ = f32[8,128]{1,0:T(8,128)S(1)} collective-permute-done((f32[8,128]{1,0:T(8,128)S(1)}, f32[8,128]{1,0:T(8,128)S(1)}, u32[]{:S(2)}, u32[]{:S(2)}) %collective-permute-start.26) | collective-permute-done | bytes 4128 | tf_op jit(solution)/shard_map/ppermute | solution.py:29
  151.8 0.7 shard_map.81
  (45 shorter events, 5.3 us)
Async XLA Ops:
  0.6 27.6 %copy-start = (bf16[1024,1024]{1,0:T(8,128)(2,1)S(1)}, bf16[1024,1024]{1,0:T(8,128)(2,1)}, u32[]{:S(2)}) copy-start(bf16[1024,1024]{1,0:T(8,128)(2,1)} %param.6) | copy-start | bytes 6291460
  0.8 1.0 copy-start.1
  2.4 11.4 %collective-permute-start.3 = (f32[32,256]{1,0:T(8,128)S(1)}, f32[32,256]{1,0:T(8,128)S(1)}, u32[]{:S(2)}, u32[]{:S(2)}) collective-permute-start(f32[32,256]{1,0:T(8,128)S(1)} %get-tuple-element.31), channel_id=1, source_target_pairs={{0,4},{4,8},{8,12},{12,0},{1,5},{5,9},{9,13},{13,1},{2,6},{6,10},{... | collective-permute-start | bytes 98312 | tf_op jit(solution)/shard_map/ppermute | solution.py:459
  6.3 7.5 %collective-permute-start.4 = (f32[32,256]{1,0:T(8,128)S(1)}, f32[32,256]{1,0:T(8,128)S(1)}, u32[]{:S(2)}, u32[]{:S(2)}) collective-permute-start(f32[32,256]{1,0:T(8,128)S(1)} %get-tuple-element.32), channel_id=1, source_target_pairs={{0,8},{4,12},{8,0},{12,4},{1,9},{5,13},{9,1},{13,5},{2,10},{6,14},... | collective-permute-start | bytes 98312 | tf_op jit(solution)/shard_map/ppermute | solution.py:459
  11.4 3.7 %collective-permute-start.5 = (f32[32,256]{1,0:T(8,128)S(1)}, f32[32,256]{1,0:T(8,128)S(1)}, u32[]{:S(2)}, u32[]{:S(2)}) collective-permute-start(f32[32,256]{1,0:T(8,128)S(1)} %get-tuple-element.33), channel_id=1, source_target_pairs={{0,12},{4,0},{8,4},{12,8},{1,13},{5,1},{9,5},{13,9},{2,14},{6,2},{... | collective-permute-start | bytes 98312 | tf_op jit(solution)/shard_map/ppermute | solution.py:459
  15.2 5.4 %collective-permute-start.6 = (f32[1,256,128]{2,1,0:T(8,128)S(1)}, f32[1,256,128]{2,1,0:T(8,128)S(1)}, u32[]{:S(2)}, u32[]{:S(2)}) collective-permute-start(f32[1,256,128]{2,1,0:T(8,128)S(1)} %shard_map.70), channel_id=1, source_target_pairs={{0,16},{16,0},{1,17},{17,1},{2,18},{18,2},{3,19},{19,3},{4,20},{20... | collective-permute-start | bytes 393224 | tf_op jit(solution)/shard_map/ppermute | solution.py:29
  20.6 12.5 %collective-permute-start.7 = (f32[2,256,128]{2,1,0:T(8,128)S(1)}, f32[2,256,128]{2,1,0:T(8,128)S(1)}, u32[]{:S(2)}, u32[]{:S(2)}) collective-permute-start(f32[2,256,128]{2,1,0:T(8,128)S(1)} %pad_maximum_fusion.f0), channel_id=1, source_target_pairs={{0,2},{2,0},{1,3},{3,1},{4,6},{6,4},{5,7},{7,5},{8,10},{10,8},{9,1... | collective-permute-start | bytes 786440 | tf_op jit(solution)/shard_map/ppermute | solution.py:29
  22.1 13.5 %collective-permute-start.1 = (s32[32,1024]{1,0:T(8,128)}, s32[32,1024]{1,0:T(8,128)S(1)}, u32[]{:S(2)}, u32[]{:S(2)}) collective-permute-start(s32[32,1024]{1,0:T(8,128)} %x0.1), channel_id=1, source_target_pairs={{0,8},{4,12},{8,0},{12,4},{1,9},{5,13},{9,1},{13,5},{2,10},{6,14},... | collective-permute-start | bytes 393224 | tf_op jit(solution)/shard_map/ppermute | solution.py:459
  24.7 15.5 %collective-permute-start = (s32[32,1024]{1,0:T(8,128)}, s32[32,1024]{1,0:T(8,128)S(1)}, u32[]{:S(2)}, u32[]{:S(2)}) collective-permute-start(s32[32,1024]{1,0:T(8,128)} %x0.1), channel_id=1, source_target_pairs={{0,4},{4,8},{8,12},{12,0},{1,5},{5,9},{9,13},{13,1},{2,6},{6,10},{... | collective-permute-start | bytes 393224 | tf_op jit(solution)/shard_map/ppermute | solution.py:459
  27.1 13.1 %collective-permute-start.2 = (s32[32,1024]{1,0:T(8,128)}, s32[32,1024]{1,0:T(8,128)S(1)}, u32[]{:S(2)}, u32[]{:S(2)}) collective-permute-start(s32[32,1024]{1,0:T(8,128)} %x0.1), channel_id=1, source_target_pairs={{0,12},{4,0},{8,4},{12,8},{1,13},{5,1},{9,5},{13,9},{2,14},{6,2},{... | collective-permute-start | bytes 393224 | tf_op jit(solution)/shard_map/ppermute | solution.py:459
  28.3 17.9 %collective-permute-start.8 = (f32[2,256,128]{2,1,0:T(8,128)S(1)}, f32[2,256,128]{2,1,0:T(8,128)S(1)}, u32[]{:S(2)}, u32[]{:S(2)}) collective-permute-start(f32[2,256,128]{2,1,0:T(8,128)S(1)} %pad_maximum_fusion.f0), channel_id=1, source_target_pairs={{0,1},{1,0},{2,3},{3,2},{4,5},{5,4},{6,7},{7,6},{8,9},{9,8},{10,11... | collective-permute-start | bytes 786440 | tf_op jit(solution)/shard_map/ppermute | solution.py:29
  33.1 13.1 %collective-permute-start.9 = (f32[2,256,128]{2,1,0:T(8,128)S(1)}, f32[2,256,128]{2,1,0:T(8,128)S(1)}, u32[]{:S(2)}, u32[]{:S(2)}) collective-permute-start(f32[2,256,128]{2,1,0:T(8,128)S(1)} %collective-permute-done.7.f1), channel_id=1, source_target_pairs={{0,1},{1,0},{2,3},{3,2},{4,5},{5,4},{6,7},{7,6},{8,9},{9,8},{10,11... | collective-permute-start | bytes 786440 | tf_op jit(solution)/shard_map/ppermute | solution.py:29
  40.1 0.9 copy-start.4
  41.1 0.7 copy-start.5
  41.7 4.5 %copy-start.3 = (f32[1024]{0:T(1024)S(1)}, f32[1024]{0:T(1024)}, u32[]{:S(2)}) copy-start(f32[1024]{0:T(1024)} %param.9) | copy-start | bytes 12292
  78.8 7.2 %collective-permute-start.10 = (f32[8,128]{1,0:T(8,128)S(1)}, f32[8,128]{1,0:T(8,128)S(1)}, u32[]{:S(2)}, u32[]{:S(2)}) collective-permute-start(f32[8,128]{1,0:T(8,128)S(1)} %get-tuple-element.35.near_ref.refs_9_.norm_ref), channel_id=1, source_target_pairs={{0,1},{1,0},{2,3},{3,2},{4,5},{5,4},{6,7},{7,6},{8,9},{9,8},{10,11... | collective-permute-start | bytes 12296 | tf_op jit(solution)/shard_map/ppermute | solution.py:29
  91.4 2.0 %collective-permute-start.11 = (f32[4,264,128]{2,1,0:T(8,128)S(1)}, f32[4,264,128]{2,1,0:T(8,128)S(1)}, u32[]{:S(2)}, u32[]{:S(2)}) collective-permute-start(f32[4,264,128]{2,1,0:T(8,128)S(1)} %get-tuple-element.37), channel_id=1, source_target_pairs={{0,1},{1,0},{2,3},{3,2},{4,5},{5,4},{6,7},{7,6},{8,9},{9,8},{10,11... | collective-permute-start | bytes 1622024 | tf_op jit(solution)/shard_map/ppermute | solution.py:29
  93.5 6.4 %collective-permute-start.12 = (f32[264,128]{1,0:T(8,128)S(1)}, f32[264,128]{1,0:T(8,128)S(1)}, u32[]{:S(2)}, u32[]{:S(2)}) collective-permute-start(f32[264,128]{1,0:T(8,128)S(1)} %get-tuple-element.39), channel_id=1, source_target_pairs={{0,16},{16,0},{1,17},{17,1},{2,18},{18,2},{3,19},{19,3},{4,20},{20... | collective-permute-start | bytes 405512 | tf_op jit(solution)/shard_map/ppermute | solution.py:29
  94.6 5.3 %collective-permute-start.13 = (f32[264,128]{1,0:T(8,128)S(1)}, f32[264,128]{1,0:T(8,128)S(1)}, u32[]{:S(2)}, u32[]{:S(2)}) collective-permute-start(f32[264,128]{1,0:T(8,128)S(1)} %get-tuple-element.40), channel_id=1, source_target_pairs={{0,2},{2,0},{1,3},{3,1},{4,6},{6,4},{5,7},{7,5},{8,10},{10,8},{9,1... | collective-permute-start | bytes 405512 | tf_op jit(solution)/shard_map/ppermute | solution.py:29
  94.9 8.8 %collective-permute-start.14 = (f32[264,128]{1,0:T(8,128)S(1)}, f32[264,128]{1,0:T(8,128)S(1)}, u32[]{:S(2)}, u32[]{:S(2)}) collective-permute-start(f32[264,128]{1,0:T(8,128)S(1)} %get-tuple-element.41), channel_id=1, source_target_pairs={{0,18},{2,16},{16,2},{18,0},{1,19},{3,17},{17,3},{19,1},{4,22},{6,... | collective-permute-start | bytes 405512 | tf_op jit(solution)/shard_map/ppermute | solution.py:411
  103.8 6.6 %collective-permute-start.17 = (f32[264,128]{1,0:T(8,128)S(1)}, f32[264,128]{1,0:T(8,128)S(1)}, u32[]{:S(2)}, u32[]{:S(2)}) collective-permute-start(f32[264,128]{1,0:T(8,128)S(1)} %get-tuple-element.42.refs_0_), channel_id=1, source_target_pairs={{0,18},{2,16},{16,2},{18,0},{1,19},{3,17},{17,3},{19,1},{4,22},{6,... | collective-permute-start | bytes 405512 | tf_op jit(solution)/shard_map/ppermute | solution.py:411
  104.6 9.2 %collective-permute-start.16 = (f32[264,128]{1,0:T(8,128)S(1)}, f32[264,128]{1,0:T(8,128)S(1)}, u32[]{:S(2)}, u32[]{:S(2)}) collective-permute-start(f32[264,128]{1,0:T(8,128)S(1)} %get-tuple-element.42.refs_0_), channel_id=1, source_target_pairs={{0,2},{2,0},{1,3},{3,1},{4,6},{6,4},{5,7},{7,5},{8,10},{10,8},{9,1... | collective-permute-start | bytes 405512 | tf_op jit(solution)/shard_map/ppermute | solution.py:29
  106.2 7.6 %collective-permute-start.15 = (f32[264,128]{1,0:T(8,128)S(1)}, f32[264,128]{1,0:T(8,128)S(1)}, u32[]{:S(2)}, u32[]{:S(2)}) collective-permute-start(f32[264,128]{1,0:T(8,128)S(1)} %get-tuple-element.42.refs_0_), channel_id=1, source_target_pairs={{0,16},{16,0},{1,17},{17,1},{2,18},{18,2},{3,19},{19,3},{4,20},{20... | collective-permute-start | bytes 405512 | tf_op jit(solution)/shard_map/ppermute | solution.py:29
  108.0 7.2 %collective-permute-start.18 = (f32[264,128]{1,0:T(8,128)S(1)}, f32[264,128]{1,0:T(8,128)S(1)}, u32[]{:S(2)}, u32[]{:S(2)}) collective-permute-start(f32[264,128]{1,0:T(8,128)S(1)} %get-tuple-element.42.refs_0_), channel_id=1, source_target_pairs={{0,1},{1,0},{2,3},{3,2},{4,5},{5,4},{6,7},{7,6},{8,9},{9,8},{10,11... | collective-permute-start | bytes 405512 | tf_op jit(solution)/shard_map/ppermute | solution.py:29
  110.3 4.8 %collective-permute-start.21 = (f32[264,128]{1,0:T(8,128)S(1)}, f32[264,128]{1,0:T(8,128)S(1)}, u32[]{:S(2)}, u32[]{:S(2)}) collective-permute-start(f32[264,128]{1,0:T(8,128)S(1)} %collective-permute-done.17.refs_3_), channel_id=1, source_target_pairs={{0,1},{1,0},{2,3},{3,2},{4,5},{5,4},{6,7},{7,6},{8,9},{9,8},{10,11... | collective-permute-start | bytes 405512 | tf_op jit(solution)/shard_map/ppermute | solution.py:29
  113.8 1.4 collective-permute-start.20
  113.8 2.3 %collective-permute-start.19 = (f32[264,128]{1,0:T(8,128)S(1)}, f32[264,128]{1,0:T(8,128)S(1)}, u32[]{:S(2)}, u32[]{:S(2)}) collective-permute-start(f32[264,128]{1,0:T(8,128)S(1)} %collective-permute-done.15.refs_1_), channel_id=1, source_target_pairs={{0,1},{1,0},{2,3},{3,2},{4,5},{5,4},{6,7},{7,6},{8,9},{9,8},{10,11... | collective-permute-start | bytes 405512 | tf_op jit(solution)/shard_map/ppermute | solution.py:29
  116.2 35.6 %copy-start.2 = (f32[32,1024]{1,0:T(8,128)S(1)}, f32[32,1024]{1,0:T(8,128)}, u32[]{:S(2)}) copy-start(f32[32,1024]{1,0:T(8,128)} %f_ref.3) | copy-start | bytes 393220
  121.5 5.2 %collective-permute-start.22 = (f32[104,128]{1,0:T(8,128)S(1)}, f32[104,128]{1,0:T(8,128)S(1)}, u32[]{:S(2)}, u32[]{:S(2)}) collective-permute-start(f32[104,128]{1,0:T(8,128)S(1)} %get-tuple-element.45), channel_id=1, source_target_pairs={{0,4},{4,8},{8,12},{12,0},{1,5},{5,9},{9,13},{13,1},{2,6},{6,10},{... | collective-permute-start | bytes 159752 | tf_op jit(solution)/shard_map/ppermute | solution.py:459
  121.6 7.1 %collective-permute-start.23 = (f32[104,128]{1,0:T(8,128)S(1)}, f32[104,128]{1,0:T(8,128)S(1)}, u32[]{:S(2)}, u32[]{:S(2)}) collective-permute-start(f32[104,128]{1,0:T(8,128)S(1)} %get-tuple-element.46), channel_id=1, source_target_pairs={{0,8},{4,12},{8,0},{12,4},{1,9},{5,13},{9,1},{13,5},{2,10},{6,14},... | collective-permute-start | bytes 159752 | tf_op jit(solution)/shard_map/ppermute | solution.py:459
  123.9 9.0 %collective-permute-start.24 = (f32[104,128]{1,0:T(8,128)S(1)}, f32[104,128]{1,0:T(8,128)S(1)}, u32[]{:S(2)}, u32[]{:S(2)}) collective-permute-start(f32[104,128]{1,0:T(8,128)S(1)} %get-tuple-element.47), channel_id=1, source_target_pairs={{0,12},{4,0},{8,4},{12,8},{1,13},{5,1},{9,5},{13,9},{2,14},{6,2},{... | collective-permute-start | bytes 159752 | tf_op jit(solution)/shard_map/ppermute | solution.py:459
  141.9 2.6 %collective-permute-start.25 = (f32[8,128]{1,0:T(8,128)S(1)}, f32[8,128]{1,0:T(8,128)S(1)}, u32[]{:S(2)}, u32[]{:S(2)}) collective-permute-start(f32[8,128]{1,0:T(8,128)S(1)} %get-tuple-element.51.st_ref), channel_id=1, source_target_pairs={{0,1},{1,0},{2,3},{3,2},{4,5},{5,4},{6,7},{7,6},{8,9},{9,8},{10,11... | collective-permute-start | bytes 12296 | tf_op jit(solution)/shard_map/ppermute | solution.py:29
  144.5 4.9 %collective-permute-start.28 = (f32[8,128]{1,0:T(8,128)S(1)}, f32[8,128]{1,0:T(8,128)S(1)}, u32[]{:S(2)}, u32[]{:S(2)}) collective-permute-start(f32[8,128]{1,0:T(8,128)S(1)} %shard_map.80.refs_0_), channel_id=1, source_target_pairs={{0,18},{2,16},{16,2},{18,0},{1,19},{3,17},{17,3},{19,1},{4,22},{6,... | collective-permute-start | bytes 12296 | tf_op jit(solution)/shard_map/ppermute | solution.py:411
  145.8 3.6 %collective-permute-start.27 = (f32[8,128]{1,0:T(8,128)S(1)}, f32[8,128]{1,0:T(8,128)S(1)}, u32[]{:S(2)}, u32[]{:S(2)}) collective-permute-start(f32[8,128]{1,0:T(8,128)S(1)} %shard_map.80.refs_0_), channel_id=1, source_target_pairs={{0,2},{2,0},{1,3},{3,1},{4,6},{6,4},{5,7},{7,5},{8,10},{10,8},{9,1... | collective-permute-start | bytes 12296 | tf_op jit(solution)/shard_map/ppermute | solution.py:29
  147.8 4.0 %collective-permute-start.26 = (f32[8,128]{1,0:T(8,128)S(1)}, f32[8,128]{1,0:T(8,128)S(1)}, u32[]{:S(2)}, u32[]{:S(2)}) collective-permute-start(f32[8,128]{1,0:T(8,128)S(1)} %shard_map.80.refs_0_), channel_id=1, source_target_pairs={{0,16},{16,0},{1,17},{17,1},{2,18},{18,2},{3,19},{19,3},{4,20},{20... | collective-permute-start | bytes 12296 | tf_op jit(solution)/shard_map/ppermute | solution.py:29
